TPU v7x, 32 devices: a whole 2x2x4 slice. The times are simulated.
32 devices in a mesh: fsdp: 32 (over z, y, x, core).
Axes of the slice: x: 2, y: 2, z: 4, core: 2. Of those that a mesh axis runs over, the one named last changes fastest.
Arguments:
- tokens: bfloat16 [2, 12288, 1024], P(None, 'fsdp'), may hold values from -6 to 6
- valid_slots: int32 [2, 12288], P(None, 'fsdp'), may hold values from 0 to 1, as said below
- cotangent: bfloat16 [2, 12288, 1024], P(None, 'fsdp'), may hold values from -6 to 6
- first_gain: bfloat16 [1024], P('fsdp'), may hold values from 0.5 to 1.5
- first_shift: bfloat16 [1024], P('fsdp'), may hold values from -3 to 3
- qkv_weight: bfloat16 [1024, 3072], P('fsdp'), may hold values from -0.1875 to 0.1875
- query_bias: bfloat16 [1024], P('fsdp'), may hold values from -3 to 3
- value_bias: bfloat16 [1024], P('fsdp'), may hold values from -3 to 3
- proj_weight: bfloat16 [1024, 1024], P('fsdp'), may hold values from -3 to 3
- proj_bias: bfloat16 [1024], P('fsdp'), may hold values from -3 to 3
- second_gain: bfloat16 [1024], P('fsdp'), may hold values from 0.5 to 1.5
- second_shift: bfloat16 [1024], P('fsdp'), may hold values from -3 to 3
- up_weight: bfloat16 [1024, 4096], P('fsdp'), may hold values from -0.1875 to 0.1875
- up_bias: bfloat16 [4096], P('fsdp'), may hold values from -3 to 3
- down_weight: bfloat16 [4096, 1024], P('fsdp'), may hold values from -0.09375 to 0.09375
- down_bias: bfloat16 [1024], P('fsdp'), may hold values from -3 to 3
Outputs:
- block_output: bfloat16 [2, 12288, 1024], P(None, 'fsdp')
- tokens_grad: float32 [2, 12288, 1024], P(None, 'fsdp')
- first_gain_grad: float32 [1024], P('fsdp')
- first_shift_grad: float32 [1024], P('fsdp')
- qkv_weight_grad: float32 [1024, 3072], P('fsdp')
- query_bias_grad: float32 [1024], P('fsdp')
- value_bias_grad: float32 [1024], P('fsdp')
- proj_weight_grad: float32 [1024, 1024], P('fsdp')
- proj_bias_grad: float32 [1024], P('fsdp')
- second_gain_grad: float32 [1024], P('fsdp')
- second_shift_grad: float32 [1024], P('fsdp')
- up_weight_grad: float32 [1024, 4096], P('fsdp')
- up_bias_grad: float32 [4096], P('fsdp')
- down_weight_grad: float32 [4096, 1024], P('fsdp')
- down_bias_grad: float32 [1024], P('fsdp')
Inputs may be any that keep to these rules, and one draw needn't show every extreme that they name: `valid_slots`: in each clip of 768 consecutive slots of a micro-batch, the slots with 1 are a prefix of 384 to 768 slots; the first clip of each micro-batch has 1 in all its slots.
All inputs are finite; a program needn't handle non-finite values.
Results may differ from a plain program's by a relative error of at most 0.0098.
Values may be sent and summed in bfloat16 or wider, within the bound.
A program may use at most 256 MiB of HBM per device.

v0:
```python
import jax
import jax.numpy as jnp
from jax import lax
from jax.sharding import PartitionSpec as P

HEAD = 64
CLIP_DEVS = 2


EPSILON = 1e-06
ROOT_HALF = 0.7071067811865476
INV_ROOT_TWO_PI = 0.3989422804014327


def partner(shard, axis, apart):
    return lax.ppermute(shard, axis, [(i, i ^ 1 << apart) for i in range(lax.axis_size(axis))])


def product(left_side, right_side):
    return jnp.dot(left_side, right_side, preferred_element_type=jnp.float32)


def product_left_t(left_side, right_side):
    return lax.dot_general(
        left_side, right_side, (((0,), (0,)), ((), ())), preferred_element_type=jnp.float32
    )


def product_right_t(left_side, right_side):
    return lax.dot_general(
        left_side, right_side, (((1,), (1,)), ((), ())), preferred_element_type=jnp.float32
    )


def normalize(values, norm_gain, norm_shift):
    average = jnp.mean(values, axis=-1, keepdims=True)
    centered = values - average
    variance = jnp.mean(centered * centered, axis=-1, keepdims=True)
    inverse = lax.rsqrt(variance + EPSILON)
    scaled = centered * inverse
    return (scaled * norm_gain + norm_shift, scaled, inverse)


def normalize_back(grad_normed, scaled, inverse, norm_gain):
    grad_scaled = grad_normed * norm_gain
    first_mean = jnp.mean(grad_scaled, axis=-1, keepdims=True)
    second_mean = jnp.mean(grad_scaled * scaled, axis=-1, keepdims=True)
    return inverse * (grad_scaled - first_mean - scaled * second_mean)


def split_heads(tile_block, feature_count):
    row_count = tile_block.shape[0]
    return tile_block.reshape(row_count, feature_count // HEAD, HEAD).transpose(1, 0, 2)


def join_heads(tile_block):
    head_count, row_count, head_width = tile_block.shape
    return tile_block.transpose(1, 0, 2).reshape(row_count, head_count * head_width)


def add_trees(earlier, later):
    if earlier is None:
        return later
    return jax.tree.map(lambda left_side, right_side: left_side + right_side, earlier, later)


def group_gather(tile_block, slot_marks):
    position = lax.axis_index("fsdp")
    other_block, other_marks = partner((tile_block, slot_marks), "fsdp", 0)
    is_upper = position >> 0 & 1 == 1
    tile_block = jnp.where(
        is_upper,
        jnp.concatenate([other_block, tile_block], 0),
        jnp.concatenate([tile_block, other_block], 0),
    )
    slot_marks = jnp.where(
        is_upper,
        jnp.concatenate([other_marks, slot_marks], 0),
        jnp.concatenate([slot_marks, other_marks], 0),
    )
    return (tile_block, slot_marks)


def group_reduce(full_block, group_bits):
    position = lax.axis_index("fsdp")
    for bit_index in reversed(range(group_bits)):
        half_rows = full_block.shape[0] // 2
        lower_half = full_block[:half_rows]
        upper_half = full_block[half_rows:]
        is_upper = position >> bit_index & 1 == 1
        kept_half = jnp.where(is_upper, upper_half, lower_half)
        sent_half = jnp.where(is_upper, lower_half, upper_half)
        full_block = kept_half + partner(sent_half.astype(jnp.bfloat16), "fsdp", bit_index).astype(
            sent_half.dtype
        )
    return full_block


def key_penalty(key_marks):
    return jnp.where(key_marks > 0, 0.0, -1000000000.0).astype(jnp.float32)


def attend(queries, keys_values, key_marks):
    feature_count = queries.shape[1]
    query_heads = split_heads(queries, feature_count)
    key_heads = split_heads(keys_values[:, :feature_count], feature_count)
    value_heads = split_heads(keys_values[:, feature_count:], feature_count)
    penalty = key_penalty(key_marks)
    score_scale = HEAD ** (-0.5)

    def one_head(operands):
        head_queries, head_keys, head_values = operands
        scores = score_scale * product_right_t(head_queries, head_keys) + penalty[None, :]
        row_max = jnp.max(scores, axis=-1, keepdims=True)
        exponent = jnp.exp(scores - row_max)
        row_total = jnp.sum(exponent, axis=-1, keepdims=True)
        probabilities = (exponent / row_total).astype(jnp.bfloat16)
        return (product(probabilities, head_values), (row_max + jnp.log(row_total))[:, 0])

    head_outputs, log_totals = lax.map(one_head, (query_heads, key_heads, value_heads))
    return (join_heads(head_outputs), log_totals)


def attend_back(queries, keys_values, key_marks, log_totals, grad_attended):
    feature_count = queries.shape[1]
    query_heads = split_heads(queries, feature_count)
    key_heads = split_heads(keys_values[:, :feature_count], feature_count)
    value_heads = split_heads(keys_values[:, feature_count:], feature_count)
    grad_heads = split_heads(grad_attended, feature_count)
    penalty = key_penalty(key_marks)
    score_scale = HEAD ** (-0.5)

    def one_head(operands):
        head_queries, head_keys, head_values, head_grads, head_logs = operands
        scores = score_scale * product_right_t(head_queries, head_keys) + penalty[None, :]
        soft_exact = jnp.exp(scores - head_logs[:, None])
        grad_soft = product_right_t(head_grads, head_values)
        correction = jnp.sum(soft_exact * grad_soft, axis=-1, keepdims=True)
        grad_scores = (soft_exact * (grad_soft - correction)).astype(jnp.bfloat16)
        grad_queries = score_scale * product(grad_scores, head_keys)
        grad_keys = score_scale * product_left_t(grad_scores, head_queries)
        grad_values = product_left_t(soft_exact.astype(jnp.bfloat16), head_grads)
        return (grad_queries, grad_keys, grad_values)

    grad_queries, grad_keys, grad_values = lax.map(
        one_head, (query_heads, key_heads, value_heads, grad_heads, log_totals)
    )
    return (
        join_heads(grad_queries),
        jnp.concatenate([join_heads(grad_keys), join_heads(grad_values)], 1),
    )


def forward_micro(weights, token_rows, slot_flags):
    (
        gain_one,
        shift_one,
        weight_qkv,
        bias_query,
        bias_value,
        weight_proj,
        bias_proj,
        gain_two,
        shift_two,
        weight_up,
        bias_up,
        weight_down,
        bias_down,
    ) = weights
    inputs = token_rows.astype(jnp.float32)
    feature_count = inputs.shape[1]
    norm_one, hat_one, inverse_one = normalize(
        inputs, gain_one.astype(jnp.float32), shift_one.astype(jnp.float32)
    )
    norm_one = norm_one.astype(jnp.bfloat16)
    qkv_bias = jnp.concatenate(
        [
            bias_query.astype(jnp.float32),
            jnp.zeros((feature_count,), jnp.float32),
            bias_value.astype(jnp.float32),
        ]
    )
    projected = (product(norm_one, weight_qkv) + qkv_bias).astype(jnp.bfloat16)
    queries = projected[:, :feature_count]
    slot_marks = slot_flags.astype(jnp.bfloat16)
    keys_values, key_marks = group_gather(projected[:, feature_count:], slot_marks)
    attended_full, log_totals = attend(queries, keys_values, key_marks)
    attended = attended_full.astype(jnp.bfloat16)
    middle = inputs + product(attended, weight_proj) + bias_proj.astype(jnp.float32)
    norm_two, hat_two, inverse_two = normalize(
        middle, gain_two.astype(jnp.float32), shift_two.astype(jnp.float32)
    )
    norm_two = norm_two.astype(jnp.bfloat16)
    pre_act = product(norm_two, weight_up) + bias_up.astype(jnp.float32)
    activation = jax.nn.gelu(pre_act, approximate=False).astype(jnp.bfloat16)
    block_rows = (middle + product(activation, weight_down) + bias_down.astype(jnp.float32)).astype(
        jnp.bfloat16
    )
    saved_values = (
        hat_one,
        inverse_one,
        norm_one,
        queries,
        keys_values,
        key_marks,
        log_totals,
        attended,
        hat_two,
        inverse_two,
        norm_two,
        pre_act,
        activation,
        slot_marks,
    )
    return (block_rows, saved_values)


def backward_mlp(weights, saved_values, cotangent_rows):
    (
        gain_one,
        shift_one,
        weight_qkv,
        bias_query,
        bias_value,
        weight_proj,
        bias_proj,
        gain_two,
        shift_two,
        weight_up,
        bias_up,
        weight_down,
        bias_down,
    ) = weights
    (
        hat_one,
        inverse_one,
        norm_one,
        queries,
        keys_values,
        key_marks,
        log_totals,
        attended,
        hat_two,
        inverse_two,
        norm_two,
        pre_act,
        activation,
        slot_marks,
    ) = saved_values
    grad_out = cotangent_rows * slot_marks[:, None]
    grad_out_full = grad_out.astype(jnp.float32)
    grad_down = product_left_t(activation, grad_out)
    grad_bias_down = jnp.sum(grad_out_full, axis=0)
    grad_act = product_right_t(grad_out, weight_down)
    normal_cdf = 0.5 * (1.0 + jax.scipy.special.erf(pre_act * ROOT_HALF))
    density = jnp.exp(-0.5 * pre_act * pre_act) * INV_ROOT_TWO_PI
    grad_pre_full = grad_act * (normal_cdf + pre_act * density)
    grad_bias_up = jnp.sum(grad_pre_full, axis=0)
    grad_pre = grad_pre_full.astype(jnp.bfloat16)
    grad_up = product_left_t(norm_two, grad_pre)
    grad_norm_two = product_right_t(grad_pre, weight_up)
    grad_gain_two = jnp.sum(grad_norm_two * hat_two, axis=0)
    grad_shift_two = jnp.sum(grad_norm_two, axis=0)
    grad_middle = grad_out_full + normalize_back(
        grad_norm_two, hat_two, inverse_two, gain_two.astype(jnp.float32)
    )
    grad_bias_proj = jnp.sum(grad_middle, axis=0)
    mlp_part = (
        grad_bias_proj,
        grad_gain_two,
        grad_shift_two,
        grad_up,
        grad_bias_up,
        grad_down,
        grad_bias_down,
    )
    return (grad_middle, mlp_part)


def backward_attention(weights, saved_values, grad_middle, group_bits):
    (
        gain_one,
        shift_one,
        weight_qkv,
        bias_query,
        bias_value,
        weight_proj,
        bias_proj,
        gain_two,
        shift_two,
        weight_up,
        bias_up,
        weight_down,
        bias_down,
    ) = weights
    (
        hat_one,
        inverse_one,
        norm_one,
        queries,
        keys_values,
        key_marks,
        log_totals,
        attended,
        hat_two,
        inverse_two,
        norm_two,
        pre_act,
        activation,
        slot_marks,
    ) = saved_values
    feature_count = queries.shape[1]
    grad_middle_low = grad_middle.astype(jnp.bfloat16)
    grad_proj = product_left_t(attended, grad_middle_low)
    grad_attended = product_right_t(grad_middle_low, weight_proj).astype(jnp.bfloat16)
    grad_queries, grad_kv_partial = attend_back(
        queries, keys_values, key_marks, log_totals, grad_attended
    )
    grad_kv = group_reduce(grad_kv_partial, group_bits)
    grad_bias_query = jnp.sum(grad_queries, axis=0)
    grad_bias_value = jnp.sum(grad_kv[:, feature_count:], axis=0)
    grad_projected = jnp.concatenate([grad_queries, grad_kv], 1).astype(jnp.bfloat16)
    grad_qkv = product_left_t(norm_one, grad_projected)
    grad_norm_one = product_right_t(grad_projected, weight_qkv)
    grad_gain_one = jnp.sum(grad_norm_one * hat_one, axis=0)
    grad_shift_one = jnp.sum(grad_norm_one, axis=0)
    grad_inputs = grad_middle + normalize_back(
        grad_norm_one, hat_one, inverse_one, gain_one.astype(jnp.float32)
    )
    attention_part = (
        grad_gain_one,
        grad_shift_one,
        grad_qkv,
        grad_bias_query,
        grad_bias_value,
        grad_proj,
    )
    return (grad_inputs, attention_part)


def per_device(
    tokens,
    valid_slots,
    cotangent,
    first_gain,
    first_shift,
    qkv_weight,
    query_bias,
    value_bias,
    proj_weight,
    proj_bias,
    second_gain,
    second_shift,
    up_weight,
    up_bias,
    down_weight,
    down_bias,
):
    group_bits = CLIP_DEVS.bit_length() - 1
    micro_count = tokens.shape[0]
    weights = (
        lax.all_gather(first_gain, "fsdp", axis=0, tiled=True),
        lax.all_gather(first_shift, "fsdp", axis=0, tiled=True),
        lax.all_gather(qkv_weight, "fsdp", axis=0, tiled=True),
        lax.all_gather(query_bias, "fsdp", axis=0, tiled=True),
        lax.all_gather(value_bias, "fsdp", axis=0, tiled=True),
        lax.all_gather(proj_weight, "fsdp", axis=0, tiled=True),
        lax.all_gather(proj_bias, "fsdp", axis=0, tiled=True),
        lax.all_gather(second_gain, "fsdp", axis=0, tiled=True),
        lax.all_gather(second_shift, "fsdp", axis=0, tiled=True),
        lax.all_gather(up_weight, "fsdp", axis=0, tiled=True),
        lax.all_gather(up_bias, "fsdp", axis=0, tiled=True),
        lax.all_gather(down_weight, "fsdp", axis=0, tiled=True),
        lax.all_gather(down_bias, "fsdp", axis=0, tiled=True),
    )
    outputs_list = []
    saved_list = []
    for micro_index in range(micro_count):
        block_rows, saved_values = forward_micro(
            weights, tokens[micro_index], valid_slots[micro_index]
        )
        outputs_list.append(block_rows)
        saved_list.append(saved_values)
    weights = (
        lax.all_gather(first_gain, "fsdp", axis=0, tiled=True),
        lax.all_gather(first_shift, "fsdp", axis=0, tiled=True),
        lax.all_gather(qkv_weight, "fsdp", axis=0, tiled=True),
        lax.all_gather(query_bias, "fsdp", axis=0, tiled=True),
        lax.all_gather(value_bias, "fsdp", axis=0, tiled=True),
        lax.all_gather(proj_weight, "fsdp", axis=0, tiled=True),
        lax.all_gather(proj_bias, "fsdp", axis=0, tiled=True),
        lax.all_gather(second_gain, "fsdp", axis=0, tiled=True),
        lax.all_gather(second_shift, "fsdp", axis=0, tiled=True),
        lax.all_gather(up_weight, "fsdp", axis=0, tiled=True),
        lax.all_gather(up_bias, "fsdp", axis=0, tiled=True),
        lax.all_gather(down_weight, "fsdp", axis=0, tiled=True),
        lax.all_gather(down_bias, "fsdp", axis=0, tiled=True),
    )
    input_grads = []
    mlp_totals = None
    attention_totals = None
    for micro_index in range(micro_count):
        grad_middle, mlp_part = backward_mlp(
            weights, saved_list[micro_index], cotangent[micro_index]
        )
        mlp_totals = add_trees(mlp_totals, mlp_part)
        grad_inputs, attention_part = backward_attention(
            weights, saved_list[micro_index], grad_middle, group_bits
        )
        attention_totals = add_trees(attention_totals, attention_part)
        input_grads.append(grad_inputs)
    reduced = (
        lax.psum_scatter(attention_totals[0], "fsdp", scatter_dimension=0, tiled=True),
        lax.psum_scatter(attention_totals[1], "fsdp", scatter_dimension=0, tiled=True),
        lax.psum_scatter(attention_totals[2], "fsdp", scatter_dimension=0, tiled=True),
        lax.psum_scatter(attention_totals[3], "fsdp", scatter_dimension=0, tiled=True),
        lax.psum_scatter(attention_totals[4], "fsdp", scatter_dimension=0, tiled=True),
        lax.psum_scatter(attention_totals[5], "fsdp", scatter_dimension=0, tiled=True),
        lax.psum_scatter(mlp_totals[0], "fsdp", scatter_dimension=0, tiled=True),
        lax.psum_scatter(mlp_totals[1], "fsdp", scatter_dimension=0, tiled=True),
        lax.psum_scatter(mlp_totals[2], "fsdp", scatter_dimension=0, tiled=True),
        lax.psum_scatter(mlp_totals[3], "fsdp", scatter_dimension=0, tiled=True),
        lax.psum_scatter(mlp_totals[4], "fsdp", scatter_dimension=0, tiled=True),
        lax.psum_scatter(mlp_totals[5], "fsdp", scatter_dimension=0, tiled=True),
        lax.psum_scatter(mlp_totals[6], "fsdp", scatter_dimension=0, tiled=True),
    )
    block_output = jnp.stack(outputs_list, 0)
    tokens_grad = jnp.stack(input_grads, 0)
    return (
        block_output,
        tokens_grad,
        reduced[0],
        reduced[1],
        reduced[2],
        reduced[3],
        reduced[4],
        reduced[5],
        reduced[6],
        reduced[7],
        reduced[8],
        reduced[9],
        reduced[10],
        reduced[11],
        reduced[12],
    )


def solution(mesh):
    return jax.shard_map(
        per_device,
        mesh=mesh,
        in_specs=(
            P(None, "fsdp", None),
            P(None, "fsdp"),
            P(None, "fsdp", None),
            P("fsdp"),
            P("fsdp"),
            P("fsdp", None),
            P("fsdp"),
            P("fsdp"),
            P("fsdp", None),
            P("fsdp"),
            P("fsdp"),
            P("fsdp"),
            P("fsdp", None),
            P("fsdp"),
            P("fsdp", None),
            P("fsdp"),
        ),
        out_specs=(
            P(None, "fsdp", None),
            P(None, "fsdp", None),
            P("fsdp"),
            P("fsdp"),
            P("fsdp", None),
            P("fsdp"),
            P("fsdp"),
            P("fsdp", None),
            P("fsdp"),
            P("fsdp"),
            P("fsdp"),
            P("fsdp", None),
            P("fsdp"),
            P("fsdp", None),
            P("fsdp"),
        ),
        check_vma=False,
    )
```

profile of v0, /device:TPU:0, one launch (start us, length us, event | category | flops | bytes accessed | tf_op | source)
XLA Modules:
  0.0 1258.5 jit_solution(1397706908398293370)
XLA Ops:
  16.2 42.4 %all-reduce.18 = (bf16[1024]{0:T(1024)(128)(2,1)S(1)}, bf16[1024]{0:T(1024)(128)(2,1)S(1)}, bf16[1024]{0:T(1024)(128)(2,1)S(1)}, bf16[1024]{0:T(1024)(128)(2,1)S...) all-reduce(bf16[1024]{0:T(1024)(128)(2,1)S(1)} %dynamic-update-slic, ...), channel_id=1, replica_groups=mesh['fsdp'=32] {'fsdp'}, use_global_device_ids=true, to_apply=%add.3 | all-reduce | flops 8192 | bytes 32768
  58.7 2.0 convert_reduce_fusion.3
  61.3 21.6 %all-gather.6.cloned.1.call-done = bf16[1024,3072]{1,0:T(8,128)(2,1)} async-done(((bf16[32,3072]{1,0:T(8,128)(2,1)}), bf16[1024,3072]{1,0:T(8,128)(2,1)}) %all-gather.6.cloned.1.call-update) | async-done | bytes 6291472 | tf_op jit(solution)/shard_map/all_gather | solution.py:364
  82.9 5.9 add_convert_fusion
  92.5 39.6 %all-gather = bf16[32,1,128]{2,1,0:T(2,128)(2,1)S(1)} all-gather(bf16[1,1,128]{2,1,0:T(2,128)(2,1)S(1)} %bitcast.391), channel_id=1, replica_groups=mesh['fsdp'=32] {'fsdp'}, dimensions={0}, use_global_device_ids=true | all-gather | bytes 8448 | tf_op jit(solution)/shard_map/all_gather | solution.py:372
  132.3 2.1 slice.91
  134.4 5.9 add_convert_fusion.1
  142.7 2.3 copy.67
  145.0 2.4 copy.70
  147.4 2.3 copy.61
  149.7 2.5 copy.64
  152.7 3.8 maximum_select_fusion.1
  156.5 2.0 fusion.189
  158.5 2.6 copy.68
  161.1 4.1 copy.71
  165.2 2.6 copy.69
  167.8 4.2 copy.72
  172.0 52.2 %while.53 = (s32[]{:T(128)}, bf16[16,384,64]{1,2,0:T(8,128)(2,1)S(1)}, f32[16,384]{1,0:T(8,128)S(1)}, bf16[16,384,64]{2,1,0:T(8,128)(2,1)}, bf16[16,768,64]{2,1,...) while((s32[]{:T(128)}, ...), condition=%wide.region_13.14_spmd, body=%wide.region_10.13_spmd.sunk | while | flops 77856384 | bytes 4153449 | solution.py:120
  224.3 3.8 maximum_select_fusion
  228.2 2.0 fusion.188
  230.2 2.6 copy.62
  232.8 4.2 copy.65
  237.0 2.6 copy.63
  239.6 4.2 copy.66
  243.8 52.2 %while.52 = (s32[]{:T(128)}, bf16[16,384,64]{1,2,0:T(8,128)(2,1)S(1)}, f32[16,384]{1,0:T(8,128)S(1)}, bf16[16,384,64]{2,1,0:T(8,128)(2,1)}, bf16[16,768,64]{2,1,...) while((s32[]{:T(128)}, bf16[16,384,64]{1,2,0:T(8,128)(2,1)S(1)}, ...), condition=%wide.region_5.6_spmd, body=%wide.region_2.5_spmd.sunk | while | flops 77856384 | bytes 4153449 | solution.py:120
  296.9 3.1 fusion.192
  303.0 6.3 fusion.180
  309.3 2.6 copy-done.64
  311.9 33.4 %fusion.88 = (bf16[384,4096]{1,0:T(8,128)(2,1)}, bf16[384,4096]{1,0:T(8,128)(2,1)}, f32[384,4096]{1,0:T(8,128)}) fusion(f32[4096]{0:T(1024)S(1)} %bitcast.388, f32[384,4096]{1,0:T(8,128)S(1)} %fusion.180, bf16[1024,4096]{1,0:T(8,128)(2,1)S(1)} %copy-done.63, f32[384,1024]{1,0:T(8,128)S(1)} %copy-done.11, f32[1024]{0:T(1024)S(1)} %convert_element_type.186, ...), kind=kOutput, calls=%fused_computation.119 | convolution fusion | flops 3430809600 | bytes 28863488 | tf_op jit(solution)/shard_map/dot_general | solution.py:20
  345.3 9.6 fusion.194
  354.8 7.0 fusion.155
  362.3 9.2 fusion.193
  371.5 7.8 multiply_reduce_fusion.3
  379.4 2.8 fusion.183
  385.3 2.3 copy.78
  387.6 5.0 fusion.168
  392.6 1.9 convolution_convert_fusion.1
  394.5 2.3 copy.73
  398.2 2.1 broadcast.313.clone.2
  400.2 2.0 broadcast.313.clone.3
  402.2 135.3 %while.54 = (s32[]{:T(128)}, f32[16,384,64]{1,2,0:T(8,128)}, f32[16,768,64]{1,2,0:T(8,128)}, f32[16,768,64]{1,2,0:T(8,128)}, bf16[16,384,64]{2,1,0:T(8,128)(2,1)...) while((s32[]{:T(128)}, f32[16,384,64]{1,2,0:T(8,128)}, ...), condition=%wide.region_20.21_spmd, body=%wide.region_18.20_spmd.sunk | while | flops 191471232 | bytes 10239609 | solution.py:145
  537.5 4.5 select_convert_fusion.1
  542.8 3.3 convolution_add_fusion.3
  547.5 2.0 broadcast.313.clone
  549.5 2.0 broadcast.313.clone.1
  551.6 146.7 %while.55 = (s32[]{:T(128)}, f32[16,384,64]{1,2,0:T(8,128)}, f32[16,768,64]{1,2,0:T(8,128)}, f32[16,768,64]{1,2,0:T(8,128)}, bf16[16,384,64]{2,1,0:T(8,128)(2,1)...) while((s32[]{:T(128)}, f32[16,384,64]{1,2,0:T(8,128)}, ...), condition=%wide.region_27.28_spmd, body=%wide.region_25.27_spmd.sunk | while | flops 191471232 | bytes 10239609 | solution.py:145
  698.3 4.4 select_convert_fusion
  705.4 3.8 fusion.184
  709.3 5.5 fusion.162
  714.8 4.2 fusion.185
  719.0 8.5 convolution_add_fusion.2
  727.6 11.2 fusion.157
  738.8 12.7 %convolution_add_fusion.1 = f32[1024,4096]{1,0:T(8,128)} fusion(f32[1024,4096]{1,0:T(8,128)} %fusion.157, bf16[384,4096]{1,0:T(8,128)(2,1)S(1)} %copy-done.35, f32[384,1024]{1,0:T(8,128)S(1)} %get-tuple-element.423, f32[384]{0:T(512)S(1)} %add_rsqrt_fusion, f32[384]{0:T(512)S(1)} %broadcast_multiply_fusion.8, f32[1024]{0:T(1024)S(1)} %convert_element_type.186, ...), kind=kOutput, calls=%fused_computation.115 | convolution fusion | flops 3227385856 | bytes 38284288 | tf_op jit(solution)/shard_map/dot_general | solution.py:24
  751.9 7.0 fusion.181
  758.9 13.4 %convolution_add_fusion = f32[4096,1024]{1,0:T(8,128)} fusion(f32[4096,1024]{1,0:T(8,128)S(1)} %fusion.181, bf16[384,4096]{1,0:T(8,128)(2,1)} %get-tuple-element.415, bf16[2,384,1024]{2,1,0:T(8,128)(2,1)} %param.26, bf16[384]{0:T(512)(128)(2,1)S(1)} %get-tuple-element.302), kind=kOutput, calls=%fused_computation.114 | convolution fusion | flops 3225812992 | bytes 37487360 | tf_op jit(solution)/shard_map/dot_general | solution.py:24
  777.6 9.1 fusion.165
  786.8 7.0 fusion.164
  796.0 2.7 fusion.161
  798.8 4.6 fusion.150
  803.9 38.1 %all-reduce.17 = (f32[1024]{0:T(1024)S(1)}, f32[1024]{0:T(1024)S(1)}, f32[1024]{0:T(1024)S(1)}, f32[1024]{0:T(1024)S(1)}, f32[1024]{0:T(1024)S(1)}, /*index=5*/f...) all-reduce(f32[1024]{0:T(1024)S(1)} %add.336, ...), channel_id=2, replica_groups=mesh['fsdp'=32] {'fsdp'}, use_global_device_ids=true, to_apply=%region_32.33.clone | all-reduce | flops 12288 | bytes 98304
  847.2 2.9 fusion.149
  852.1 27.2 %reduce-scatter.5.cloned.1.call-done = f32[32,3072]{1,0:T(8,128)} async-done(((f32[1024,3072]{1,0:T(8,128)}), f32[32,3072]{1,0:T(8,128)}) %reduce-scatter.5.cloned.1.call-update) | async-done | bytes 393232 | tf_op jit(solution)/shard_map/reduce_scatter | solution.py:415
  879.2 184.7 %reduce-scatter.9.cloned.1.call-done = f32[32,4096]{1,0:T(8,128)} async-done(((f32[1024,4096]{1,0:T(8,128)}), f32[32,4096]{1,0:T(8,128)}) %reduce-scatter.9.cloned.1.call-update) | async-done | bytes 524304 | tf_op jit(solution)/shard_map/reduce_scatter | solution.py:422
  1063.9 187.5 %reduce-scatter.11.cloned.1.call-done = f32[128,1024]{1,0:T(8,128)} async-done(((f32[4096,1024]{1,0:T(8,128)}), f32[128,1024]{1,0:T(8,128)}) %reduce-scatter.11.cloned.1.call-update) | async-done | bytes 524304 | tf_op jit(solution)/shard_map/reduce_scatter | solution.py:424
  (670 shorter events, 429.6 us)
Async XLA Ops:
  7.2 53.5 %copy-start = (bf16[2,384,1024]{2,1,0:T(8,128)(2,1)S(1)}, bf16[2,384,1024]{2,1,0:T(8,128)(2,1)}, u32[]{:S(2)}) copy-start(bf16[2,384,1024]{2,1,0:T(8,128)(2,1)} %param.24) | copy-start | bytes 4718596
  7.2 75.7 %all-gather.6.cloned.1.call-start = ((), (), s32[]{:S(2)}) async-start(), calls=%async_computation.4 | async-start | bytes 6488064 | tf_op jit(solution)/shard_map/all_gather | solution.py:364
  7.9 288.1 %all-gather.8.cloned.1.call-start = ((), (), s32[]{:S(2)}) async-start(), calls=%async_computation.5 | async-start | bytes 2162688 | tf_op jit(solution)/shard_map/all_gather | solution.py:367
  8.7 294.3 %all-gather.10.cloned.1.call-start = ((), (), s32[]{:S(2)}) async-start(), calls=%async_computation.6 | async-start | bytes 8650752 | tf_op jit(solution)/shard_map/all_gather | solution.py:371
  9.4 335.8 %all-gather.12.cloned.1.call-start = ((), (), s32[]{:S(2)}) async-start(), calls=%async_computation.7 | async-start | bytes 8650752 | tf_op jit(solution)/shard_map/all_gather | solution.py:373
  58.6 75.7 %copy-start.43 = (f32[1024]{0:T(1024)}, f32[1024]{0:T(1024)S(1)}, u32[]{:S(2)}) copy-start(f32[1024]{0:T(1024)S(1)} %convert_element_type.175) | copy-start | bytes 12292
  58.6 75.7 %copy-start.41 = (f32[1024]{0:T(1024)}, f32[1024]{0:T(1024)S(1)}, u32[]{:S(2)}) copy-start(f32[1024]{0:T(1024)S(1)} %convert_element_type.174) | copy-start | bytes 12292
  60.7 28.1 %copy-start.51 = (f32[384]{0:T(512)}, f32[384]{0:T(512)S(1)}, u32[]{:S(2)}) copy-start(f32[384]{0:T(512)S(1)} %get-tuple-element.431) | copy-start | bytes 4612
  60.7 73.7 %copy-start.47 = (f32[384]{0:T(512)}, f32[384]{0:T(512)S(1)}, u32[]{:S(2)}) copy-start(f32[384]{0:T(512)S(1)} %get-tuple-element.432) | copy-start | bytes 4612
  61.3 27.5 %copy-start.54 = (f32[384]{0:T(512)}, f32[384]{0:T(512)S(1)}, u32[]{:S(2)}) copy-start(f32[384]{0:T(512)S(1)} %add_rsqrt_fusion.1) | copy-start | bytes 4612
  91.4 61.2 %collective-permute-start.2 = (bf16[384,2048]{1,0:T(8,128)(2,1)}, bf16[384,2048]{1,0:T(8,128)(2,1)}, u32[]{:S(2)}, u32[]{:S(2)}) collective-permute-start(bf16[384,2048]{1,0:T(8,128)(2,1)} %slice.92), channel_id=1, source_target_pairs={{0,1},{1,0},{2,3},{3,2},{4,5},{5,4},{6,7},{7,6},{8,9},{9,8},{10,11... | collective-permute-start | bytes 4718600 | tf_op jit(solution)/shard_map/ppermute | solution.py:16
  91.7 48.6 %copy-start.56 = (bf16[384]{0:T(512)(128)(2,1)}, bf16[384]{0:T(512)(128)(2,1)S(1)}, u32[]{:S(2)}) copy-start(bf16[384]{0:T(512)(128)(2,1)S(1)} %get-tuple-element.301) | copy-start | bytes 2308
  91.7 40.5 %collective-permute-start.3 = (bf16[384]{0:T(512)(128)(2,1)S(1)}, bf16[384]{0:T(512)(128)(2,1)S(1)}, u32[]{:S(2)}, u32[]{:S(2)}) collective-permute-start(bf16[384]{0:T(512)(128)(2,1)S(1)} %get-tuple-element.302), channel_id=1, source_target_pairs={{0,1},{1,0},{2,3},{3,2},{4,5},{5,4},{6,7},{7,6},{8,9},{9,8},{10,11... | collective-permute-start | bytes 2312 | tf_op jit(solution)/shard_map/ppermute | solution.py:16
  92.0 40.2 %collective-permute-start.1 = (bf16[384]{0:T(512)(128)(2,1)S(1)}, bf16[384]{0:T(512)(128)(2,1)S(1)}, u32[]{:S(2)}, u32[]{:S(2)}) collective-permute-start(bf16[384]{0:T(512)(128)(2,1)S(1)} %get-tuple-element.301), channel_id=1, source_target_pairs={{0,1},{1,0},{2,3},{3,2},{4,5},{5,4},{6,7},{7,6},{8,9},{9,8},{10,11... | collective-permute-start | bytes 2312 | tf_op jit(solution)/shard_map/ppermute | solution.py:16
  92.3 759.8 %reduce-scatter.7.cloned.1.call-start = ((), (), s32[]{:S(2)}) async-start(), calls=%async_computation.9 | async-start | bytes 4325376 | tf_op jit(solution)/shard_map/reduce_scatter | solution.py:418
  132.2 8.1 copy-start.49
  152.2 72.0 %collective-permute-start = (bf16[384,2048]{1,0:T(8,128)(2,1)}, bf16[384,2048]{1,0:T(8,128)(2,1)}, u32[]{:S(2)}, u32[]{:S(2)}) collective-permute-start(bf16[384,2048]{1,0:T(8,128)(2,1)} %slice.87), channel_id=1, source_target_pairs={{0,1},{1,0},{2,3},{3,2},{4,5},{5,4},{6,7},{7,6},{8,9},{9,8},{10,11... | collective-permute-start | bytes 4718600 | tf_op jit(solution)/shard_map/ppermute | solution.py:16
  224.2 3.9 copy-start.21
  224.2 3.9 copy-start.45
  224.3 3.9 copy-start.53
  296.9 3.4 copy-start.24
  296.9 3.4 copy-start.25
  300.0 438.8 %copy-start.4 = (f32[384,1024]{1,0:T(8,128)}, f32[384,1024]{1,0:T(8,128)S(1)}, u32[]{:S(2)}) copy-start(f32[384,1024]{1,0:T(8,128)S(1)} %get-tuple-element.423) | copy-start | bytes 4718596
  302.9 9.0 copy-start.11
  302.9 8.9 copy-start.63
  354.8 7.1 copy-start.34
  354.8 7.1 copy-start.13
  354.8 7.1 copy-start.57
  354.8 7.5 copy-start.62
  371.5 7.8 copy-start.36
  379.4 4.0 copy-start.26
  387.6 5.0 copy-start.15
  387.6 5.0 copy-start.27
  537.5 4.5 copy-start.3
  537.5 5.1 copy-start.18
  537.5 5.3 copy-start.22
  542.0 163.5 %collective-permute-start.4 = (bf16[384,2048]{0,1:T(8,128)(2,1)}, bf16[384,2048]{0,1:T(8,128)(2,1)}, u32[]{:S(2)}, u32[]{:S(2)}) collective-permute-start(bf16[384,2048]{0,1:T(8,128)(2,1)} %select_convert_fusion.1), channel_id=1, source_target_pairs={{0,1},{1,0},{2,3},{3,2},{4,5},{5,4},{6,7},{7,6},{8,9},{9,8},{10,11... | collective-permute-start | bytes 4718600 | tf_op jit(solution)/shard_map/ppermute | solution.py:16
  546.2 333.1 %reduce-scatter.5.cloned.1.call-start = ((), (), s32[]{:S(2)}) async-start(), calls=%async_computation.8 | async-start | bytes 12976128 | tf_op jit(solution)/shard_map/reduce_scatter | solution.py:415
  698.3 4.5 copy-start.19
  698.3 7.2 copy-start.9
  702.7 12.1 collective-permute-start.5
  705.4 3.8 copy-start.1
  705.4 3.8 copy-start.42
  705.4 3.8 copy-start.44
  705.4 3.8 copy-start.48
  705.4 3.8 copy-start.50
  709.2 5.5 copy-start.31
  709.3 5.5 copy-start.6
  709.3 5.5 copy-start.7
  714.8 4.3 copy-start.52
  714.8 4.2 copy-start.55
  727.6 336.4 %reduce-scatter.9.cloned.1.call-start = ((), (), s32[]{:S(2)}) async-start(), calls=%async_computation.10 | async-start | bytes 17301504 | tf_op jit(solution)/shard_map/reduce_scatter | solution.py:422
  727.6 11.2 copy-start.35
  751.5 499.9 %reduce-scatter.11.cloned.1.call-start = ((), (), s32[]{:S(2)}) async-start(), calls=%async_computation.11 | async-start | bytes 17301504 | tf_op jit(solution)/shard_map/reduce_scatter | solution.py:424
  773.7 3.8 copy-start.58
  773.7 3.9 copy-start.5
  777.6 9.2 copy-start.12
  777.6 9.2 copy-start.33
  777.6 17.5 %slice-start = ((s8[6291456]{0:T(1024)(128)(4,1)}), s8[4194304]{0:T(1024)(128)(4,1)S(1)}, s32[]{:S(2)}) async-start(s8[6291456]{0:T(1024)(128)(4,1)} %bitcast.392), calls=%async_computation.12 | async-start | bytes 8388608
  786.8 8.3 slice-start.1
  798.7 4.7 copy-start.40
  798.8 4.7 copy-start.28
  798.8 4.9 copy-start.29
  803.4 43.8 %copy-start.16 = (f32[384,1024]{1,0:T(8,128)S(1)}, f32[384,1024]{1,0:T(8,128)}, u32[]{:S(2)}) copy-start(f32[384,1024]{1,0:T(8,128)} %get-tuple-element.391) | copy-start | bytes 4718596
  (17 other events, 32.0 us)
Sparse Core Ops, SparseCore 0:
  10.9 71.9 all-gather.5
  85.7 54.7 all-gather.7
  143.4 75.8 all-gather.9
  222.0 75.6 all-gather.11
  546.3 138.5 reduce-scatter.6
  727.7 151.5 reduce-scatter.4
  882.1 181.7 reduce-scatter.8
  1066.8 184.5 reduce-scatter.10
where the time goes:
time: 1270 us; the launch traced here: 1260 us
  matrix products  537 us (42%)
  waiting for transfers between devices  423 us (33%)
  blocking collectives  120 us (9%)
  local copies, waits for them, and re-layouts  99.2 us (8%)
  other arithmetic  60 us (5%)
  between operations  15.4 us (1%)
    reduce_scatter x1, waiting for transfers between devices, per_device(): lax.psum_scatter(mlp_totals[5], 'fsdp', scatter_dimension=0, tiled=True)  188 us
    reduce_scatter x1, waiting for transfers between devices, per_device(): lax.psum_scatter(mlp_totals[3], 'fsdp', scatter_dimension=0, tiled=True)  185 us
    dot_general x104, matrix products, product_right_t(): lax.dot_general(left_side, right_side, (((1,), (1,)), ((), ())), preferre...  179 us
    dot_general x72, matrix products, product_left_t(): lax.dot_general(left_side, right_side, (((0,), (0,)), ((), ())), preferre...  179 us
    dot_general x72, matrix products, product(): return jnp.dot(left_side, right_side, preferred_element_type=jnp.float32)  178 us
    unnamed x2, blocking collectives  80.5 us
    all_gather x1, blocking collectives, per_device(): lax.all_gather(up_bias, 'fsdp', axis=0, tiled=True)  39.6 us
    reduce_scatter x1, waiting for transfers between devices, per_device(): lax.psum_scatter(attention_totals[2], 'fsdp', scatter_dimension=0, tiled=...  27.2 us
  transfers between devices with their start and end apart: 14, of which 4 were waited for; matrix products, arithmetic and copies ran while one was open for 39% of the time, Pallas kernels for 0%

commit v1 on v0

v1 whole, which is shorter than its diff:
```python
import functools

import jax
import jax.numpy as jnp
from jax import lax
from jax.experimental import pallas as pl
from jax.experimental.pallas import tpu as pltpu
from jax.sharding import PartitionSpec as P

AX = "fsdp"
MESH = pl.DeviceIdType.MESH
HEAD = 64
EPSILON = 1e-06
ROOT_HALF = 0.7071067811865476
INV_ROOT_TWO_PI = 0.3989422804014327
BF = jnp.bfloat16
F32 = jnp.float32
PARAM_COLS = 128


def product(left_side, right_side):
    return jnp.dot(left_side, right_side, preferred_element_type=F32)


def product_left_t(left_side, right_side):
    return lax.dot_general(left_side, right_side, (((0,), (0,)), ((), ())), preferred_element_type=F32)


def product_right_t(left_side, right_side):
    return lax.dot_general(left_side, right_side, (((1,), (1,)), ((), ())), preferred_element_type=F32)


def swap(shard):
    return lax.ppermute(shard, AX, [(i, i ^ 1) for i in range(lax.axis_size(AX))])


def same_core_groups():
    count = lax.axis_size(AX)
    return [[i for i in range(count) if i % 2 == core] for core in (0, 1)]


def flip(index, step):
    return index + step - 2 * step * ((index // step) % 2)


def peers_of(me):
    return flip(me, 1), flip(me, 2), flip(me, 4), [flip(me, 8), flip(me, 16), flip(flip(me, 8), 16)]


def zflip(chip, j):
    return [chip, flip(chip, 4), flip(chip, 8), flip(flip(chip, 4), 8)][j]


def meet(peers):
    barrier = pltpu.get_barrier_semaphore()
    for peer in peers:
        pl.semaphore_signal(barrier, inc=1, device_id=(peer,), device_id_type=MESH)
    pl.semaphore_wait(barrier, len(peers))


def gather_kernel(count, *refs):
    ins, outs = refs[:count], refs[count : 2 * count]
    local_sem, send_sem, recv_sem = refs[2 * count :]
    me = lax.axis_index(AX)
    chip, core = me // 2, me % 2
    mate, peer_x, peer_y, peers_z = peers_of(me)
    meet([mate, peer_x, peer_y] + peers_z)
    chip_x, chip_y = flip(chip, 1), flip(chip, 2)
    chip_xy = flip(chip_x, 2)
    pending = []

    def send(w, slot, block, target, peer):
        copy = pltpu.make_async_remote_copy(
            src_ref=block, dst_ref=target, send_sem=send_sem.at[w, slot], recv_sem=recv_sem.at[w, slot],
            device_id=(peer,), device_id_type=MESH,
        )
        copy.start()
        pending.append(copy)

    def arrive(w, slot, block):
        pltpu.make_async_remote_copy(
            src_ref=block, dst_ref=block, send_sem=send_sem.at[w, slot], recv_sem=recv_sem.at[w, slot],
            device_id=(mate,), device_id_type=MESH,
        ).wait_recv()

    local = []
    for w in range(count):
        copy = pltpu.make_async_copy(ins[w].at[core], outs[w].at[chip, core], local_sem.at[w])
        copy.start()
        local.append(copy)
        send(w, 0, ins[w].at[1 - core], outs[w].at[chip, core], mate)
    for w in range(count):
        local[w].wait()
        arrive(w, 0, outs[w].at[chip, 1 - core])
        block = outs[w].at[chip]
        for j in range(3):
            send(w, 1 + j, block, block, peers_z[j])
        send(w, 4, block, block, peer_x)
        send(w, 8, block, block, peer_y)
    for w in range(count):
        for j in (1, 2, 3):
            block = outs[w].at[zflip(chip, j)]
            arrive(w, j, block)
            send(w, 4 + j, block, block, peer_x)
            send(w, 8 + j, block, block, peer_y)
        for j in range(4):
            block = outs[w].at[zflip(chip_x, j)]
            arrive(w, 4 + j, block)
            send(w, 12 + j, block.at[0], block.at[0], peer_y)
            block = outs[w].at[zflip(chip_y, j)]
            arrive(w, 8 + j, block)
            send(w, 16 + j, block.at[1], block.at[1], peer_x)
    for w in range(count):
        for j in range(4):
            block = outs[w].at[zflip(chip_xy, j)]
            arrive(w, 12 + j, block.at[0])
            arrive(w, 16 + j, block.at[1])
    for copy in pending:
        copy.wait_send()


def gather_chips(shards):
    devices = lax.axis_size(AX)
    if devices != 32:
        core = lax.axis_index(AX) % 2
        gathered = []
        for shard in shards:
            own = lax.dynamic_index_in_dim(shard, core, 0, keepdims=False)
            other = swap(lax.dynamic_index_in_dim(shard, 1 - core, 0, keepdims=False))
            block = jnp.where(core == 0, jnp.stack([own, other]), jnp.stack([other, own]))
            gathered.append(lax.all_gather(block, AX, axis=0, axis_index_groups=same_core_groups()))
        return gathered
    count = len(shards)
    return pl.pallas_call(
        functools.partial(gather_kernel, count),
        out_shape=[jax.ShapeDtypeStruct((devices // 2,) + s.shape, s.dtype) for s in shards],
        in_specs=[pl.BlockSpec(memory_space=pltpu.VMEM)] * count,
        out_specs=[pl.BlockSpec(memory_space=pl.ANY)] * count,
        scratch_shapes=[
            pltpu.SemaphoreType.DMA((count,)),
            pltpu.SemaphoreType.DMA((count, 20)),
            pltpu.SemaphoreType.DMA((count, 20)),
        ],
        compiler_params=pltpu.CompilerParams(collective_id=0, has_side_effects=True),
        name="gather_chips",
    )(*shards)


def scatter_kernel(count, *refs):
    ins, outs = refs[:count], refs[count : 2 * count]
    scratch = refs[2 * count :]
    recv_a, recv_b = scratch[:count], scratch[count : 2 * count]
    recv_x, recv_y = scratch[2 * count : 3 * count], scratch[3 * count : 4 * count]
    recv_z, stage = scratch[4 * count : 5 * count], scratch[5 * count : 6 * count]
    send_sem, recv_sem = scratch[6 * count :]
    me = lax.axis_index(AX)
    chip, core = me // 2, me % 2
    mate, peer_x, peer_y, peers_z = peers_of(me)
    meet([mate, peer_x, peer_y] + peers_z)
    chip_x, chip_y = flip(chip, 1), flip(chip, 2)
    chip_xy = flip(chip_x, 2)
    pending = []

    def send(w, slot, block, target, peer):
        copy = pltpu.make_async_remote_copy(
            src_ref=block, dst_ref=target, send_sem=send_sem.at[w, slot], recv_sem=recv_sem.at[w, slot],
            device_id=(peer,), device_id_type=MESH,
        )
        copy.start()
        pending.append(copy)

    def arrive(w, slot, block):
        pltpu.make_async_remote_copy(
            src_ref=block, dst_ref=block, send_sem=send_sem.at[w, slot], recv_sem=recv_sem.at[w, slot],
            device_id=(mate,), device_id_type=MESH,
        ).wait_recv()

    order = (1, 2, 3, 0)

    def first(w):
        for j in order:
            block = ins[w].at[zflip(chip_xy, j)]
            send(w, j, block.at[0], recv_a[w].at[j], peer_y)
            send(w, 4 + j, block.at[1], recv_b[w].at[j], peer_x)
        for j in order:
            send(w, 8 + j, ins[w].at[zflip(chip_x, j), 1], recv_x[w].at[j, 1], peer_x)
            send(w, 12 + j, ins[w].at[zflip(chip_y, j), 0], recv_y[w].at[j, 0], peer_y)

    def second(w):
        rows = ins[w].shape[2]
        for j in order:
            arrive(w, j, recv_a[w].at[j])

            @pl.loop(0, rows // 16)
            def _(i):
                part = pl.ds(pl.multiple_of(i * 16, 16), 16)
                total = recv_a[w][j, part].astype(F32) + ins[w][zflip(chip_x, j), 0, part].astype(F32)
                recv_a[w][j, part] = total.astype(BF)

            send(w, 16 + j, recv_a[w].at[j], recv_x[w].at[j, 0], peer_x)
            arrive(w, 4 + j, recv_b[w].at[j])

            @pl.loop(0, rows // 16)
            def _(i):
                part = pl.ds(pl.multiple_of(i * 16, 16), 16)
                total = recv_b[w][j, part].astype(F32) + ins[w][zflip(chip_y, j), 1, part].astype(F32)
                recv_b[w][j, part] = total.astype(BF)

            send(w, 20 + j, recv_b[w].at[j], recv_y[w].at[j, 1], peer_y)

    def third(w):
        rows = ins[w].shape[2]
        for j in (1, 2, 3):
            arrive(w, 8 + j, recv_x[w].at[j, 1])
            arrive(w, 12 + j, recv_y[w].at[j, 0])
            arrive(w, 16 + j, recv_x[w].at[j, 0])
            arrive(w, 20 + j, recv_y[w].at[j, 1])

            @pl.loop(0, 2 * (rows // 16))
            def _(i):
                half = i // (rows // 16)
                part = pl.ds(pl.multiple_of((i % (rows // 16)) * 16, 16), 16)
                total = recv_x[w][j, half, part].astype(F32) + recv_y[w][j, half, part].astype(F32)
                total = total + ins[w][zflip(chip, j), half, part].astype(F32)
                recv_x[w][j, half, part] = total.astype(BF)

            send(w, 23 + j, recv_x[w].at[j], recv_z[w].at[j - 1], peers_z[j - 1])

    def last(w):
        rows = ins[w].shape[2]
        for slot, block in ((8, recv_x[w].at[0, 1]), (12, recv_y[w].at[0, 0]), (16, recv_x[w].at[0, 0]), (20, recv_y[w].at[0, 1])):
            arrive(w, slot, block)
        for j in range(3):
            arrive(w, 24 + j, recv_z[w].at[j])

        def total_of(half, part):
            total = recv_x[w][0, half, part].astype(F32) + recv_y[w][0, half, part].astype(F32)
            total = total + ins[w][chip, half, part].astype(F32)
            for j in range(3):
                total = total + recv_z[w][j, half, part].astype(F32)
            return total

        @pl.loop(0, rows // 16)
        def _(i):
            part = pl.ds(pl.multiple_of(i * 16, 16), 16)
            stage[w][part] = total_of(1 - core, part)

        send(w, 27, stage[w], outs[w].at[core], mate)

        @pl.loop(0, rows // 16)
        def _(i):
            part = pl.ds(pl.multiple_of(i * 16, 16), 16)
            outs[w][core, part] = total_of(core, part)

    for w in range(count):
        first(w)
        if w >= 1:
            second(w - 1)
        if w >= 2:
            third(w - 2)
    second(count - 1)
    for w in range(max(count - 2, 0), count):
        third(w)
    for w in range(count):
        last(w)
    for w in range(count):
        arrive(w, 27, outs[w].at[1 - core])
    for copy in pending:
        copy.wait_send()


def scatter_chips(grads):
    devices = lax.axis_size(AX)
    if devices != 32:
        core = lax.axis_index(AX) % 2
        summed = []
        for grad in grads:
            block = lax.psum_scatter(grad, AX, scatter_dimension=0, axis_index_groups=same_core_groups())
            block = block.astype(F32)
            own = lax.dynamic_index_in_dim(block, core, 0, keepdims=False)
            other = swap(lax.dynamic_index_in_dim(block, 1 - core, 0, keepdims=False))
            summed.append(jnp.where(core == 0, jnp.stack([own, other]), jnp.stack([other, own])))
        return summed
    count = len(grads)
    shapes = [g.shape for g in grads]
    scratch = [pltpu.VMEM((4,) + s[2:], BF) for s in shapes] * 2
    scratch += [pltpu.VMEM((4, 2) + s[2:], BF) for s in shapes] * 2
    scratch += [pltpu.VMEM((3, 2) + s[2:], BF) for s in shapes]
    scratch += [pltpu.VMEM(s[2:], F32) for s in shapes]
    scratch += [pltpu.SemaphoreType.DMA((count, 28)), pltpu.SemaphoreType.DMA((count, 28))]
    return pl.pallas_call(
        functools.partial(scatter_kernel, count),
        out_shape=[jax.ShapeDtypeStruct((2,) + s[2:], F32) for s in shapes],
        in_specs=[pl.BlockSpec(memory_space=pltpu.VMEM)] * count,
        out_specs=[pl.BlockSpec(memory_space=pltpu.VMEM)] * count,
        scratch_shapes=scratch,
        compiler_params=pltpu.CompilerParams(
            collective_id=1, has_side_effects=True, vmem_limit_bytes=56 << 20
        ),
        name="scatter_chips",
    )(*grads)


def head_masks():
    lane = lax.broadcasted_iota(jnp.int32, (1, 2 * HEAD), 1)
    return [(lane < HEAD).astype(BF), (lane >= HEAD).astype(BF)]


def attend_kernel(chunk, q_ref, k_ref, v_ref, penalty_ref, out_ref, log_ref):
    slots = q_ref.shape[1]
    keys, values = k_ref[0], v_ref[0]
    values_t = values.T
    penalty = penalty_ref[0]
    masks = head_masks()
    for start in range(0, slots, chunk):
        queries = q_ref[0, start : start + chunk] * jnp.asarray(0.125, BF)
        parts = []
        for h in range(2):
            scores = product_right_t(keys, queries * masks[h]) + penalty
            top = jnp.max(scores, axis=0, keepdims=True)
            exponent = jnp.exp(scores - top)
            total = jnp.sum(exponent, axis=0, keepdims=True)
            mixed = product(values_t[h * HEAD : (h + 1) * HEAD], exponent.astype(BF))
            parts.append(mixed * (1.0 / total))
            log_ref[0, 0, h : h + 1, start : start + chunk] = top + jnp.log(total)
        out_ref[0, start : start + chunk] = jnp.concatenate(parts, 0).T.astype(BF)


def attend(projected, penalty):
    clips, slots, triple = projected.shape
    width = triple // 3
    pairs = width // (2 * HEAD)

    def block(offset):
        return pl.BlockSpec((1, slots, 2 * HEAD), lambda i, j: (i, 0, offset * pairs + j))

    return pl.pallas_call(
        functools.partial(attend_kernel, 256),
        grid=(clips, pairs),
        in_specs=[block(0), block(1), block(2), pl.BlockSpec((1, slots, 1), lambda i, j: (i, 0, 0))],
        out_specs=[block(0), pl.BlockSpec((1, 1, 2, slots), lambda i, j: (i, j, 0, 0))],
        out_shape=[
            jax.ShapeDtypeStruct((clips, slots, width), BF),
            jax.ShapeDtypeStruct((clips, pairs, 2, slots), F32),
        ],
        compiler_params=pltpu.CompilerParams(vmem_limit_bytes=48 << 20),
        cost_estimate=pl.CostEstimate(
            flops=4 * clips * pairs * slots * slots * 2 * HEAD, bytes_accessed=8 * clips * slots * width,
            transcendentals=clips * pairs * 2 * slots * slots,
        ),
        name="attend",
    )(projected, projected, projected, penalty)


def attend_back_kernel(chunk, q_ref, k_ref, v_ref, penalty_ref, log_ref, att_ref, grad_ref, out_ref, bias_ref):
    slots = q_ref.shape[1]
    pair = pl.program_id(1)
    width = out_ref.shape[2] // 3
    keys, values = k_ref[0], v_ref[0]
    keys_t = keys.T
    penalty = penalty_ref[0]
    masks = head_masks()
    grad_keys = jnp.zeros((slots, 2 * HEAD), F32)
    grad_values = jnp.zeros((slots, 2 * HEAD), F32)
    query_bias = jnp.zeros((1, 2 * HEAD), F32)
    for start in range(0, slots, chunk):
        queries = q_ref[0, start : start + chunk] * jnp.asarray(0.125, BF)
        grads = grad_ref[0, start : start + chunk]
        overlap = (grads.astype(F32) * att_ref[0, start : start + chunk].astype(F32)).T
        parts = []
        for h in range(2):
            head_queries = queries * masks[h]
            head_grads = grads * masks[h]
            correction = jnp.sum(overlap[h * HEAD : (h + 1) * HEAD], axis=0, keepdims=True)
            logs = log_ref[0, 0, h : h + 1, start : start + chunk]
            soft = jnp.exp(product_right_t(keys, head_queries) + penalty - logs)
            grad_soft = product_right_t(values, head_grads)
            grad_values += product(soft.astype(BF), head_grads)
            grad_scores = (soft * (grad_soft - correction)).astype(BF)
            grad_keys += product(grad_scores, head_queries)
            parts.append(product(keys_t[h * HEAD : (h + 1) * HEAD], grad_scores))
        grad_queries = jnp.concatenate(parts, 0).T * 0.125
        query_bias += jnp.sum(grad_queries, axis=0, keepdims=True)
        out_ref[0, start : start + chunk, pl.ds(pl.multiple_of(pair * 2 * HEAD, 128), 2 * HEAD)] = grad_queries.astype(BF)
    out_ref[0, :, pl.ds(pl.multiple_of(width + pair * 2 * HEAD, 128), 2 * HEAD)] = grad_keys.astype(BF)
    out_ref[0, :, pl.ds(pl.multiple_of(2 * width + pair * 2 * HEAD, 128), 2 * HEAD)] = grad_values.astype(BF)
    bias_ref[0, 0, 0:1] = query_bias
    bias_ref[0, 0, 1:2] = jnp.sum(grad_values, axis=0, keepdims=True)


def attend_back(projected, penalty, logs, attended, grad_attended):
    clips, slots, triple = projected.shape
    width = triple // 3
    pairs = width // (2 * HEAD)

    def block(offset):
        return pl.BlockSpec((1, slots, 2 * HEAD), lambda i, j: (i, 0, offset * pairs + j))

    return pl.pallas_call(
        functools.partial(attend_back_kernel, 256),
        grid=(clips, pairs),
        in_specs=[
            block(0), block(1), block(2),
            pl.BlockSpec((1, slots, 1), lambda i, j: (i, 0, 0)),
            pl.BlockSpec((1, 1, 2, slots), lambda i, j: (i, j, 0, 0)),
            block(0), block(0),
        ],
        out_specs=[
            pl.BlockSpec((1, slots, triple), lambda i, j: (i, 0, 0)),
            pl.BlockSpec((1, 1, 2, 2 * HEAD), lambda i, j: (i, j, 0, 0)),
        ],
        out_shape=[
            jax.ShapeDtypeStruct((clips, slots, triple), BF),
            jax.ShapeDtypeStruct((clips, pairs, 2, 2 * HEAD), F32),
        ],
        compiler_params=pltpu.CompilerParams(vmem_limit_bytes=56 << 20),
        cost_estimate=pl.CostEstimate(
            flops=10 * clips * pairs * slots * slots * 2 * HEAD, bytes_accessed=18 * clips * slots * width,
            transcendentals=clips * pairs * 2 * slots * slots,
        ),
        name="attend_back",
    )(projected, projected, projected, penalty, logs, attended, grad_attended)


def normalize(values, norm_gain, norm_shift):
    average = jnp.mean(values, axis=-1, keepdims=True)
    centered = values - average
    variance = jnp.mean(centered * centered, axis=-1, keepdims=True)
    inverse = lax.rsqrt(variance + EPSILON)
    scaled = centered * inverse
    return scaled * norm_gain + norm_shift, scaled, inverse


def normalize_back(grad_normed, scaled, inverse, norm_gain):
    grad_scaled = grad_normed * norm_gain
    first_mean = jnp.mean(grad_scaled, axis=-1, keepdims=True)
    second_mean = jnp.mean(grad_scaled * scaled, axis=-1, keepdims=True)
    return inverse * (grad_scaled - first_mean - scaled * second_mean)


def by_core(core, own, other, axis):
    return jnp.where(core == 0, jnp.concatenate([own, other], axis), jnp.concatenate([other, own], axis))


def per_device(
    tokens, valid_slots, cotangent, first_gain, first_shift, qkv_weight, query_bias, value_bias, proj_weight,
    proj_bias, second_gain, second_shift, up_weight, up_bias, down_weight, down_bias,
):
    devices = lax.axis_size(AX)
    chips = devices // 2
    core = lax.axis_index(AX) % 2
    micro, rows, features = tokens.shape
    shard = qkv_weight.shape[0]
    width = features // 2
    hidden = up_weight.shape[1] // 2
    unit = hidden // chips
    slots = 2 * rows
    every = micro * slots

    vectors = jnp.stack(
        [first_gain, first_shift, query_bias, value_bias, proj_bias, second_gain, second_shift, down_bias], 1
    )
    packed = jnp.concatenate([vectors, up_bias.reshape(shard, 4)], 1)
    packed = jnp.pad(packed, ((0, 0), (0, PARAM_COLS - packed.shape[1])))
    split = qkv_weight.reshape(shard, 3, 2, width).transpose(2, 0, 1, 3).reshape(2, shard, 3 * width)
    qkv_in = jnp.concatenate([split, jnp.broadcast_to(packed, (2,) + packed.shape)], 2)
    up_in = up_weight.reshape(shard, chips, 2, unit).transpose(2, 0, 1, 3).reshape(2, shard, hidden)
    proj_in = proj_weight.reshape(shard, 2, width).transpose(1, 0, 2)
    weight_down = lax.all_gather(down_weight, AX, axis=0, tiled=True, axis_index_groups=same_core_groups())
    qkv_all, proj_all, up_all = gather_chips([qkv_in, proj_in, up_in])
    qkv_all = qkv_all.reshape(features, 3 * width + PARAM_COLS)
    weight_qkv = qkv_all[:, : 3 * width]
    params = qkv_all[:, 3 * width : 3 * width + 12].astype(F32).T
    gain_one, shift_one, bias_query, bias_value, bias_proj, gain_two, shift_two, bias_down = params[:8]
    bias_up = params[8:].T.reshape(chips, 2, unit)
    bias_up = lax.dynamic_index_in_dim(bias_up, core, 1, keepdims=False).reshape(hidden)
    weight_up = up_all.reshape(features, hidden)
    proj_cols = proj_all.reshape(2, width, width)
    proj_own = lax.dynamic_index_in_dim(proj_cols, core, 0, keepdims=False)
    proj_other = swap(lax.dynamic_index_in_dim(proj_cols, 1 - core, 0, keepdims=False))
    weight_proj = by_core(core, proj_own, proj_other, 1)
    qkv_bias = jnp.concatenate(
        [
            lax.dynamic_slice_in_dim(bias_query, core * width, width),
            jnp.zeros((width,), F32),
            lax.dynamic_slice_in_dim(bias_value, core * width, width),
        ]
    )

    def both(own):
        return jnp.concatenate([own, swap(own)], 1)

    inputs_low = both(tokens)
    marks = both(valid_slots)
    grad_out = both(cotangent)
    inputs = tokens.astype(F32)
    norm_one, hat_one, inverse_one = normalize(inputs_low.astype(F32), gain_one, shift_one)
    norm_one = norm_one.astype(BF).reshape(every, features)
    projected = (product(norm_one, weight_qkv) + qkv_bias).astype(BF).reshape(micro, slots, 3 * width)
    penalty = jnp.where(marks > 0, 0.0, -1000000000.0).astype(F32)[:, :, None]
    attended, logs = attend(projected, penalty)
    attended_flat = attended.reshape(every, width)
    mixed = product(attended_flat, weight_proj).reshape(micro, slots, features)
    middle = inputs + mixed[:, :rows] + swap(mixed[:, rows:].astype(BF)).astype(F32) + bias_proj
    norm_two, hat_two, inverse_two = normalize(middle, gain_two, shift_two)
    norm_two = both(norm_two.astype(BF)).reshape(every, features)
    pre_act = product(norm_two, weight_up) + bias_up
    normal_cdf = 0.5 * (1.0 + jax.scipy.special.erf(pre_act * ROOT_HALF))
    density = jnp.exp(-0.5 * pre_act * pre_act) * INV_ROOT_TWO_PI
    activation = (pre_act * normal_cdf).astype(BF)
    slope = (normal_cdf + pre_act * density).astype(BF)
    lifted = product(activation, weight_down).reshape(micro, slots, features)
    block_output = (middle + lifted[:, :rows] + swap(lifted[:, rows:].astype(BF)).astype(F32) + bias_down).astype(BF)

    grad_out = (grad_out * (marks > 0).astype(BF)[:, :, None])
    grad_out_own = grad_out[:, :rows].astype(F32)
    grad_out = grad_out.reshape(every, features)
    grad_down = product_left_t(activation, grad_out).astype(BF)
    down_weight_grad = lax.psum_scatter(
        grad_down, AX, scatter_dimension=0, tiled=True, axis_index_groups=same_core_groups()
    ).astype(F32)
    grad_pre_full = product_right_t(grad_out, weight_down) * slope.astype(F32)
    grad_bias_up = jnp.sum(grad_pre_full, axis=0)
    grad_pre = grad_pre_full.astype(BF)
    grad_up = product_left_t(norm_two, grad_pre).astype(BF)
    grad_norm_two = product_right_t(grad_pre, weight_up).reshape(micro, slots, features)
    grad_norm_two = grad_norm_two[:, :rows] + swap(grad_norm_two[:, rows:].astype(BF)).astype(F32)
    grad_middle = grad_out_own + normalize_back(grad_norm_two, hat_two, inverse_two, gain_two)
    grad_middle_low = both(grad_middle.astype(BF)).reshape(every, features)
    grad_proj = product_left_t(attended_flat, grad_middle_low).astype(BF)
    grad_proj_own = lax.dynamic_slice_in_dim(grad_proj, core * width, width, 1)
    grad_proj_other = swap(lax.dynamic_slice_in_dim(grad_proj, (1 - core) * width, width, 1))
    grad_proj = by_core(core, grad_proj_own, grad_proj_other, 0)
    grad_attended = product_right_t(grad_middle_low, weight_proj).astype(BF).reshape(micro, slots, width)
    grad_projected, grad_bias = attend_back(projected, penalty, logs, attended, grad_attended)
    grad_projected = grad_projected.reshape(every, 3 * width)
    grad_bias = jnp.sum(grad_bias, axis=0)
    grad_qkv = product_left_t(norm_one, grad_projected).astype(BF)
    grad_norm_one = product_right_t(grad_projected, weight_qkv).reshape(micro, slots, features)
    grad_norm_one = grad_norm_one[:, :rows] + swap(grad_norm_one[:, rows:].astype(BF)).astype(F32)
    hat_own, inverse_own = hat_one[:, :rows], inverse_one[:, :rows]
    tokens_grad = grad_middle + normalize_back(grad_norm_one, hat_own, inverse_own, gain_one)

    def over_rows(value):
        return jnp.sum(value, axis=(0, 1))

    def whole(half):
        empty = jnp.zeros_like(half)
        return by_core(core, half, empty, 0)

    up_units = grad_bias_up.reshape(chips, 1, unit)
    up_units = by_core(core, up_units, jnp.zeros_like(up_units), 1).reshape(features, 4)
    sums = jnp.stack(
        [
            over_rows(grad_norm_one * hat_own),
            over_rows(grad_norm_one),
            whole(grad_bias[:, 0].reshape(width)),
            whole(grad_bias[:, 1].reshape(width)),
            over_rows(grad_middle),
            over_rows(grad_norm_two * hat_two),
            over_rows(grad_norm_two),
            over_rows(grad_out_own),
        ],
        1,
    )
    sums = jnp.concatenate([sums, up_units], 1)
    sums = jnp.pad(sums, ((0, 0), (0, PARAM_COLS - sums.shape[1]))).astype(BF)
    qkv_part = jnp.concatenate([grad_qkv, sums], 1).reshape(chips, 2, shard, 3 * width + PARAM_COLS)
    up_sum, qkv_sum, proj_sum = scatter_chips(
        [
            grad_up.reshape(chips, 2, shard, hidden),
            qkv_part,
            grad_proj.reshape(chips, 2, shard, width),
        ]
    )
    qkv_weight_grad = qkv_sum[:, :, : 3 * width].reshape(2, shard, 3, width).transpose(1, 2, 0, 3)
    qkv_weight_grad = qkv_weight_grad.reshape(shard, 6 * width)
    up_weight_grad = up_sum.reshape(2, shard, chips, unit).transpose(1, 2, 0, 3).reshape(shard, 2 * hidden)
    proj_weight_grad = jnp.concatenate([proj_sum[0], proj_sum[1]], 1)
    vector_sum = qkv_sum[0, :, 3 * width : 3 * width + 12] + qkv_sum[1, :, 3 * width : 3 * width + 12]
    up_bias_grad = vector_sum[:, 8:].reshape(4 * shard)
    vector_sum = vector_sum.T
    return (
        block_output, tokens_grad, vector_sum[0], vector_sum[1], qkv_weight_grad, vector_sum[2], vector_sum[3],
        proj_weight_grad, vector_sum[4], vector_sum[5], vector_sum[6], up_weight_grad, up_bias_grad,
        down_weight_grad, vector_sum[7],
    )


def solution(mesh):
    row = P(None, AX, None)
    vec = P(AX)
    mat = P(AX, None)
    return jax.shard_map(
        per_device,
        mesh=mesh,
        in_specs=(row, P(None, AX), row, vec, vec, mat, vec, vec, mat, vec, vec, vec, mat, vec, mat, vec),
        out_specs=(row, row, vec, vec, mat, vec, vec, mat, vec, vec, vec, mat, vec, mat, vec),
        check_vma=False,
    )
```

time: 1270 us -> 489 us (0.39)
  matrix products: 537 us -> 98 us
  waiting for transfers between devices: 423 us -> 0.07 us
  Pallas kernels: 0 us -> 246 us
  blocking collectives: 120 us -> 0 us
  local copies, waits for them, and re-layouts: 99.2 us -> 67.2 us
    reduce_scatter x4 -> x1, waiting for transfers between devices: 399 us -> 0.01 us  [per_device(): lax.psum_scatter(grad_down, AX, scatter_dimension=0, tiled=True, axis_ind...]
    pallas_call x0 -> x4, Pallas kernels: none -> 246 us  [the longest x1 105 us: scatter_chips(): pl.pallas_call(functools.partial(scatter_kernel, count), out_shape=[jax.S...]
    dot_general x72 -> x4, matrix products: 179 us -> 29.9 us  [product_left_t(): lax.dot_general(left_side, right_side, (((0,), (0,)), ((), ())), preferre...]
    dot_general x72 -> x4, matrix products: 178 us -> 31.8 us  [product(): return jnp.dot(left_side, right_side, preferred_element_type=F32)]
    dot_general x104 -> x4, matrix products: 179 us -> 36.3 us  [product_right_t(): lax.dot_general(left_side, right_side, (((1,), (1,)), ((), ())), preferre...]
    unnamed x2 -> x0, blocking collectives: 80.5 us -> none
    all_gather x1 -> x0, blocking collectives: 39.6 us -> none  [per_device(): lax.all_gather(up_bias, 'fsdp', axis=0, tiled=True)]
    while x6 -> x0, local copies, waits for them, and re-layouts: 21.7 us -> none  [attend(): lax.map(one_head, (query_heads, key_heads, value_heads))]
  transfers between devices with their start and end apart: 14 -> 13, of which waited for: 4 -> 0; matrix products, arithmetic and copies ran while one was open for 39% -> 38% of each run, Pallas kernels for 0% -> 51%
where the time goes in v1:
time: 489 us; the launch traced here: 483 us
  Pallas kernels  246 us (50%)
  matrix products  98 us (20%)
  local copies, waits for them, and re-layouts  67.2 us (14%)
  other arithmetic  54.1 us (11%)
  between operations  15.4 us (3%)
    pallas_call x1, Pallas kernels, scatter_chips(): pl.pallas_call(functools.partial(scatter_kernel, count), out_shape=[jax.S...  105 us
    pallas_call x1, Pallas kernels, gather_chips(): pl.pallas_call(functools.partial(gather_kernel, count), out_shape=[jax.Sh...  81.8 us
    dot_general x4, matrix products, product_right_t(): lax.dot_general(left_side, right_side, (((1,), (1,)), ((), ())), preferre...  36.3 us
    dot_general x4, matrix products, product(): return jnp.dot(left_side, right_side, preferred_element_type=F32)  31.8 us
    dot_general x4, matrix products, product_left_t(): lax.dot_general(left_side, right_side, (((0,), (0,)), ((), ())), preferre...  29.9 us
    pallas_call x1, Pallas kernels, attend_back(): pl.pallas_call(functools.partial(attend_back_kernel, 256), grid=(clips, p...  29.3 us
    pallas_call x1, Pallas kernels, attend(): pl.pallas_call(functools.partial(attend_kernel, 256), grid=(clips, pairs)...  28.9 us
    unnamed x80, local copies, waits for them, and re-layouts  16.3 us
  transfers between devices with their start and end apart: 13, of which 0 were waited for; matrix products, arithmetic and copies ran while one was open for 38% of the time, Pallas kernels for 51%

profile of v1, /device:TPU:0, one launch (start us, length us, event | category | flops | bytes accessed | tf_op | source)
XLA Modules:
  0.0 483.5 jit_solution(10505902667799502457)
XLA Ops:
  7.9 1.1 reshape.250
  16.1 1.1 reshape.254
  18.1 1.5 copy.145
  20.4 81.8 %gather_chips.1 = (bf16[16,2,32,1664]{3,2,1,0:T(8,128)(2,1)}, bf16[16,2,32,512]{3,2,1,0:T(8,128)(2,1)}, bf16[16,2,32,2048]{3,2,1,0:T(8,128)(2,1)}) custom-call(bf16[2,32,1664]{2,1,0:T(8,128)(2,1)} %pad_maximum_fusion.3.refs_0_, bf16[2,32,512]{2,1,0:T(8,128)(2,1)} %bitcast.127, bf16[2,32,2048]{2,1,0:T(8,128)(2,1)} %reshape.255.refs_2_), custom_call_target="tpu_custom_call" | custom-call | tf_op jit(solution)/shard_map/gather_chips/pallas_call | solution.py:134
  102.2 2.1 dynamic-slice_bitcast_fusion.1
  104.3 1.1 convert_bitcast_fusion
  105.5 1.9 fusion.36
  108.3 2.2 convert_reduce_fusion
  110.5 2.5 multiply_reduce_fusion
  113.0 2.7 fusion.9
  115.8 6.8 %add_convert_fusion = bf16[1536,1536]{1,0:T(8,128)(2,1)} fusion(bf16[1536,1024]{1,0:T(8,128)(2,1)S(1)} %fusion.9, f32[1536]{0:T(1024)S(1)} %pad_maximum_fusion.5, bf16[1024,1664]{1,0:T(8,128)(2,1)S(1)} %bitcast.130), kind=kOutput, calls=%fused_computation.9 | convolution fusion | flops 4836556800 | bytes 11018240 | tf_op jit(solution)/shard_map/dot_general | solution.py:22
  122.6 28.9 %attend.1 = (bf16[2,768,512]{2,1,0:T(8,128)(2,1)S(1)}, f32[2,4,2,768]{3,2,1,0:T(2,128)S(1)}) custom-call(bf16[2,768,1536]{2,1,0:T(8,128)(2,1)} %bitcast.152, bf16[2,768,1536]{2,1,0:T(8,128)(2,1)} %bitcast.153, bf16[2,768,1536]{2,1,0:T(8,128)(2,1)} %bitcast.154, f32[2,768,1]{2,1,0:T(8,128)S(1)} %broadcast_select_fusion.penalty_ref), custom_call_target="tpu_custom_call" | custom-call | flops 2415919104 | bytes 6291456 | tf_op jit(solution)/shard_map/attend/pallas_call | solution.py:337
  151.6 3.7 fusion.23
  155.3 1.5 slice.237
  156.8 1.6 copy-done.14
  158.9 1.0 slice_bitcast_fusion
  159.9 1.5 reshape.261
  161.4 2.7 constant_dynamic-update-slice_fusion.1
  164.2 3.1 fusion.33
  170.3 1.5 constant_dynamic-update-slice_fusion
  172.4 5.0 %subtract_multiply_fusion = f32[2,768,1024]{2,1,0:T(8,128)} fusion(f32[2,768]{1,0:T(2,128)S(1)} %get-tuple-element.83, f32[2,768]{1,0:T(2,128)S(1)} %broadcast_multiply_fusion, bf16[2,384,1024]{2,1,0:T(8,128)(2,1)} %collective-permute-done, bf16[2,384,1024]{2,1,0:T(8,128)(2,1)S(1)} %copy-done.6), kind=kLoop, calls=%fused_computation.20 | loop fusion | flops 9437184 | bytes 9449472 | tf_op jit(solution)/shard_map/mul | solution.py:430
  177.5 2.2 bitcast_multiply_fusion
  180.0 1.7 copy-done.16
  181.6 1.3 copy-done.30
  183.0 10.8 %multiply_convert_fusion = (bf16[1536,2048]{1,0:T(8,128)(2,1)}, f32[1536,2048]{1,0:T(8,128)}) fusion(f32[2048]{0:T(1024)S(1)} %bitcast.135, bf16[1536,1024]{1,0:T(8,128)(2,1)S(1)} %bitcast.118, bf16[1024,2048]{1,0:T(8,128)(2,1)S(1)} %bitcast.147), kind=kOutput, calls=%fused_computation.7 | convolution fusion | flops 6461325312 | bytes 26222592 | tf_op jit(solution)/shard_map/dot_general | solution.py:22
  193.7 15.4 %fusion.35 = (f32[2048]{0:T(1024)S(1)}, bf16[1536,2048]{1,0:T(8,128)(2,1)S(1)}) fusion(f32[1536,2048]{1,0:T(8,128)} %get-tuple-element.88, f32[2048]{0:T(1024)S(1)} %bitcast.136, bf16[1536,1024]{1,0:T(8,128)(2,1)} %bitcast_multiply_fusion, bf16[2048,1024]{1,0:T(8,128)(2,1)} %all-gather.2.cloned.1.call-done), kind=kOutput, calls=%fused_computation.128 | convolution fusion | flops 6486489088 | bytes 26230784 | tf_op jit(solution)/shard_map/dot_general | solution.py:30
  209.1 6.9 %fusion.39 = f32[2,768,1024]{2,1,0:T(8,128)S(1)} fusion(bf16[2,768,2048]{2,1,0:T(8,128)(2,1)S(1)} %bitcast.149, bf16[1024,2048,1]{1,0,2:T(8,128)(2,1)S(1)} %bitcast.148), kind=kOutput, calls=%fused_computation.132 | convolution fusion | flops 6442450944 | bytes 16777216 | tf_op jit(solution)/shard_map/dot_general | solution.py:30
  216.1 1.4 slice.235
  218.0 10.6 %fusion.38 = f32[1536,1024]{1,0:T(8,128)S(1)} fusion(bf16[1536,2048]{1,0:T(8,128)(2,1)} %get-tuple-element.87, bf16[2048,1024]{1,0:T(8,128)(2,1)S(1)} %copy-done.32), kind=kOutput, calls=%fused_computation.131 | convolution fusion | flops 6442450944 | bytes 16777216 | tf_op jit(solution)/shard_map/dot_general | solution.py:22
  228.6 3.2 copy-done.15
  231.8 1.4 slice.236
  233.8 8.5 %convolution_convert_fusion = bf16[2048,1024]{1,0:T(8,128)(2,1)} fusion(bf16[1536,2048]{1,0:T(8,128)(2,1)S(1)} %bitcast.160, bf16[1536,1024]{1,0:T(8,128)(2,1)S(1)} %copy-done.19), kind=kOutput, calls=%fused_computation.22 | convolution fusion | flops 6444548096 | bytes 13631488 | tf_op jit(solution)/shard_map/dot_general | solution.py:26
  242.4 4.2 multiply_reduce_fusion.1
  247.5 6.0 %fusion.32 = (bf16[1024]{0:T(1024)(128)(2,1)S(1)}, f32[2,384,1024]{2,1,0:T(8,128)S(1)}, bf16[2,384,1024]{2,1,0:T(8,128)(2,1)}) fusion(f32[2,384]{1,0:T(2,128)S(1)} %broadcast_multiply_fusion.3, f32[2,384,1024]{2,1,0:T(8,128)S(1)} %copy-done.4, f32[2,384]{1,0:T(2,128)S(1)} %broadcast_multiply_fusion.5, f32[2,384]{1,0:T(2,128)S(1)} %broadcast_multiply_fusion.4, ...), kind=kLoop, calls=%fused_computation.126 | loop fusion | flops 15727616 | bytes 18898432 | tf_op jit(solution)/shard_map/reduce_sum | solution.py:545
  253.5 1.4 convert_element_type.117
  254.9 2.2 copy-done.17
  257.1 8.9 %convolution_convert_fusion.1 = bf16[1024,2048]{1,0:T(8,128)(2,1)} fusion(bf16[1536,1024]{1,0:T(8,128)(2,1)S(1)} %bitcast.119, bf16[1536,2048]{1,0:T(8,128)(2,1)S(1)} %bitcast.151), kind=kOutput, calls=%fused_computation.23 | convolution fusion | flops 6444548096 | bytes 13631488 | tf_op jit(solution)/shard_map/dot_general | solution.py:26
  266.0 1.3 reshape.267
  268.2 0.9 stack.77
  269.1 0.9 stack.78
  270.1 3.7 bitcast_convert_fusion.1
  273.8 1.1 constant_dynamic-slice_fusion.1
  274.9 2.3 pad_maximum_fusion.2
  277.2 4.2 convolution_convert_fusion.2
  281.4 29.3 %attend_back.1 = (bf16[2,768,1536]{2,1,0:T(8,128)(2,1)}, f32[2,4,2,128]{3,2,1,0:T(2,128)}) custom-call(bf16[2,768,1536]{2,1,0:T(8,128)(2,1)} %bitcast.155, bf16[2,768,1536]{2,1,0:T(8,128)(2,1)} %bitcast.156, bf16[2,768,1536]{2,1,0:T(8,128)(2,1)} %bitcast.157, f32[2,768,1]{2,1,0:T(8,128)} %copy-done, f32[2,4,2,768]{3,2,1,0:T(2,128)} %copy-done.2, ...), custom_call_target="tpu_custom_call" | custom-call | flops 6039797760 | bytes 14155776 | tf_op jit(solution)/shard_map/attend_back/pallas_call | solution.py:399
  310.7 9.8 %fusion.16 = f32[2,768,1024]{2,1,0:T(8,128)} fusion(bf16[2,768,1536]{2,1,0:T(8,128)(2,1)} %get-tuple-element.30, bf16[1024,1664]{1,0:T(8,128)(2,1)S(1)} %bitcast.131), kind=kOutput, calls=%fused_computation.41 | convolution fusion | flops 4831838208 | bytes 14155776 | tf_op jit(solution)/shard_map/dot_general | solution.py:30
  320.6 3.3 slice.234
  324.3 8.7 %bitcast_convert_fusion = bf16[1024,1536]{1,0:T(8,128)(2,1)} fusion(bf16[2,768,1536]{2,1,0:T(8,128)(2,1)S(1)} %copy-done.34, f32[1024]{0:T(1024)S(1)} %copy-done.27, f32[1024]{0:T(1024)S(1)} %copy-done.23, f32[2,768]{1,0:T(2,128)S(1)} %get-tuple-element.83, f32[2,768]{1,0:T(2,128)S(1)} %broadcast_multiply_fusion, ...), kind=kOutput, calls=%fused_computation.12 | convolution fusion | flops 4847566848 | bytes 11030528 | tf_op jit(solution)/shard_map/dot_general | solution.py:26
  333.0 0.9 stack.74
  333.9 0.9 stack.75
  334.9 2.9 maximum_select_fusion.1
  337.8 4.6 multiply_reduce_fusion.2
  344.2 3.7 concatenate.102
  347.9 3.0 fusion.10
  350.9 105.5 %scatter_chips.1 = (f32[2,32,2048]{2,1,0:T(8,128)}, f32[2,32,1664]{2,1,0:T(8,128)}, f32[2,32,512]{2,1,0:T(8,128)}) custom-call(bf16[16,2,32,2048]{3,2,1,0:T(8,128)(2,1)} %bitcast.115, bf16[16,2,32,1664]{3,2,1,0:T(8,128)(2,1)} %bitcast.113, bf16[16,2,32,512]{3,2,1,0:T(8,128)(2,1)} %bitcast.114), custom_call_target="tpu_custom_call" | custom-call | tf_op jit(solution)/shard_map/scatter_chips/pallas_call | solution.py:291
  456.4 1.1 copy.139
  457.6 1.2 copy.135
  458.8 2.3 reshape.272
  461.0 1.0 slice.123
  462.1 1.1 reshape.269
  463.1 1.3 copy.134
  464.5 1.1 reshape.270
  469.4 4.9 %multiply_add_fusion = f32[2,384,1024]{2,1,0:T(8,128)} fusion(f32[2,384,1024]{2,1,0:T(8,128)S(1)} %copy-done.8, f32[2,768,1024]{2,1,0:T(8,128)} %subtract_multiply_fusion, f32[2,384]{1,0:T(2,128)S(1)} %broadcast_multiply_fusion.1, f32[2,384]{1,0:T(2,128)S(1)} %broadcast_multiply_fusion.2, f32[1024]{0:T(1024)S(1)} %copy-done.23, ...), kind=kLoop, calls=%fused_computation.48 | loop fusion | flops 6291456 | bytes 14169088 | tf_op jit(solution)/shard_map/add | solution.py:542
  474.3 1.8 convert_element_type.125
  (162 shorter events, 24.1 us)
Async XLA Ops:
  7.2 186.5 %all-gather.2.cloned.1.call-start = ((), (), s32[]{:S(2)}) async-start(), calls=%async_computation.1 | async-start | bytes 4456448 | tf_op jit(solution)/shard_map/all_gather | solution.py:469
  7.2 101.1 %collective-permute-start = (bf16[2,384,1024]{2,1,0:T(8,128)(2,1)}, bf16[2,384,1024]{2,1,0:T(8,128)(2,1)}, u32[]{:S(2)}, u32[]{:S(2)}) collective-permute-start(bf16[2,384,1024]{2,1,0:T(8,128)(2,1)} %param.16), channel_id=1, source_target_pairs={{0,1},{1,0},{2,3},{3,2},{4,5},{5,4},{6,7},{7,6},{8,9},{9,8},{10,11... | collective-permute-start | bytes 4718600 | tf_op jit(solution)/shard_map/ppermute | solution.py:34
  7.8 99.8 %collective-permute-start.1 = (s32[2,384]{1,0:T(2,128)}, s32[2,384]{1,0:T(2,128)S(1)}, u32[]{:S(2)}, u32[]{:S(2)}) collective-permute-start(s32[2,384]{1,0:T(2,128)} %param.17), channel_id=1, source_target_pairs={{0,1},{1,0},{2,3},{3,2},{4,5},{5,4},{6,7},{7,6},{8,9},{9,8},{10,11... | collective-permute-start | bytes 9224 | tf_op jit(solution)/shard_map/ppermute | solution.py:34
  104.2 47.4 %copy-start.20 = (bf16[512,512]{1,0:T(8,128)(2,1)}, bf16[512,512]{1,0:T(8,128)(2,1)S(1)}, u32[]{:S(2)}) copy-start(bf16[512,512]{1,0:T(8,128)(2,1)S(1)} %get-tuple-element.68) | copy-start | bytes 1572868
  104.2 47.4 %collective-permute-start.2 = (bf16[512,512]{1,0:T(8,128)(2,1)}, bf16[512,512]{1,0:T(8,128)(2,1)}, u32[]{:S(2)}, u32[]{:S(2)}) collective-permute-start(bf16[512,512]{1,0:T(8,128)(2,1)} %get-tuple-element.69), channel_id=1, source_target_pairs={{0,1},{1,0},{2,3},{3,2},{4,5},{5,4},{6,7},{7,6},{8,9},{9,8},{10,11... | collective-permute-start | bytes 1572872 | tf_op jit(solution)/shard_map/ppermute | solution.py:34
  104.3 370.1 %reduce-scatter.2.cloned.1.call-start = ((), (), s32[]{:S(2)}) async-start(), calls=%async_computation.2 | async-start | bytes 4456448 | tf_op jit(solution)/shard_map/reduce_scatter | solution.py:519
  104.3 3.3 copy-start.28
  105.4 2.9 copy-start.5
  107.3 5.7 %copy-start.22 = (f32[1024]{0:T(1024)}, f32[1024]{0:T(1024)S(1)}, u32[]{:S(2)}) copy-start(f32[1024]{0:T(1024)S(1)} %get-tuple-element.72) | copy-start | bytes 12292
  107.3 5.7 %copy-start.26 = (f32[1024]{0:T(1024)}, f32[1024]{0:T(1024)S(1)}, u32[]{:S(2)}) copy-start(f32[1024]{0:T(1024)S(1)} %get-tuple-element.73) | copy-start | bytes 12292
  108.3 14.4 %copy-start = (f32[2,768,1]{2,1,0:T(8,128)}, f32[2,768,1]{2,1,0:T(8,128)S(1)}, u32[]{:S(2)}) copy-start(f32[2,768,1]{2,1,0:T(8,128)S(1)} %broadcast_select_fusion.penalty_ref) | copy-start | bytes 18436
  113.0 2.8 copy-start.24
  151.6 3.7 copy-start.2
  151.6 118.5 %copy-start.1 = (bf16[2,768,512]{2,1,0:T(8,128)(2,1)}, bf16[2,768,512]{2,1,0:T(8,128)(2,1)S(1)}, u32[]{:S(2)}) copy-start(bf16[2,768,512]{2,1,0:T(8,128)(2,1)S(1)} %get-tuple-element.26.att_ref) | copy-start | bytes 4718596
  155.3 3.1 copy-start.14
  158.4 5.8 %collective-permute-start.3 = (bf16[2,384,1024]{2,1,0:T(8,128)(2,1)}, bf16[2,384,1024]{2,1,0:T(8,128)(2,1)}, u32[]{:S(2)}, u32[]{:S(2)}) collective-permute-start(bf16[2,384,1024]{2,1,0:T(8,128)(2,1)} %slice.237), channel_id=1, source_target_pairs={{0,1},{1,0},{2,3},{3,2},{4,5},{5,4},{6,7},{7,6},{8,9},{9,8},{10,11... | collective-permute-start | bytes 4718600 | tf_op jit(solution)/shard_map/ppermute | solution.py:34
  158.8 10.6 %collective-permute-start.6 = (bf16[2,384,1024]{2,1,0:T(8,128)(2,1)}, bf16[2,384,1024]{2,1,0:T(8,128)(2,1)}, u32[]{:S(2)}, u32[]{:S(2)}) collective-permute-start(bf16[2,384,1024]{2,1,0:T(8,128)(2,1)} %param.18), channel_id=1, source_target_pairs={{0,1},{1,0},{2,3},{3,2},{4,5},{5,4},{6,7},{7,6},{8,9},{9,8},{10,11... | collective-permute-start | bytes 4718600 | tf_op jit(solution)/shard_map/ppermute | solution.py:34
  159.9 4.3 copy-start.6
  167.3 1.7 copy-start.3
  167.8 2.5 copy-start.9
  168.9 10.7 %collective-permute-start.4 = (bf16[2,384,1024]{2,1,0:T(8,128)(2,1)S(1)}, bf16[2,384,1024]{2,1,0:T(8,128)(2,1)S(1)}, u32[]{:S(2)}, u32[]{:S(2)}) collective-permute-start(bf16[2,384,1024]{2,1,0:T(8,128)(2,1)S(1)} %add_convert_fusion.3), channel_id=1, source_target_pairs={{0,1},{1,0},{2,3},{3,2},{4,5},{5,4},{6,7},{7,6},{8,9},{9,8},{10,11... | collective-permute-start | bytes 4718600 | tf_op jit(solution)/shard_map/ppermute | solution.py:34
  171.8 5.6 %copy-start.10 = (bf16[2,768,1024]{2,1,0:T(8,128)(2,1)}, bf16[2,768,1024]{2,1,0:T(8,128)(2,1)S(1)}, u32[]{:S(2)}) copy-start(bf16[2,768,1024]{2,1,0:T(8,128)(2,1)S(1)} %constant_dynamic-update-slice_fusion) | copy-start | bytes 9437188
  179.6 3.3 copy-start.30
  179.9 1.7 copy-start.16
  193.7 15.4 %copy-start.31 = (bf16[16,2,32,2048]{3,2,1,0:T(8,128)(2,1)S(1)}, bf16[16,2,32,2048]{3,2,1,0:T(8,128)(2,1)}, u32[]{:S(2)}) copy-start(bf16[16,2,32,2048]{3,2,1,0:T(8,128)(2,1)} %get-tuple-element.28) | copy-start | bytes 12582916
  209.1 7.0 %copy-start.33 = (bf16[1536,2048]{1,0:T(8,128)(2,1)}, bf16[1536,2048]{1,0:T(8,128)(2,1)S(1)}, u32[]{:S(2)}) copy-start(bf16[1536,2048]{1,0:T(8,128)(2,1)S(1)} %get-tuple-element.64) | copy-start | bytes 18874372
  209.1 8.9 %copy-start.32 = (bf16[2048,1024]{1,0:T(8,128)(2,1)S(1)}, bf16[2048,1024]{1,0:T(8,128)(2,1)}, u32[]{:S(2)}) copy-start(bf16[2048,1024]{1,0:T(8,128)(2,1)} %all-gather.2.cloned.1.call-done) | copy-start | bytes 12582916
  216.1 12.5 %copy-start.12 = (f32[2,768,1024]{2,1,0:T(8,128)}, f32[2,768,1024]{2,1,0:T(8,128)S(1)}, u32[]{:S(2)}) copy-start(f32[2,768,1024]{2,1,0:T(8,128)S(1)} %fusion.39) | copy-start | bytes 18874372
  216.1 17.7 %slice-start.2 = ((s8[6291456]{0:T(1024)(128)(4,1)}), s8[2097152]{0:T(1024)(128)(4,1)S(1)}, s32[]{:S(2)}) async-start(s8[6291456]{0:T(1024)(128)(4,1)} %bitcast.159), calls=%async_computation.5 | async-start | bytes 4194304
  217.5 24.9 %collective-permute-start.7 = (bf16[2,384,1024]{2,1,0:T(8,128)(2,1)}, bf16[2,384,1024]{2,1,0:T(8,128)(2,1)}, u32[]{:S(2)}, u32[]{:S(2)}) collective-permute-start(bf16[2,384,1024]{2,1,0:T(8,128)(2,1)} %slice.235), channel_id=1, source_target_pairs={{0,1},{1,0},{2,3},{3,2},{4,5},{5,4},{6,7},{7,6},{8,9},{9,8},{10,11... | collective-permute-start | bytes 4718600 | tf_op jit(solution)/shard_map/ppermute | solution.py:34
  218.0 15.7 %slice-start.3 = ((s8[6291456]{0:T(1024)(128)(4,1)}), s8[4194304]{0:T(1024)(128)(4,1)S(1)}, s32[]{:S(2)}) async-start(s8[6291456]{0:T(1024)(128)(4,1)} %bitcast.159), calls=%async_computation.6 | async-start | bytes 8388608
  228.6 3.2 copy-start.15
  228.6 5.1 %copy-start.19 = (bf16[1536,1024]{1,0:T(8,128)(2,1)S(1)}, bf16[1536,1024]{1,0:T(8,128)(2,1)}, u32[]{:S(2)}) copy-start(bf16[1536,1024]{1,0:T(8,128)(2,1)} %bitcast_multiply_fusion) | copy-start | bytes 9437188
  233.2 13.4 %collective-permute-start.5 = (bf16[2,384,1024]{2,1,0:T(8,128)(2,1)}, bf16[2,384,1024]{2,1,0:T(8,128)(2,1)}, u32[]{:S(2)}, u32[]{:S(2)}) collective-permute-start(bf16[2,384,1024]{2,1,0:T(8,128)(2,1)} %slice.236), channel_id=1, source_target_pairs={{0,1},{1,0},{2,3},{3,2},{4,5},{5,4},{6,7},{7,6},{8,9},{9,8},{10,11... | collective-permute-start | bytes 4718600 | tf_op jit(solution)/shard_map/ppermute | solution.py:34
  242.3 4.3 copy-start.4
  242.3 5.2 %copy-start.11 = (bf16[2,768,1024]{2,1,0:T(8,128)(2,1)S(1)}, bf16[2,768,1024]{2,1,0:T(8,128)(2,1)}, u32[]{:S(2)}) copy-start(bf16[2,768,1024]{2,1,0:T(8,128)(2,1)} %copy-done.10) | copy-start | bytes 9437188
  242.4 12.6 %slice-start = ((s8[6291456]{0:T(1024)(128)(4,1)}), s8[4194304]{0:T(1024)(128)(4,1)S(1)}, s32[]{:S(2)}) async-start(s8[6291456]{0:T(1024)(128)(4,1)} %bitcast.150), calls=%async_computation.3 | async-start | bytes 8388608
  247.5 7.4 %slice-start.1 = ((s8[6291456]{0:T(1024)(128)(4,1)}), s8[2097152]{0:T(1024)(128)(4,1)S(1)}, s32[]{:S(2)}) async-start(s8[6291456]{0:T(1024)(128)(4,1)} %bitcast.150), calls=%async_computation.4 | async-start | bytes 4194304
  253.5 12.5 %copy-start.7 = (f32[2,384,1024]{2,1,0:T(8,128)}, f32[2,384,1024]{2,1,0:T(8,128)S(1)}, u32[]{:S(2)}) copy-start(f32[2,384,1024]{2,1,0:T(8,128)S(1)} %get-tuple-element.58) | copy-start | bytes 9437188
  253.5 3.6 copy-start.17
  254.9 15.2 %collective-permute-start.8 = (bf16[2,384,1024]{2,1,0:T(8,128)(2,1)}, bf16[2,384,1024]{2,1,0:T(8,128)(2,1)}, u32[]{:S(2)}, u32[]{:S(2)}) collective-permute-start(bf16[2,384,1024]{2,1,0:T(8,128)(2,1)} %convert_element_type.117), channel_id=1, source_target_pairs={{0,1},{1,0},{2,3},{3,2},{4,5},{5,4},{6,7},{7,6},{8,9},{9,8},{10,11... | collective-permute-start | bytes 4718600 | tf_op jit(solution)/shard_map/ppermute | solution.py:34
  274.9 2.3 copy-start.21
  274.9 60.0 %collective-permute-start.10 = (bf16[512,512]{1,0:T(8,128)(2,1)}, bf16[512,512]{1,0:T(8,128)(2,1)}, u32[]{:S(2)}, u32[]{:S(2)}) collective-permute-start(bf16[512,512]{1,0:T(8,128)(2,1)} %get-tuple-element.67), channel_id=1, source_target_pairs={{0,1},{1,0},{2,3},{3,2},{4,5},{5,4},{6,7},{7,6},{8,9},{9,8},{10,11... | collective-permute-start | bytes 1572872 | tf_op jit(solution)/shard_map/ppermute | solution.py:34
  281.4 29.3 %copy-start.25 = (bf16[16,2,32,1664]{3,2,1,0:T(8,128)(2,1)S(1)}, bf16[16,2,32,1664]{3,2,1,0:T(8,128)(2,1)}, u32[]{:S(2)}) copy-start(bf16[16,2,32,1664]{3,2,1,0:T(8,128)(2,1)} %get-tuple-element.25) | copy-start | bytes 10223620
  310.7 13.6 %copy-start.34 = (bf16[2,768,1536]{2,1,0:T(8,128)(2,1)S(1)}, bf16[2,768,1536]{2,1,0:T(8,128)(2,1)}, u32[]{:S(2)}) copy-start(bf16[2,768,1536]{2,1,0:T(8,128)(2,1)} %get-tuple-element.30) | copy-start | bytes 14155780
  320.5 3.7 copy-start.23
  320.5 3.7 copy-start.27
  323.9 9.1 %copy-start.29 = (f32[2,4,2,128]{3,2,1,0:T(2,128)S(1)}, f32[2,4,2,128]{3,2,1,0:T(2,128)}, u32[]{:S(2)}) copy-start(f32[2,4,2,128]{3,2,1,0:T(2,128)} %get-tuple-element.31) | copy-start | bytes 24580
  323.9 13.9 %collective-permute-start.9 = (bf16[2,384,1024]{2,1,0:T(8,128)(2,1)}, bf16[2,384,1024]{2,1,0:T(8,128)(2,1)S(1)}, u32[]{:S(2)}, u32[]{:S(2)}) collective-permute-start(bf16[2,384,1024]{2,1,0:T(8,128)(2,1)} %slice.234), channel_id=1, source_target_pairs={{0,1},{1,0},{2,3},{3,2},{4,5},{5,4},{6,7},{7,6},{8,9},{9,8},{10,11... | collective-permute-start | bytes 4718600 | tf_op jit(solution)/shard_map/ppermute | solution.py:34
  337.8 4.6 copy-start.13
  342.4 5.5 %copy-start.18 = (bf16[1024,1536]{1,0:T(8,128)(2,1)S(1)}, bf16[1024,1536]{1,0:T(8,128)(2,1)}, u32[]{:S(2)}) copy-start(bf16[1024,1536]{1,0:T(8,128)(2,1)} %bitcast_convert_fusion) | copy-start | bytes 9437188
  457.6 11.8 %copy-start.8 = (f32[2,384,1024]{2,1,0:T(8,128)S(1)}, f32[2,384,1024]{2,1,0:T(8,128)}, u32[]{:S(2)}) copy-start(f32[2,384,1024]{2,1,0:T(8,128)} %copy-done.7) | copy-start | bytes 9437188
Sparse Core Ops, SparseCore 0:
  104.4 75.8 all-gather.1
  242.5 95.1 reduce-scatter.1

commit v2 on v1

v2 whole, which is shorter than its diff:
```python
import functools

import jax
import jax.numpy as jnp
from jax import lax
from jax.experimental import pallas as pl
from jax.experimental.pallas import tpu as pltpu
from jax.sharding import PartitionSpec as P

AX = "fsdp"
MESH = pl.DeviceIdType.MESH
HEAD = 64
EPSILON = 1e-06
ROOT_HALF = 0.7071067811865476
INV_ROOT_TWO_PI = 0.3989422804014327
BF = jnp.bfloat16
F32 = jnp.float32
PARAM_COLS = 128


def product(left_side, right_side):
    return jnp.dot(left_side, right_side, preferred_element_type=F32)


def product_left_t(left_side, right_side):
    return lax.dot_general(left_side, right_side, (((0,), (0,)), ((), ())), preferred_element_type=F32)


def product_right_t(left_side, right_side):
    return lax.dot_general(left_side, right_side, (((1,), (1,)), ((), ())), preferred_element_type=F32)


def swap(shard):
    return lax.ppermute(shard, AX, [(i, i ^ 1) for i in range(lax.axis_size(AX))])


def same_core_groups():
    count = lax.axis_size(AX)
    return [[i for i in range(count) if i % 2 == core] for core in (0, 1)]


def flip(index, step):
    return index + step - 2 * step * ((index // step) % 2)


def peers_of(me):
    return flip(me, 1), flip(me, 2), flip(me, 4), [flip(me, 8), flip(me, 16), flip(flip(me, 8), 16)]


def zflip(chip, j):
    return [chip, flip(chip, 4), flip(chip, 8), flip(flip(chip, 4), 8)][j]


def meet(peers):
    barrier = pltpu.get_barrier_semaphore()
    for peer in peers:
        pl.semaphore_signal(barrier, inc=1, device_id=(peer,), device_id_type=MESH)
    pl.semaphore_wait(barrier, len(peers))


def gather_kernel(qkv_ref, proj_ref, packed_ref, qkv_out, proj_out, packed_out, local_sem, send_sem, recv_sem):
    me = lax.axis_index(AX)
    chip, core = me // 2, me % 2
    mate, peer_x, peer_y, peers_z = peers_of(me)
    meet([mate, peer_x, peer_y] + peers_z)
    chip_x, chip_y = flip(chip, 1), flip(chip, 2)
    chip_xy = flip(chip_x, 2)
    outs = (qkv_out, packed_out, proj_out)
    count = len(outs)
    width = qkv_ref.shape[1] // 6
    pending = []

    def remote(w, slot, block, target, peer):
        return pltpu.make_async_remote_copy(
            src_ref=block, dst_ref=target, send_sem=send_sem.at[w, slot], recv_sem=recv_sem.at[w, slot],
            device_id=(peer,), device_id_type=MESH,
        )

    def send(w, slot, block, target, peer):
        copy = remote(w, slot, block, target, peer)
        copy.start()
        pending.append(copy)

    def arrive(w, slot, block):
        remote(w, slot, block, block, mate).wait_recv()

    def columns(start, size):
        return pl.ds(pl.multiple_of(start, 128), size)

    def pieces(w, half, target):
        if w == 0:
            return [
                (qkv_ref.at[:, columns((2 * t + half) * width, width)], target.at[:, pl.ds(t * width, width)])
                for t in range(3)
            ]
        if w == 1:
            return [(packed_ref, target)]
        return [(proj_ref.at[:, columns(half * width, width)], target)]

    for w in range(count):
        for source, target in pieces(w, 1 - core, outs[w].at[chip, core]):
            remote(w, 0, source, target, mate).start()
        for source, target in pieces(w, core, outs[w].at[chip, core]):
            pltpu.make_async_copy(source, target, local_sem.at[w]).start()
    for w in range(count):
        own = outs[w].at[chip, core]
        pltpu.make_async_copy(own, own, local_sem.at[w]).wait()
        arrive(w, 0, outs[w].at[chip, 1 - core])
        block = outs[w].at[chip]
        for j in range(3):
            send(w, 1 + j, block, block, peers_z[j])
        send(w, 4, block, block, peer_x)
        send(w, 8, block, block, peer_y)
    for w in range(count):
        for j in (1, 2, 3):
            block = outs[w].at[zflip(chip, j)]
            arrive(w, j, block)
            send(w, 4 + j, block, block, peer_x)
            send(w, 8 + j, block, block, peer_y)
        for j in range(4):
            block = outs[w].at[zflip(chip_x, j)]
            arrive(w, 4 + j, block)
            send(w, 12 + j, block.at[0], block.at[0], peer_y)
            block = outs[w].at[zflip(chip_y, j)]
            arrive(w, 8 + j, block)
            send(w, 16 + j, block.at[1], block.at[1], peer_x)
    for w in range(count):
        for j in range(4):
            block = outs[w].at[zflip(chip_xy, j)]
            arrive(w, 12 + j, block.at[0])
            arrive(w, 16 + j, block.at[1])
    for w in range(count):
        own = outs[w].at[chip, core]
        remote(w, 0, own, own, mate).wait_send()
    for copy in pending:
        copy.wait_send()


def gather_chips(qkv, proj, packed):
    devices = lax.axis_size(AX)
    shard, features = proj.shape
    width = features // 2
    if devices != 32:
        core = lax.axis_index(AX) % 2
        split = qkv.reshape(shard, 3, 2, width).transpose(2, 0, 1, 3).reshape(2, shard, 3 * width)
        gathered = []
        for halves in (split, proj.reshape(shard, 2, width).transpose(1, 0, 2), jnp.stack([packed, packed])):
            own = lax.dynamic_index_in_dim(halves, core, 0, keepdims=False)
            other = swap(lax.dynamic_index_in_dim(halves, 1 - core, 0, keepdims=False))
            block = jnp.where(core == 0, jnp.stack([own, other]), jnp.stack([other, own]))
            gathered.append(lax.all_gather(block, AX, axis=0, axis_index_groups=same_core_groups()))
        return gathered
    chips = devices // 2
    return pl.pallas_call(
        gather_kernel,
        out_shape=[
            jax.ShapeDtypeStruct((chips, 2, shard, 3 * width), BF),
            jax.ShapeDtypeStruct((chips, 2, shard, width), BF),
            jax.ShapeDtypeStruct((chips, 2) + packed.shape, BF),
        ],
        in_specs=[pl.BlockSpec(memory_space=pltpu.VMEM)] * 3,
        out_specs=[pl.BlockSpec(memory_space=pl.ANY)] * 3,
        scratch_shapes=[
            pltpu.SemaphoreType.DMA((3,)),
            pltpu.SemaphoreType.DMA((3, 20)),
            pltpu.SemaphoreType.DMA((3, 20)),
        ],
        compiler_params=pltpu.CompilerParams(collective_id=0, has_side_effects=True),
        cost_estimate=pl.CostEstimate(flops=int(4e10), bytes_accessed=int(1.5e8), transcendentals=0),
        name="gather_chips",
    )(qkv, proj, packed)


def scatter_kernel(kinds, *refs):
    count = len(kinds)
    ins, outs = refs[:count], refs[count : 2 * count]
    scratch = refs[2 * count :]
    recv_a, recv_b = scratch[:count], scratch[count : 2 * count]
    recv_x, recv_y = scratch[2 * count : 3 * count], scratch[3 * count : 4 * count]
    recv_z, stage = scratch[4 * count : 5 * count], scratch[5 * count : 6 * count]
    land = scratch[6 * count : 7 * count]
    send_sem, recv_sem = scratch[7 * count :]
    me = lax.axis_index(AX)
    chip, core = me // 2, me % 2
    mate, peer_x, peer_y, peers_z = peers_of(me)
    meet([mate, peer_x, peer_y] + peers_z)
    chip_x, chip_y = flip(chip, 1), flip(chip, 2)
    chip_xy = flip(chip_x, 2)
    pending = []

    def send(w, slot, block, target, peer):
        copy = pltpu.make_async_remote_copy(
            src_ref=block, dst_ref=target, send_sem=send_sem.at[w, slot], recv_sem=recv_sem.at[w, slot],
            device_id=(peer,), device_id_type=MESH,
        )
        copy.start()
        pending.append(copy)

    def arrive(w, slot, block):
        pltpu.make_async_remote_copy(
            src_ref=block, dst_ref=block, send_sem=send_sem.at[w, slot], recv_sem=recv_sem.at[w, slot],
            device_id=(mate,), device_id_type=MESH,
        ).wait_recv()

    order = (1, 2, 3, 0)

    def first(w):
        for j in order:
            block = ins[w].at[zflip(chip_xy, j)]
            send(w, j, block.at[0], recv_a[w].at[j], peer_y)
            send(w, 4 + j, block.at[1], recv_b[w].at[j], peer_x)
        for j in order:
            send(w, 8 + j, ins[w].at[zflip(chip_x, j), 1], recv_x[w].at[j, 1], peer_x)
            send(w, 12 + j, ins[w].at[zflip(chip_y, j), 0], recv_y[w].at[j, 0], peer_y)

    def second(w):
        rows = ins[w].shape[2]
        for j in order:
            arrive(w, j, recv_a[w].at[j])

            @pl.loop(0, rows // 16)
            def _(i):
                part = pl.ds(pl.multiple_of(i * 16, 16), 16)
                total = recv_a[w][j, part].astype(F32) + ins[w][zflip(chip_x, j), 0, part].astype(F32)
                recv_a[w][j, part] = total.astype(BF)

            send(w, 16 + j, recv_a[w].at[j], recv_x[w].at[j, 0], peer_x)
            arrive(w, 4 + j, recv_b[w].at[j])

            @pl.loop(0, rows // 16)
            def _(i):
                part = pl.ds(pl.multiple_of(i * 16, 16), 16)
                total = recv_b[w][j, part].astype(F32) + ins[w][zflip(chip_y, j), 1, part].astype(F32)
                recv_b[w][j, part] = total.astype(BF)

            send(w, 20 + j, recv_b[w].at[j], recv_y[w].at[j, 1], peer_y)

    def third(w):
        rows = ins[w].shape[2]
        for j in (1, 2, 3):
            arrive(w, 8 + j, recv_x[w].at[j, 1])
            arrive(w, 12 + j, recv_y[w].at[j, 0])
            arrive(w, 16 + j, recv_x[w].at[j, 0])
            arrive(w, 20 + j, recv_y[w].at[j, 1])

            @pl.loop(0, 2 * (rows // 16))
            def _(i):
                half = i // (rows // 16)
                part = pl.ds(pl.multiple_of((i % (rows // 16)) * 16, 16), 16)
                total = recv_x[w][j, half, part].astype(F32) + recv_y[w][j, half, part].astype(F32)
                total = total + ins[w][zflip(chip, j), half, part].astype(F32)
                recv_x[w][j, half, part] = total.astype(BF)

            send(w, 23 + j, recv_x[w].at[j], recv_z[w].at[j - 1], peers_z[j - 1])

    def last(w):
        rows = ins[w].shape[2]
        for slot, block in ((8, recv_x[w].at[0, 1]), (12, recv_y[w].at[0, 0]), (16, recv_x[w].at[0, 0]), (20, recv_y[w].at[0, 1])):
            arrive(w, slot, block)
        for j in range(3):
            arrive(w, 24 + j, recv_z[w].at[j])

        def total_of(half, part):
            total = recv_x[w][0, half, part].astype(F32) + recv_y[w][0, half, part].astype(F32)
            total = total + ins[w][chip, half, part].astype(F32)
            for j in range(3):
                total = total + recv_z[w][j, half, part].astype(F32)
            return total

        @pl.loop(0, rows // 16)
        def _(i):
            part = pl.ds(pl.multiple_of(i * 16, 16), 16)
            stage[w][part] = total_of(1 - core, part)

        send(w, 27, stage[w], land[w], mate)

        @pl.loop(0, rows // 16)
        def _(i):
            part = pl.ds(pl.multiple_of(i * 16, 16), 16)
            place(w, part, total_of(core, part), core)

    def place(w, part, total, half):
        if kinds[w] == "sum":
            outs[w][part] = total
            return
        size = total.shape[1] // kinds[w]
        for t in range(kinds[w]):
            start = pl.multiple_of((2 * t + half) * size, 128)
            outs[w][part, pl.ds(start, size)] = total[:, t * size : (t + 1) * size]

    for w in range(count):
        first(w)
        if w >= 1:
            second(w - 1)
        if w >= 2:
            third(w - 2)
    second(count - 1)
    for w in range(max(count - 2, 0), count):
        third(w)
    for w in range(count):
        last(w)
    for w in range(count):
        arrive(w, 27, land[w])

        @pl.loop(0, stage[w].shape[0] // 16)
        def _(i):
            part = pl.ds(pl.multiple_of(i * 16, 16), 16)
            other = land[w][part]
            if kinds[w] == "sum":
                other = other + outs[w][part]
            place(w, part, other, 1 - core)

    for copy in pending:
        copy.wait_send()


def scatter_chips(grads, kinds):
    devices = lax.axis_size(AX)
    shapes = [g.shape for g in grads]
    if devices != 32:
        core = lax.axis_index(AX) % 2
        summed = []
        for grad, kind in zip(grads, kinds):
            block = lax.psum_scatter(grad, AX, scatter_dimension=0, axis_index_groups=same_core_groups())
            block = block.astype(F32)
            own = lax.dynamic_index_in_dim(block, core, 0, keepdims=False)
            other = swap(lax.dynamic_index_in_dim(block, 1 - core, 0, keepdims=False))
            if kind == "sum":
                summed.append(own + other)
                continue
            rows, columns = own.shape
            own = own.reshape(rows, kind, 1, columns // kind)
            other = other.reshape(rows, kind, 1, columns // kind)
            summed.append(by_core(core, own, other, 2).reshape(rows, 2 * columns))
        return summed
    count = len(grads)
    scratch = [pltpu.VMEM((4,) + s[2:], BF) for s in shapes] * 2
    scratch += [pltpu.VMEM((4, 2) + s[2:], BF) for s in shapes] * 2
    scratch += [pltpu.VMEM((3, 2) + s[2:], BF) for s in shapes]
    scratch += [pltpu.VMEM(s[2:], F32) for s in shapes] * 2
    scratch += [pltpu.SemaphoreType.DMA((count, 28)), pltpu.SemaphoreType.DMA((count, 28))]
    return pl.pallas_call(
        functools.partial(scatter_kernel, kinds),
        out_shape=[
            jax.ShapeDtypeStruct((s[2], s[3] * (1 if kind == "sum" else 2)), F32) for s, kind in zip(shapes, kinds)
        ],
        in_specs=[pl.BlockSpec(memory_space=pltpu.VMEM)] * count,
        out_specs=[pl.BlockSpec(memory_space=pltpu.VMEM)] * count,
        scratch_shapes=scratch,
        compiler_params=pltpu.CompilerParams(
            collective_id=1, has_side_effects=True, vmem_limit_bytes=56 << 20
        ),
        name="scatter_chips",
    )(*grads)


def flat(ref):
    return ref[...].reshape(-1, ref.shape[-1])


def head_masks():
    lane = lax.broadcasted_iota(jnp.int32, (1, 2 * HEAD), 1)
    return [(lane < HEAD).astype(BF), (lane >= HEAD).astype(BF)]


def attend_kernel(chunk, q_ref, k_ref, v_ref, penalty_ref, out_ref, log_ref):
    slots = 2 * q_ref.shape[2]
    all_queries, keys, values = flat(q_ref), flat(k_ref), flat(v_ref)
    values_t = values.T
    penalty = flat(penalty_ref)
    masks = head_masks()
    mixed_all = []
    for start in range(0, slots, chunk):
        queries = all_queries[start : start + chunk] * jnp.asarray(0.125, BF)
        parts = []
        for h in range(2):
            scores = product_right_t(keys, queries * masks[h]) + penalty
            top = jnp.max(scores, axis=0, keepdims=True)
            exponent = jnp.exp(scores - top)
            total = jnp.sum(exponent, axis=0, keepdims=True)
            mixed = product(values_t[h * HEAD : (h + 1) * HEAD], exponent.astype(BF))
            parts.append(mixed * (1.0 / total))
            log_ref[0, 0, h : h + 1, start : start + chunk] = top + jnp.log(total)
        mixed_all.append(jnp.concatenate(parts, 0).T.astype(BF))
    out_ref[...] = jnp.concatenate(mixed_all, 0).reshape(out_ref.shape)


def attend(projected, penalty):
    _, clips, rows, triple = projected.shape
    slots = 2 * rows
    width = triple // 3
    pairs = width // (2 * HEAD)

    def block(offset):
        return pl.BlockSpec((2, 1, rows, 2 * HEAD), lambda i, j: (0, i, 0, offset * pairs + j))

    return pl.pallas_call(
        functools.partial(attend_kernel, 256),
        grid=(clips, pairs),
        in_specs=[block(0), block(1), block(2), pl.BlockSpec((2, 1, rows, 1), lambda i, j: (0, i, 0, 0))],
        out_specs=[block(0), pl.BlockSpec((1, 1, 2, slots), lambda i, j: (i, j, 0, 0))],
        out_shape=[
            jax.ShapeDtypeStruct((2, clips, rows, width), BF),
            jax.ShapeDtypeStruct((clips, pairs, 2, slots), F32),
        ],
        compiler_params=pltpu.CompilerParams(vmem_limit_bytes=48 << 20),
        cost_estimate=pl.CostEstimate(
            flops=4 * clips * pairs * slots * slots * 2 * HEAD, bytes_accessed=8 * clips * slots * width,
            transcendentals=clips * pairs * 2 * slots * slots,
        ),
        name="attend",
    )(projected, projected, projected, penalty)


def attend_back_kernel(chunk, q_ref, k_ref, v_ref, penalty_ref, log_ref, att_ref, grad_ref, out_ref, bias_ref):
    rows = q_ref.shape[2]
    slots = 2 * rows
    pair = pl.program_id(1)
    width = out_ref.shape[3] // 3
    all_queries, keys, values = flat(q_ref), flat(k_ref), flat(v_ref)
    all_grads, all_mixed = flat(grad_ref), flat(att_ref)
    keys_t = keys.T
    penalty = flat(penalty_ref)
    query_grads = []

    def keep(offset, value):
        columns = pl.ds(pl.multiple_of(offset + pair * 2 * HEAD, 128), 2 * HEAD)
        for side in range(2):
            out_ref[side, 0, :, columns] = value[side * rows : (side + 1) * rows]

    masks = head_masks()
    grad_keys = jnp.zeros((slots, 2 * HEAD), F32)
    grad_values = jnp.zeros((slots, 2 * HEAD), F32)
    query_bias = jnp.zeros((1, 2 * HEAD), F32)
    for start in range(0, slots, chunk):
        queries = all_queries[start : start + chunk] * jnp.asarray(0.125, BF)
        grads = all_grads[start : start + chunk]
        overlap = (grads.astype(F32) * all_mixed[start : start + chunk].astype(F32)).T
        parts = []
        for h in range(2):
            head_queries = queries * masks[h]
            head_grads = grads * masks[h]
            correction = jnp.sum(overlap[h * HEAD : (h + 1) * HEAD], axis=0, keepdims=True)
            logs = log_ref[0, 0, h : h + 1, start : start + chunk]
            soft = jnp.exp(product_right_t(keys, head_queries) + penalty - logs)
            grad_soft = product_right_t(values, head_grads)
            grad_values += product(soft.astype(BF), head_grads)
            grad_scores = (soft * (grad_soft - correction)).astype(BF)
            grad_keys += product(grad_scores, head_queries)
            parts.append(product(keys_t[h * HEAD : (h + 1) * HEAD], grad_scores))
        grad_queries = jnp.concatenate(parts, 0).T * 0.125
        query_bias += jnp.sum(grad_queries, axis=0, keepdims=True)
        query_grads.append(grad_queries.astype(BF))
    keep(0, jnp.concatenate(query_grads, 0))
    keep(width, grad_keys.astype(BF))
    keep(2 * width, grad_values.astype(BF))
    bias_ref[0, 0, 0:1] = query_bias
    bias_ref[0, 0, 1:2] = jnp.sum(grad_values, axis=0, keepdims=True)


def attend_back(projected, penalty, logs, attended, grad_attended):
    _, clips, rows, triple = projected.shape
    slots = 2 * rows
    width = triple // 3
    pairs = width // (2 * HEAD)

    def block(offset):
        return pl.BlockSpec((2, 1, rows, 2 * HEAD), lambda i, j: (0, i, 0, offset * pairs + j))

    return pl.pallas_call(
        functools.partial(attend_back_kernel, 256),
        grid=(clips, pairs),
        in_specs=[
            block(0), block(1), block(2),
            pl.BlockSpec((2, 1, rows, 1), lambda i, j: (0, i, 0, 0)),
            pl.BlockSpec((1, 1, 2, slots), lambda i, j: (i, j, 0, 0)),
            block(0), block(0),
        ],
        out_specs=[
            pl.BlockSpec((2, 1, rows, triple), lambda i, j: (0, i, 0, 0)),
            pl.BlockSpec((1, 1, 2, 2 * HEAD), lambda i, j: (i, j, 0, 0)),
        ],
        out_shape=[
            jax.ShapeDtypeStruct((2, clips, rows, triple), BF),
            jax.ShapeDtypeStruct((clips, pairs, 2, 2 * HEAD), F32),
        ],
        compiler_params=pltpu.CompilerParams(vmem_limit_bytes=56 << 20),
        cost_estimate=pl.CostEstimate(
            flops=10 * clips * pairs * slots * slots * 2 * HEAD, bytes_accessed=18 * clips * slots * width,
            transcendentals=clips * pairs * 2 * slots * slots,
        ),
        name="attend_back",
    )(projected, projected, projected, penalty, logs, attended, grad_attended)


def normal_parts(values):
    average = jnp.mean(values, axis=-1, keepdims=True)
    centered = values - average
    inverse = lax.rsqrt(jnp.mean(centered * centered, axis=-1, keepdims=True) + EPSILON)
    return centered * inverse, inverse


def normal_back(grad_normed, scaled, inverse, gain):
    grad_scaled = grad_normed * gain
    first_mean = jnp.mean(grad_scaled, axis=-1, keepdims=True)
    second_mean = jnp.mean(grad_scaled * scaled, axis=-1, keepdims=True)
    return inverse * (grad_scaled - first_mean - scaled * second_mean)


def rows_spec(size, columns):
    return pl.BlockSpec((size, columns), lambda i: (i, 0))


def whole_spec(shape):
    return pl.BlockSpec(shape, lambda i: (0,) * len(shape), pipeline_mode=pl.Buffered(1))


PARAMS = pltpu.CompilerParams(vmem_limit_bytes=56 << 20)


def first_norm_kernel(steps, own_ref, other_ref, gain_ref, shift_ref, out_ref):
    def put(ref):
        scaled, _ = normal_parts(ref[...].astype(F32))
        out_ref[...] = (scaled * gain_ref[...] + shift_ref[...]).astype(BF)

    pl.when(pl.program_id(0) < steps)(lambda: put(own_ref))
    pl.when(pl.program_id(0) >= steps)(lambda: put(other_ref))


def first_norm(own, other, gain, shift):
    rows, features = own.shape
    steps = 3
    size = rows // steps
    return pl.pallas_call(
        functools.partial(first_norm_kernel, steps),
        grid=(2 * steps,),
        in_specs=[
            pl.BlockSpec((size, features), lambda i: (jnp.minimum(i, steps - 1), 0)),
            pl.BlockSpec((size, features), lambda i: (jnp.maximum(i - steps, 0), 0)),
            whole_spec((1, features)),
            whole_spec((1, features)),
        ],
        out_specs=rows_spec(size, features),
        out_shape=jax.ShapeDtypeStruct((2 * rows, features), BF),
        compiler_params=PARAMS,
        name="first_norm",
    )(own, other, gain, shift)


def second_norm_kernel(att_ref, weight_ref, token_ref, recv_ref, bias_ref, gain_ref, shift_ref, middle_ref, out_ref):
    middle = token_ref[...].astype(F32) + product(att_ref[...], weight_ref[...])
    middle = middle + recv_ref[...].astype(F32) + bias_ref[...]
    middle_ref[...] = middle
    scaled, _ = normal_parts(middle)
    out_ref[...] = (scaled * gain_ref[...] + shift_ref[...]).astype(BF)


def second_norm(attended, weight, tokens, received, bias, gain, shift):
    rows, features = tokens.shape
    width = weight.shape[0]
    size = rows // 4
    return pl.pallas_call(
        second_norm_kernel,
        grid=(4,),
        in_specs=[
            rows_spec(size, width), whole_spec((width, features)), rows_spec(size, features), rows_spec(size, features),
            whole_spec((1, features)), whole_spec((1, features)), whole_spec((1, features)),
        ],
        out_specs=[rows_spec(size, features), rows_spec(size, features)],
        out_shape=[jax.ShapeDtypeStruct((rows, features), F32), jax.ShapeDtypeStruct((rows, features), BF)],
        compiler_params=PARAMS,
        name="second_norm",
    )(attended, weight, tokens, received, bias, gain, shift)


def lift_kernel(steps, unit, own_ref, other_ref, weight_ref, bias_ref, act_ref, slope_ref, norm_ref, half_ref):
    step = pl.program_id(0)
    hidden = half_ref.shape[1]

    @pl.when(step == 0)
    def _():
        if weight_ref.shape[1] == hidden:
            half_ref[...] = weight_ref[...]
        else:
            core = lax.axis_index(AX) % 2
            for k in range(hidden // unit):
                start = pl.multiple_of((2 * k + core) * unit, unit)
                half_ref[:, k * unit : (k + 1) * unit] = weight_ref[:, pl.ds(start, unit)]

    def put(ref):
        rows = ref[...]
        norm_ref[...] = rows
        size = 512
        for start in range(0, hidden, size):
            part = slice(start, start + size)
            pre = product(rows, half_ref[:, part]) + bias_ref[:, part]
            normal_cdf = 0.5 * (1.0 + lax.erf(pre * ROOT_HALF))
            density = jnp.exp(-0.5 * pre * pre) * INV_ROOT_TWO_PI
            act_ref[:, part] = (pre * normal_cdf).astype(BF)
            slope_ref[:, part] = (normal_cdf + pre * density).astype(BF)

    pl.when(step < steps)(lambda: put(own_ref))
    pl.when(step >= steps)(lambda: put(other_ref))


def lift(own, other, weight, bias, unit):
    rows, features = own.shape
    hidden = bias.shape[1]
    steps = 3
    size = rows // steps
    return pl.pallas_call(
        functools.partial(lift_kernel, steps, unit),
        grid=(2 * steps,),
        in_specs=[
            pl.BlockSpec((size, features), lambda i: (jnp.minimum(i, steps - 1), 0)),
            pl.BlockSpec((size, features), lambda i: (jnp.maximum(i - steps, 0), 0)),
            whole_spec(weight.shape),
            whole_spec((1, hidden)),
        ],
        out_specs=[
            rows_spec(size, hidden), rows_spec(size, hidden), rows_spec(size, features),
            pl.BlockSpec((features, hidden), lambda i: (0, 0)),
        ],
        out_shape=[
            jax.ShapeDtypeStruct((2 * rows, hidden), BF), jax.ShapeDtypeStruct((2 * rows, hidden), BF),
            jax.ShapeDtypeStruct((2 * rows, features), BF), jax.ShapeDtypeStruct((features, hidden), BF),
        ],
        compiler_params=PARAMS,
        cost_estimate=pl.CostEstimate(
            flops=4 * rows * features * hidden, bytes_accessed=4 * features * hidden, transcendentals=4 * rows * hidden
        ),
        name="lift",
    )(own, other, weight, bias)


def gather_sums(sums_ref, values):
    @pl.when(pl.program_id(0) == 0)
    def _():
        sums_ref[...] = jnp.zeros_like(sums_ref)

    for index, value in enumerate(values):
        sums_ref[index : index + 1] += jnp.sum(value, axis=0, keepdims=True)


def second_back_kernel(
    grad_ref, weight_ref, recv_ref, middle_ref, out_ref, gain_ref, full_ref, low_ref, sums_ref
):
    grad_normed = product_right_t(grad_ref[...], weight_ref[...]) + recv_ref[...].astype(F32)
    scaled, inverse = normal_parts(middle_ref[...])
    grad_out = out_ref[...].astype(F32)
    grad_middle = grad_out + normal_back(grad_normed, scaled, inverse, gain_ref[...])
    full_ref[...] = grad_middle
    low_ref[...] = grad_middle.astype(BF)
    gather_sums(sums_ref, [grad_normed * scaled, grad_normed, grad_middle, grad_out])


def second_back(grad_pre, weight, received, middle, grad_out, gain):
    rows, features = middle.shape
    hidden = weight.shape[1]
    size = rows // 4
    return pl.pallas_call(
        second_back_kernel,
        grid=(4,),
        in_specs=[
            rows_spec(size, hidden), whole_spec((features, hidden)), rows_spec(size, features),
            rows_spec(size, features), rows_spec(size, features), whole_spec((1, features)),
        ],
        out_specs=[rows_spec(size, features), rows_spec(size, features), pl.BlockSpec((8, features), lambda i: (0, 0))],
        out_shape=[
            jax.ShapeDtypeStruct((rows, features), F32), jax.ShapeDtypeStruct((rows, features), BF),
            jax.ShapeDtypeStruct((8, features), F32),
        ],
        compiler_params=PARAMS,
        name="second_back",
    )(grad_pre, weight, received, middle, grad_out, gain)


def first_back_kernel(grad_ref, weight_ref, recv_ref, token_ref, middle_ref, gain_ref, full_ref, sums_ref):
    grad_normed = product_right_t(grad_ref[...], weight_ref[...]) + recv_ref[...].astype(F32)
    scaled, inverse = normal_parts(token_ref[...].astype(F32))
    full_ref[...] = middle_ref[...] + normal_back(grad_normed, scaled, inverse, gain_ref[...])
    gather_sums(sums_ref, [grad_normed * scaled, grad_normed])


def first_back(grad_projected, weight, received, tokens, grad_middle, gain):
    rows, features = tokens.shape
    triple = weight.shape[1]
    size = rows // 4
    return pl.pallas_call(
        first_back_kernel,
        grid=(4,),
        in_specs=[
            rows_spec(size, triple), whole_spec((features, triple)), rows_spec(size, features),
            rows_spec(size, features), rows_spec(size, features), whole_spec((1, features)),
        ],
        out_specs=[rows_spec(size, features), pl.BlockSpec((8, features), lambda i: (0, 0))],
        out_shape=[jax.ShapeDtypeStruct((rows, features), F32), jax.ShapeDtypeStruct((8, features), F32)],
        compiler_params=PARAMS,
        name="first_back",
    )(grad_projected, weight, received, tokens, grad_middle, gain)


def by_core(core, own, other, axis):
    return jnp.where(core == 0, jnp.concatenate([own, other], axis), jnp.concatenate([other, own], axis))


def per_device(
    tokens, valid_slots, cotangent, first_gain, first_shift, qkv_weight, query_bias, value_bias, proj_weight,
    proj_bias, second_gain, second_shift, up_weight, up_bias, down_weight, down_bias,
):
    devices = lax.axis_size(AX)
    chips = devices // 2
    core = lax.axis_index(AX) % 2
    micro, rows, features = tokens.shape
    shard = qkv_weight.shape[0]
    width = features // 2
    hidden = up_weight.shape[1] // 2
    unit = hidden // chips
    own_rows = micro * rows
    every = 2 * own_rows

    weight_up = lax.all_gather(up_weight, AX, axis=0, tiled=True)
    weight_down = lax.all_gather(down_weight, AX, axis=0, tiled=True, axis_index_groups=same_core_groups())
    if unit % 128 != 0:
        weight_up = lax.dynamic_index_in_dim(weight_up.reshape(features, chips, 2, unit), core, 2, keepdims=False)
        weight_up = weight_up.reshape(features, hidden)
    vectors = jnp.stack(
        [first_gain, first_shift, query_bias, value_bias, proj_bias, second_gain, second_shift, down_bias], 0
    )
    lanes = max(PARAM_COLS, unit)
    vectors = jnp.pad(vectors.T, ((0, 16), (0, lanes - 8)))
    packed = lax.dynamic_update_slice(vectors, up_bias[None, :], (shard, 0))
    qkv_all, proj_all, packed_all = gather_chips(qkv_weight, proj_weight, packed)
    weight_qkv = qkv_all.reshape(features, 3 * width)
    params = packed_all[:, :, :shard, :8].astype(F32).reshape(features, 8).T
    gain_one, shift_one, bias_query, bias_value, bias_proj, gain_two, shift_two, bias_down = [
        params[i : i + 1] for i in range(8)
    ]
    bias_up = lax.dynamic_index_in_dim(packed_all[:, :, shard, :unit], core, 1, keepdims=False)
    bias_up = bias_up.astype(F32).reshape(1, hidden)
    proj_cols = proj_all.reshape(2, width, width)
    proj_own = lax.dynamic_index_in_dim(proj_cols, core, 0, keepdims=False)
    proj_other = swap(lax.dynamic_index_in_dim(proj_cols, 1 - core, 0, keepdims=False))
    weight_proj = by_core(core, proj_own, proj_other, 1)
    qkv_bias = jnp.concatenate(
        [
            lax.dynamic_slice_in_dim(bias_query, core * width, width, 1),
            jnp.zeros((1, width), F32),
            lax.dynamic_slice_in_dim(bias_value, core * width, width, 1),
        ],
        1,
    )

    own_tokens = tokens.reshape(own_rows, features)
    other_tokens = swap(own_tokens)
    marks = jnp.stack([valid_slots, swap(valid_slots)])
    own_cotangent = cotangent.reshape(own_rows, features)
    grad_out = jnp.concatenate([own_cotangent, swap(own_cotangent)], 0)
    grad_out = grad_out * (marks > 0).astype(BF).reshape(every, 1)
    penalty = jnp.where(marks > 0, 0.0, -1000000000.0).astype(F32)[..., None]
    norm_one = first_norm(own_tokens, other_tokens, gain_one, shift_one)
    projected = (product(norm_one, weight_qkv) + qkv_bias).astype(BF).reshape(2, micro, rows, 3 * width)
    attended, logs = attend(projected, penalty)
    attended_flat = attended.reshape(every, width)
    mixed = swap(product(attended_flat[own_rows:], weight_proj).astype(BF))
    middle, norm_own = second_norm(
        attended_flat, weight_proj, own_tokens, mixed, bias_proj, gain_two, shift_two
    )
    activation, slope, norm_two, weight_half = lift(norm_own, swap(norm_own), weight_up, bias_up, unit)
    lifted = swap(product(activation[own_rows:], weight_down).astype(BF))
    lifted = product(activation[:own_rows], weight_down) + lifted.astype(F32)
    block_output = (middle + lifted + bias_down).astype(BF).reshape(micro, rows, features)

    grad_pre_full = product_right_t(grad_out, weight_down) * slope.astype(F32)
    grad_bias_up = jnp.sum(grad_pre_full, axis=0)
    grad_pre = grad_pre_full.astype(BF)
    grad_down = product_left_t(activation, grad_out).astype(BF)
    down_weight_grad = lax.psum_scatter(
        grad_down, AX, scatter_dimension=0, tiled=True, axis_index_groups=same_core_groups()
    ).astype(F32)
    passed = swap(product_right_t(grad_pre[own_rows:], weight_half).astype(BF))
    grad_middle, grad_low, second_sums = second_back(
        grad_pre, weight_half, passed, middle, grad_out, gain_two
    )
    grad_up = product_left_t(norm_two, grad_pre).astype(BF)
    grad_low = jnp.concatenate([grad_low, swap(grad_low)], 0)
    grad_attended = product_right_t(grad_low, weight_proj).astype(BF).reshape(2, micro, rows, width)
    grad_proj = product_left_t(attended_flat, grad_low).astype(BF)
    grad_proj_own = lax.dynamic_slice_in_dim(grad_proj, core * width, width, 1)
    grad_proj_other = swap(lax.dynamic_slice_in_dim(grad_proj, (1 - core) * width, width, 1))
    grad_proj = by_core(core, grad_proj_own, grad_proj_other, 0)
    grad_projected, grad_bias = attend_back(projected, penalty, logs, attended, grad_attended)
    grad_projected = grad_projected.reshape(every, 3 * width)
    passed = swap(product_right_t(grad_projected[own_rows:], weight_qkv).astype(BF))
    grad_qkv = product_left_t(norm_one, grad_projected).astype(BF)
    tokens_grad, first_sums = first_back(
        grad_projected, weight_qkv, passed, own_tokens, grad_middle, gain_one
    )
    tokens_grad = tokens_grad.reshape(micro, rows, features)

    grad_bias = jnp.sum(grad_bias, axis=0).transpose(1, 0, 2).reshape(2, width)
    grad_bias = by_core(core, grad_bias, jnp.zeros_like(grad_bias), 1)
    sums = jnp.concatenate([first_sums[:2], grad_bias, second_sums[2:3], second_sums[:2], second_sums[3:4]], 0)
    sums = sums.astype(BF).T.reshape(chips, 2, shard, 8)
    sums = jnp.pad(sums, ((0, 0), (0, 0), (0, 16), (0, lanes - 8)))
    up_units = grad_bias_up.astype(BF).reshape(chips, 1, unit)
    up_units = by_core(core, up_units, jnp.zeros_like(up_units), 1)
    sums = lax.dynamic_update_slice(sums, up_units.reshape(chips, 2, 1, unit), (0, 0, shard, 0))
    up_weight_grad, qkv_weight_grad, proj_weight_grad, packed_sum = scatter_chips(
        [
            grad_up.reshape(chips, 2, shard, hidden),
            grad_qkv.reshape(chips, 2, shard, 3 * width),
            grad_proj.reshape(chips, 2, shard, width),
            sums,
        ],
        (chips, 3, 1, "sum"),
    )
    up_bias_grad = packed_sum[shard, :unit]
    vector_sum = packed_sum[:shard, :8].T
    return (
        block_output, tokens_grad, vector_sum[0], vector_sum[1], qkv_weight_grad, vector_sum[2], vector_sum[3],
        proj_weight_grad, vector_sum[4], vector_sum[5], vector_sum[6], up_weight_grad, up_bias_grad,
        down_weight_grad, vector_sum[7],
    )


def solution(mesh):
    row = P(None, AX, None)
    vec = P(AX)
    mat = P(AX, None)
    return jax.shard_map(
        per_device,
        mesh=mesh,
        in_specs=(row, P(None, AX), row, vec, vec, mat, vec, vec, mat, vec, vec, vec, mat, vec, mat, vec),
        out_specs=(row, row, vec, vec, mat, vec, vec, mat, vec, vec, vec, mat, vec, mat, vec),
        check_vma=False,
    )
```

time: 489 us -> 444 us (0.908)
  other arithmetic: 54.1 us -> 9.4 us
  local copies, waits for them, and re-layouts: 67.2 us -> 28.2 us
  Pallas kernels: 246 us -> 282 us
  waiting for transfers between devices: 0.07 us -> 25.9 us
  matrix products: 98 us -> 72.3 us
    pallas_call x2 -> x7, Pallas kernels: 187 us -> 223 us  [the longest x1 104 us: scatter_chips(): pl.pallas_call(functools.partial(scatter_kernel, kinds), out_shape=[jax.S...]
    reduce_sum x9 -> x1, other arithmetic: 23.4 us -> 0.02 us  [per_device(): grad_bias = jnp.sum(grad_bias, axis=0).transpose(1, 0, 2).reshape(2, width)]
    all_gather x1, waiting for transfers between devices: 0.01 us -> 23 us  [per_device(): lax.all_gather(down_weight, AX, axis=0, tiled=True, axis_index_groups=sam...]
    dot_general x4, matrix products: 36.3 us -> 21.7 us  [product_right_t(): lax.dot_general(left_side, right_side, (((1,), (1,)), ((), ())), preferre...]
    reshape x14 -> x1, local copies, waits for them, and re-layouts: 13.4 us -> 0.02 us  [per_device(): up_units.reshape(chips, 2, 1, unit)]
    another operation x10 -> x0, local copies, waits for them, and re-layouts: 8.43 us -> none  [the longest x8 6.57 us: per_device(): jnp.stack([over_rows(grad_norm_one * hat_own), over_rows(grad_norm_one),...]
    dot_general x4, matrix products: 31.8 us -> 24.4 us  [product(): return jnp.dot(left_side, right_side, preferred_element_type=F32)]
    concatenate x6 -> x0, other arithmetic: 6.91 us -> none  [the longest x1 2.98 us: per_device(): jnp.concatenate([grad_qkv, sums], 1)]
  transfers between devices with their start and end apart: 13 -> 14, of which waited for: 0 -> 2; matrix products, arithmetic and copies ran while one was open for 38% -> 18% of each run, Pallas kernels for 51% -> 65%
where the time goes in v2:
time: 444 us; the launch traced here: 435 us
  Pallas kernels  282 us (64%)
  matrix products  72.3 us (16%)
  local copies, waits for them, and re-layouts  28.2 us (6%)
  waiting for transfers between devices  25.9 us (6%)
  between operations  14.5 us (3%)
  other arithmetic  9.4 us (2%)
    pallas_call x1, Pallas kernels, scatter_chips(): pl.pallas_call(functools.partial(scatter_kernel, kinds), out_shape=[jax.S...  104 us
    pallas_call x1, Pallas kernels, gather_chips(): pl.pallas_call(gather_kernel, out_shape=[jax.ShapeDtypeStruct((chips, 2,...  62.6 us
    pallas_call x1, Pallas kernels, attend_back(): pl.pallas_call(functools.partial(attend_back_kernel, 256), grid=(clips, p...  29.4 us
    pallas_call x1, Pallas kernels, attend(): pl.pallas_call(functools.partial(attend_kernel, 256), grid=(clips, pairs)...  29.1 us
    dot_general x4, matrix products, product_left_t(): lax.dot_general(left_side, right_side, (((0,), (0,)), ((), ())), preferre...  26.2 us
    dot_general x4, matrix products, product(): return jnp.dot(left_side, right_side, preferred_element_type=F32)  24.4 us
    all_gather x1, waiting for transfers between devices, per_device(): lax.all_gather(down_weight, AX, axis=0, tiled=True, axis_index_groups=sam...  23 us
    dot_general x4, matrix products, product_right_t(): lax.dot_general(left_side, right_side, (((1,), (1,)), ((), ())), preferre...  21.7 us
  transfers between devices with their start and end apart: 14, of which 2 were waited for; matrix products, arithmetic and copies ran while one was open for 18% of the time, Pallas kernels for 65%

profile of v2, /device:TPU:0, one launch (start us, length us, event | category | flops | bytes accessed | tf_op | source)
XLA Modules:
  0.0 435.5 jit_solution(8687389660327586393)
XLA Ops:
  7.2 0.7 all-gather.3.cloned.1.call-update
  8.0 0.6 collective-permute-start
  8.7 0.8 stack.50
  9.6 0.7 dynamic_update_slice.6.packed_ref
  10.3 0.6 copy-done.19
  10.9 62.6 %gather_chips.1 = (bf16[16,2,32,1536]{3,2,1,0:T(8,128)(2,1)}, bf16[16,2,32,512]{3,2,1,0:T(8,128)(2,1)}, bf16[16,2,48,128]{3,2,1,0:T(8,128)(2,1)}) custom-call(bf16[32,3072]{1,0:T(8,128)(2,1)} %qkv_ref.1, bf16[32,1024]{1,0:T(8,128)(2,1)} %proj_ref.1, bf16[48,128]{1,0:T(8,128)(2,1)} %copy-done.19), custom_call_target="tpu_custom_call" | custom-call | flops 40000000000 | bytes 150000000 | tf_op jit(solution)/shard_map/gather_chips/pallas_call | solution.py:154
  73.5 2.1 dynamic-slice_bitcast_fusion.1
  75.6 1.0 slice.97
  76.6 0.2 copy.65
  76.8 0.6 fusion.17
  77.5 0.4 copy.62
  78.0 1.8 maximum_select_fusion.weight_ref
  79.9 1.2 copy-done.15
  81.0 6.4 %first_norm.1 = bf16[1536,1024]{1,0:T(8,128)(2,1)} custom-call(bf16[768,1024]{1,0:T(8,128)(2,1)} %bitcast.79, bf16[768,1024]{1,0:T(8,128)(2,1)} %copy-done.15, f32[1,1024]{1,0:T(1,128)} %get-tuple-element.80.gain_ref, f32[1,1024]{1,0:T(1,128)} %get-tuple-element.79.shift_ref), custom_call_target="tpu_custom_call" | custom-call | tf_op jit(solution)/shard_map/first_norm/pallas_call | solution.py:534
  87.5 8.7 %add_convert_fusion = bf16[1536,1536]{1,0:T(8,128)(2,1)} fusion(bf16[1536,1024]{1,0:T(8,128)(2,1)} %first_norm.1, bf16[1024,1536]{1,0:T(8,128)(2,1)S(1)} %bitcast.92, f32[1536]{0:T(1024)S(1)} %fusion.15), kind=kOutput, calls=%fused_computation.1 | convolution fusion | flops 4836556800 | bytes 11016192 | tf_op jit(solution)/shard_map/dot_general | solution.py:22
  96.2 29.1 %attend.1 = (bf16[2,2,384,512]{3,2,1,0:T(8,128)(2,1)S(1)}, f32[2,4,2,768]{3,2,1,0:T(2,128)S(1)}) custom-call(bf16[2,2,384,1536]{3,2,1,0:T(8,128)(2,1)} %bitcast.120, bf16[2,2,384,1536]{3,2,1,0:T(8,128)(2,1)} %bitcast.121, bf16[2,2,384,1536]{3,2,1,0:T(8,128)(2,1)} %bitcast.122, f32[2,2,384,1]{3,2,1,0:T(8,128)S(1)} %broadcast_select_fusion.penalty_ref), custom_call_target="tpu_custom_call" | custom-call | flops 2415919104 | bytes 6291456 | tf_op jit(solution)/shard_map/attend/pallas_call | solution.py:397
  125.3 0.6 copy-done.3
  126.0 1.0 convolution_convert_fusion.4
  126.9 0.5 collective-permute-start.3
  127.5 0.4 copy-done.14
  127.9 0.5 collective-permute-start.6
  128.4 2.2 collective-permute-done.3.recv_ref
  130.5 1.1 copy-done.16
  131.7 6.0 %second_norm.1 = (f32[768,1024]{1,0:T(8,128)}, bf16[768,1024]{1,0:T(8,128)(2,1)}) custom-call(bf16[1536,512]{1,0:T(8,128)(2,1)} %bitcast.76, bf16[512,1024]{1,0:T(8,128)(2,1)} %copy-done.7, bf16[768,1024]{1,0:T(8,128)(2,1)} %bitcast.80, bf16[768,1024]{1,0:T(8,128)(2,1)} %copy-done.16, f32[1,1024]{1,0:T(1,128)} %get-tuple-element.76.bias_ref, ...), custom_call_target="tpu_custom_call" | custom-call | tf_op jit(solution)/shard_map/second_norm/pallas_call | solution.py:562
  137.7 0.4 collective-permute-start.4
  138.1 0.8 slice.107
  138.9 0.6 bitcast_convert_fusion.1.bias_ref
  139.6 2.5 maximum_multiply_fusion.out_ref
  142.1 21.5 %lift.1 = (bf16[1536,2048]{1,0:T(8,128)(2,1)}, bf16[1536,2048]{1,0:T(8,128)(2,1)}, bf16[1536,1024]{1,0:T(8,128)(2,1)}, bf16[1024,2048]{1,0:T(8,128)(2,1)}) custom-call(bf16[768,1024]{1,0:T(8,128)(2,1)} %get-tuple-element.42.own_ref, bf16[768,1024]{1,0:T(8,128)(2,1)} %collective-permute-done.4.other_ref, ...), custom_call_target="tpu_custom_call" | custom-call | flops 6442450944 | bytes 8388608 | tf_op jit(solution)/shard_map/lift/pallas_call | solution.py:611
  163.6 23.0 %all-gather.5.cloned.1.call-done = bf16[2048,1024]{1,0:T(8,128)(2,1)} async-done(((bf16[128,1024]{1,0:T(8,128)(2,1)}), bf16[2048,1024]{1,0:T(8,128)(2,1)}) %all-gather.5.cloned.1.call-update) | async-done | bytes 4194320 | tf_op jit(solution)/shard_map/all_gather | solution.py:723
  186.5 10.2 %fusion.16 = (bf16[2048]{0:T(1024)(128)(2,1)S(1)}, bf16[1536,2048]{1,0:T(8,128)(2,1)S(1)}) fusion(bf16[1536,2048]{1,0:T(8,128)(2,1)} %get-tuple-element.45, bf16[1536,1024]{1,0:T(8,128)(2,1)S(1)} %maximum_multiply_fusion.out_ref, bf16[2048,1024]{1,0:T(8,128)(2,1)} %all-gather.5.cloned.1.call-done), kind=kOutput, calls=%fused_computation.51 | convolution fusion | flops 6455031808 | bytes 19927040 | tf_op jit(solution)/shard_map/dot_general | solution.py:30
  196.8 4.6 %fusion.9 = bf16[768,1024]{1,0:T(8,128)(2,1)} fusion(bf16[1024,2048]{1,0:T(8,128)(2,1)S(1)} %copy-done.6, bf16[1536,2048]{1,0:T(8,128)(2,1)S(1)} %get-tuple-element.68.grad_ref), kind=kOutput, calls=%fused_computation.16 | convolution fusion | flops 3222011904 | bytes 8912896 | tf_op jit(solution)/shard_map/dot_general | solution.py:30
  201.4 1.0 copy-done.23
  202.4 9.0 %convolution_convert_fusion = bf16[2048,1024]{1,0:T(8,128)(2,1)} fusion(bf16[1536,2048]{1,0:T(8,128)(2,1)S(1)} %copy-done.23, bf16[1536,1024]{1,0:T(8,128)(2,1)S(1)} %maximum_multiply_fusion.out_ref), kind=kOutput, calls=%fused_computation.2 | convolution fusion | flops 6444548096 | bytes 13631488 | tf_op jit(solution)/shard_map/dot_general | solution.py:26
  211.4 7.8 %fusion.6 = bf16[768,1024]{1,0:T(8,128)(2,1)} fusion(bf16[2048,1024]{1,0:T(8,128)(2,1)} %all-gather.5.cloned.1.call-done, bf16[1536,2048]{1,0:T(8,128)(2,1)} %get-tuple-element.43), kind=kOutput, calls=%fused_computation.15 | convolution fusion | flops 3222011904 | bytes 8912896 | tf_op jit(solution)/shard_map/dot_general | solution.py:22
  219.3 8.6 %convolution_convert_fusion.1 = bf16[1024,2048]{1,0:T(8,128)(2,1)} fusion(bf16[1536,1024]{1,0:T(8,128)(2,1)S(1)} %copy-done.24, bf16[1536,2048]{1,0:T(8,128)(2,1)S(1)} %bitcast.87), kind=kOutput, calls=%fused_computation.3 | convolution fusion | flops 6444548096 | bytes 13631488 | tf_op jit(solution)/shard_map/dot_general | solution.py:26
  227.9 12.5 %second_back.1 = (f32[768,1024]{1,0:T(8,128)}, bf16[768,1024]{1,0:T(8,128)(2,1)}, f32[8,1024]{1,0:T(8,128)}) custom-call(bf16[1536,2048]{1,0:T(8,128)(2,1)} %copy-done.5, bf16[1024,2048]{1,0:T(8,128)(2,1)} %get-tuple-element.46.weight_ref, bf16[768,1024]{1,0:T(8,128)(2,1)} %collective-permute-done.7.recv_ref, f32[768,1024]{1,0:T(8,128)} %get-tuple-element.41.middle_ref, ...), custom_call_target="tpu_custom_call" | custom-call | tf_op jit(solution)/shard_map/second_back/pallas_call | solution.py:661
  240.4 0.6 collective-permute-start.8
  241.0 1.1 convert.21
  242.0 1.5 constant_dynamic-update-slice_fusion.1
  243.6 7.0 %add_convert_fusion.1 = bf16[768,1024]{1,0:T(8,128)(2,1)} fusion(f32[768,1024]{1,0:T(8,128)S(1)} %copy-done.9, bf16[768,1024]{1,0:T(8,128)(2,1)} %collective-permute-done.5, f32[1024]{0:T(1024)S(1)} %bitcast.108, bf16[2048,1024]{1,0:T(8,128)(2,1)S(1)} %copy-done.22, bf16[1536,2048]{1,0:T(8,128)(2,1)} %get-tuple-element.43), kind=kOutput, calls=%fused_computation.8 | convolution fusion | flops 3225157632 | bytes 13635584 | tf_op jit(solution)/shard_map/dot_general | solution.py:22
  250.7 1.1 copy-done.8
  251.8 3.1 convolution_convert_fusion.3
  254.9 29.4 %attend_back.1 = (bf16[2,2,384,1536]{3,2,1,0:T(8,128)(2,1)}, f32[2,4,2,128]{3,2,1,0:T(2,128)}) custom-call(bf16[2,2,384,1536]{3,2,1,0:T(8,128)(2,1)} %bitcast.123, bf16[2,2,384,1536]{3,2,1,0:T(8,128)(2,1)} %bitcast.124, bf16[2,2,384,1536]{3,2,1,0:T(8,128)(2,1)} %bitcast.125, f32[2,2,384,1]{3,2,1,0:T(8,128)} %copy-done.2, f32[2,4,2,768]{3,2,1,0:T(2,128)} %copy-done.3, ...), custom_call_target="tpu_custom_call" | custom-call | flops 6039797760 | bytes 14155776 | tf_op jit(solution)/shard_map/attend_back/pallas_call | solution.py:470
  284.4 2.0 slice.112
  286.3 0.6 copy-done.12
  287.0 3.8 convolution_convert_fusion.5
  290.7 1.8 convolution_convert_fusion.6
  292.7 0.6 collective-permute-start.10
  293.3 6.8 %convolution_convert_fusion.2 = bf16[1024,1536]{1,0:T(8,128)(2,1)} fusion(bf16[1536,1024]{1,0:T(8,128)(2,1)S(1)} %copy-done.10, bf16[1536,1536]{1,0:T(8,128)(2,1)S(1)} %bitcast.85), kind=kOutput, calls=%fused_computation.4 | convolution fusion | flops 4833411072 | bytes 11010048 | tf_op jit(solution)/shard_map/dot_general | solution.py:26
  300.2 1.5 maximum_select_fusion.1
  301.6 1.2 copy-done.17
  302.8 9.9 %first_back.1 = (f32[768,1024]{1,0:T(8,128)}, f32[8,1024]{1,0:T(8,128)}) custom-call(bf16[1536,1536]{1,0:T(8,128)(2,1)} %bitcast.82, bf16[1024,1536]{1,0:T(8,128)(2,1)} %bitcast.91, bf16[768,1024]{1,0:T(8,128)(2,1)} %copy-done.17, bf16[768,1024]{1,0:T(8,128)(2,1)} %bitcast.81, f32[768,1024]{1,0:T(8,128)} %get-tuple-element.49.middle_ref, ...), custom_call_target="tpu_custom_call" | custom-call | tf_op jit(solution)/shard_map/first_back/pallas_call | solution.py:689
  312.7 0.8 slice.172
  313.5 0.2 copy.63
  313.8 0.7 copy-done.13
  314.6 104.4 %scatter_chips.1 = (f32[32,4096]{1,0:T(8,128)}, f32[32,3072]{1,0:T(8,128)}, f32[32,1024]{1,0:T(8,128)}, f32[48,128]{1,0:T(8,128)}) custom-call(bf16[16,2,32,2048]{3,2,1,0:T(8,128)(2,1)} %bitcast.89, bf16[16,2,32,1536]{3,2,1,0:T(8,128)(2,1)} %bitcast.90, bf16[16,2,32,512]{3,2,1,0:T(8,128)(2,1)} %bitcast.88, bf16[16,2,48,128]{3,2,1,0:T(8,128)(2,1)} %copy-done.13), custom_call_target="tpu_custom_call" | custom-call | tf_op jit(solution)/shard_map/scatter_chips/pallas_call | solution.py:342
  419.0 0.7 slice_bitcast_fusion
  419.7 0.8 slice_reduce_fusion
  420.6 1.2 slice_bitcast_fusion.1
  421.7 1.8 convert_element_type.107
  423.5 1.8 copy.72
  425.3 1.6 copy.73
  426.9 1.9 copy.74
  (96 shorter events, 1.3 us)
Async XLA Ops:
  7.2 134.9 %all-gather.3.cloned.1.call-start = ((), (), s32[]{:S(2)}) async-start(), calls=%async_computation.1 | async-start | bytes 8650752 | tf_op jit(solution)/shard_map/all_gather | solution.py:722
  7.9 178.6 %all-gather.5.cloned.1.call-start = ((), (), s32[]{:S(2)}) async-start(), calls=%async_computation.2 | async-start | bytes 4456448 | tf_op jit(solution)/shard_map/all_gather | solution.py:723
  8.0 71.9 %collective-permute-start = (bf16[768,1024]{1,0:T(8,128)(2,1)}, bf16[768,1024]{1,0:T(8,128)(2,1)S(1)}, u32[]{:S(2)}, u32[]{:S(2)}) collective-permute-start(bf16[768,1024]{1,0:T(8,128)(2,1)} %bitcast.78), channel_id=1, source_target_pairs={{0,1},{1,0},{2,3},{3,2},{4,5},{5,4},{6,7},{7,6},{8,9},{9,8},{10,11... | collective-permute-start | bytes 4718600 | tf_op jit(solution)/shard_map/ppermute | solution.py:34
  8.5 69.0 %collective-permute-start.1 = (s32[2,384]{1,0:T(2,128)}, s32[2,384]{1,0:T(2,128)S(1)}, u32[]{:S(2)}, u32[]{:S(2)}) collective-permute-start(s32[2,384]{1,0:T(2,128)} %param.17), channel_id=1, source_target_pairs={{0,1},{1,0},{2,3},{3,2},{4,5},{5,4},{6,7},{7,6},{8,9},{9,8},{10,11... | collective-permute-start | bytes 9224 | tf_op jit(solution)/shard_map/ppermute | solution.py:34
  8.7 413.1 %reduce-scatter.2.cloned.1.call-start = ((), (), s32[]{:S(2)}) async-start(), calls=%async_computation.3 | async-start | bytes 4456448 | tf_op jit(solution)/shard_map/reduce_scatter | solution.py:778
  10.3 0.6 copy-start.19
  73.5 4.0 copy-start.20
  75.6 2.4 collective-permute-start.2
  78.0 18.2 %copy-start.2 = (f32[2,2,384,1]{3,2,1,0:T(8,128)}, f32[2,2,384,1]{3,2,1,0:T(8,128)S(1)}, u32[]{:S(2)}) copy-start(f32[2,2,384,1]{3,2,1,0:T(8,128)S(1)} %broadcast_select_fusion.penalty_ref) | copy-start | bytes 18436
  79.8 46.1 %copy-start.7 = (bf16[512,1024]{1,0:T(8,128)(2,1)}, bf16[512,1024]{1,0:T(8,128)(2,1)S(1)}, u32[]{:S(2)}) copy-start(bf16[512,1024]{1,0:T(8,128)(2,1)S(1)} %maximum_select_fusion.weight_ref) | copy-start | bytes 3145732
  79.9 1.2 copy-start.15
  81.0 6.4 %copy-start.11 = (bf16[16,2,32,1536]{3,2,1,0:T(8,128)(2,1)S(1)}, bf16[16,2,32,1536]{3,2,1,0:T(8,128)(2,1)}, u32[]{:S(2)}) copy-start(bf16[16,2,32,1536]{3,2,1,0:T(8,128)(2,1)} %get-tuple-element.38) | copy-start | bytes 9437188
  125.3 0.6 copy-start.3
  125.9 4.6 %copy-start = (bf16[2,2,384,512]{3,2,1,0:T(8,128)(2,1)}, bf16[2,2,384,512]{3,2,1,0:T(8,128)(2,1)S(1)}, u32[]{:S(2)}) copy-start(bf16[2,2,384,512]{3,2,1,0:T(8,128)(2,1)S(1)} %get-tuple-element.39.att_ref) | copy-start | bytes 4718596
  125.9 2.0 copy-start.14
  126.9 3.6 collective-permute-start.3
  127.9 11.7 %collective-permute-start.6 = (bf16[768,1024]{1,0:T(8,128)(2,1)S(1)}, bf16[768,1024]{1,0:T(8,128)(2,1)}, u32[]{:S(2)}, u32[]{:S(2)}) collective-permute-start(bf16[768,1024]{1,0:T(8,128)(2,1)S(1)} %bitcast.96), channel_id=1, source_target_pairs={{0,1},{1,0},{2,3},{3,2},{4,5},{5,4},{6,7},{7,6},{8,9},{9,8},{10,11... | collective-permute-start | bytes 4718600 | tf_op jit(solution)/shard_map/ppermute | solution.py:34
  130.5 1.1 copy-start.16
  137.7 4.4 collective-permute-start.4
  142.0 59.4 %copy-start.4 = (bf16[1536,1024]{1,0:T(8,128)(2,1)}, bf16[1536,1024]{1,0:T(8,128)(2,1)S(1)}, u32[]{:S(2)}) copy-start(bf16[1536,1024]{1,0:T(8,128)(2,1)S(1)} %maximum_multiply_fusion.out_ref) | copy-start | bytes 9437188
  186.5 10.3 %copy-start.6 = (bf16[1024,2048]{1,0:T(8,128)(2,1)S(1)}, bf16[1024,2048]{1,0:T(8,128)(2,1)}, u32[]{:S(2)}) copy-start(bf16[1024,2048]{1,0:T(8,128)(2,1)} %get-tuple-element.46.weight_ref) | copy-start | bytes 12582916
  196.8 4.6 %copy-start.5 = (bf16[1536,2048]{1,0:T(8,128)(2,1)}, bf16[1536,2048]{1,0:T(8,128)(2,1)S(1)}, u32[]{:S(2)}) copy-start(bf16[1536,2048]{1,0:T(8,128)(2,1)S(1)} %get-tuple-element.68.grad_ref) | copy-start | bytes 18874372
  196.8 5.6 %copy-start.23 = (bf16[1536,2048]{1,0:T(8,128)(2,1)S(1)}, bf16[1536,2048]{1,0:T(8,128)(2,1)}, u32[]{:S(2)}) copy-start(bf16[1536,2048]{1,0:T(8,128)(2,1)} %get-tuple-element.43) | copy-start | bytes 18874372
  201.4 26.5 %collective-permute-start.7 = (bf16[768,1024]{1,0:T(8,128)(2,1)}, bf16[768,1024]{1,0:T(8,128)(2,1)}, u32[]{:S(2)}, u32[]{:S(2)}) collective-permute-start(bf16[768,1024]{1,0:T(8,128)(2,1)} %fusion.9), channel_id=1, source_target_pairs={{0,1},{1,0},{2,3},{3,2},{4,5},{5,4},{6,7},{7,6},{8,9},{9,8},{10,11... | collective-permute-start | bytes 4718600 | tf_op jit(solution)/shard_map/ppermute | solution.py:34
  211.4 7.9 %slice-start.2 = ((s8[6291456]{0:T(1024)(128)(4,1)}), s8[2097152]{0:T(1024)(128)(4,1)S(1)}, s32[]{:S(2)}) async-start(s8[6291456]{0:T(1024)(128)(4,1)} %bitcast.86), calls=%async_computation.6 | async-start | bytes 4194304
  211.4 7.9 %slice-start.3 = ((s8[6291456]{0:T(1024)(128)(4,1)}), s8[4194304]{0:T(1024)(128)(4,1)S(1)}, s32[]{:S(2)}) async-start(s8[6291456]{0:T(1024)(128)(4,1)} %bitcast.86), calls=%async_computation.7 | async-start | bytes 8388608
  211.4 7.9 %copy-start.24 = (bf16[1536,1024]{1,0:T(8,128)(2,1)S(1)}, bf16[1536,1024]{1,0:T(8,128)(2,1)}, u32[]{:S(2)}) copy-start(bf16[1536,1024]{1,0:T(8,128)(2,1)} %get-tuple-element.51) | copy-start | bytes 9437188
  219.3 24.3 %collective-permute-start.5 = (bf16[768,1024]{1,0:T(8,128)(2,1)}, bf16[768,1024]{1,0:T(8,128)(2,1)}, u32[]{:S(2)}, u32[]{:S(2)}) collective-permute-start(bf16[768,1024]{1,0:T(8,128)(2,1)} %fusion.6), channel_id=1, source_target_pairs={{0,1},{1,0},{2,3},{3,2},{4,5},{5,4},{6,7},{7,6},{8,9},{9,8},{10,11... | collective-permute-start | bytes 4718600 | tf_op jit(solution)/shard_map/ppermute | solution.py:34
  227.9 15.7 %copy-start.22 = (bf16[2048,1024]{1,0:T(8,128)(2,1)S(1)}, bf16[2048,1024]{1,0:T(8,128)(2,1)}, u32[]{:S(2)}) copy-start(bf16[2048,1024]{1,0:T(8,128)(2,1)} %all-gather.5.cloned.1.call-done) | copy-start | bytes 12582916
  240.4 3.3 copy-start.9
  240.4 10.2 %collective-permute-start.8 = (bf16[768,1024]{1,0:T(8,128)(2,1)}, bf16[768,1024]{1,0:T(8,128)(2,1)S(1)}, u32[]{:S(2)}, u32[]{:S(2)}) collective-permute-start(bf16[768,1024]{1,0:T(8,128)(2,1)} %get-tuple-element.47), channel_id=1, source_target_pairs={{0,1},{1,0},{2,3},{3,2},{4,5},{5,4},{6,7},{7,6},{8,9},{9,8},{10,11... | collective-permute-start | bytes 4718600 | tf_op jit(solution)/shard_map/ppermute | solution.py:34
  242.0 8.6 %copy-start.18 = (bf16[8,1024]{1,0:T(8,128)(2,1)}, bf16[8,1024]{1,0:T(8,128)(2,1)S(1)}, u32[]{:S(2)}) copy-start(bf16[8,1024]{1,0:T(8,128)(2,1)S(1)} %convert.21) | copy-start | bytes 49156
  250.6 1.2 copy-start.8
  284.3 2.6 copy-start.12
  284.3 8.9 %slice-start = ((s8[4718592]{0:T(1024)(128)(4,1)}), s8[4194304]{0:T(1024)(128)(4,1)S(1)}, s32[]{:S(2)}) async-start(s8[4718592]{0:T(1024)(128)(4,1)} %bitcast.83), calls=%async_computation.4 | async-start | bytes 8388608
  287.0 3.8 copy-start.1
  287.0 6.3 %slice-start.1 = ((s8[4718592]{0:T(1024)(128)(4,1)}), s8[524288]{0:T(1024)(128)(4,1)S(1)}, s32[]{:S(2)}) async-start(s8[4718592]{0:T(1024)(128)(4,1)} %bitcast.83), calls=%async_computation.5 | async-start | bytes 1048576
  290.7 2.5 copy-start.10
  290.7 10.9 %collective-permute-start.9 = (bf16[768,1024]{1,0:T(8,128)(2,1)}, bf16[768,1024]{1,0:T(8,128)(2,1)S(1)}, u32[]{:S(2)}, u32[]{:S(2)}) collective-permute-start(bf16[768,1024]{1,0:T(8,128)(2,1)} %convolution_convert_fusion.5), channel_id=1, source_target_pairs={{0,1},{1,0},{2,3},{3,2},{4,5},{5,4},{6,7},{7,6},{8,9},{9,8},{10,11... | collective-permute-start | bytes 4718600 | tf_op jit(solution)/shard_map/ppermute | solution.py:34
  292.7 7.5 %collective-permute-start.10 = (bf16[512,512]{1,0:T(8,128)(2,1)S(1)}, bf16[512,512]{1,0:T(8,128)(2,1)S(1)}, u32[]{:S(2)}, u32[]{:S(2)}) collective-permute-start(bf16[512,512]{1,0:T(8,128)(2,1)S(1)} %get-tuple-element.70), channel_id=1, source_target_pairs={{0,1},{1,0},{2,3},{3,2},{4,5},{5,4},{6,7},{7,6},{8,9},{9,8},{10,11... | collective-permute-start | bytes 1572872 | tf_op jit(solution)/shard_map/ppermute | solution.py:34
  293.3 6.8 %copy-start.21 = (f32[2,4,2,128]{3,2,1,0:T(2,128)S(1)}, f32[2,4,2,128]{3,2,1,0:T(2,128)}, u32[]{:S(2)}) copy-start(f32[2,4,2,128]{3,2,1,0:T(2,128)} %get-tuple-element.53) | copy-start | bytes 24580
  301.6 1.2 copy-start.17
  302.8 10.7 %slice-start.4 = ((bf16[8,1024]{1,0:T(8,128)(2,1)}), bf16[2,1024]{1,0:T(2,128)(2,1)S(1)}, s32[]{:S(2)}) async-start(bf16[8,1024]{1,0:T(8,128)(2,1)} %copy-done.18), calls=%async_computation.8 | async-start | bytes 8192 | tf_op jit(solution)/shard_map/slice | solution.py:803
  313.8 0.7 copy-start.13
Sparse Core Ops, SparseCore 0:
  10.9 98.6 all-gather.2
  112.3 74.1 all-gather.4
  211.5 93.8 reduce-scatter.1

commit v3 on v2

v3 whole, which is shorter than its diff:
```python
import functools

import jax
import jax.numpy as jnp
from jax import lax
from jax.experimental import pallas as pl
from jax.experimental.pallas import tpu as pltpu
from jax.sharding import PartitionSpec as P

AX = "fsdp"
MESH = pl.DeviceIdType.MESH
HEAD = 64
EPSILON = 1e-06
ROOT_HALF = 0.7071067811865476
INV_ROOT_TWO_PI = 0.3989422804014327
BF = jnp.bfloat16
F32 = jnp.float32
PARAM_COLS = 128


def product(left_side, right_side):
    return jnp.dot(left_side, right_side, preferred_element_type=F32)


def product_left_t(left_side, right_side):
    return lax.dot_general(left_side, right_side, (((0,), (0,)), ((), ())), preferred_element_type=F32)


def product_right_t(left_side, right_side):
    return lax.dot_general(left_side, right_side, (((1,), (1,)), ((), ())), preferred_element_type=F32)


def swap(shard):
    return lax.ppermute(shard, AX, [(i, i ^ 1) for i in range(lax.axis_size(AX))])


def same_core_groups():
    count = lax.axis_size(AX)
    return [[i for i in range(count) if i % 2 == core] for core in (0, 1)]


def flip(index, step):
    return index + step - 2 * step * ((index // step) % 2)


def peers_of(me):
    return flip(me, 1), flip(me, 2), flip(me, 4), [flip(me, 8), flip(me, 16), flip(flip(me, 8), 16)]


def zflip(chip, j):
    return [chip, flip(chip, 4), flip(chip, 8), flip(flip(chip, 4), 8)][j]


def meet(peers):
    barrier = pltpu.get_barrier_semaphore()
    for peer in peers:
        pl.semaphore_signal(barrier, inc=1, device_id=(peer,), device_id_type=MESH)
    pl.semaphore_wait(barrier, len(peers))


def gather_kernel(qkv_ref, proj_ref, packed_ref, qkv_out, proj_out, packed_out, local_sem, send_sem, recv_sem):
    me = lax.axis_index(AX)
    chip, core = me // 2, me % 2
    mate, peer_x, peer_y, peers_z = peers_of(me)
    meet([mate, peer_x, peer_y] + peers_z)
    chip_x, chip_y = flip(chip, 1), flip(chip, 2)
    chip_xy = flip(chip_x, 2)
    outs = (qkv_out, packed_out, proj_out)
    count = len(outs)
    width = qkv_ref.shape[1] // 6
    pending = []

    def remote(w, slot, block, target, peer):
        return pltpu.make_async_remote_copy(
            src_ref=block, dst_ref=target, send_sem=send_sem.at[w, slot], recv_sem=recv_sem.at[w, slot],
            device_id=(peer,), device_id_type=MESH,
        )

    def send(w, slot, block, target, peer):
        copy = remote(w, slot, block, target, peer)
        copy.start()
        pending.append(copy)

    def arrive(w, slot, block):
        remote(w, slot, block, block, mate).wait_recv()

    def columns(start, size):
        return pl.ds(pl.multiple_of(start, 128), size)

    def pieces(w, half, target):
        if w == 0:
            return [
                (qkv_ref.at[:, columns((2 * t + half) * width, width)], target.at[:, pl.ds(t * width, width)])
                for t in range(3)
            ]
        if w == 1:
            return [(packed_ref, target)]
        return [(proj_ref.at[:, columns(half * width, width)], target)]

    for w in range(count):
        for source, target in pieces(w, 1 - core, outs[w].at[chip, core]):
            remote(w, 0, source, target, mate).start()
        for source, target in pieces(w, core, outs[w].at[chip, core]):
            pltpu.make_async_copy(source, target, local_sem.at[w]).start()
    for w in range(count):
        own = outs[w].at[chip, core]
        pltpu.make_async_copy(own, own, local_sem.at[w]).wait()
        arrive(w, 0, outs[w].at[chip, 1 - core])
        block = outs[w].at[chip]
        for j in range(3):
            send(w, 1 + j, block, block, peers_z[j])
        send(w, 4, block, block, peer_x)
        send(w, 8, block, block, peer_y)
    for w in range(count):
        for j in (1, 2, 3):
            block = outs[w].at[zflip(chip, j)]
            arrive(w, j, block)
            send(w, 4 + j, block, block, peer_x)
            send(w, 8 + j, block, block, peer_y)
        for j in range(4):
            block = outs[w].at[zflip(chip_x, j)]
            arrive(w, 4 + j, block)
            send(w, 12 + j, block.at[0], block.at[0], peer_y)
            block = outs[w].at[zflip(chip_y, j)]
            arrive(w, 8 + j, block)
            send(w, 16 + j, block.at[1], block.at[1], peer_x)
    for w in range(count):
        for j in range(4):
            block = outs[w].at[zflip(chip_xy, j)]
            arrive(w, 12 + j, block.at[0])
            arrive(w, 16 + j, block.at[1])
    for w in range(count):
        own = outs[w].at[chip, core]
        remote(w, 0, own, own, mate).wait_send()
    for copy in pending:
        copy.wait_send()


def gather_chips(qkv, proj, packed):
    devices = lax.axis_size(AX)
    shard, features = proj.shape
    width = features // 2
    if devices != 32:
        core = lax.axis_index(AX) % 2
        split = qkv.reshape(shard, 3, 2, width).transpose(2, 0, 1, 3).reshape(2, shard, 3 * width)
        gathered = []
        for halves in (split, proj.reshape(shard, 2, width).transpose(1, 0, 2), jnp.stack([packed, packed])):
            own = lax.dynamic_index_in_dim(halves, core, 0, keepdims=False)
            other = swap(lax.dynamic_index_in_dim(halves, 1 - core, 0, keepdims=False))
            block = jnp.where(core == 0, jnp.stack([own, other]), jnp.stack([other, own]))
            gathered.append(lax.all_gather(block, AX, axis=0, axis_index_groups=same_core_groups()))
        return gathered
    chips = devices // 2
    return pl.pallas_call(
        gather_kernel,
        out_shape=[
            jax.ShapeDtypeStruct((chips, 2, shard, 3 * width), BF),
            jax.ShapeDtypeStruct((chips, 2, shard, width), BF),
            jax.ShapeDtypeStruct((chips, 2) + packed.shape, BF),
        ],
        in_specs=[pl.BlockSpec(memory_space=pltpu.VMEM)] * 3,
        out_specs=[pl.BlockSpec(memory_space=pl.ANY)] * 3,
        scratch_shapes=[
            pltpu.SemaphoreType.DMA((3,)),
            pltpu.SemaphoreType.DMA((3, 20)),
            pltpu.SemaphoreType.DMA((3, 20)),
        ],
        compiler_params=pltpu.CompilerParams(collective_id=0, has_side_effects=True),
        cost_estimate=pl.CostEstimate(flops=int(4e10), bytes_accessed=int(1.5e8), transcendentals=0),
        name="gather_chips",
    )(qkv, proj, packed)


class Scatter:
    def __init__(self, kinds, ins, outs, scratch):
        count = len(kinds)
        self.kinds, self.ins, self.outs = kinds, ins, outs
        names = ("recv_a", "recv_b", "recv_x", "recv_y", "recv_z", "stage", "land")
        for place, name in enumerate(names):
            setattr(self, name, scratch[place * count : (place + 1) * count])
        self.send_sem, self.recv_sem = scratch[len(names) * count :]
        me = lax.axis_index(AX)
        self.chip, self.core = me // 2, me % 2
        self.mate, self.peer_x, self.peer_y, self.peers_z = peers_of(me)
        chip_x, chip_y = flip(self.chip, 1), flip(self.chip, 2)
        self.own = [zflip(self.chip, j) for j in range(4)]
        self.at_x = [zflip(chip_x, j) for j in range(4)]
        self.at_y = [zflip(chip_y, j) for j in range(4)]
        self.at_xy = [zflip(flip(chip_x, 2), j) for j in range(4)]
        self.sent = []

    def meet(self):
        meet([self.mate, self.peer_x, self.peer_y] + self.peers_z)

    def remote(self, w, slot, block, target, peer):
        return pltpu.make_async_remote_copy(
            src_ref=block, dst_ref=target, send_sem=self.send_sem.at[w, slot], recv_sem=self.recv_sem.at[w, slot],
            device_id=(peer,), device_id_type=MESH,
        )

    def send(self, w, slot, block, target, peer):
        self.remote(w, slot, block, target, peer).start()
        self.sent.append((w, slot))

    def arrive(self, w, slot, block):
        self.remote(w, slot, block, block, self.mate).wait_recv()

    def far(self, w, j):
        block = self.ins[w].at[self.at_xy[j]]
        self.send(w, j, block.at[0], self.recv_a[w].at[j], self.peer_y)
        self.send(w, 4 + j, block.at[1], self.recv_b[w].at[j], self.peer_x)

    def near(self, w, j):
        self.send(w, 8 + j, self.ins[w].at[self.at_x[j], 1], self.recv_x[w].at[j, 1], self.peer_x)
        self.send(w, 12 + j, self.ins[w].at[self.at_y[j], 0], self.recv_y[w].at[j, 0], self.peer_y)

    def strips(self, w, body):
        @pl.loop(0, self.ins[w].shape[2] // 16)
        def _(i):
            body(pl.ds(pl.multiple_of(i * 16, 16), 16))

    def relay(self, w, j):
        for slot, recv, block, half in (
            (j, self.recv_a[w], self.at_x[j], 0),
            (4 + j, self.recv_b[w], self.at_y[j], 1),
        ):
            self.arrive(w, slot, recv.at[j])

            def body(part):
                total = recv[j, part].astype(F32) + self.ins[w][block, half, part].astype(F32)
                recv[j, part] = total.astype(BF)

            self.strips(w, body)
            if half == 0:
                self.send(w, 16 + j, recv.at[j], self.recv_x[w].at[j, 0], self.peer_x)
            else:
                self.send(w, 20 + j, recv.at[j], self.recv_y[w].at[j, 1], self.peer_y)

    def arrive_near(self, w, j):
        self.arrive(w, 8 + j, self.recv_x[w].at[j, 1])
        self.arrive(w, 12 + j, self.recv_y[w].at[j, 0])
        self.arrive(w, 16 + j, self.recv_x[w].at[j, 0])
        self.arrive(w, 20 + j, self.recv_y[w].at[j, 1])

    def near_sum(self, w, j, half, part):
        total = self.recv_x[w][j, half, part].astype(F32) + self.recv_y[w][j, half, part].astype(F32)
        return total + self.ins[w][self.own[j], half, part].astype(F32)

    def cross(self, w, j):
        self.arrive_near(w, j)

        def body(part):
            for half in range(2):
                self.recv_x[w][j, half, part] = self.near_sum(w, j, half, part).astype(BF)

        self.strips(w, body)
        self.send(w, 23 + j, self.recv_x[w].at[j], self.recv_z[w].at[j - 1], self.peers_z[j - 1])

    def place(self, w, part, total, half):
        kind = self.kinds[w]
        if kind == "sum":
            self.outs[w][part] = total
            return
        size = total.shape[1] // kind
        for t in range(kind):
            start = pl.multiple_of((2 * t + half) * size, 128)
            self.outs[w][part, pl.ds(start, size)] = total[:, t * size : (t + 1) * size]

    def last(self, w):
        self.arrive_near(w, 0)
        for j in range(3):
            self.arrive(w, 24 + j, self.recv_z[w].at[j])

        def total_of(half, part):
            total = self.near_sum(w, 0, half, part)
            for j in range(3):
                total = total + self.recv_z[w][j, half, part].astype(F32)
            return total

        def other(part):
            self.stage[w][part] = total_of(1 - self.core, part)

        self.strips(w, other)
        self.send(w, 27, self.stage[w], self.land[w], self.mate)
        self.strips(w, lambda part: self.place(w, part, total_of(self.core, part), self.core))

    def finish(self, w):
        self.arrive(w, 27, self.land[w])

        def body(part):
            other = self.land[w][part]
            if self.kinds[w] == "sum":
                other = other + self.outs[w][part]
            self.place(w, part, other, 1 - self.core)

        self.strips(w, body)

    def drain(self):
        for w, slot in self.sent:
            if slot == 27:
                block = self.stage[w]
            elif slot >= 24:
                block = self.recv_x[w].at[0]
            else:
                block = self.recv_a[w].at[0]
            self.remote(w, slot, block, block, self.mate).wait_send()

    def run(self):
        small = range(2, len(self.kinds))

        def opening(w):
            self.far(w, 1), self.far(w, 2), self.near(w, 1)

        self.meet()
        opening(0)
        for w in small:
            for j in (1, 2, 3, 0):
                self.far(w, j), self.near(w, j)
        self.relay(0, 1), self.far(0, 3), self.near(0, 2)
        self.relay(0, 2), self.far(0, 0), self.near(0, 3)
        for w in small:
            for j in (1, 2, 3, 0):
                self.relay(w, j)
        self.relay(0, 3), self.near(0, 0), self.cross(0, 1)
        opening(1)
        for w in small:
            for j in (1, 2, 3):
                self.cross(w, j)
        self.relay(0, 0), self.cross(0, 2), self.cross(0, 3)
        self.relay(1, 1), self.far(1, 3), self.near(1, 2)
        self.relay(1, 2), self.far(1, 0), self.near(1, 3)
        for w in small:
            self.last(w)
        self.relay(1, 3), self.near(1, 0), self.cross(1, 1)
        self.relay(1, 0)
        self.last(0)
        self.cross(1, 2), self.cross(1, 3)
        for w in small:
            self.finish(w)
        self.finish(0)
        self.last(1)
        self.finish(1)
        self.drain()


def scatter_scratch(shapes):
    count = len(shapes)
    scratch = [pltpu.VMEM((4,) + s[2:], BF) for s in shapes] * 2
    scratch += [pltpu.VMEM((4, 2) + s[2:], BF) for s in shapes] * 2
    scratch += [pltpu.VMEM((3, 2) + s[2:], BF) for s in shapes]
    scratch += [pltpu.VMEM(s[2:], F32) for s in shapes] * 2
    return scratch + [pltpu.SemaphoreType.DMA((count, 28)), pltpu.SemaphoreType.DMA((count, 28))]


def scatter_shapes(shapes, kinds):
    return [
        jax.ShapeDtypeStruct((s[2], s[3] * (1 if kind == "sum" else 2)), F32) for s, kind in zip(shapes, kinds)
    ]


def scatter_kernel(kinds, *refs):
    count = len(kinds)
    Scatter(kinds, refs[:count], refs[count : 2 * count], refs[2 * count :]).run()


def scatter_chips(grads, kinds):
    devices = lax.axis_size(AX)
    shapes = [g.shape for g in grads]
    if devices != 32:
        core = lax.axis_index(AX) % 2
        summed = []
        for grad, kind in zip(grads, kinds):
            block = lax.psum_scatter(grad, AX, scatter_dimension=0, axis_index_groups=same_core_groups())
            block = block.astype(F32)
            own = lax.dynamic_index_in_dim(block, core, 0, keepdims=False)
            other = swap(lax.dynamic_index_in_dim(block, 1 - core, 0, keepdims=False))
            if kind == "sum":
                summed.append(own + other)
                continue
            rows, columns = own.shape
            own = own.reshape(rows, kind, 1, columns // kind)
            other = other.reshape(rows, kind, 1, columns // kind)
            summed.append(by_core(core, own, other, 2).reshape(rows, 2 * columns))
        return summed
    count = len(grads)
    return pl.pallas_call(
        functools.partial(scatter_kernel, kinds),
        out_shape=scatter_shapes(shapes, kinds),
        in_specs=[pl.BlockSpec(memory_space=pltpu.VMEM)] * count,
        out_specs=[pl.BlockSpec(memory_space=pltpu.VMEM)] * count,
        scratch_shapes=scatter_scratch(shapes),
        compiler_params=pltpu.CompilerParams(
            collective_id=1, has_side_effects=True, vmem_limit_bytes=56 << 20
        ),
        name="scatter_chips",
    )(*grads)


def flat(ref):
    return ref[...].reshape(-1, ref.shape[-1])


def head_masks():
    lane = lax.broadcasted_iota(jnp.int32, (1, 2 * HEAD), 1)
    return [(lane < HEAD).astype(BF), (lane >= HEAD).astype(BF)]


def attend_kernel(chunk, q_ref, k_ref, v_ref, penalty_ref, out_ref, log_ref, query_buf, mixed_buf):
    query_buf[...] = flat(q_ref) * jnp.asarray(0.125, BF)
    keys, values = flat(k_ref), flat(v_ref)
    values_t = values.T
    penalty = flat(penalty_ref)
    masks = head_masks()

    @pl.loop(0, query_buf.shape[0] // chunk)
    def _(i):
        part = pl.ds(pl.multiple_of(i * chunk, chunk), chunk)
        queries = query_buf[part]
        parts = []
        for h in range(2):
            scores = product_right_t(keys, queries * masks[h]) + penalty
            top = jnp.max(scores, axis=0, keepdims=True)
            exponent = jnp.exp(scores - top)
            total = jnp.sum(exponent, axis=0, keepdims=True)
            mixed = product(values_t[h * HEAD : (h + 1) * HEAD], exponent.astype(BF))
            parts.append(mixed * (1.0 / total))
            log_ref[0, 0, h : h + 1, part] = top + jnp.log(total)
        mixed_buf[part] = jnp.concatenate(parts, 0).T.astype(BF)

    out_ref[...] = mixed_buf[...].reshape(out_ref.shape)


def attend(projected, penalty):
    _, clips, rows, triple = projected.shape
    slots = 2 * rows
    width = triple // 3
    pairs = width // (2 * HEAD)

    def block(offset):
        return pl.BlockSpec((2, 1, rows, 2 * HEAD), lambda i, j: (0, i, 0, offset * pairs + j))

    return pl.pallas_call(
        functools.partial(attend_kernel, 256),
        grid=(clips, pairs),
        in_specs=[block(0), block(1), block(2), pl.BlockSpec((2, 1, rows, 1), lambda i, j: (0, i, 0, 0))],
        out_specs=[block(0), pl.BlockSpec((1, 1, 2, slots), lambda i, j: (i, j, 0, 0))],
        out_shape=[
            jax.ShapeDtypeStruct((2, clips, rows, width), BF),
            jax.ShapeDtypeStruct((clips, pairs, 2, slots), F32),
        ],
        scratch_shapes=[pltpu.VMEM((slots, 2 * HEAD), BF)] * 2,
        compiler_params=pltpu.CompilerParams(vmem_limit_bytes=48 << 20),
        cost_estimate=pl.CostEstimate(
            flops=4 * clips * pairs * slots * slots * 2 * HEAD, bytes_accessed=8 * clips * slots * width,
            transcendentals=clips * pairs * 2 * slots * slots,
        ),
        name="attend",
    )(projected, projected, projected, penalty)


def attend_back_kernel(
    chunk, q_ref, k_ref, v_ref, penalty_ref, log_ref, att_ref, grad_ref, out_ref, bias_ref,
    query_buf, grad_buf, mixed_buf, back_buf, key_sum, value_sum, bias_sum,
):
    rows = q_ref.shape[2]
    pair = pl.program_id(1)
    width = out_ref.shape[3] // 3
    query_buf[...] = flat(q_ref) * jnp.asarray(0.125, BF)
    grad_buf[...] = flat(grad_ref)
    mixed_buf[...] = flat(att_ref)
    keys, values = flat(k_ref), flat(v_ref)
    keys_t = keys.T
    penalty = flat(penalty_ref)
    masks = head_masks()
    for total in (key_sum, value_sum, bias_sum):
        total[...] = jnp.zeros_like(total)

    def keep(offset, value):
        columns = pl.ds(pl.multiple_of(offset + pair * 2 * HEAD, 128), 2 * HEAD)
        for side in range(2):
            out_ref[side, 0, :, columns] = value[side * rows : (side + 1) * rows]

    for start in range(0, query_buf.shape[0], chunk):
        part = pl.ds(start, chunk)
        queries, grads = query_buf[part], grad_buf[part]
        overlap = (grads.astype(F32) * mixed_buf[part].astype(F32)).T
        parts = []
        for h in range(2):
            head_queries = queries * masks[h]
            head_grads = grads * masks[h]
            correction = jnp.sum(overlap[h * HEAD : (h + 1) * HEAD], axis=0, keepdims=True)
            logs = log_ref[0, 0, h : h + 1, part]
            soft = jnp.exp(product_right_t(keys, head_queries) + penalty - logs)
            grad_soft = product_right_t(values, head_grads)
            value_sum[...] += product(soft.astype(BF), head_grads)
            grad_scores = (soft * (grad_soft - correction)).astype(BF)
            key_sum[...] += product(grad_scores, head_queries)
            parts.append(product(keys_t[h * HEAD : (h + 1) * HEAD], grad_scores))
        grad_queries = jnp.concatenate(parts, 0).T * 0.125
        bias_sum[0:1] += jnp.sum(grad_queries, axis=0, keepdims=True)
        back_buf[part] = grad_queries.astype(BF)

    keep(0, back_buf[...])
    keep(width, key_sum[...].astype(BF))
    keep(2 * width, value_sum[...].astype(BF))
    bias_ref[0, 0, 0:1] = bias_sum[0:1]
    bias_ref[0, 0, 1:2] = jnp.sum(value_sum[...], axis=0, keepdims=True)


def attend_back(projected, penalty, logs, attended, grad_attended):
    _, clips, rows, triple = projected.shape
    slots = 2 * rows
    width = triple // 3
    pairs = width // (2 * HEAD)

    def block(offset):
        return pl.BlockSpec((2, 1, rows, 2 * HEAD), lambda i, j: (0, i, 0, offset * pairs + j))

    return pl.pallas_call(
        functools.partial(attend_back_kernel, 256),
        grid=(clips, pairs),
        in_specs=[
            block(0), block(1), block(2),
            pl.BlockSpec((2, 1, rows, 1), lambda i, j: (0, i, 0, 0)),
            pl.BlockSpec((1, 1, 2, slots), lambda i, j: (i, j, 0, 0)),
            block(0), block(0),
        ],
        out_specs=[
            pl.BlockSpec((2, 1, rows, triple), lambda i, j: (0, i, 0, 0)),
            pl.BlockSpec((1, 1, 2, 2 * HEAD), lambda i, j: (i, j, 0, 0)),
        ],
        out_shape=[
            jax.ShapeDtypeStruct((2, clips, rows, triple), BF),
            jax.ShapeDtypeStruct((clips, pairs, 2, 2 * HEAD), F32),
        ],
        scratch_shapes=[pltpu.VMEM((slots, 2 * HEAD), BF)] * 4
        + [pltpu.VMEM((slots, 2 * HEAD), F32)] * 2
        + [pltpu.VMEM((8, 2 * HEAD), F32)],
        compiler_params=pltpu.CompilerParams(vmem_limit_bytes=56 << 20),
        cost_estimate=pl.CostEstimate(
            flops=10 * clips * pairs * slots * slots * 2 * HEAD, bytes_accessed=18 * clips * slots * width,
            transcendentals=clips * pairs * 2 * slots * slots,
        ),
        name="attend_back",
    )(projected, projected, projected, penalty, logs, attended, grad_attended)


def normal_parts(values):
    average = jnp.mean(values, axis=-1, keepdims=True)
    centered = values - average
    inverse = lax.rsqrt(jnp.mean(centered * centered, axis=-1, keepdims=True) + EPSILON)
    return centered * inverse, inverse


def normal_back(grad_normed, scaled, inverse, gain):
    grad_scaled = grad_normed * gain
    first_mean = jnp.mean(grad_scaled, axis=-1, keepdims=True)
    second_mean = jnp.mean(grad_scaled * scaled, axis=-1, keepdims=True)
    return inverse * (grad_scaled - first_mean - scaled * second_mean)


def rows_spec(size, columns):
    return pl.BlockSpec((size, columns), lambda i: (i, 0))


def whole_spec(shape):
    return pl.BlockSpec(shape, lambda i: (0,) * len(shape), pipeline_mode=pl.Buffered(1))


PARAMS = pltpu.CompilerParams(vmem_limit_bytes=56 << 20)


def strips_of(ref):
    return [pl.ds(start, 32) for start in range(0, ref.shape[0], 32)]


def project_kernel(steps, own_ref, other_ref, gain_ref, shift_ref, weight_ref, bias_ref, norm_ref, out_ref):
    is_own = pl.program_id(0) < steps
    for part in strips_of(own_ref):
        rows = jnp.where(is_own, own_ref[part].astype(F32), other_ref[part].astype(F32))
        scaled, _ = normal_parts(rows)
        norm_ref[part] = (scaled * gain_ref[...] + shift_ref[...]).astype(BF)
    out_ref[...] = (product(norm_ref[...], weight_ref[...]) + bias_ref[...]).astype(BF)


def project(own, other, gain, shift, weight, bias):
    rows, features = own.shape
    columns = weight.shape[1]
    steps = 3
    size = rows // steps
    return pl.pallas_call(
        functools.partial(project_kernel, steps),
        grid=(2 * steps,),
        in_specs=[
            pl.BlockSpec((size, features), lambda i: (jnp.minimum(i, steps - 1), 0)),
            pl.BlockSpec((size, features), lambda i: (jnp.maximum(i - steps, 0), 0)),
            whole_spec((1, features)),
            whole_spec((1, features)),
            whole_spec((features, columns)),
            whole_spec((1, columns)),
        ],
        out_specs=[rows_spec(size, features), rows_spec(size, columns)],
        out_shape=[
            jax.ShapeDtypeStruct((2 * rows, features), BF),
            jax.ShapeDtypeStruct((2 * rows, columns), BF),
        ],
        compiler_params=PARAMS,
        name="project",
    )(own, other, gain, shift, weight, bias)


def second_norm_kernel(att_ref, weight_ref, token_ref, recv_ref, bias_ref, gain_ref, shift_ref, middle_ref, out_ref):
    mixed = product(att_ref[...], weight_ref[...])
    for part in strips_of(token_ref):
        middle = token_ref[part].astype(F32) + mixed[part.start : part.start + part.size]
        middle = middle + recv_ref[part].astype(F32) + bias_ref[...]
        middle_ref[part] = middle
        scaled, _ = normal_parts(middle)
        out_ref[part] = (scaled * gain_ref[...] + shift_ref[...]).astype(BF)


def second_norm(attended, weight, tokens, received, bias, gain, shift):
    rows, features = tokens.shape
    width = weight.shape[0]
    size = rows // 4
    return pl.pallas_call(
        second_norm_kernel,
        grid=(4,),
        in_specs=[
            rows_spec(size, width), whole_spec((width, features)), rows_spec(size, features), rows_spec(size, features),
            whole_spec((1, features)), whole_spec((1, features)), whole_spec((1, features)),
        ],
        out_specs=[rows_spec(size, features), rows_spec(size, features)],
        out_shape=[jax.ShapeDtypeStruct((rows, features), F32), jax.ShapeDtypeStruct((rows, features), BF)],
        compiler_params=PARAMS,
        name="second_norm",
    )(attended, weight, tokens, received, bias, gain, shift)


def feed_kernel(
    steps, unit, own_ref, other_ref, grad_own_ref, grad_other_ref, mark_ref, bias_ref, *refs
):
    if len(refs) == 14:
        both_ref, refs = refs[0], refs[1:]
        sources = None
    else:
        sources, refs = refs[:2], refs[2:]
    act_ref, pre_ref, norm_ref, grad_ref, lift_own_ref, lift_other_ref, pass_own_ref, pass_other_ref = refs[:8]
    sums_ref, up_ref, down_ref, up_sem, down_sem = refs[8:]
    step = pl.program_id(0)
    features, hidden = up_ref.shape

    @pl.when(step == 0)
    def _():
        sums_ref[...] = jnp.zeros_like(sums_ref)
        if sources is not None:
            pltpu.make_async_copy(sources[0], up_ref, up_sem).start()
            pltpu.make_async_copy(sources[1], down_ref, down_sem).start()
        else:
            core = lax.axis_index(AX) % 2
            chips = hidden // unit
            shard = features // (2 * chips)
            for k in range(chips):
                device = 2 * k + core
                pltpu.make_async_copy(
                    both_ref.at[:, pl.ds(pl.multiple_of(device * unit, 128), unit)],
                    up_ref.at[:, k * unit : (k + 1) * unit],
                    up_sem,
                ).start()
            for k in range(chips):
                device = 2 * k + core
                for q in range(unit // shard):
                    pltpu.make_async_copy(
                        both_ref.at[
                            pl.ds(pl.multiple_of(device * shard, 16), shard),
                            pl.ds(2 * hidden + q * features, features),
                        ],
                        down_ref.at[k * unit + q * shard : k * unit + (q + 1) * shard],
                        down_sem,
                    ).start()
        pltpu.make_async_copy(up_ref, up_ref, up_sem).wait()
        pltpu.make_async_copy(down_ref, down_ref, down_sem).wait()

    rows = jnp.where(step < steps, other_ref[...], own_ref[...])
    grads = jnp.where(step < steps, grad_other_ref[...], grad_own_ref[...]) * mark_ref[...].astype(BF)
    norm_ref[...] = rows
    grad_ref[...] = grads
    size = 512
    for start in range(0, hidden, size):
        part = slice(start, start + size)
        pre = product(rows, up_ref[:, part]) + bias_ref[:, part]
        normal_cdf = 0.5 * (1.0 + lax.erf(pre * ROOT_HALF))
        density = jnp.exp(-0.5 * pre * pre) * INV_ROOT_TWO_PI
        act_ref[:, part] = (pre * normal_cdf).astype(BF)
        grad_pre = product_right_t(grads, down_ref[part]) * (normal_cdf + pre * density)
        sums_ref[0:1, part] += jnp.sum(grad_pre, axis=0, keepdims=True)
        pre_ref[:, part] = grad_pre.astype(BF)
    lifted = product(act_ref[...], down_ref[...])
    passed = product_right_t(pre_ref[...], up_ref[...])
    lift_own_ref[...] = lifted
    pass_own_ref[...] = passed

    @pl.when(step < steps)
    def _():
        lift_other_ref[...] = lifted.astype(BF)
        pass_other_ref[...] = passed.astype(BF)


def feed(own, other, grad_own, grad_other, marks, weights, bias, unit):
    rows, features = own.shape
    hidden = bias.shape[1]
    steps = 3
    size = rows // steps

    def side(i):
        return jnp.where(i < steps, i + steps, i - steps)

    def both_spec(columns):
        return pl.BlockSpec((size, columns), lambda i: (side(i), 0))

    own_spec = pl.BlockSpec((size, features), lambda i: (jnp.maximum(i - steps, 0), 0))
    other_spec = pl.BlockSpec((size, features), lambda i: (jnp.minimum(i, steps - 1), 0))
    return pl.pallas_call(
        functools.partial(feed_kernel, steps, unit),
        grid=(2 * steps,),
        in_specs=[own_spec, other_spec, own_spec, other_spec, both_spec(1), whole_spec((1, hidden))]
        + [pl.BlockSpec(memory_space=pl.ANY)] * len(weights),
        out_specs=[
            both_spec(hidden), both_spec(hidden), both_spec(features), both_spec(features),
            own_spec, other_spec, own_spec, other_spec,
            pl.BlockSpec((8, hidden), lambda i: (0, 0)),
        ],
        out_shape=[
            jax.ShapeDtypeStruct((2 * rows, hidden), BF), jax.ShapeDtypeStruct((2 * rows, hidden), BF),
            jax.ShapeDtypeStruct((2 * rows, features), BF), jax.ShapeDtypeStruct((2 * rows, features), BF),
            jax.ShapeDtypeStruct((rows, features), F32), jax.ShapeDtypeStruct((rows, features), BF),
            jax.ShapeDtypeStruct((rows, features), F32), jax.ShapeDtypeStruct((rows, features), BF),
            jax.ShapeDtypeStruct((8, hidden), F32),
        ],
        scratch_shapes=[
            pltpu.VMEM((features, hidden), BF), pltpu.VMEM((hidden, features), BF),
            pltpu.SemaphoreType.DMA(()), pltpu.SemaphoreType.DMA(()),
        ],
        compiler_params=PARAMS,
        cost_estimate=pl.CostEstimate(
            flops=16 * rows * features * hidden, bytes_accessed=8 * features * hidden,
            transcendentals=4 * rows * hidden,
        ),
        name="feed",
    )(own, other, grad_own, grad_other, marks, bias, *weights)


def outer_kernel(left_ref, right_ref, out_ref):
    out_ref[...] = product_left_t(left_ref[...], right_ref[...]).astype(BF)


def outer(left, right):
    rows, columns = left.shape
    width = right.shape[1]
    size = 256
    return pl.pallas_call(
        outer_kernel,
        grid=(columns // size,),
        in_specs=[pl.BlockSpec((rows, size), lambda i: (0, i)), whole_spec((rows, width))],
        out_specs=rows_spec(size, width),
        out_shape=jax.ShapeDtypeStruct((columns, width), BF),
        compiler_params=PARAMS,
        cost_estimate=pl.CostEstimate(
            flops=2 * rows * columns * width, bytes_accessed=2 * (rows * columns + rows * width + columns * width),
            transcendentals=0,
        ),
        name="outer",
    )(left, right)


def gather_sums(sums_ref, values):
    for index, value in enumerate(values):
        sums_ref[index : index + 1] += jnp.sum(value, axis=0, keepdims=True)


def clear_first(sums_ref):
    @pl.when(pl.program_id(0) == 0)
    def _():
        sums_ref[...] = jnp.zeros_like(sums_ref)


def second_back_kernel(
    grad_ref, recv_ref, middle_ref, out_ref, lift_ref, lift_recv_ref, gain_ref, bias_ref,
    full_ref, low_ref, block_ref, sums_ref,
):
    clear_first(sums_ref)
    for part in strips_of(grad_ref):
        lifted = lift_ref[part] + lift_recv_ref[part].astype(F32)
        block_ref[part] = (middle_ref[part] + lifted + bias_ref[...]).astype(BF)
        grad_normed = grad_ref[part] + recv_ref[part].astype(F32)
        scaled, inverse = normal_parts(middle_ref[part])
        grad_out = out_ref[part].astype(F32)
        grad_middle = grad_out + normal_back(grad_normed, scaled, inverse, gain_ref[...])
        full_ref[part] = grad_middle
        low_ref[part] = grad_middle.astype(BF)
        gather_sums(sums_ref, [grad_normed * scaled, grad_normed, grad_middle, grad_out])


def second_back(passed, received, middle, grad_out, lifted, lift_received, gain, bias):
    rows, features = middle.shape
    size = rows // 4
    return pl.pallas_call(
        second_back_kernel,
        grid=(4,),
        in_specs=[rows_spec(size, features)] * 6 + [whole_spec((1, features))] * 2,
        out_specs=[rows_spec(size, features)] * 3 + [pl.BlockSpec((8, features), lambda i: (0, 0))],
        out_shape=[
            jax.ShapeDtypeStruct((rows, features), F32), jax.ShapeDtypeStruct((rows, features), BF),
            jax.ShapeDtypeStruct((rows, features), BF), jax.ShapeDtypeStruct((8, features), F32),
        ],
        compiler_params=PARAMS,
        name="second_back",
    )(passed, received, middle, grad_out, lifted, lift_received, gain, bias)


def first_back_kernel(grad_ref, weight_ref, recv_ref, token_ref, middle_ref, gain_ref, full_ref, sums_ref):
    clear_first(sums_ref)
    passed = product_right_t(grad_ref[...], weight_ref[...])
    for part in strips_of(grad_ref):
        grad_normed = passed[part.start : part.start + part.size] + recv_ref[part].astype(F32)
        scaled, inverse = normal_parts(token_ref[part].astype(F32))
        full_ref[part] = middle_ref[part] + normal_back(grad_normed, scaled, inverse, gain_ref[...])
        gather_sums(sums_ref, [grad_normed * scaled, grad_normed])


def first_back(grad_projected, weight, received, tokens, grad_middle, gain):
    rows, features = tokens.shape
    triple = weight.shape[1]
    size = rows // 4
    return pl.pallas_call(
        first_back_kernel,
        grid=(4,),
        in_specs=[
            rows_spec(size, triple), whole_spec((features, triple)), rows_spec(size, features),
            rows_spec(size, features), rows_spec(size, features), whole_spec((1, features)),
        ],
        out_specs=[rows_spec(size, features), pl.BlockSpec((8, features), lambda i: (0, 0))],
        out_shape=[jax.ShapeDtypeStruct((rows, features), F32), jax.ShapeDtypeStruct((8, features), F32)],
        compiler_params=PARAMS,
        name="first_back",
    )(grad_projected, weight, received, tokens, grad_middle, gain)


def pack_kernel(up_ref, down_ref, out_ref):
    shard, columns = up_ref.shape
    features = down_ref.shape[1]
    out_ref[:, :columns] = up_ref[...]
    for i in range(down_ref.shape[0] // shard):
        out_ref[:, columns + i * features : columns + (i + 1) * features] = down_ref[i * shard : (i + 1) * shard]


def pack(up, down):
    shard, columns = up.shape
    fold = down.shape[0] // shard
    if shard % 16 != 0:
        return jnp.concatenate([up] + [down[shard * i : shard * (i + 1)] for i in range(fold)], 1)
    return pl.pallas_call(
        pack_kernel,
        out_shape=jax.ShapeDtypeStruct((shard, columns + fold * down.shape[1]), BF),
        in_specs=[pl.BlockSpec(memory_space=pltpu.VMEM)] * 2,
        out_specs=pl.BlockSpec(memory_space=pltpu.VMEM),
        name="pack",
    )(up, down)


def finish_kernel(up_ref, qkv_ref, proj_ref, down_ref, packed_ref, up_out, qkv_out, proj_out, down_out, vec_out, bias_out):
    up_out[...] = up_ref[...]
    qkv_out[...] = qkv_ref[...]
    proj_out[...] = proj_ref[...]
    down_out[...] = down_ref[...].astype(F32)
    shard = vec_out.shape[1]
    vec_out[...] = packed_ref[:shard].T[:8]
    bias_out[...] = packed_ref[shard : shard + 1]


def finish(up, qkv, proj, down, packed, shard, unit):
    if lax.axis_size(AX) != 32:
        return up, qkv, proj, down.astype(F32), packed[:shard, :8].T, packed[shard : shard + 1, :unit]
    return pl.pallas_call(
        finish_kernel,
        out_shape=[jax.ShapeDtypeStruct(a.shape, F32) for a in (up, qkv, proj, down)]
        + [jax.ShapeDtypeStruct((8, shard), F32), jax.ShapeDtypeStruct((1, unit), F32)],
        in_specs=[pl.BlockSpec(memory_space=pltpu.VMEM)] * 5,
        out_specs=[pl.BlockSpec(memory_space=pltpu.VMEM)] * 6,
        compiler_params=PARAMS,
        name="finish",
    )(up, qkv, proj, down, packed)


def by_core(core, own, other, axis):
    return jnp.where(core == 0, jnp.concatenate([own, other], axis), jnp.concatenate([other, own], axis))


def per_device(
    tokens, valid_slots, cotangent, first_gain, first_shift, qkv_weight, query_bias, value_bias, proj_weight,
    proj_bias, second_gain, second_shift, up_weight, up_bias, down_weight, down_bias,
):
    devices = lax.axis_size(AX)
    chips = devices // 2
    core = lax.axis_index(AX) % 2
    micro, rows, features = tokens.shape
    shard = qkv_weight.shape[0]
    width = features // 2
    hidden = up_weight.shape[1] // 2
    unit = hidden // chips
    own_rows = micro * rows
    every = 2 * own_rows

    fold = unit // shard
    both_weights = lax.all_gather(pack(up_weight, down_weight), AX, axis=0, tiled=True)
    feed_weights = [both_weights]
    if unit % 128 != 0 or shard % 16 != 0:
        half_up = both_weights[:, : 2 * hidden].reshape(features, chips, 2, unit)
        half_up = lax.dynamic_index_in_dim(half_up, core, 2, keepdims=False).reshape(features, hidden)
        half_down = both_weights[:, 2 * hidden :].reshape(chips, 2, shard, fold, features)
        half_down = lax.dynamic_index_in_dim(half_down, core, 1, keepdims=False)
        half_down = half_down.transpose(0, 2, 1, 3).reshape(hidden, features)
        feed_weights = [half_up, half_down]
    vectors = jnp.stack(
        [first_gain, first_shift, query_bias, value_bias, proj_bias, second_gain, second_shift, down_bias], 0
    )
    lanes = max(PARAM_COLS, unit)
    vectors = jnp.pad(vectors.T, ((0, 16), (0, lanes - 8)))
    packed = lax.dynamic_update_slice(vectors, up_bias[None, :], (shard, 0))
    qkv_all, proj_all, packed_all = gather_chips(qkv_weight, proj_weight, packed)
    weight_qkv = qkv_all.reshape(features, 3 * width)
    params = packed_all[:, :, :shard, :8].astype(F32).reshape(features, 8).T
    gain_one, shift_one, bias_query, bias_value, bias_proj, gain_two, shift_two, bias_down = [
        params[i : i + 1] for i in range(8)
    ]
    bias_up = lax.dynamic_index_in_dim(packed_all[:, :, shard, :unit], core, 1, keepdims=False)
    bias_up = bias_up.astype(F32).reshape(1, hidden)
    proj_cols = proj_all.reshape(2, width, width)
    proj_own = lax.dynamic_index_in_dim(proj_cols, core, 0, keepdims=False)
    proj_other = swap(lax.dynamic_index_in_dim(proj_cols, 1 - core, 0, keepdims=False))
    weight_proj = by_core(core, proj_own, proj_other, 1)
    qkv_bias = jnp.concatenate(
        [
            lax.dynamic_slice_in_dim(bias_query, core * width, width, 1),
            jnp.zeros((1, width), F32),
            lax.dynamic_slice_in_dim(bias_value, core * width, width, 1),
        ],
        1,
    )

    own_tokens = tokens.reshape(own_rows, features)
    other_tokens = swap(own_tokens)
    marks = jnp.stack([valid_slots, swap(valid_slots)])
    own_cotangent = cotangent.reshape(own_rows, features)
    penalty = jnp.where(marks > 0, 0.0, -1000000000.0).astype(F32)[..., None]
    norm_one, projected = project(own_tokens, other_tokens, gain_one, shift_one, weight_qkv, qkv_bias)
    projected = projected.reshape(2, micro, rows, 3 * width)
    attended, logs = attend(projected, penalty)
    attended_flat = attended.reshape(every, width)
    mixed = swap(product(attended_flat[own_rows:], weight_proj).astype(BF))
    middle, norm_own = second_norm(
        attended_flat, weight_proj, own_tokens, mixed, bias_proj, gain_two, shift_two
    )
    activation, grad_pre, norm_two, grad_out, lifted, lifted_other, passed, passed_other, up_sums = feed(
        norm_own, swap(norm_own), own_cotangent, swap(own_cotangent),
        (marks > 0).astype(F32).reshape(every, 1), feed_weights, bias_up, unit,
    )
    grad_bias_up = up_sums[0]
    passed_other = swap(passed_other)
    lifted_other = swap(lifted_other)

    grad_down = outer(activation, grad_out)
    down_weight_grad = lax.psum_scatter(
        grad_down, AX, scatter_dimension=0, tiled=True, axis_index_groups=same_core_groups()
    )
    grad_middle, grad_low, block_output, second_sums = second_back(
        passed, passed_other, middle, grad_out, lifted, lifted_other, gain_two, bias_down
    )
    block_output = block_output.reshape(micro, rows, features)
    grad_up = outer(norm_two, grad_pre)
    grad_low = jnp.concatenate([grad_low, swap(grad_low)], 0)
    grad_attended = product_right_t(grad_low, weight_proj).astype(BF).reshape(2, micro, rows, width)
    grad_proj = product_left_t(attended_flat, grad_low).astype(BF)
    grad_proj_own = lax.dynamic_slice_in_dim(grad_proj, core * width, width, 1)
    grad_proj_other = swap(lax.dynamic_slice_in_dim(grad_proj, (1 - core) * width, width, 1))
    grad_proj = by_core(core, grad_proj_own, grad_proj_other, 0)
    grad_projected, grad_bias = attend_back(projected, penalty, logs, attended, grad_attended)
    grad_projected = grad_projected.reshape(every, 3 * width)
    passed = swap(product_right_t(grad_projected[own_rows:], weight_qkv).astype(BF))
    grad_qkv = outer(norm_one, grad_projected)
    tokens_grad, first_sums = first_back(
        grad_projected, weight_qkv, passed, own_tokens, grad_middle, gain_one
    )
    tokens_grad = tokens_grad.reshape(micro, rows, features)

    grad_bias = jnp.sum(grad_bias, axis=0).transpose(1, 0, 2).reshape(2, width)
    grad_bias = by_core(core, grad_bias, jnp.zeros_like(grad_bias), 1)
    sums = jnp.concatenate([first_sums[:2], grad_bias, second_sums[2:3], second_sums[:2], second_sums[3:4]], 0)
    sums = sums.astype(BF).T.reshape(chips, 2, shard, 8)
    sums = jnp.pad(sums, ((0, 0), (0, 0), (0, 16), (0, lanes - 8)))
    up_units = grad_bias_up.astype(BF).reshape(chips, 1, unit)
    up_units = by_core(core, up_units, jnp.zeros_like(up_units), 1)
    sums = lax.dynamic_update_slice(sums, up_units.reshape(chips, 2, 1, unit), (0, 0, shard, 0))
    up_weight_grad, qkv_weight_grad, proj_weight_grad, packed_sum = scatter_chips(
        [
            grad_up.reshape(chips, 2, shard, hidden),
            grad_qkv.reshape(chips, 2, shard, 3 * width),
            grad_proj.reshape(chips, 2, shard, width),
            sums,
        ],
        (chips, 3, 1, "sum"),
    )
    up_weight_grad, qkv_weight_grad, proj_weight_grad, down_weight_grad, vector_sum, up_bias_grad = finish(
        up_weight_grad, qkv_weight_grad, proj_weight_grad, down_weight_grad, packed_sum, shard, unit
    )
    up_bias_grad = up_bias_grad[0]
    return (
        block_output, tokens_grad, vector_sum[0], vector_sum[1], qkv_weight_grad, vector_sum[2], vector_sum[3],
        proj_weight_grad, vector_sum[4], vector_sum[5], vector_sum[6], up_weight_grad, up_bias_grad,
        down_weight_grad, vector_sum[7],
    )


def solution(mesh):
    row = P(None, AX, None)
    vec = P(AX)
    mat = P(AX, None)
    return jax.shard_map(
        per_device,
        mesh=mesh,
        in_specs=(row, P(None, AX), row, vec, vec, mat, vec, vec, mat, vec, vec, vec, mat, vec, mat, vec),
        out_specs=(row, row, vec, vec, mat, vec, vec, mat, vec, vec, vec, mat, vec, mat, vec),
        check_vma=False,
    )
```

time: 444 us -> 415 us (0.935); the launches traced: 435 us -> 413 us
  matrix products: 72.3 us -> 11.5 us
  Pallas kernels: 282 us -> 338 us
  local copies, waits for them, and re-layouts: 28.2 us -> 20.5 us
  other arithmetic: 9.4 us -> 3.15 us
    pallas_call x4 -> x9, Pallas kernels: 145 us -> 190 us  [the longest x1 93.3 us: scatter_chips(): pl.pallas_call(functools.partial(scatter_kernel, kinds), out_shape=scatte...]
    dot_general x4 -> x1, matrix products: 24.4 us -> 0.98 us  [product(): return jnp.dot(left_side, right_side, preferred_element_type=F32)]
    dot_general x4 -> x1, matrix products: 26.2 us -> 3.71 us  [product_left_t(): lax.dot_general(left_side, right_side, (((0,), (0,)), ((), ())), preferre...]
    dot_general x4 -> x2, matrix products: 21.7 us -> 6.78 us  [product_right_t(): lax.dot_general(left_side, right_side, (((1,), (1,)), ((), ())), preferre...]
    all_gather x2 -> x1, waiting for transfers between devices: 23 us -> 11.8 us  [per_device(): lax.all_gather(pack(up_weight, down_weight), AX, axis=0, tiled=True)]
    ppermute x11, waiting for transfers between devices: 2.2 us -> 9.58 us  [swap(): lax.ppermute(shard, AX, [(i, i ^ 1) for i in range(lax.axis_size(AX))])]
    unnamed x62 -> x47, local copies, waits for them, and re-layouts: 15.3 us -> 8.82 us
    pallas_call x1, Pallas kernels: 29.1 us -> 34.2 us  [attend(): pl.pallas_call(functools.partial(attend_kernel, 256), grid=(clips, pairs)...]
  transfers between devices with their start and end apart: 14 -> 13, of which waited for: 2 -> 5; matrix products, arithmetic and copies ran while one was open for 18% -> 6% of each run, Pallas kernels for 65% -> 69%
where the time goes in v3:
time: 415 us; the launch traced here: 413 us
  Pallas kernels  338 us (81%)
  waiting for transfers between devices  21.5 us (5%)
  local copies, waits for them, and re-layouts  20.5 us (5%)
  between operations  14.5 us (3%)
  matrix products  11.5 us (3%)
    pallas_call x1, Pallas kernels, scatter_chips(): pl.pallas_call(functools.partial(scatter_kernel, kinds), out_shape=scatte...  93.3 us
    pallas_call x1, Pallas kernels, gather_chips(): pl.pallas_call(gather_kernel, out_shape=[jax.ShapeDtypeStruct((chips, 2,...  67.4 us
    pallas_call x1, Pallas kernels, feed(): pl.pallas_call(functools.partial(feed_kernel, steps, unit), grid=(2 * ste...  38.9 us
    pallas_call x1, Pallas kernels, attend(): pl.pallas_call(functools.partial(attend_kernel, 256), grid=(clips, pairs)...  34.2 us
    pallas_call x3, Pallas kernels, outer(): pl.pallas_call(outer_kernel, grid=(columns // size,), in_specs=[pl.BlockS...  33.2 us
    pallas_call x1, Pallas kernels, attend_back(): pl.pallas_call(functools.partial(attend_back_kernel, 256), grid=(clips, p...  30.2 us
    all_gather x1, waiting for transfers between devices, per_device(): lax.all_gather(pack(up_weight, down_weight), AX, axis=0, tiled=True)  11.8 us
    pallas_call x1, Pallas kernels, project(): pl.pallas_call(functools.partial(project_kernel, steps), grid=(2 * steps,...  11.3 us
  transfers between devices with their start and end apart: 13, of which 5 were waited for; matrix products, arithmetic and copies ran while one was open for 6% of the time, Pallas kernels for 69%

profile of v3, /device:TPU:0, one launch (start us, length us, event | category | flops | bytes accessed | tf_op | source)
XLA Modules:
  0.0 413.1 jit_solution(2031416546673466279)
XLA Ops:
  7.2 1.9 pack.1
  9.2 0.6 collective-permute-start.1
  9.8 0.8 stack.50
  10.6 0.1 copy.76
  10.7 0.7 dynamic_update_slice.6.packed_ref
  11.4 0.6 copy-done.17
  12.0 67.4 %gather_chips.1 = (bf16[16,2,32,1536]{3,2,1,0:T(8,128)(2,1)}, bf16[16,2,32,512]{3,2,1,0:T(8,128)(2,1)}, bf16[16,2,48,128]{3,2,1,0:T(8,128)(2,1)}) custom-call(bf16[32,3072]{1,0:T(8,128)(2,1)} %qkv_ref.1, bf16[32,1024]{1,0:T(8,128)(2,1)} %proj_ref.1, bf16[48,128]{1,0:T(8,128)(2,1)} %copy-done.17), custom_call_target="tpu_custom_call" | custom-call | flops 40000000000 | bytes 150000000 | tf_op jit(solution)/shard_map/gather_chips/pallas_call | solution.py:154
  79.4 1.3 dynamic-slice_bitcast_fusion.1
  80.9 0.2 copy.82
  81.1 0.6 fusion.2
  81.7 0.6 fusion.1.bias_ref
  82.4 0.4 copy.78
  82.8 0.3 maximum_select_fusion.weight_ref
  83.2 11.3 %project.1 = (bf16[1536,1024]{1,0:T(8,128)(2,1)}, bf16[1536,1536]{1,0:T(8,128)(2,1)}) custom-call(bf16[768,1024]{1,0:T(8,128)(2,1)} %bitcast.76, bf16[768,1024]{1,0:T(8,128)(2,1)} %collective-permute-done.other_ref, f32[1,1024]{1,0:T(1,128)} %get-tuple-element.98.gain_ref, f32[1,1024]{1,0:T(1,128)} %get-tuple-element.97.shift_ref, ...), custom_call_target="tpu_custom_call" | custom-call | tf_op jit(solution)/shard_map/project/pallas_call | solution.py:591
  94.5 34.2 %attend.1 = (bf16[2,2,384,512]{3,2,1,0:T(8,128)(2,1)S(1)}, f32[2,4,2,768]{3,2,1,0:T(2,128)S(1)}) custom-call(bf16[2,2,384,1536]{3,2,1,0:T(8,128)(2,1)} %bitcast.109, bf16[2,2,384,1536]{3,2,1,0:T(8,128)(2,1)} %bitcast.110, bf16[2,2,384,1536]{3,2,1,0:T(8,128)(2,1)} %bitcast.111, f32[2,2,384,1]{3,2,1,0:T(8,128)S(1)} %broadcast_select_fusion.penalty_ref), custom_call_target="tpu_custom_call" | custom-call | flops 2415919104 | bytes 6291456 | tf_op jit(solution)/shard_map/attend/pallas_call | solution.py:442
  128.8 1.0 convolution_convert_fusion.1
  129.8 0.1 copy-done
  129.9 0.5 collective-permute-start.3
  130.4 0.3 copy-done.20
  130.7 0.5 collective-permute-start.5
  131.2 2.3 collective-permute-done.3.recv_ref
  133.5 1.1 copy-done.11
  134.7 6.2 %second_norm.1 = (f32[768,1024]{1,0:T(8,128)}, bf16[768,1024]{1,0:T(8,128)(2,1)}) custom-call(bf16[1536,512]{1,0:T(8,128)(2,1)} %bitcast.73, bf16[512,1024]{1,0:T(8,128)(2,1)} %copy-done.5, bf16[768,1024]{1,0:T(8,128)(2,1)} %bitcast.77, bf16[768,1024]{1,0:T(8,128)(2,1)} %copy-done.11, f32[1,1024]{1,0:T(1,128)} %get-tuple-element.94.bias_ref, ...), custom_call_target="tpu_custom_call" | custom-call | tf_op jit(solution)/shard_map/second_norm/pallas_call | solution.py:626
  140.9 0.6 collective-permute-start.4
  141.5 0.6 bitcast_convert_fusion.1.bias_ref
  142.1 1.5 reshape.184.mark_ref
  143.6 2.3 collective-permute-done.4.other_ref
  145.9 11.8 %all-gather.2.cloned.1.call-done.refs_0_ = bf16[1024,8192]{1,0:T(8,128)(2,1)} async-done(((bf16[32,8192]{1,0:T(8,128)(2,1)}), bf16[1024,8192]{1,0:T(8,128)(2,1)}) %all-gather.2.cloned.1.call-update) | async-done | bytes 16777232 | tf_op jit(solution)/shard_map/all_gather | solution.py:915
  157.8 38.9 %feed.1 = (bf16[1536,2048]{1,0:T(8,128)(2,1)}, bf16[1536,2048]{1,0:T(8,128)(2,1)}, bf16[1536,1024]{1,0:T(8,128)(2,1)}, bf16[1536,1024]{1,0:T(8,128)(2,1)}, f32[7...) custom-call(bf16[768,1024]{1,0:T(8,128)(2,1)} %get-tuple-element.56., ...), custom_call_target="tpu_custom_call" | custom-call | flops 25769803776 | bytes 16777216 | tf_op jit(solution)/shard_map/feed/pallas_call | solution.py:723
  196.7 12.2 %outer.5 = bf16[2048,1024]{1,0:T(8,128)(2,1)} custom-call(bf16[1536,2048]{1,0:T(8,128)(2,1)} %get-tuple-element.79.left_ref, bf16[1536,1024]{1,0:T(8,128)(2,1)} %get-tuple-element.60.out_ref.right_ref), custom_call_target="tpu_custom_call" | custom-call | flops 6442450944 | bytes 13631488 | tf_op jit(solution)/shard_map/outer/pallas_call | solution.py:761
  208.9 1.4 copy-done.22
  210.3 0.2 collective-permute-start.6
  210.5 0.2 copy-done.21
  210.8 0.2 collective-permute-start.7
  211.0 2.7 collective-permute-done.6.recv_ref
  213.7 2.2 collective-permute-done.7.lift_recv_ref
  215.9 1.2 copy-done.9
  217.2 9.2 %second_back.1 = (f32[768,1024]{1,0:T(8,128)}, bf16[768,1024]{1,0:T(8,128)(2,1)}, bf16[768,1024]{1,0:T(8,128)(2,1)}, f32[8,1024]{1,0:T(8,128)}) custom-call(f32[768,1024]{1,0:T(8,128)} %get-tuple-element.57.grad_ref, bf16[768,1024]{1,0:T(8,128)(2,1)} %copy-done.8, f32[768,1024]{1,0:T(8,128)} %get-tuple-element.59.middle_ref, ...), custom_call_target="tpu_custom_call" | custom-call | tf_op jit(solution)/shard_map/second_back/pallas_call | solution.py:807
  226.4 0.3 collective-permute-start.8
  226.7 0.9 fusion
  227.6 11.7 %outer.3 = bf16[1024,2048]{1,0:T(8,128)(2,1)} custom-call(bf16[1536,1024]{1,0:T(8,128)(2,1)} %get-tuple-element.69.left_ref, bf16[1536,2048]{1,0:T(8,128)(2,1)} %get-tuple-element.70.right_ref), custom_call_target="tpu_custom_call" | custom-call | flops 6442450944 | bytes 13631488 | tf_op jit(solution)/shard_map/outer/pallas_call | solution.py:761
  239.4 0.1 constant_dynamic-update-slice_fusion.1
  239.5 0.1 constant_dynamic-update-slice_fusion
  239.7 1.1 copy-done.6
  240.8 3.0 convolution_convert_fusion
  243.8 30.2 %attend_back.1 = (bf16[2,2,384,1536]{3,2,1,0:T(8,128)(2,1)}, f32[2,4,2,128]{3,2,1,0:T(2,128)}) custom-call(bf16[2,2,384,1536]{3,2,1,0:T(8,128)(2,1)} %bitcast.112, bf16[2,2,384,1536]{3,2,1,0:T(8,128)(2,1)} %bitcast.113, bf16[2,2,384,1536]{3,2,1,0:T(8,128)(2,1)} %bitcast.114, f32[2,2,384,1]{3,2,1,0:T(8,128)} %copy-done.2, f32[2,4,2,768]{3,2,1,0:T(2,128)} %copy-done.3, ...), custom_call_target="tpu_custom_call" | custom-call | flops 6039797760 | bytes 14155776 | tf_op jit(solution)/shard_map/attend_back/pallas_call | solution.py:519
  274.0 2.0 slice.98
  276.0 0.6 copy-done.4
  276.6 3.8 convolution_convert_fusion.2
  280.4 0.2 collective-permute-start.9
  280.7 3.7 convolution_convert_fusion.3
  284.4 0.1 constant_dynamic-slice_fusion.1
  284.5 0.3 collective-permute-start.10
  284.9 9.2 %outer.4 = bf16[1024,1536]{1,0:T(8,128)(2,1)} custom-call(bf16[1536,1024]{1,0:T(8,128)(2,1)} %get-tuple-element.71.left_ref, bf16[1536,1536]{1,0:T(8,128)(2,1)} %bitcast.82), custom_call_target="tpu_custom_call" | custom-call | flops 4831838208 | bytes 11010048 | tf_op jit(solution)/shard_map/outer/pallas_call | solution.py:761
  294.1 1.4 maximum_select_fusion.1
  295.5 1.2 copy-done.12
  296.7 10.2 %first_back.1 = (f32[768,1024]{1,0:T(8,128)}, f32[8,1024]{1,0:T(8,128)}) custom-call(bf16[1536,1536]{1,0:T(8,128)(2,1)} %bitcast.83, bf16[1024,1536]{1,0:T(8,128)(2,1)} %bitcast.80, bf16[768,1024]{1,0:T(8,128)(2,1)} %copy-done.12, bf16[768,1024]{1,0:T(8,128)(2,1)} %bitcast.78, f32[768,1024]{1,0:T(8,128)} %get-tuple-element.67.middle_ref, ...), custom_call_target="tpu_custom_call" | custom-call | tf_op jit(solution)/shard_map/first_back/pallas_call | solution.py:835
  306.9 0.8 slice.138
  307.7 0.2 copy.80
  308.0 0.3 dynamic_update_slice.7.refs_3_
  308.3 0.7 copy-done.7
  309.1 93.3 %scatter_chips.1 = (f32[32,4096]{1,0:T(8,128)}, f32[32,3072]{1,0:T(8,128)}, f32[32,1024]{1,0:T(8,128)}, f32[48,128]{1,0:T(8,128)}) custom-call(bf16[16,2,32,2048]{3,2,1,0:T(8,128)(2,1)} %bitcast.85, bf16[16,2,32,1536]{3,2,1,0:T(8,128)(2,1)} %bitcast.86, bf16[16,2,32,512]{3,2,1,0:T(8,128)(2,1)} %bitcast.84, bf16[16,2,48,128]{3,2,1,0:T(8,128)(2,1)} %copy-done.7), custom_call_target="tpu_custom_call" | custom-call | tf_op jit(solution)/shard_map/scatter_chips/pallas_call | solution.py:386
  402.4 2.4 finish.1
  404.8 1.5 slice_bitcast_fusion
  (70 shorter events, 0.8 us)
Async XLA Ops:
  7.2 150.6 %all-gather.2.cloned.1.call-start = ((), (), s32[]{:S(2)}) async-start(), calls=%async_computation.1 | async-start | bytes 17301504 | tf_op jit(solution)/shard_map/all_gather | solution.py:915
  9.1 393.2 %reduce-scatter.2.cloned.1.call-start = ((), (), s32[]{:S(2)}) async-start(), calls=%async_computation.2 | async-start | bytes 4456448 | tf_op jit(solution)/shard_map/reduce_scatter | solution.py:973
  9.2 73.2 %collective-permute-start.1 = (s32[2,384]{1,0:T(2,128)}, s32[2,384]{1,0:T(2,128)S(1)}, u32[]{:S(2)}, u32[]{:S(2)}) collective-permute-start(s32[2,384]{1,0:T(2,128)} %param.17), channel_id=1, source_target_pairs={{0,1},{1,0},{2,3},{3,2},{4,5},{5,4},{6,7},{7,6},{8,9},{9,8},{10,11... | collective-permute-start | bytes 9224 | tf_op jit(solution)/shard_map/ppermute | solution.py:34
  9.7 73.5 %collective-permute-start = (bf16[768,1024]{1,0:T(8,128)(2,1)}, bf16[768,1024]{1,0:T(8,128)(2,1)}, u32[]{:S(2)}, u32[]{:S(2)}) collective-permute-start(bf16[768,1024]{1,0:T(8,128)(2,1)} %bitcast.75), channel_id=1, source_target_pairs={{0,1},{1,0},{2,3},{3,2},{4,5},{5,4},{6,7},{7,6},{8,9},{9,8},{10,11... | collective-permute-start | bytes 4718600 | tf_op jit(solution)/shard_map/ppermute | solution.py:34
  11.4 0.6 copy-start.17
  79.4 1.5 copy-start.14
  79.4 3.0 copy-start.18
  80.7 2.1 collective-permute-start.2
  82.8 11.7 %copy-start.2 = (f32[2,2,384,1]{3,2,1,0:T(8,128)}, f32[2,2,384,1]{3,2,1,0:T(8,128)S(1)}, u32[]{:S(2)}) copy-start(f32[2,2,384,1]{3,2,1,0:T(8,128)S(1)} %broadcast_select_fusion.penalty_ref) | copy-start | bytes 18436
  83.2 45.6 %copy-start.5 = (bf16[512,1024]{1,0:T(8,128)(2,1)}, bf16[512,1024]{1,0:T(8,128)(2,1)S(1)}, u32[]{:S(2)}) copy-start(bf16[512,1024]{1,0:T(8,128)(2,1)S(1)} %maximum_select_fusion.weight_ref) | copy-start | bytes 3145732
  128.7 1.2 copy-start
  128.7 1.2 copy-start.3
  128.8 1.9 copy-start.20
  129.9 3.6 collective-permute-start.3
  130.7 12.9 %collective-permute-start.5 = (bf16[768,1024]{1,0:T(8,128)(2,1)S(1)}, bf16[768,1024]{1,0:T(8,128)(2,1)}, u32[]{:S(2)}, u32[]{:S(2)}) collective-permute-start(bf16[768,1024]{1,0:T(8,128)(2,1)S(1)} %bitcast.117), channel_id=1, source_target_pairs={{0,1},{1,0},{2,3},{3,2},{4,5},{5,4},{6,7},{7,6},{8,9},{9,8},{10,11... | collective-permute-start | bytes 4718600 | tf_op jit(solution)/shard_map/ppermute | solution.py:34
  133.5 1.1 copy-start.11
  140.9 5.1 %collective-permute-start.4 = (bf16[768,1024]{1,0:T(8,128)(2,1)}, bf16[768,1024]{1,0:T(8,128)(2,1)}, u32[]{:S(2)}, u32[]{:S(2)}) collective-permute-start(bf16[768,1024]{1,0:T(8,128)(2,1)} %get-tuple-element.56.own_ref), channel_id=1, source_target_pairs={{0,1},{1,0},{2,3},{3,2},{4,5},{5,4},{6,7},{7,6},{8,9},{9,8},{10,11... | collective-permute-start | bytes 4718600 | tf_op jit(solution)/shard_map/ppermute | solution.py:34
  208.9 1.4 copy-start.22
  208.9 1.9 copy-start.21
  210.3 3.4 collective-permute-start.6
  210.8 5.2 %collective-permute-start.7 = (bf16[768,1024]{1,0:T(8,128)(2,1)S(1)}, bf16[768,1024]{1,0:T(8,128)(2,1)S(1)}, u32[]{:S(2)}, u32[]{:S(2)}) collective-permute-start(bf16[768,1024]{1,0:T(8,128)(2,1)S(1)} %copy-done.21), channel_id=1, source_target_pairs={{0,1},{1,0},{2,3},{3,2},{4,5},{5,4},{6,7},{7,6},{8,9},{9,8},{10,11... | collective-permute-start | bytes 4718600 | tf_op jit(solution)/shard_map/ppermute | solution.py:34
  213.7 2.3 copy-start.8
  215.9 1.2 copy-start.9
  226.4 13.1 %collective-permute-start.8 = (bf16[768,1024]{1,0:T(8,128)(2,1)}, bf16[768,1024]{1,0:T(8,128)(2,1)S(1)}, u32[]{:S(2)}, u32[]{:S(2)}) collective-permute-start(bf16[768,1024]{1,0:T(8,128)(2,1)} %get-tuple-element.65), channel_id=1, source_target_pairs={{0,1},{1,0},{2,3},{3,2},{4,5},{5,4},{6,7},{7,6},{8,9},{9,8},{10,11... | collective-permute-start | bytes 4718600 | tf_op jit(solution)/shard_map/ppermute | solution.py:34
  227.6 11.8 %copy-start.16 = (f32[8,1024]{1,0:T(8,128)S(1)}, f32[8,1024]{1,0:T(8,128)}, u32[]{:S(2)}) copy-start(f32[8,1024]{1,0:T(8,128)} %get-tuple-element.74) | copy-start | bytes 98308
  227.6 11.8 %copy-start.10 = (bf16[768,1024]{1,0:T(8,128)(2,1)S(1)}, bf16[768,1024]{1,0:T(8,128)(2,1)}, u32[]{:S(2)}) copy-start(bf16[768,1024]{1,0:T(8,128)(2,1)} %get-tuple-element.65) | copy-start | bytes 4718596
  239.4 41.3 %copy-start.15 = (bf16[8,1024]{1,0:T(8,128)(2,1)}, bf16[8,1024]{1,0:T(8,128)(2,1)S(1)}, u32[]{:S(2)}) copy-start(bf16[8,1024]{1,0:T(8,128)(2,1)S(1)} %convert.24) | copy-start | bytes 49156
  239.5 1.2 copy-start.6
  240.7 3.0 copy-start.13
  274.0 2.6 copy-start.4
  276.6 4.0 copy-start.19
  276.6 4.1 copy-start.1
  280.4 15.1 %collective-permute-start.9 = (bf16[768,1024]{1,0:T(8,128)(2,1)}, bf16[768,1024]{1,0:T(8,128)(2,1)S(1)}, u32[]{:S(2)}, u32[]{:S(2)}) collective-permute-start(bf16[768,1024]{1,0:T(8,128)(2,1)} %convolution_convert_fusion.2), channel_id=1, source_target_pairs={{0,1},{1,0},{2,3},{3,2},{4,5},{5,4},{6,7},{7,6},{8,9},{9,8},{10,11... | collective-permute-start | bytes 4718600 | tf_op jit(solution)/shard_map/ppermute | solution.py:34
  284.5 9.6 %collective-permute-start.10 = (bf16[512,512]{1,0:T(8,128)(2,1)S(1)}, bf16[512,512]{1,0:T(8,128)(2,1)S(1)}, u32[]{:S(2)}, u32[]{:S(2)}) collective-permute-start(bf16[512,512]{1,0:T(8,128)(2,1)S(1)} %get-tuple-element.88), channel_id=1, source_target_pairs={{0,1},{1,0},{2,3},{3,2},{4,5},{5,4},{6,7},{7,6},{8,9},{9,8},{10,11... | collective-permute-start | bytes 1572872 | tf_op jit(solution)/shard_map/ppermute | solution.py:34
  295.5 1.2 copy-start.12
  296.7 11.0 %slice-start = ((bf16[8,1024]{1,0:T(8,128)(2,1)}), bf16[2,1024]{1,0:T(2,128)(2,1)S(1)}, s32[]{:S(2)}) async-start(bf16[8,1024]{1,0:T(8,128)(2,1)} %copy-done.15), calls=%async_computation.3 | async-start | bytes 8192 | tf_op jit(solution)/shard_map/slice | solution.py:998
  308.3 0.7 copy-start.7
Sparse Core Ops, SparseCore 0:
  11.4 146.3 all-gather.1
  209.0 93.8 reduce-scatter.1

commit v4 on v3

--- a/solution.py
+++ b/solution.py
@@ -305,12 +305,12 @@
                 block = self.recv_a[w].at[0]
             self.remote(w, slot, block, block, self.mate).wait_send()
 
+    def opening(self, w):
+        self.far(w, 1), self.far(w, 2), self.near(w, 1)
+
     def run(self):
         small = range(2, len(self.kinds))
-
-        def opening(w):
-            self.far(w, 1), self.far(w, 2), self.near(w, 1)
-
+        opening = self.opening
         self.meet()
         opening(0)
         for w in small:
@@ -844,6 +844,123 @@
         compiler_params=PARAMS,
         name="first_back",
     )(grad_projected, weight, received, tokens, grad_middle, gain)
+
+
+def tail_kernel(
+    kinds, up_ref, proj_ref, sums_ref, bias_ref, gain_ref, back_hbm, weight_hbm, norm_hbm, token_hbm, middle_hbm,
+    up_out, qkv_out, proj_out, packed_out, tokens_out, *refs
+):
+    back, weight, norm, token, middle, qkv, packed, vectors, stage, land, load_sem, pass_sem = refs[:12]
+    scatter = Scatter(kinds, (up_ref, qkv, proj_ref, packed), (up_out, qkv_out, proj_out, packed_out), refs[12:])
+    chips, _, shard, triple = qkv.shape
+    own_rows = token.shape[0]
+    loads = [
+        pltpu.make_async_copy(source, target, load_sem.at[i])
+        for i, (source, target) in enumerate(
+            ((back_hbm, back), (weight_hbm, weight), (norm_hbm, norm), (token_hbm, token), (middle_hbm, middle))
+        )
+    ]
+    for load in loads:
+        load.start()
+    scatter.meet()
+    scatter.opening(0)
+    for j in (1, 2, 3, 0):
+        scatter.far(2, j), scatter.near(2, j)
+    vectors[...] = jnp.zeros_like(vectors)
+    vectors[0:8] = sums_ref[...]
+    loads[0].wait(), loads[1].wait()
+
+    @pl.loop(0, own_rows // 256)
+    def _(i):
+        part = pl.ds(pl.multiple_of(own_rows + i * 256, 256), 256)
+        stage[pl.ds(pl.multiple_of(i * 256, 256), 256)] = product_right_t(back[part], weight[...]).astype(BF)
+
+    passing = pltpu.make_async_remote_copy(
+        src_ref=stage, dst_ref=land, send_sem=pass_sem.at[0], recv_sem=pass_sem.at[1],
+        device_id=(scatter.mate,), device_id_type=MESH,
+    )
+    passing.start()
+    scatter.relay(0, 1), scatter.far(0, 3), scatter.near(0, 2)
+    loads[2].wait()
+
+    @pl.loop(0, norm.shape[1] // 256)
+    def _(i):
+        part = pl.ds(pl.multiple_of(i * 256, 256), 256)
+        count = 256 // (2 * shard)
+        grad = product_left_t(norm[:, part], back[...]).astype(BF)
+        qkv[pl.ds(i * count, count)] = grad.reshape(count, 2, shard, triple)
+
+    scatter.relay(0, 2), scatter.far(0, 0), scatter.near(0, 3)
+    for j in (1, 2, 3, 0):
+        scatter.relay(2, j)
+    scatter.opening(1)
+    loads[3].wait(), loads[4].wait()
+    passing.wait()
+
+    @pl.loop(0, own_rows // 256)
+    def _(i):
+        start = pl.multiple_of(i * 256, 256)
+        passed = product_right_t(back[pl.ds(start, 256)], weight[...])
+        for strip in range(0, 256, 32):
+            part = pl.ds(start + strip, 32)
+            grad_normed = passed[strip : strip + 32] + land[part].astype(F32)
+            scaled, inverse = normal_parts(token[part].astype(F32))
+            tokens_out[part] = middle[part] + normal_back(grad_normed, scaled, inverse, gain_ref[...])
+            vectors[0:1] += jnp.sum(grad_normed * scaled, axis=0, keepdims=True)
+            vectors[1:2] += jnp.sum(grad_normed, axis=0, keepdims=True)
+
+    scatter.relay(0, 3), scatter.near(0, 0), scatter.cross(0, 1), scatter.cross(0, 2)
+    packed[:, :, :shard] = vectors[...].T.astype(BF).reshape(chips, 2, shard, PARAM_COLS)
+    packed[:, :, shard:] = bias_ref[...]
+    for j in (1, 2, 3, 0):
+        scatter.far(3, j), scatter.near(3, j)
+    scatter.relay(0, 0), scatter.cross(0, 3)
+    for j in (1, 2, 3):
+        scatter.cross(2, j)
+    scatter.relay(1, 1), scatter.far(1, 3), scatter.near(1, 2)
+    scatter.relay(1, 2), scatter.far(1, 0), scatter.near(1, 3)
+    for j in (1, 2, 3, 0):
+        scatter.relay(3, j)
+    scatter.last(2)
+    scatter.relay(1, 3), scatter.near(1, 0), scatter.cross(1, 1)
+    for j in (1, 2, 3):
+        scatter.cross(3, j)
+    scatter.relay(1, 0)
+    scatter.last(0)
+    scatter.cross(1, 2), scatter.cross(1, 3)
+    scatter.finish(2), scatter.finish(0)
+    scatter.last(3)
+    scatter.last(1)
+    scatter.finish(3), scatter.finish(1)
+    scatter.drain()
+
+
+def tail(grad_up, grad_proj, sums, bias_rows, gain, back, weight, norm, tokens, middle):
+    chips, _, shard, hidden = grad_up.shape
+    rows, triple = back.shape
+    own_rows, features = tokens.shape
+    extra = bias_rows.shape[2]
+    kinds = (chips, 3, 1, "sum")
+    shapes = [
+        grad_up.shape, (chips, 2, shard, triple), grad_proj.shape, (chips, 2, shard + extra, PARAM_COLS),
+    ]
+    vmem = pl.BlockSpec(memory_space=pltpu.VMEM)
+    return pl.pallas_call(
+        functools.partial(tail_kernel, kinds),
+        out_shape=scatter_shapes(shapes, kinds) + [jax.ShapeDtypeStruct((own_rows, features), F32)],
+        in_specs=[vmem] * 5 + [pl.BlockSpec(memory_space=pl.ANY)] * 5,
+        out_specs=[vmem] * 5,
+        scratch_shapes=[
+            pltpu.VMEM(back.shape, BF), pltpu.VMEM(weight.shape, BF), pltpu.VMEM(norm.shape, BF),
+            pltpu.VMEM(tokens.shape, BF), pltpu.VMEM(middle.shape, F32),
+            pltpu.VMEM(shapes[1], BF), pltpu.VMEM(shapes[3], BF), pltpu.VMEM((PARAM_COLS, features), F32),
+            pltpu.VMEM((own_rows, features), BF), pltpu.VMEM((own_rows, features), BF),
+            pltpu.SemaphoreType.DMA((5,)), pltpu.SemaphoreType.DMA((2,)),
+        ]
+        + scatter_scratch(shapes),
+        compiler_params=pltpu.CompilerParams(collective_id=1, has_side_effects=True, vmem_limit_bytes=62 << 20),
+        name="tail",
+    )(grad_up, grad_proj, sums, bias_rows, gain, back, weight, norm, tokens, middle)
 
 
 def pack_kernel(up_ref, down_ref, out_ref):
@@ -981,35 +1098,40 @@
     grad_low = jnp.concatenate([grad_low, swap(grad_low)], 0)
     grad_attended = product_right_t(grad_low, weight_proj).astype(BF).reshape(2, micro, rows, width)
     grad_proj = product_left_t(attended_flat, grad_low).astype(BF)
+    grad_attended, grad_proj, grad_up = lax.optimization_barrier((grad_attended, grad_proj, grad_up))
     grad_proj_own = lax.dynamic_slice_in_dim(grad_proj, core * width, width, 1)
     grad_proj_other = swap(lax.dynamic_slice_in_dim(grad_proj, (1 - core) * width, width, 1))
     grad_proj = by_core(core, grad_proj_own, grad_proj_other, 0)
     grad_projected, grad_bias = attend_back(projected, penalty, logs, attended, grad_attended)
     grad_projected = grad_projected.reshape(every, 3 * width)
-    passed = swap(product_right_t(grad_projected[own_rows:], weight_qkv).astype(BF))
-    grad_qkv = outer(norm_one, grad_projected)
-    tokens_grad, first_sums = first_back(
-        grad_projected, weight_qkv, passed, own_tokens, grad_middle, gain_one
-    )
-    tokens_grad = tokens_grad.reshape(micro, rows, features)
 
     grad_bias = jnp.sum(grad_bias, axis=0).transpose(1, 0, 2).reshape(2, width)
     grad_bias = by_core(core, grad_bias, jnp.zeros_like(grad_bias), 1)
-    sums = jnp.concatenate([first_sums[:2], grad_bias, second_sums[2:3], second_sums[:2], second_sums[3:4]], 0)
-    sums = sums.astype(BF).T.reshape(chips, 2, shard, 8)
-    sums = jnp.pad(sums, ((0, 0), (0, 0), (0, 16), (0, lanes - 8)))
+    sums = [grad_bias, second_sums[2:3], second_sums[:2], second_sums[3:4]]
     up_units = grad_bias_up.astype(BF).reshape(chips, 1, unit)
-    up_units = by_core(core, up_units, jnp.zeros_like(up_units), 1)
-    sums = lax.dynamic_update_slice(sums, up_units.reshape(chips, 2, 1, unit), (0, 0, shard, 0))
-    up_weight_grad, qkv_weight_grad, proj_weight_grad, packed_sum = scatter_chips(
-        [
-            grad_up.reshape(chips, 2, shard, hidden),
-            grad_qkv.reshape(chips, 2, shard, 3 * width),
-            grad_proj.reshape(chips, 2, shard, width),
-            sums,
-        ],
-        (chips, 3, 1, "sum"),
-    )
+    up_units = by_core(core, up_units, jnp.zeros_like(up_units), 1).reshape(chips, 2, 1, unit)
+    grad_up = grad_up.reshape(chips, 2, shard, hidden)
+    grad_proj = grad_proj.reshape(chips, 2, shard, width)
+    if devices == 32:
+        bias_rows = jnp.pad(up_units, ((0, 0), (0, 0), (0, 15), (0, 0)))
+        sums = jnp.concatenate([jnp.zeros((2, features), F32)] + sums, 0)
+        up_weight_grad, qkv_weight_grad, proj_weight_grad, packed_sum, tokens_grad = tail(
+            grad_up, grad_proj, sums, bias_rows, gain_one, grad_projected, weight_qkv, norm_one, own_tokens, grad_middle
+        )
+    else:
+        passed = swap(product_right_t(grad_projected[own_rows:], weight_qkv).astype(BF))
+        grad_qkv = outer(norm_one, grad_projected)
+        tokens_grad, first_sums = first_back(
+            grad_projected, weight_qkv, passed, own_tokens, grad_middle, gain_one
+        )
+        sums = jnp.concatenate([first_sums[:2]] + sums, 0)
+        sums = sums.astype(BF).T.reshape(chips, 2, shard, 8)
+        sums = jnp.pad(sums, ((0, 0), (0, 0), (0, 16), (0, lanes - 8)))
+        sums = lax.dynamic_update_slice(sums, up_units, (0, 0, shard, 0))
+        up_weight_grad, qkv_weight_grad, proj_weight_grad, packed_sum = scatter_chips(
+            [grad_up, grad_qkv.reshape(chips, 2, shard, 3 * width), grad_proj, sums], (chips, 3, 1, "sum")
+        )
+    tokens_grad = tokens_grad.reshape(micro, rows, features)
     up_weight_grad, qkv_weight_grad, proj_weight_grad, down_weight_grad, vector_sum, up_bias_grad = finish(
         up_weight_grad, qkv_weight_grad, proj_weight_grad, down_weight_grad, packed_sum, shard, unit
     )

time: 415 us -> 406 us (0.978)
  matrix products: 11.5 us -> 5.84 us
    pallas_call x3 -> x2, Pallas kernels: 33.2 us -> 23.8 us  [outer(): pl.pallas_call(outer_kernel, grid=(columns // size,), in_specs=[pl.BlockS...]
    pallas_call x2 -> x1, Pallas kernels: 103 us -> 109 us  [tail(): pl.pallas_call(functools.partial(tail_kernel, kinds), out_shape=scatter_s...]
    unnamed x47 -> x38, local copies, waits for them, and re-layouts: 8.82 us -> 9.84 us
    ppermute x11 -> x10, waiting for transfers between devices: 9.58 us -> 9.31 us  [swap(): lax.ppermute(shard, AX, [(i, i ^ 1) for i in range(lax.axis_size(AX))])]
  transfers between devices with their start and end apart: 13 -> 12, of which waited for: 5 -> 5; matrix products, arithmetic and copies ran while one was open for 6% -> 5% of each run, Pallas kernels for 69% -> 69%
where the time goes in v4:
time: 406 us; the launch traced here: 403 us
  Pallas kernels  334 us (82%)
  waiting for transfers between devices  21.4 us (5%)
  local copies, waits for them, and re-layouts  20.4 us (5%)
  between operations  14.4 us (4%)
  matrix products  5.84 us (1%)
    pallas_call x1, Pallas kernels, tail(): pl.pallas_call(functools.partial(tail_kernel, kinds), out_shape=scatter_s...  109 us
    pallas_call x1, Pallas kernels, gather_chips(): pl.pallas_call(gather_kernel, out_shape=[jax.ShapeDtypeStruct((chips, 2,...  67.4 us
    pallas_call x1, Pallas kernels, feed(): pl.pallas_call(functools.partial(feed_kernel, steps, unit), grid=(2 * ste...  38.9 us
    pallas_call x1, Pallas kernels, attend(): pl.pallas_call(functools.partial(attend_kernel, 256), grid=(clips, pairs)...  34.2 us
    pallas_call x1, Pallas kernels, attend_back(): pl.pallas_call(functools.partial(attend_back_kernel, 256), grid=(clips, p...  30.1 us
    pallas_call x2, Pallas kernels, outer(): pl.pallas_call(outer_kernel, grid=(columns // size,), in_specs=[pl.BlockS...  23.8 us
    all_gather x1, waiting for transfers between devices, per_device(): lax.all_gather(pack(up_weight, down_weight), AX, axis=0, tiled=True)  12 us
    pallas_call x1, Pallas kernels, project(): pl.pallas_call(functools.partial(project_kernel, steps), grid=(2 * steps,...  11.3 us
  transfers between devices with their start and end apart: 12, of which 5 were waited for; matrix products, arithmetic and copies ran while one was open for 5% of the time, Pallas kernels for 69%

profile of v4, /device:TPU:0, one launch (start us, length us, event | category | flops | bytes accessed | tf_op | source)
XLA Modules:
  0.0 403.2 jit_solution(2353942598234115743)
XLA Ops:
  7.2 0.0 all-gather.2.cloned.1.call-start
  7.2 1.9 pack.1
  9.1 0.0 reduce-scatter.2.cloned.1.call-start
  9.2 0.6 collective-permute-start
  9.7 0.1 collective-permute-start.1
  9.8 0.8 stack.50
  10.6 0.1 copy.72
  10.7 0.7 dynamic_update_slice.3.packed_ref
  11.4 0.6 copy-done.11
  12.0 67.4 %gather_chips.1 = (bf16[16,2,32,1536]{3,2,1,0:T(8,128)(2,1)}, bf16[16,2,32,512]{3,2,1,0:T(8,128)(2,1)}, bf16[16,2,48,128]{3,2,1,0:T(8,128)(2,1)}) custom-call(bf16[32,3072]{1,0:T(8,128)(2,1)} %qkv_ref.1, bf16[32,1024]{1,0:T(8,128)(2,1)} %proj_ref.1, bf16[48,128]{1,0:T(8,128)(2,1)} %copy-done.11), custom_call_target="tpu_custom_call" | custom-call | flops 40000000000 | bytes 150000000 | tf_op jit(solution)/shard_map/gather_chips/pallas_call | solution.py:154
  79.5 1.3 dynamic-slice_bitcast_fusion.1
  80.8 0.1 collective-permute-start.2
  80.9 0.1 bitcast_convert_fusion
  81.0 0.2 copy.77
  81.1 0.6 fusion.3
  81.8 0.6 fusion.1.bias_ref
  82.4 0.4 copy.74
  82.8 0.1 broadcast_select_fusion.penalty_ref
  82.9 0.3 maximum_select_fusion.weight_ref
  83.2 11.3 %project.1 = (bf16[1536,1024]{1,0:T(8,128)(2,1)}, bf16[1536,1536]{1,0:T(8,128)(2,1)}) custom-call(bf16[768,1024]{1,0:T(8,128)(2,1)} %bitcast.70, bf16[768,1024]{1,0:T(8,128)(2,1)} %collective-permute-done.other_ref, f32[1,1024]{1,0:T(1,128)} %get-tuple-element.104.gain_ref, f32[1,1024]{1,0:T(1,128)} %get-tuple-element.103.shift_ref, ...), custom_call_target="tpu_custom_call" | custom-call | tf_op jit(solution)/shard_map/project/pallas_call | solution.py:591
  94.6 34.2 %attend.1 = (bf16[2,2,384,512]{3,2,1,0:T(8,128)(2,1)S(1)}, f32[2,4,2,768]{3,2,1,0:T(2,128)S(1)}) custom-call(bf16[2,2,384,1536]{3,2,1,0:T(8,128)(2,1)} %bitcast.98, bf16[2,2,384,1536]{3,2,1,0:T(8,128)(2,1)} %bitcast.99, bf16[2,2,384,1536]{3,2,1,0:T(8,128)(2,1)} %bitcast.100, f32[2,2,384,1]{3,2,1,0:T(8,128)S(1)} %broadcast_select_fusion.penalty_ref), custom_call_target="tpu_custom_call" | custom-call | flops 2415919104 | bytes 6291456 | tf_op jit(solution)/shard_map/attend/pallas_call | solution.py:442
  128.8 0.1 slice.78
  128.9 1.0 convolution_convert_fusion.1
  129.8 0.1 copy-done
  129.9 0.5 collective-permute-start.3
  130.4 0.1 collective-permute-start.5
  130.5 3.0 collective-permute-done.3.recv_ref
  133.5 1.1 copy-done.9
  134.6 6.1 %second_norm.1 = (f32[768,1024]{1,0:T(8,128)}, bf16[768,1024]{1,0:T(8,128)(2,1)}) custom-call(bf16[1536,512]{1,0:T(8,128)(2,1)} %bitcast.67, bf16[512,1024]{1,0:T(8,128)(2,1)} %copy-done.4, bf16[768,1024]{1,0:T(8,128)(2,1)} %bitcast.71, bf16[768,1024]{1,0:T(8,128)(2,1)} %copy-done.9, f32[1,1024]{1,0:T(1,128)} %get-tuple-element.100.bias_ref, ...), custom_call_target="tpu_custom_call" | custom-call | tf_op jit(solution)/shard_map/second_norm/pallas_call | solution.py:626
  140.8 0.7 collective-permute-start.4
  141.4 0.8 slice.83
  142.3 0.6 bitcast_convert_fusion.1.bias_ref
  142.9 1.5 reshape.175.mark_ref
  144.4 1.4 collective-permute-done.4.other_ref
  145.8 12.0 %all-gather.2.cloned.1.call-done.refs_0_ = bf16[1024,8192]{1,0:T(8,128)(2,1)} async-done(((bf16[32,8192]{1,0:T(8,128)(2,1)}), bf16[1024,8192]{1,0:T(8,128)(2,1)}) %all-gather.2.cloned.1.call-update) | async-done | bytes 16777232 | tf_op jit(solution)/shard_map/all_gather | solution.py:1032
  157.8 38.9 %feed.1 = (bf16[1536,2048]{1,0:T(8,128)(2,1)}, bf16[1536,2048]{1,0:T(8,128)(2,1)}, bf16[1536,1024]{1,0:T(8,128)(2,1)}, bf16[1536,1024]{1,0:T(8,128)(2,1)}, f32[7...) custom-call(bf16[768,1024]{1,0:T(8,128)(2,1)} %get-tuple-element.58., ...), custom_call_target="tpu_custom_call" | custom-call | flops 25769803776 | bytes 16777216 | tf_op jit(solution)/shard_map/feed/pallas_call | solution.py:723
  196.7 12.3 %outer.3 = bf16[2048,1024]{1,0:T(8,128)(2,1)} custom-call(bf16[1536,2048]{1,0:T(8,128)(2,1)} %get-tuple-element.83.left_ref, bf16[1536,1024]{1,0:T(8,128)(2,1)} %get-tuple-element.62.out_ref.right_ref), custom_call_target="tpu_custom_call" | custom-call | flops 6442450944 | bytes 13631488 | tf_op jit(solution)/shard_map/outer/pallas_call | solution.py:761
  209.0 1.4 copy-done.17
  210.4 0.3 collective-permute-start.6
  210.6 0.2 copy-done.15
  210.8 0.3 collective-permute-start.7
  211.1 2.7 collective-permute-done.6.recv_ref
  213.8 2.2 collective-permute-done.7.lift_recv_ref
  216.0 1.2 copy-done.7
  217.2 9.2 %second_back.1 = (f32[768,1024]{1,0:T(8,128)}, bf16[768,1024]{1,0:T(8,128)(2,1)}, bf16[768,1024]{1,0:T(8,128)(2,1)}, f32[8,1024]{1,0:T(8,128)}) custom-call(f32[768,1024]{1,0:T(8,128)} %get-tuple-element.59.grad_ref, bf16[768,1024]{1,0:T(8,128)(2,1)} %copy-done.6, f32[768,1024]{1,0:T(8,128)} %get-tuple-element.61.middle_ref, ...), custom_call_target="tpu_custom_call" | custom-call | tf_op jit(solution)/shard_map/second_back/pallas_call | solution.py:807
  226.4 0.3 collective-permute-start.8
  226.8 0.9 fusion
  227.7 0.7 pad.13.bias_ref
  228.4 11.5 %outer.2 = bf16[1024,2048]{1,0:T(8,128)(2,1)} custom-call(bf16[1536,1024]{1,0:T(8,128)(2,1)} %get-tuple-element.67.left_ref, bf16[1536,2048]{1,0:T(8,128)(2,1)} %get-tuple-element.68.right_ref), custom_call_target="tpu_custom_call" | custom-call | flops 6442450944 | bytes 13631488 | tf_op jit(solution)/shard_map/outer/pallas_call | solution.py:761
  239.9 0.1 constant_dynamic-update-slice_fusion.1
  240.1 0.1 constant_dynamic-update-slice_fusion
  240.2 1.1 copy-done.5
  241.3 3.1 convolution_convert_fusion
  244.3 1.8 convolution_convert_fusion.2
  246.2 0.1 constant_dynamic-slice_fusion.1
  246.3 0.3 collective-permute-start.9
  246.6 30.1 %attend_back.1 = (bf16[2,2,384,1536]{3,2,1,0:T(8,128)(2,1)}, f32[2,4,2,128]{3,2,1,0:T(2,128)}) custom-call(bf16[2,2,384,1536]{3,2,1,0:T(8,128)(2,1)} %bitcast.101, bf16[2,2,384,1536]{3,2,1,0:T(8,128)(2,1)} %bitcast.102, bf16[2,2,384,1536]{3,2,1,0:T(8,128)(2,1)} %bitcast.103, f32[2,2,384,1]{3,2,1,0:T(8,128)} %copy-done.2, f32[2,4,2,768]{3,2,1,0:T(2,128)} %copy-done.3, ...), custom_call_target="tpu_custom_call" | custom-call | flops 6039797760 | bytes 14155776 | tf_op jit(solution)/shard_map/attend_back/pallas_call | solution.py:519
  276.7 0.7 reduce_sum.9
  277.4 0.7 concatenate.48.sums_ref
  278.1 1.5 maximum_select_fusion.1
  279.6 108.9 %tail.1 = (f32[32,4096]{1,0:T(8,128)}, f32[32,3072]{1,0:T(8,128)}, f32[32,1024]{1,0:T(8,128)}, f32[48,128]{1,0:T(8,128)}, f32[768,1024]{1,0:T(8,128)}) custom-call(bf16[16,2,32,2048]{3,2,1,0:T(8,128)(2,1)} %bitcast.77, bf16[16,2,32,512]{3,2,1,0:T(8,128)(2,1)} %bitcast.76, f32[8,1024]{1,0:T(8,128)} %concatenate.48.sums_ref, ...), custom_call_target="tpu_custom_call" | custom-call | tf_op jit(solution)/shard_map/tail/pallas_call | solution.py:948
  388.5 2.4 finish.1
  390.9 1.5 slice_bitcast_fusion
  392.4 4.0 copy.81
  (51 shorter events, 0.2 us)
Async XLA Ops:
  7.2 150.7 %all-gather.2.cloned.1.call-start = ((), (), s32[]{:S(2)}) async-start(), calls=%async_computation.1 | async-start | bytes 17301504 | tf_op jit(solution)/shard_map/all_gather | solution.py:1032
  9.1 379.4 %reduce-scatter.2.cloned.1.call-start = ((), (), s32[]{:S(2)}) async-start(), calls=%async_computation.2 | async-start | bytes 4456448 | tf_op jit(solution)/shard_map/reduce_scatter | solution.py:1090
  9.2 74.1 %collective-permute-start = (bf16[768,1024]{1,0:T(8,128)(2,1)}, bf16[768,1024]{1,0:T(8,128)(2,1)}, u32[]{:S(2)}, u32[]{:S(2)}) collective-permute-start(bf16[768,1024]{1,0:T(8,128)(2,1)} %bitcast.69), channel_id=1, source_target_pairs={{0,1},{1,0},{2,3},{3,2},{4,5},{5,4},{6,7},{7,6},{8,9},{9,8},{10,11... | collective-permute-start | bytes 4718600 | tf_op jit(solution)/shard_map/ppermute | solution.py:34
  9.7 72.7 %collective-permute-start.1 = (s32[2,384]{1,0:T(2,128)}, s32[2,384]{1,0:T(2,128)S(1)}, u32[]{:S(2)}, u32[]{:S(2)}) collective-permute-start(s32[2,384]{1,0:T(2,128)} %param.17), channel_id=1, source_target_pairs={{0,1},{1,0},{2,3},{3,2},{4,5},{5,4},{6,7},{7,6},{8,9},{9,8},{10,11... | collective-permute-start | bytes 9224 | tf_op jit(solution)/shard_map/ppermute | solution.py:34
  11.4 0.6 copy-start.11
  79.4 1.5 copy-start.10
  79.4 3.0 copy-start.12
  80.8 2.1 collective-permute-start.2
  82.9 11.7 %copy-start.2 = (f32[2,2,384,1]{3,2,1,0:T(8,128)}, f32[2,2,384,1]{3,2,1,0:T(8,128)S(1)}, u32[]{:S(2)}) copy-start(f32[2,2,384,1]{3,2,1,0:T(8,128)S(1)} %broadcast_select_fusion.penalty_ref) | copy-start | bytes 18436
  83.2 45.7 %copy-start.4 = (bf16[512,1024]{1,0:T(8,128)(2,1)}, bf16[512,1024]{1,0:T(8,128)(2,1)S(1)}, u32[]{:S(2)}) copy-start(bf16[512,1024]{1,0:T(8,128)(2,1)S(1)} %maximum_select_fusion.weight_ref) | copy-start | bytes 3145732
  128.8 1.2 copy-start
  128.8 1.2 copy-start.3
  129.9 3.6 collective-permute-start.3
  130.4 14.0 %collective-permute-start.5 = (bf16[768,1024]{1,0:T(8,128)(2,1)}, bf16[768,1024]{1,0:T(8,128)(2,1)S(1)}, u32[]{:S(2)}, u32[]{:S(2)}) collective-permute-start(bf16[768,1024]{1,0:T(8,128)(2,1)} %bitcast.23.grad_own_ref), channel_id=1, source_target_pairs={{0,1},{1,0},{2,3},{3,2},{4,5},{5,4},{6,7},{7,6},{8,9},{9,8},{10,11... | collective-permute-start | bytes 4718600 | tf_op jit(solution)/shard_map/ppermute | solution.py:34
  133.5 1.1 copy-start.9
  140.8 5.0 %collective-permute-start.4 = (bf16[768,1024]{1,0:T(8,128)(2,1)}, bf16[768,1024]{1,0:T(8,128)(2,1)S(1)}, u32[]{:S(2)}, u32[]{:S(2)}) collective-permute-start(bf16[768,1024]{1,0:T(8,128)(2,1)} %get-tuple-element.58.own_ref), channel_id=1, source_target_pairs={{0,1},{1,0},{2,3},{3,2},{4,5},{5,4},{6,7},{7,6},{8,9},{9,8},{10,11... | collective-permute-start | bytes 4718600 | tf_op jit(solution)/shard_map/ppermute | solution.py:34
  144.4 13.4 %copy-start.14 = (bf16[768,1024]{1,0:T(8,128)(2,1)}, bf16[768,1024]{1,0:T(8,128)(2,1)S(1)}, u32[]{:S(2)}) copy-start(bf16[768,1024]{1,0:T(8,128)(2,1)S(1)} %collective-permute-done.5.grad_other_ref) | copy-start | bytes 4718596
  145.8 12.0 %copy-start.16 = (bf16[768,1024]{1,0:T(8,128)(2,1)}, bf16[768,1024]{1,0:T(8,128)(2,1)S(1)}, u32[]{:S(2)}) copy-start(bf16[768,1024]{1,0:T(8,128)(2,1)S(1)} %collective-permute-done.4.other_ref) | copy-start | bytes 4718596
  209.0 1.4 copy-start.17
  209.0 1.9 copy-start.15
  210.4 3.4 collective-permute-start.6
  210.8 5.2 %collective-permute-start.7 = (bf16[768,1024]{1,0:T(8,128)(2,1)S(1)}, bf16[768,1024]{1,0:T(8,128)(2,1)S(1)}, u32[]{:S(2)}, u32[]{:S(2)}) collective-permute-start(bf16[768,1024]{1,0:T(8,128)(2,1)S(1)} %copy-done.15), channel_id=1, source_target_pairs={{0,1},{1,0},{2,3},{3,2},{4,5},{5,4},{6,7},{7,6},{8,9},{9,8},{10,11... | collective-permute-start | bytes 4718600 | tf_op jit(solution)/shard_map/ppermute | solution.py:34
  213.8 2.3 copy-start.6
  216.0 1.2 copy-start.7
  226.4 13.6 %collective-permute-start.8 = (bf16[768,1024]{1,0:T(8,128)(2,1)}, bf16[768,1024]{1,0:T(8,128)(2,1)S(1)}, u32[]{:S(2)}, u32[]{:S(2)}) collective-permute-start(bf16[768,1024]{1,0:T(8,128)(2,1)} %get-tuple-element.66), channel_id=1, source_target_pairs={{0,1},{1,0},{2,3},{3,2},{4,5},{5,4},{6,7},{7,6},{8,9},{9,8},{10,11... | collective-permute-start | bytes 4718600 | tf_op jit(solution)/shard_map/ppermute | solution.py:34
  228.4 11.5 %copy-start.13 = (f32[8,1024]{1,0:T(8,128)S(1)}, f32[8,1024]{1,0:T(8,128)}, u32[]{:S(2)}) copy-start(f32[8,1024]{1,0:T(8,128)} %get-tuple-element.74) | copy-start | bytes 98308
  228.4 11.5 %copy-start.8 = (bf16[768,1024]{1,0:T(8,128)(2,1)S(1)}, bf16[768,1024]{1,0:T(8,128)(2,1)}, u32[]{:S(2)}) copy-start(bf16[768,1024]{1,0:T(8,128)(2,1)} %get-tuple-element.66) | copy-start | bytes 4718596
  240.0 1.2 copy-start.5
  241.3 3.1 copy-start.1
  246.3 31.8 %collective-permute-start.9 = (bf16[512,512]{1,0:T(8,128)(2,1)S(1)}, bf16[512,512]{1,0:T(8,128)(2,1)S(1)}, u32[]{:S(2)}, u32[]{:S(2)}) collective-permute-start(bf16[512,512]{1,0:T(8,128)(2,1)S(1)} %get-tuple-element.92), channel_id=1, source_target_pairs={{0,1},{1,0},{2,3},{3,2},{4,5},{5,4},{6,7},{7,6},{8,9},{9,8},{10,11... | collective-permute-start | bytes 1572872 | tf_op jit(solution)/shard_map/ppermute | solution.py:34
Sparse Core Ops, SparseCore 0:
  11.4 146.3 all-gather.1
  209.1 107.4 reduce-scatter.1

commit v5 on v4

--- a/solution.py
+++ b/solution.py
@@ -270,12 +270,23 @@
         self.arrive_near(w, 0)
         for j in range(3):
             self.arrive(w, 24 + j, self.recv_z[w].at[j])
+        rows = self.ins[w].shape[2]
 
         def total_of(half, part):
             total = self.near_sum(w, 0, half, part)
             for j in range(3):
                 total = total + self.recv_z[w][j, half, part].astype(F32)
             return total
+
+        if self.kinds[w] == "rows":
+
+            @pl.loop(0, rows // 16)
+            def _(i):
+                for half in range(2):
+                    part = pl.ds(pl.multiple_of(i * 16, 16), 16)
+                    self.outs[w][pl.ds(pl.multiple_of(half * rows + i * 16, 16), 16)] = total_of(half, part)
+
+            return
 
         def other(part):
             self.stage[w][part] = total_of(1 - self.core, part)
@@ -353,9 +364,9 @@
 
 
 def scatter_shapes(shapes, kinds):
-    return [
-        jax.ShapeDtypeStruct((s[2], s[3] * (1 if kind == "sum" else 2)), F32) for s, kind in zip(shapes, kinds)
-    ]
+    factors = {"sum": (1, 1), "rows": (2, 1)}
+    sizes = [factors.get(kind, (1, 2)) for kind in kinds]
+    return [jax.ShapeDtypeStruct((s[2] * a, s[3] * b), F32) for s, (a, b) in zip(shapes, sizes)]
 
 
 def scatter_kernel(kinds, *refs):
@@ -458,7 +469,57 @@
     )(projected, projected, projected, penalty)
 
 
-def attend_back_kernel(
+def attend_back_kernel(chunk, *refs):
+    if len(refs) == 16:
+        attend_back_step(chunk, *refs)
+        return
+    inputs, (down_ref, norm_hbm, pre_hbm), (back_out, bias_out, down_out, up_out) = refs[:7], refs[7:10], refs[10:14]
+    buffers, (norm, pre, load_sem), scratch = refs[14:21], refs[21:24], refs[24:]
+    scatter = Scatter(("rows",), (down_ref,), (down_out,), scratch)
+    step = pl.program_id(0) * pl.num_programs(1) + pl.program_id(1)
+    total = pl.num_programs(0) * pl.num_programs(1)
+
+    def start():
+        pltpu.make_async_copy(norm_hbm, norm, load_sem.at[0]).start()
+        pltpu.make_async_copy(pre_hbm, pre, load_sem.at[1]).start()
+        scatter.meet()
+        scatter.opening(0)
+
+    def two():
+        scatter.relay(0, 1), scatter.far(0, 3), scatter.near(0, 2)
+
+    def four():
+        scatter.relay(0, 2), scatter.far(0, 0), scatter.near(0, 3), scatter.cross(0, 1)
+
+    def five():
+        scatter.relay(0, 3), scatter.near(0, 0)
+
+    def six():
+        scatter.cross(0, 2)
+
+    def seven():
+        scatter.relay(0, 0)
+
+    def end():
+        scatter.cross(0, 3)
+        pltpu.make_async_copy(norm_hbm, norm, load_sem.at[0]).wait()
+        pltpu.make_async_copy(pre_hbm, pre, load_sem.at[1]).wait()
+
+        @pl.loop(0, norm.shape[1] // 256)
+        def _(i):
+            part = pl.ds(pl.multiple_of(i * 256, 256), 256)
+            up_out[part] = product_left_t(norm[:, part], pre[...]).astype(BF)
+
+        scatter.last(0)
+        scatter.drain()
+
+    for place, work in ((0, start), (2, two), (4, four), (5, five), (6, six), (7, seven)):
+        pl.when(step == place)(work)
+    attend_back_step(chunk, *inputs, back_out, bias_out, *buffers)
+    pl.when(step == total - 1)(end)
+
+
+def attend_back_step(
     chunk, q_ref, k_ref, v_ref, penalty_ref, log_ref, att_ref, grad_ref, out_ref, bias_ref,
     query_buf, grad_buf, mixed_buf, back_buf, key_sum, value_sum, bias_sum,
 ):
@@ -507,42 +568,64 @@
     bias_ref[0, 0, 1:2] = jnp.sum(value_sum[...], axis=0, keepdims=True)
 
 
-def attend_back(projected, penalty, logs, attended, grad_attended):
+def attend_back(projected, penalty, logs, attended, grad_attended, grad_down, norm_two, grad_pre):
     _, clips, rows, triple = projected.shape
     slots = 2 * rows
     width = triple // 3
     pairs = width // (2 * HEAD)
+    fused = lax.axis_size(AX) == 32 and clips * pairs == 8
 
     def block(offset):
         return pl.BlockSpec((2, 1, rows, 2 * HEAD), lambda i, j: (0, i, 0, offset * pairs + j))
 
-    return pl.pallas_call(
+    in_specs = [
+        block(0), block(1), block(2),
+        pl.BlockSpec((2, 1, rows, 1), lambda i, j: (0, i, 0, 0)),
+        pl.BlockSpec((1, 1, 2, slots), lambda i, j: (i, j, 0, 0)),
+        block(0), block(0),
+    ]
+    out_specs = [
+        pl.BlockSpec((2, 1, rows, triple), lambda i, j: (0, i, 0, 0)),
+        pl.BlockSpec((1, 1, 2, 2 * HEAD), lambda i, j: (i, j, 0, 0)),
+    ]
+    out_shape = [
+        jax.ShapeDtypeStruct((2, clips, rows, triple), BF),
+        jax.ShapeDtypeStruct((clips, pairs, 2, 2 * HEAD), F32),
+    ]
+    operands = [projected, projected, projected, penalty, logs, attended, grad_attended]
+    scratch = [pltpu.VMEM((slots, 2 * HEAD), BF)] * 4 + [pltpu.VMEM((slots, 2 * HEAD), F32)] * 2
+    scratch += [pltpu.VMEM((8, 2 * HEAD), F32)]
+    params = pltpu.CompilerParams(vmem_limit_bytes=60 << 20)
+    if fused:
+        up_shape = (norm_two.shape[1], grad_pre.shape[1])
+        sums = scatter_shapes([grad_down.shape], ("rows",))
+        in_specs += [pl.BlockSpec(grad_down.shape, lambda i, j: (0, 0, 0, 0), pipeline_mode=pl.Buffered(1))]
+        in_specs += [pl.BlockSpec(memory_space=pl.ANY)] * 2
+        out_specs += [pl.BlockSpec(sums[0].shape, lambda i, j: (0, 0)), pl.BlockSpec(up_shape, lambda i, j: (0, 0))]
+        out_shape += [sums[0], jax.ShapeDtypeStruct(up_shape, BF)]
+        operands += [grad_down, norm_two, grad_pre]
+        scratch += [pltpu.VMEM(norm_two.shape, BF), pltpu.VMEM(grad_pre.shape, BF), pltpu.SemaphoreType.DMA((2,))]
+        scratch += scatter_scratch([grad_down.shape])
+        params = pltpu.CompilerParams(vmem_limit_bytes=60 << 20, collective_id=2, has_side_effects=True)
+    outs = pl.pallas_call(
         functools.partial(attend_back_kernel, 256),
         grid=(clips, pairs),
-        in_specs=[
-            block(0), block(1), block(2),
-            pl.BlockSpec((2, 1, rows, 1), lambda i, j: (0, i, 0, 0)),
-            pl.BlockSpec((1, 1, 2, slots), lambda i, j: (i, j, 0, 0)),
-            block(0), block(0),
-        ],
-        out_specs=[
-            pl.BlockSpec((2, 1, rows, triple), lambda i, j: (0, i, 0, 0)),
-            pl.BlockSpec((1, 1, 2, 2 * HEAD), lambda i, j: (i, j, 0, 0)),
-        ],
-        out_shape=[
-            jax.ShapeDtypeStruct((2, clips, rows, triple), BF),
-            jax.ShapeDtypeStruct((clips, pairs, 2, 2 * HEAD), F32),
-        ],
-        scratch_shapes=[pltpu.VMEM((slots, 2 * HEAD), BF)] * 4
-        + [pltpu.VMEM((slots, 2 * HEAD), F32)] * 2
-        + [pltpu.VMEM((8, 2 * HEAD), F32)],
-        compiler_params=pltpu.CompilerParams(vmem_limit_bytes=56 << 20),
+        in_specs=in_specs,
+        out_specs=out_specs,
+        out_shape=out_shape,
+        scratch_shapes=scratch,
+        compiler_params=params,
         cost_estimate=pl.CostEstimate(
             flops=10 * clips * pairs * slots * slots * 2 * HEAD, bytes_accessed=18 * clips * slots * width,
             transcendentals=clips * pairs * 2 * slots * slots,
         ),
         name="attend_back",
-    )(projected, projected, projected, penalty, logs, attended, grad_attended)
+    )(*operands)
+    if not fused:
+        total = lax.psum_scatter(grad_down, AX, scatter_dimension=0, axis_index_groups=same_core_groups())
+        total = total.astype(F32).reshape(-1, total.shape[-1])
+        outs = [*outs, total, outer(norm_two, grad_pre)]
+    return outs
 
 
 def normal_parts(values):
@@ -645,8 +728,8 @@
         sources = None
     else:
         sources, refs = refs[:2], refs[2:]
-    act_ref, pre_ref, norm_ref, grad_ref, lift_own_ref, lift_other_ref, pass_own_ref, pass_other_ref = refs[:8]
-    sums_ref, up_ref, down_ref, up_sem, down_sem = refs[8:]
+    act_ref, pre_ref, norm_ref, grad_ref, pass_own_ref, pass_other_ref, sums_ref, down_hbm = refs[:8]
+    up_ref, down_ref, up_sem, down_sem, out_sem = refs[8:]
     step = pl.program_id(0)
     features, hidden = up_ref.shape
 
@@ -680,6 +763,7 @@
                     ).start()
         pltpu.make_async_copy(up_ref, up_ref, up_sem).wait()
         pltpu.make_async_copy(down_ref, down_ref, down_sem).wait()
+        pltpu.make_async_copy(down_ref, down_hbm, out_sem).start()
 
     rows = jnp.where(step < steps, other_ref[...], own_ref[...])
     grads = jnp.where(step < steps, grad_other_ref[...], grad_own_ref[...]) * mark_ref[...].astype(BF)
@@ -695,15 +779,16 @@
         grad_pre = product_right_t(grads, down_ref[part]) * (normal_cdf + pre * density)
         sums_ref[0:1, part] += jnp.sum(grad_pre, axis=0, keepdims=True)
         pre_ref[:, part] = grad_pre.astype(BF)
-    lifted = product(act_ref[...], down_ref[...])
     passed = product_right_t(pre_ref[...], up_ref[...])
-    lift_own_ref[...] = lifted
     pass_own_ref[...] = passed
 
     @pl.when(step < steps)
     def _():
-        lift_other_ref[...] = lifted.astype(BF)
         pass_other_ref[...] = passed.astype(BF)
+
+    @pl.when(step == 2 * steps - 1)
+    def _():
+        pltpu.make_async_copy(down_ref, down_hbm, out_sem).wait()
 
 
 def feed(own, other, grad_own, grad_other, marks, weights, bias, unit):
@@ -727,23 +812,22 @@
         + [pl.BlockSpec(memory_space=pl.ANY)] * len(weights),
         out_specs=[
             both_spec(hidden), both_spec(hidden), both_spec(features), both_spec(features),
-            own_spec, other_spec, own_spec, other_spec,
-            pl.BlockSpec((8, hidden), lambda i: (0, 0)),
+            own_spec, other_spec,
+            pl.BlockSpec((8, hidden), lambda i: (0, 0)), pl.BlockSpec(memory_space=pl.ANY),
         ],
         out_shape=[
             jax.ShapeDtypeStruct((2 * rows, hidden), BF), jax.ShapeDtypeStruct((2 * rows, hidden), BF),
             jax.ShapeDtypeStruct((2 * rows, features), BF), jax.ShapeDtypeStruct((2 * rows, features), BF),
             jax.ShapeDtypeStruct((rows, features), F32), jax.ShapeDtypeStruct((rows, features), BF),
-            jax.ShapeDtypeStruct((rows, features), F32), jax.ShapeDtypeStruct((rows, features), BF),
-            jax.ShapeDtypeStruct((8, hidden), F32),
+            jax.ShapeDtypeStruct((8, hidden), F32), jax.ShapeDtypeStruct((hidden, features), BF),
         ],
         scratch_shapes=[
             pltpu.VMEM((features, hidden), BF), pltpu.VMEM((hidden, features), BF),
-            pltpu.SemaphoreType.DMA(()), pltpu.SemaphoreType.DMA(()),
+            pltpu.SemaphoreType.DMA(()), pltpu.SemaphoreType.DMA(()), pltpu.SemaphoreType.DMA(()),
         ],
         compiler_params=PARAMS,
         cost_estimate=pl.CostEstimate(
-            flops=16 * rows * features * hidden, bytes_accessed=8 * features * hidden,
+            flops=12 * rows * features * hidden, bytes_accessed=8 * features * hidden,
             transcendentals=4 * rows * hidden,
         ),
         name="feed",
@@ -785,13 +869,10 @@
 
 
 def second_back_kernel(
-    grad_ref, recv_ref, middle_ref, out_ref, lift_ref, lift_recv_ref, gain_ref, bias_ref,
-    full_ref, low_ref, block_ref, sums_ref,
+    grad_ref, recv_ref, middle_ref, out_ref, gain_ref, full_ref, low_ref, sums_ref
 ):
     clear_first(sums_ref)
     for part in strips_of(grad_ref):
-        lifted = lift_ref[part] + lift_recv_ref[part].astype(F32)
-        block_ref[part] = (middle_ref[part] + lifted + bias_ref[...]).astype(BF)
         grad_normed = grad_ref[part] + recv_ref[part].astype(F32)
         scaled, inverse = normal_parts(middle_ref[part])
         grad_out = out_ref[part].astype(F32)
@@ -801,21 +882,21 @@
         gather_sums(sums_ref, [grad_normed * scaled, grad_normed, grad_middle, grad_out])
 
 
-def second_back(passed, received, middle, grad_out, lifted, lift_received, gain, bias):
+def second_back(passed, received, middle, grad_out, gain):
     rows, features = middle.shape
     size = rows // 4
     return pl.pallas_call(
         second_back_kernel,
         grid=(4,),
-        in_specs=[rows_spec(size, features)] * 6 + [whole_spec((1, features))] * 2,
-        out_specs=[rows_spec(size, features)] * 3 + [pl.BlockSpec((8, features), lambda i: (0, 0))],
+        in_specs=[rows_spec(size, features)] * 4 + [whole_spec((1, features))],
+        out_specs=[rows_spec(size, features)] * 2 + [pl.BlockSpec((8, features), lambda i: (0, 0))],
         out_shape=[
             jax.ShapeDtypeStruct((rows, features), F32), jax.ShapeDtypeStruct((rows, features), BF),
-            jax.ShapeDtypeStruct((rows, features), BF), jax.ShapeDtypeStruct((8, features), F32),
+            jax.ShapeDtypeStruct((8, features), F32),
         ],
         compiler_params=PARAMS,
         name="second_back",
-    )(passed, received, middle, grad_out, lifted, lift_received, gain, bias)
+    )(passed, received, middle, grad_out, gain)
 
 
 def first_back_kernel(grad_ref, weight_ref, recv_ref, token_ref, middle_ref, gain_ref, full_ref, sums_ref):
@@ -847,17 +928,22 @@
 
 
 def tail_kernel(
-    kinds, up_ref, proj_ref, sums_ref, bias_ref, gain_ref, back_hbm, weight_hbm, norm_hbm, token_hbm, middle_hbm,
-    up_out, qkv_out, proj_out, packed_out, tokens_out, *refs
+    kinds, up_ref, proj_ref, sums_ref, bias_ref, gain_ref, shift_ref,
+    back_hbm, weight_hbm, norm_hbm, token_hbm, middle_hbm, down_hbm, act_hbm, sum_hbm,
+    up_out, qkv_out, proj_out, packed_out, tokens_out, block_out, *refs
 ):
-    back, weight, norm, token, middle, qkv, packed, vectors, stage, land, load_sem, pass_sem = refs[:12]
-    scatter = Scatter(kinds, (up_ref, qkv, proj_ref, packed), (up_out, qkv_out, proj_out, packed_out), refs[12:])
+    back, weight, norm, token, middle, down, qkv, packed, vectors, stage, land, load_sem, pass_sem = refs[:13]
+    act, total, lift_stage, lift_land, block_sem = refs[13:18]
+    scatter = Scatter(kinds, (up_ref, qkv, proj_ref, packed), (up_out, qkv_out, proj_out, packed_out), refs[18:])
     chips, _, shard, triple = qkv.shape
     own_rows = token.shape[0]
     loads = [
         pltpu.make_async_copy(source, target, load_sem.at[i])
         for i, (source, target) in enumerate(
-            ((back_hbm, back), (weight_hbm, weight), (norm_hbm, norm), (token_hbm, token), (middle_hbm, middle))
+            (
+                (back_hbm, back), (weight_hbm, weight), (norm_hbm, norm), (token_hbm, token), (middle_hbm, middle),
+                (down_hbm, down),
+            )
         )
     ]
     for load in loads:
@@ -917,8 +1003,36 @@
     scatter.relay(0, 0), scatter.cross(0, 3)
     for j in (1, 2, 3):
         scatter.cross(2, j)
+    loads[5].wait()
+
+    def fetch(source, start, target, slot):
+        copy = pltpu.make_async_copy(source.at[pl.ds(start, 256)], target, block_sem.at[slot])
+        copy.start()
+        return copy
+
+    @pl.loop(0, own_rows // 256)
+    def _(i):
+        fetch(act_hbm, pl.multiple_of(own_rows + i * 256, 256), act, 0).wait()
+        lift_stage[pl.ds(pl.multiple_of(i * 256, 256), 256)] = product(act[...], down[...]).astype(BF)
+
+    lifting = pltpu.make_async_remote_copy(
+        src_ref=lift_stage, dst_ref=lift_land, send_sem=pass_sem.at[2], recv_sem=pass_sem.at[3],
+        device_id=(scatter.mate,), device_id_type=MESH,
+    )
+    lifting.start()
     scatter.relay(1, 1), scatter.far(1, 3), scatter.near(1, 2)
     scatter.relay(1, 2), scatter.far(1, 0), scatter.near(1, 3)
+    lifting.wait()
+
+    @pl.loop(0, own_rows // 256)
+    def _(i):
+        start = pl.multiple_of(i * 256, 256)
+        copies = fetch(act_hbm, start, act, 0), fetch(sum_hbm, start, total, 1)
+        for copy in copies:
+            copy.wait()
+        lifted = product(act[...], down[...]) + lift_land[pl.ds(start, 256)].astype(F32)
+        block_out[pl.ds(start, 256)] = (total[...] + lifted + shift_ref[...]).astype(BF)
+
     for j in (1, 2, 3, 0):
         scatter.relay(3, j)
     scatter.last(2)
@@ -935,7 +1049,7 @@
     scatter.drain()
 
 
-def tail(grad_up, grad_proj, sums, bias_rows, gain, back, weight, norm, tokens, middle):
+def tail(grad_up, grad_proj, sums, bias_rows, gain, shift, back, weight, norm, tokens, grad_middle, down, act, middle):
     chips, _, shard, hidden = grad_up.shape
     rows, triple = back.shape
     own_rows, features = tokens.shape
@@ -947,20 +1061,23 @@
     vmem = pl.BlockSpec(memory_space=pltpu.VMEM)
     return pl.pallas_call(
         functools.partial(tail_kernel, kinds),
-        out_shape=scatter_shapes(shapes, kinds) + [jax.ShapeDtypeStruct((own_rows, features), F32)],
-        in_specs=[vmem] * 5 + [pl.BlockSpec(memory_space=pl.ANY)] * 5,
-        out_specs=[vmem] * 5,
+        out_shape=scatter_shapes(shapes, kinds)
+        + [jax.ShapeDtypeStruct((own_rows, features), F32), jax.ShapeDtypeStruct((own_rows, features), BF)],
+        in_specs=[vmem] * 6 + [pl.BlockSpec(memory_space=pl.ANY)] * 8,
+        out_specs=[vmem] * 6,
         scratch_shapes=[
             pltpu.VMEM(back.shape, BF), pltpu.VMEM(weight.shape, BF), pltpu.VMEM(norm.shape, BF),
-            pltpu.VMEM(tokens.shape, BF), pltpu.VMEM(middle.shape, F32),
+            pltpu.VMEM(tokens.shape, BF), pltpu.VMEM(middle.shape, F32), pltpu.VMEM(down.shape, BF),
             pltpu.VMEM(shapes[1], BF), pltpu.VMEM(shapes[3], BF), pltpu.VMEM((PARAM_COLS, features), F32),
             pltpu.VMEM((own_rows, features), BF), pltpu.VMEM((own_rows, features), BF),
-            pltpu.SemaphoreType.DMA((5,)), pltpu.SemaphoreType.DMA((2,)),
+            pltpu.SemaphoreType.DMA((6,)), pltpu.SemaphoreType.DMA((4,)),
+            pltpu.VMEM((256, act.shape[1]), BF), pltpu.VMEM((256, features), F32),
+            pltpu.VMEM((own_rows, features), BF), pltpu.VMEM((own_rows, features), BF), pltpu.SemaphoreType.DMA((2,)),
         ]
         + scatter_scratch(shapes),
         compiler_params=pltpu.CompilerParams(collective_id=1, has_side_effects=True, vmem_limit_bytes=62 << 20),
         name="tail",
-    )(grad_up, grad_proj, sums, bias_rows, gain, back, weight, norm, tokens, middle)
+    )(grad_up, grad_proj, sums, bias_rows, gain, shift, back, weight, norm, tokens, grad_middle, down, act, middle)
 
 
 def pack_kernel(up_ref, down_ref, out_ref):
@@ -985,28 +1102,33 @@
     )(up, down)
 
 
-def finish_kernel(up_ref, qkv_ref, proj_ref, down_ref, packed_ref, up_out, qkv_out, proj_out, down_out, vec_out, bias_out):
+def finish_kernel(
+    up_ref, qkv_ref, proj_ref, down_ref, token_ref, block_ref, packed_ref,
+    up_out, qkv_out, proj_out, down_out, token_out, block_out, vec_out, bias_out,
+):
+    token_out[...] = token_ref[...]
+    block_out[...] = block_ref[...]
     up_out[...] = up_ref[...]
     qkv_out[...] = qkv_ref[...]
     proj_out[...] = proj_ref[...]
-    down_out[...] = down_ref[...].astype(F32)
+    down_out[...] = down_ref[...]
     shard = vec_out.shape[1]
     vec_out[...] = packed_ref[:shard].T[:8]
     bias_out[...] = packed_ref[shard : shard + 1]
 
 
-def finish(up, qkv, proj, down, packed, shard, unit):
+def finish(up, qkv, proj, down, tokens, block, packed, shard, unit):
     if lax.axis_size(AX) != 32:
-        return up, qkv, proj, down.astype(F32), packed[:shard, :8].T, packed[shard : shard + 1, :unit]
+        return up, qkv, proj, down, tokens, block, packed[:shard, :8].T, packed[shard : shard + 1, :unit]
     return pl.pallas_call(
         finish_kernel,
-        out_shape=[jax.ShapeDtypeStruct(a.shape, F32) for a in (up, qkv, proj, down)]
+        out_shape=[jax.ShapeDtypeStruct(a.shape, a.dtype) for a in (up, qkv, proj, down, tokens, block)]
         + [jax.ShapeDtypeStruct((8, shard), F32), jax.ShapeDtypeStruct((1, unit), F32)],
-        in_specs=[pl.BlockSpec(memory_space=pltpu.VMEM)] * 5,
-        out_specs=[pl.BlockSpec(memory_space=pltpu.VMEM)] * 6,
+        in_specs=[pl.BlockSpec(memory_space=pltpu.VMEM)] * 7,
+        out_specs=[pl.BlockSpec(memory_space=pltpu.VMEM)] * 8,
         compiler_params=PARAMS,
         name="finish",
-    )(up, qkv, proj, down, packed)
+    )(up, qkv, proj, down, tokens, block, packed)
 
 
 def by_core(core, own, other, axis):
@@ -1078,31 +1200,27 @@
     middle, norm_own = second_norm(
         attended_flat, weight_proj, own_tokens, mixed, bias_proj, gain_two, shift_two
     )
-    activation, grad_pre, norm_two, grad_out, lifted, lifted_other, passed, passed_other, up_sums = feed(
+    activation, grad_pre, norm_two, grad_out, passed, passed_other, up_sums, weight_down = feed(
         norm_own, swap(norm_own), own_cotangent, swap(own_cotangent),
         (marks > 0).astype(F32).reshape(every, 1), feed_weights, bias_up, unit,
     )
     grad_bias_up = up_sums[0]
     passed_other = swap(passed_other)
-    lifted_other = swap(lifted_other)
 
     grad_down = outer(activation, grad_out)
-    down_weight_grad = lax.psum_scatter(
-        grad_down, AX, scatter_dimension=0, tiled=True, axis_index_groups=same_core_groups()
-    )
-    grad_middle, grad_low, block_output, second_sums = second_back(
-        passed, passed_other, middle, grad_out, lifted, lifted_other, gain_two, bias_down
-    )
-    block_output = block_output.reshape(micro, rows, features)
-    grad_up = outer(norm_two, grad_pre)
+    passed_other, grad_down = lax.optimization_barrier((passed_other, grad_down))
+    grad_middle, grad_low, second_sums = second_back(passed, passed_other, middle, grad_out, gain_two)
     grad_low = jnp.concatenate([grad_low, swap(grad_low)], 0)
     grad_attended = product_right_t(grad_low, weight_proj).astype(BF).reshape(2, micro, rows, width)
     grad_proj = product_left_t(attended_flat, grad_low).astype(BF)
-    grad_attended, grad_proj, grad_up = lax.optimization_barrier((grad_attended, grad_proj, grad_up))
+    grad_attended, grad_proj = lax.optimization_barrier((grad_attended, grad_proj))
     grad_proj_own = lax.dynamic_slice_in_dim(grad_proj, core * width, width, 1)
     grad_proj_other = swap(lax.dynamic_slice_in_dim(grad_proj, (1 - core) * width, width, 1))
     grad_proj = by_core(core, grad_proj_own, grad_proj_other, 0)
-    grad_projected, grad_bias = attend_back(projected, penalty, logs, attended, grad_attended)
+    grad_projected, grad_bias, down_weight_grad, grad_up = attend_back(
+        projected, penalty, logs, attended, grad_attended, grad_down.reshape(chips, 2, unit // 2, features),
+        norm_two, grad_pre,
+    )
     grad_projected = grad_projected.reshape(every, 3 * width)
 
     grad_bias = jnp.sum(grad_bias, axis=0).transpose(1, 0, 2).reshape(2, width)
@@ -1115,10 +1233,13 @@
     if devices == 32:
         bias_rows = jnp.pad(up_units, ((0, 0), (0, 0), (0, 15), (0, 0)))
         sums = jnp.concatenate([jnp.zeros((2, features), F32)] + sums, 0)
-        up_weight_grad, qkv_weight_grad, proj_weight_grad, packed_sum, tokens_grad = tail(
-            grad_up, grad_proj, sums, bias_rows, gain_one, grad_projected, weight_qkv, norm_one, own_tokens, grad_middle
+        up_weight_grad, qkv_weight_grad, proj_weight_grad, packed_sum, tokens_grad, block_output = tail(
+            grad_up, grad_proj, sums, bias_rows, gain_one, bias_down, grad_projected, weight_qkv, norm_one, own_tokens,
+            grad_middle, weight_down, activation, middle,
         )
     else:
+        lifted = swap(product(activation[own_rows:], weight_down).astype(BF)).astype(F32)
+        block_output = (middle + product(activation[:own_rows], weight_down) + lifted + bias_down).astype(BF)
         passed = swap(product_right_t(grad_projected[own_rows:], weight_qkv).astype(BF))
         grad_qkv = outer(norm_one, grad_projected)
         tokens_grad, first_sums = first_back(
@@ -1131,10 +1252,15 @@
         up_weight_grad, qkv_weight_grad, proj_weight_grad, packed_sum = scatter_chips(
             [grad_up, grad_qkv.reshape(chips, 2, shard, 3 * width), grad_proj, sums], (chips, 3, 1, "sum")
         )
+    (
+        up_weight_grad, qkv_weight_grad, proj_weight_grad, down_weight_grad, tokens_grad, block_output,
+        vector_sum, up_bias_grad,
+    ) = finish(
+        up_weight_grad, qkv_weight_grad, proj_weight_grad, down_weight_grad, tokens_grad, block_output,
+        packed_sum, shard, unit,
+    )
     tokens_grad = tokens_grad.reshape(micro, rows, features)
-    up_weight_grad, qkv_weight_grad, proj_weight_grad, down_weight_grad, vector_sum, up_bias_grad = finish(
-        up_weight_grad, qkv_weight_grad, proj_weight_grad, down_weight_grad, packed_sum, shard, unit
-    )
+    block_output = block_output.reshape(micro, rows, features)
     up_bias_grad = up_bias_grad[0]
     return (
         block_output, tokens_grad, vector_sum[0], vector_sum[1], qkv_weight_grad, vector_sum[2], vector_sum[3],

time: 406 us -> 392 us (0.966)
  waiting for transfers between devices: 21.4 us -> 16 us
    pallas_call x1, Pallas kernels: 30.1 us -> 51.7 us  [attend_back(): pl.pallas_call(functools.partial(attend_back_kernel, 256), grid=(clips, p...]
    pallas_call x2 -> x1, Pallas kernels: 23.8 us -> 12.2 us  [outer(): pl.pallas_call(outer_kernel, grid=(columns // size,), in_specs=[pl.BlockS...]
    pallas_call x1, Pallas kernels: 109 us -> 99.1 us  [tail(): pl.pallas_call(functools.partial(tail_kernel, kinds), out_shape=scatter_s...]
    pallas_call x1, Pallas kernels: 38.9 us -> 31.7 us  [feed(): pl.pallas_call(functools.partial(feed_kernel, steps, unit), grid=(2 * ste...]
    unnamed x38 -> x27, local copies, waits for them, and re-layouts: 9.84 us -> 4.79 us
    ppermute x10 -> x9, waiting for transfers between devices: 9.31 us -> 4.36 us  [swap(): lax.ppermute(shard, AX, [(i, i ^ 1) for i in range(lax.axis_size(AX))])]
  transfers between devices with their start and end apart: 12 -> 10, of which waited for: 5 -> 3; matrix products, arithmetic and copies ran while one was open for 5% -> 4% of each run, Pallas kernels for 69% -> 47%
where the time goes in v5:
time: 392 us; the launch traced here: 389 us
  Pallas kernels  330 us (84%)
  local copies, waits for them, and re-layouts  17 us (4%)
  waiting for transfers between devices  16 us (4%)
  between operations  14.4 us (4%)
  matrix products  5.83 us (1%)
    pallas_call x1, Pallas kernels, tail(): pl.pallas_call(functools.partial(tail_kernel, kinds), out_shape=scatter_s...  99.1 us
    pallas_call x1, Pallas kernels, gather_chips(): pl.pallas_call(gather_kernel, out_shape=[jax.ShapeDtypeStruct((chips, 2,...  67.5 us
    pallas_call x1, Pallas kernels, attend_back(): pl.pallas_call(functools.partial(attend_back_kernel, 256), grid=(clips, p...  51.7 us
    pallas_call x1, Pallas kernels, attend(): pl.pallas_call(functools.partial(attend_kernel, 256), grid=(clips, pairs)...  34.2 us
    pallas_call x1, Pallas kernels, feed(): pl.pallas_call(functools.partial(feed_kernel, steps, unit), grid=(2 * ste...  31.7 us
    pallas_call x1, Pallas kernels, outer(): pl.pallas_call(outer_kernel, grid=(columns // size,), in_specs=[pl.BlockS...  12.2 us
    all_gather x1, waiting for transfers between devices, per_device(): lax.all_gather(pack(up_weight, down_weight), AX, axis=0, tiled=True)  11.7 us
    pallas_call x1, Pallas kernels, project(): pl.pallas_call(functools.partial(project_kernel, steps), grid=(2 * steps,...  11.3 us
  transfers between devices with their start and end apart: 10, of which 3 were waited for; matrix products, arithmetic and copies ran while one was open for 4% of the time, Pallas kernels for 47%

profile of v5, /device:TPU:0, one launch (start us, length us, event | category | flops | bytes accessed | tf_op | source)
XLA Modules:
  0.0 389.2 jit_solution(10815212041570584570)
XLA Ops:
  7.2 0.0 all-gather.2.cloned.1.call-start
  7.2 1.9 pack.1
  9.1 0.0 all-gather.2.cloned.1.call-update
  9.1 0.6 collective-permute-start
  9.7 0.1 collective-permute-start.1
  9.7 0.8 stack.50
  10.5 0.1 copy.72
  10.6 0.7 dynamic_update_slice.3.packed_ref
  11.3 0.6 copy-done.9
  11.9 67.5 %gather_chips.1 = (bf16[16,2,32,1536]{3,2,1,0:T(8,128)(2,1)}, bf16[16,2,32,512]{3,2,1,0:T(8,128)(2,1)}, bf16[16,2,48,128]{3,2,1,0:T(8,128)(2,1)}) custom-call(bf16[32,3072]{1,0:T(8,128)(2,1)} %qkv_ref.1, bf16[32,1024]{1,0:T(8,128)(2,1)} %proj_ref.1, bf16[48,128]{1,0:T(8,128)(2,1)} %copy-done.9), custom_call_target="tpu_custom_call" | custom-call | flops 40000000000 | bytes 150000000 | tf_op jit(solution)/shard_map/gather_chips/pallas_call | solution.py:154
  79.4 0.0 copy-start.10
  79.4 1.3 dynamic-slice_bitcast_fusion.1
  80.8 0.1 collective-permute-start.2
  80.9 0.1 bitcast_convert_fusion
  80.9 0.2 copy.77
  81.1 0.6 fusion.2
  81.7 0.6 fusion.1.bias_ref
  82.4 0.4 copy.74
  82.7 0.1 broadcast_select_fusion.penalty_ref.refs_3_
  82.8 0.0 collective-permute-done.2
  82.9 0.3 maximum_select_fusion.weight_ref
  83.2 11.3 %project.1 = (bf16[1536,1024]{1,0:T(8,128)(2,1)}, bf16[1536,1536]{1,0:T(8,128)(2,1)}) custom-call(bf16[768,1024]{1,0:T(8,128)(2,1)} %bitcast.77, bf16[768,1024]{1,0:T(8,128)(2,1)} %collective-permute-done.other_ref, f32[1,1024]{1,0:T(1,128)} %get-tuple-element.110.gain_ref, f32[1,1024]{1,0:T(1,128)} %get-tuple-element.109.shift_ref, ...), custom_call_target="tpu_custom_call" | custom-call | tf_op jit(solution)/shard_map/project/pallas_call | solution.py:674
  94.5 34.2 %attend.1 = (bf16[2,2,384,512]{3,2,1,0:T(8,128)(2,1)S(1)}, f32[2,4,2,768]{3,2,1,0:T(2,128)S(1)}) custom-call(bf16[2,2,384,1536]{3,2,1,0:T(8,128)(2,1)} %bitcast.70, bf16[2,2,384,1536]{3,2,1,0:T(8,128)(2,1)} %bitcast.71, bf16[2,2,384,1536]{3,2,1,0:T(8,128)(2,1)} %bitcast.72, f32[2,2,384,1]{3,2,1,0:T(8,128)S(1)} %broadcast_select_fusion.penalty_ref.refs_3_), custom_call_target="tpu_custom_call" | custom-call | flops 2415919104 | bytes 6291456 | tf_op jit(solution)/shard_map/attend/pallas_call | solution.py:453
  128.7 0.0 copy-start
  128.7 0.0 copy-start.3
  128.7 0.1 slice.78
  128.8 1.0 convolution_convert_fusion.1
  129.8 0.1 copy-done
  129.9 0.5 collective-permute-start.3
  130.4 0.1 collective-permute-start.5
  130.4 3.0 collective-permute-done.3.recv_ref
  133.4 1.1 copy-done.7
  134.5 6.3 %second_norm.1 = (f32[768,1024]{1,0:T(8,128)}, bf16[768,1024]{1,0:T(8,128)(2,1)}) custom-call(bf16[1536,512]{1,0:T(8,128)(2,1)} %bitcast.68, bf16[512,1024]{1,0:T(8,128)(2,1)} %copy-done.4, bf16[768,1024]{1,0:T(8,128)(2,1)} %bitcast.78, bf16[768,1024]{1,0:T(8,128)(2,1)} %copy-done.7, f32[1,1024]{1,0:T(1,128)} %get-tuple-element.106.bias_ref, ...), custom_call_target="tpu_custom_call" | custom-call | tf_op jit(solution)/shard_map/second_norm/pallas_call | solution.py:709
  140.9 0.5 collective-permute-start.4
  141.3 0.8 slice.83
  142.2 0.6 bitcast_convert_fusion.1.bias_ref
  142.8 1.6 reshape.179.mark_ref
  144.4 0.0 collective-permute-done.5.grad_other_ref
  144.4 1.4 collective-permute-done.4.other_ref
  145.8 11.7 %all-gather.2.cloned.1.call-done.refs_0_ = bf16[1024,8192]{1,0:T(8,128)(2,1)} async-done(((bf16[32,8192]{1,0:T(8,128)(2,1)}), bf16[1024,8192]{1,0:T(8,128)(2,1)}) %all-gather.2.cloned.1.call-update) | async-done | bytes 16777232 | tf_op jit(solution)/shard_map/all_gather | solution.py:1154
  157.4 31.7 %feed.1 = (bf16[1536,2048]{1,0:T(8,128)(2,1)}, bf16[1536,2048]{1,0:T(8,128)(2,1)}, bf16[1536,1024]{1,0:T(8,128)(2,1)}, bf16[1536,1024]{1,0:T(8,128)(2,1)}, f32[7...) custom-call(bf16[768,1024]{1,0:T(8,128)(2,1)} %get-tuple-element.63.own_ref, ...), custom_call_target="tpu_custom_call" | custom-call | flops 19327352832 | bytes 16777216 | tf_op jit(solution)/shard_map/feed/pallas_call | solution.py:808
  189.2 0.3 collective-permute-start.6
  189.5 12.2 %outer.1 = bf16[2048,1024]{1,0:T(8,128)(2,1)} custom-call(bf16[1536,2048]{1,0:T(8,128)(2,1)} %get-tuple-element.66.left_ref.act_hbm, bf16[1536,1024]{1,0:T(8,128)(2,1)} %get-tuple-element.67.right_ref.out_ref), custom_call_target="tpu_custom_call" | custom-call | flops 6442450944 | bytes 13631488 | tf_op jit(solution)/shard_map/outer/pallas_call | solution.py:845
  201.7 1.2 copy-done.6
  202.9 8.0 %second_back.1 = (f32[768,1024]{1,0:T(8,128)}, bf16[768,1024]{1,0:T(8,128)(2,1)}, f32[8,1024]{1,0:T(8,128)}) custom-call(f32[768,1024]{1,0:T(8,128)} %get-tuple-element.64.grad_ref, bf16[768,1024]{1,0:T(8,128)(2,1)} %copy-done.6, f32[768,1024]{1,0:T(8,128)} %get-tuple-element.69.middle_ref.sum_hbm, bf16[1536,1024]{1,0:T(8,128)(2,1)} %get-tuple-element.67.right_ref.out_ref, ...), custom_call_target="tpu_custom_call" | custom-call | tf_op jit(solution)/shard_map/second_back/pallas_call | solution.py:888
  210.9 0.3 collective-permute-start.7
  211.2 0.9 fusion
  212.1 0.7 pad.13.bias_ref
  212.8 0.8 slice.85
  213.6 1.5 constant_dynamic-update-slice_fusion.1
  215.1 0.9 fusion.3
  216.0 0.1 constant_dynamic-update-slice_fusion
  216.1 0.2 copy-done.5
  216.3 3.0 convolution_convert_fusion
  219.4 1.8 convolution_convert_fusion.2
  221.2 0.1 constant_dynamic-slice_fusion.1
  221.3 0.3 collective-permute-start.8
  221.6 51.7 %attend_back.1 = (bf16[2,2,384,1536]{3,2,1,0:T(8,128)(2,1)}, f32[2,4,2,128]{3,2,1,0:T(2,128)}, f32[128,1024]{1,0:T(8,128)}, bf16[1024,2048]{1,0:T(8,128)(2,1)}) custom-call(bf16[2,2,384,1536]{3,2,1,0:T(8,128)(2,1)} %bitcast.73, bf16[2,2,384,1536]{3,2,1,0:T(8,128)(2,1)} %bitcast.74, bf16[2,2,384,1536]{3,2,1,0:T(8,128)(2,1)} %bitcast.75, ...), custom_call_target="tpu_custom_call" | custom-call | flops 6039797760 | bytes 14155776 | tf_op jit(solution)/shard_map/attend_back/pallas_call | solution.py:610
  273.4 0.7 reduce_sum.9
  274.1 0.7 concatenate.48.sums_ref
  274.8 1.4 maximum_select_fusion.1
  276.2 99.1 %tail.1 = (f32[32,4096]{1,0:T(8,128)}, f32[32,3072]{1,0:T(8,128)}, f32[32,1024]{1,0:T(8,128)}, f32[48,128]{1,0:T(8,128)}, f32[768,1024]{1,0:T(8,128)}, /*index=5*/bf16[768,1024]{1,0:T(8,128)(2,1)}) custom-call(bf16[16,2,32,2048]{3,2,1,0:T(8,128)(2,1)} %bitcast.85, bf16[16,2,32,512]{3,2,1,0:T(8,128)(2,1)} %bitcast.84, f32[8,1024]{1,0:T(8,128)} %concatenate.48.sums_ref, ...), custom_call_target="tpu_custom_call" | custom-call | tf_op jit(solution)/shard_map/tail/pallas_call | solution.py:1062
  375.3 5.6 %finish.1 = (f32[32,4096]{1,0:T(8,128)}, f32[32,3072]{1,0:T(8,128)}, f32[32,1024]{1,0:T(8,128)}, f32[128,1024]{1,0:T(8,128)}, f32[768,1024]{1,0:T(8,128)}, /*ind...) custom-call(f32[32,4096]{1,0:T(8,128)} %get-tuple-element.84.up_ref, ...), custom_call_target="tpu_custom_call" | custom-call | tf_op jit(solution)/shard_map/finish/pallas_call | solution.py:1123
  380.8 1.5 slice_bitcast_fusion
  (34 shorter events, 0.1 us)
Async XLA Ops:
  7.2 150.2 %all-gather.2.cloned.1.call-start = ((), (), s32[]{:S(2)}) async-start(), calls=%async_computation | async-start | bytes 17301504 | tf_op jit(solution)/shard_map/all_gather | solution.py:1154
  9.1 74.1 %collective-permute-start = (bf16[768,1024]{1,0:T(8,128)(2,1)}, bf16[768,1024]{1,0:T(8,128)(2,1)}, u32[]{:S(2)}, u32[]{:S(2)}) collective-permute-start(bf16[768,1024]{1,0:T(8,128)(2,1)} %bitcast.76), channel_id=1, source_target_pairs={{0,1},{1,0},{2,3},{3,2},{4,5},{5,4},{6,7},{7,6},{8,9},{9,8},{10,11... | collective-permute-start | bytes 4718600 | tf_op jit(solution)/shard_map/ppermute | solution.py:34
  9.7 72.7 %collective-permute-start.1 = (s32[2,384]{1,0:T(2,128)}, s32[2,384]{1,0:T(2,128)S(1)}, u32[]{:S(2)}, u32[]{:S(2)}) collective-permute-start(s32[2,384]{1,0:T(2,128)} %param.17), channel_id=1, source_target_pairs={{0,1},{1,0},{2,3},{3,2},{4,5},{5,4},{6,7},{7,6},{8,9},{9,8},{10,11... | collective-permute-start | bytes 9224 | tf_op jit(solution)/shard_map/ppermute | solution.py:34
  11.3 0.6 copy-start.9
  79.4 1.4 copy-start.8
  79.4 3.0 copy-start.10
  80.8 2.1 collective-permute-start.2
  82.8 11.7 %copy-start.2 = (f32[2,2,384,1]{3,2,1,0:T(8,128)}, f32[2,2,384,1]{3,2,1,0:T(8,128)S(1)}, u32[]{:S(2)}) copy-start(f32[2,2,384,1]{3,2,1,0:T(8,128)S(1)} %broadcast_select_fusion.penalty_ref.refs_3_) | copy-start | bytes 18436
  83.2 45.6 %copy-start.4 = (bf16[512,1024]{1,0:T(8,128)(2,1)}, bf16[512,1024]{1,0:T(8,128)(2,1)S(1)}, u32[]{:S(2)}) copy-start(bf16[512,1024]{1,0:T(8,128)(2,1)S(1)} %maximum_select_fusion.weight_ref) | copy-start | bytes 3145732
  128.7 1.1 copy-start
  128.7 1.1 copy-start.3
  129.9 3.5 collective-permute-start.3
  130.4 14.0 %collective-permute-start.5 = (bf16[768,1024]{1,0:T(8,128)(2,1)}, bf16[768,1024]{1,0:T(8,128)(2,1)S(1)}, u32[]{:S(2)}, u32[]{:S(2)}) collective-permute-start(bf16[768,1024]{1,0:T(8,128)(2,1)} %bitcast.23.grad_own_ref), channel_id=1, source_target_pairs={{0,1},{1,0},{2,3},{3,2},{4,5},{5,4},{6,7},{7,6},{8,9},{9,8},{10,11... | collective-permute-start | bytes 4718600 | tf_op jit(solution)/shard_map/ppermute | solution.py:34
  133.4 1.1 copy-start.7
  140.9 4.9 %collective-permute-start.4 = (bf16[768,1024]{1,0:T(8,128)(2,1)}, bf16[768,1024]{1,0:T(8,128)(2,1)S(1)}, u32[]{:S(2)}, u32[]{:S(2)}) collective-permute-start(bf16[768,1024]{1,0:T(8,128)(2,1)} %get-tuple-element.63.own_ref), channel_id=1, source_target_pairs={{0,1},{1,0},{2,3},{3,2},{4,5},{5,4},{6,7},{7,6},{8,9},{9,8},{10,11... | collective-permute-start | bytes 4718600 | tf_op jit(solution)/shard_map/ppermute | solution.py:34
  144.4 13.0 %copy-start.11 = (bf16[768,1024]{1,0:T(8,128)(2,1)}, bf16[768,1024]{1,0:T(8,128)(2,1)S(1)}, u32[]{:S(2)}) copy-start(bf16[768,1024]{1,0:T(8,128)(2,1)S(1)} %collective-permute-done.5.grad_other_ref) | copy-start | bytes 4718596
  145.8 11.7 %copy-start.12 = (bf16[768,1024]{1,0:T(8,128)(2,1)}, bf16[768,1024]{1,0:T(8,128)(2,1)S(1)}, u32[]{:S(2)}) copy-start(bf16[768,1024]{1,0:T(8,128)(2,1)S(1)} %collective-permute-done.4.other_ref) | copy-start | bytes 4718596
  189.2 12.5 %collective-permute-start.6 = (bf16[768,1024]{1,0:T(8,128)(2,1)}, bf16[768,1024]{1,0:T(8,128)(2,1)S(1)}, u32[]{:S(2)}, u32[]{:S(2)}) collective-permute-start(bf16[768,1024]{1,0:T(8,128)(2,1)} %get-tuple-element.65), channel_id=1, source_target_pairs={{0,1},{1,0},{2,3},{3,2},{4,5},{5,4},{6,7},{7,6},{8,9},{9,8},{10,11... | collective-permute-start | bytes 4718600 | tf_op jit(solution)/shard_map/ppermute | solution.py:34
  201.7 1.2 copy-start.6
  210.9 5.0 %collective-permute-start.7 = (bf16[768,1024]{1,0:T(8,128)(2,1)}, bf16[768,1024]{1,0:T(8,128)(2,1)S(1)}, u32[]{:S(2)}, u32[]{:S(2)}) collective-permute-start(bf16[768,1024]{1,0:T(8,128)(2,1)} %get-tuple-element.70), channel_id=1, source_target_pairs={{0,1},{1,0},{2,3},{3,2},{4,5},{5,4},{6,7},{7,6},{8,9},{9,8},{10,11... | collective-permute-start | bytes 4718600 | tf_op jit(solution)/shard_map/ppermute | solution.py:34
  215.1 1.3 copy-start.5
  216.3 3.0 copy-start.1
  221.3 53.5 %collective-permute-start.8 = (bf16[512,512]{1,0:T(8,128)(2,1)S(1)}, bf16[512,512]{1,0:T(8,128)(2,1)S(1)}, u32[]{:S(2)}, u32[]{:S(2)}) collective-permute-start(bf16[512,512]{1,0:T(8,128)(2,1)S(1)} %get-tuple-element.100), channel_id=1, source_target_pairs={{0,1},{1,0},{2,3},{3,2},{4,5},{5,4},{6,7},{7,6},{8,9},{9,8},{10,11... | collective-permute-start | bytes 1572872 | tf_op jit(solution)/shard_map/ppermute | solution.py:34
Sparse Core Ops, SparseCore 0:
  11.4 145.9 all-gather.1

commit v6 on v5

--- a/solution.py
+++ b/solution.py
@@ -172,8 +172,11 @@
 
 
 class Scatter:
-    def __init__(self, kinds, ins, outs, scratch):
+    def __init__(self, kinds, ins, outs, scratch, early=None):
         count = len(kinds)
+        self.early = early
+        if early is not None:
+            self.plane, scratch = scratch[-1], scratch[:-1]
         self.kinds, self.ins, self.outs = kinds, ins, outs
         names = ("recv_a", "recv_b", "recv_x", "recv_y", "recv_z", "stage", "land")
         for place, name in enumerate(names):
@@ -205,14 +208,41 @@
     def arrive(self, w, slot, block):
         self.remote(w, slot, block, block, self.mate).wait_recv()
 
+    def source(self, w, chip):
+        return (self.plane, chip % 4) if w == self.early else (self.ins[w], chip)
+
+    def along(self, w):
+        for j in (1, 2, 3):
+            layer = pl.multiple_of(self.own[j] // 4 * 4, 4)
+            self.send(w, 23 + j, self.ins[w].at[pl.ds(layer, 4)], self.recv_z[w].at[j - 1], self.peers_z[j - 1])
+
+    def layer_sum(self, w):
+        for j in range(3):
+            self.arrive(w, 24 + j, self.recv_z[w].at[j])
+        layer = self.chip // 4 * 4
+
+        @pl.loop(0, 4)
+        def _(block):
+            def body(part):
+                for half in range(2):
+                    total = self.ins[w][layer + block, half, part].astype(F32)
+                    for j in range(3):
+                        total = total + self.recv_z[w][j, block, half, part].astype(F32)
+                    self.plane[block, half, part] = total.astype(BF)
+
+            self.strips(w, body)
+
     def far(self, w, j):
-        block = self.ins[w].at[self.at_xy[j]]
+        ref, at = self.source(w, self.at_xy[j])
+        block = ref.at[at]
         self.send(w, j, block.at[0], self.recv_a[w].at[j], self.peer_y)
         self.send(w, 4 + j, block.at[1], self.recv_b[w].at[j], self.peer_x)
 
     def near(self, w, j):
-        self.send(w, 8 + j, self.ins[w].at[self.at_x[j], 1], self.recv_x[w].at[j, 1], self.peer_x)
-        self.send(w, 12 + j, self.ins[w].at[self.at_y[j], 0], self.recv_y[w].at[j, 0], self.peer_y)
+        ref, at = self.source(w, self.at_x[j])
+        self.send(w, 8 + j, ref.at[at, 1], self.recv_x[w].at[j, 1], self.peer_x)
+        ref, at = self.source(w, self.at_y[j])
+        self.send(w, 12 + j, ref.at[at, 0], self.recv_y[w].at[j, 0], self.peer_y)
 
     def strips(self, w, body):
         @pl.loop(0, self.ins[w].shape[2] // 16)
@@ -226,8 +256,10 @@
         ):
             self.arrive(w, slot, recv.at[j])
 
+            ref, at = self.source(w, block)
+
             def body(part):
-                total = recv[j, part].astype(F32) + self.ins[w][block, half, part].astype(F32)
+                total = recv[j, part].astype(F32) + ref[at, half, part].astype(F32)
                 recv[j, part] = total.astype(BF)
 
             self.strips(w, body)
@@ -244,7 +276,8 @@
 
     def near_sum(self, w, j, half, part):
         total = self.recv_x[w][j, half, part].astype(F32) + self.recv_y[w][j, half, part].astype(F32)
-        return total + self.ins[w][self.own[j], half, part].astype(F32)
+        ref, at = self.source(w, self.own[j])
+        return total + ref[at, half, part].astype(F32)
 
     def cross(self, w, j):
         self.arrive_near(w, j)
@@ -268,13 +301,14 @@
 
     def last(self, w):
         self.arrive_near(w, 0)
-        for j in range(3):
+        layers = 0 if w == self.early else 3
+        for j in range(layers):
             self.arrive(w, 24 + j, self.recv_z[w].at[j])
         rows = self.ins[w].shape[2]
 
         def total_of(half, part):
             total = self.near_sum(w, 0, half, part)
-            for j in range(3):
+            for j in range(layers):
                 total = total + self.recv_z[w][j, half, part].astype(F32)
             return total
 
@@ -311,7 +345,7 @@
             if slot == 27:
                 block = self.stage[w]
             elif slot >= 24:
-                block = self.recv_x[w].at[0]
+                block = self.recv_z[w].at[0]
             else:
                 block = self.recv_a[w].at[0]
             self.remote(w, slot, block, block, self.mate).wait_send()
@@ -354,13 +388,16 @@
         self.drain()
 
 
-def scatter_scratch(shapes):
+def scatter_scratch(shapes, early=None):
     count = len(shapes)
     scratch = [pltpu.VMEM((4,) + s[2:], BF) for s in shapes] * 2
     scratch += [pltpu.VMEM((4, 2) + s[2:], BF) for s in shapes] * 2
-    scratch += [pltpu.VMEM((3, 2) + s[2:], BF) for s in shapes]
+    scratch += [pltpu.VMEM(((3, 4, 2) if w == early else (3, 2)) + s[2:], BF) for w, s in enumerate(shapes)]
     scratch += [pltpu.VMEM(s[2:], F32) for s in shapes] * 2
-    return scratch + [pltpu.SemaphoreType.DMA((count, 28)), pltpu.SemaphoreType.DMA((count, 28))]
+    scratch += [pltpu.SemaphoreType.DMA((count, 28)), pltpu.SemaphoreType.DMA((count, 28))]
+    if early is not None:
+        scratch += [pltpu.VMEM((4, 2) + shapes[early][2:], BF)]
+    return scratch
 
 
 def scatter_shapes(shapes, kinds):
@@ -841,7 +878,7 @@
 def outer(left, right):
     rows, columns = left.shape
     width = right.shape[1]
-    size = 256
+    size = 512
     return pl.pallas_call(
         outer_kernel,
         grid=(columns // size,),
@@ -934,7 +971,7 @@
 ):
     back, weight, norm, token, middle, down, qkv, packed, vectors, stage, land, load_sem, pass_sem = refs[:13]
     act, total, lift_stage, lift_land, block_sem = refs[13:18]
-    scatter = Scatter(kinds, (up_ref, qkv, proj_ref, packed), (up_out, qkv_out, proj_out, packed_out), refs[18:])
+    scatter = Scatter(kinds, (up_ref, qkv, proj_ref, packed), (up_out, qkv_out, proj_out, packed_out), refs[18:], 2)
     chips, _, shard, triple = qkv.shape
     own_rows = token.shape[0]
     loads = [
@@ -950,8 +987,7 @@
         load.start()
     scatter.meet()
     scatter.opening(0)
-    for j in (1, 2, 3, 0):
-        scatter.far(2, j), scatter.near(2, j)
+    scatter.along(2)
     vectors[...] = jnp.zeros_like(vectors)
     vectors[0:8] = sums_ref[...]
     loads[0].wait(), loads[1].wait()
@@ -977,8 +1013,6 @@
         qkv[pl.ds(i * count, count)] = grad.reshape(count, 2, shard, triple)
 
     scatter.relay(0, 2), scatter.far(0, 0), scatter.near(0, 3)
-    for j in (1, 2, 3, 0):
-        scatter.relay(2, j)
     scatter.opening(1)
     loads[3].wait(), loads[4].wait()
     passing.wait()
@@ -1000,9 +1034,9 @@
     packed[:, :, shard:] = bias_ref[...]
     for j in (1, 2, 3, 0):
         scatter.far(3, j), scatter.near(3, j)
+    scatter.layer_sum(2)
+    scatter.far(2, 0), scatter.near(2, 0)
     scatter.relay(0, 0), scatter.cross(0, 3)
-    for j in (1, 2, 3):
-        scatter.cross(2, j)
     loads[5].wait()
 
     def fetch(source, start, target, slot):
@@ -1020,6 +1054,7 @@
         device_id=(scatter.mate,), device_id_type=MESH,
     )
     lifting.start()
+    scatter.relay(2, 0)
     scatter.relay(1, 1), scatter.far(1, 3), scatter.near(1, 2)
     scatter.relay(1, 2), scatter.far(1, 0), scatter.near(1, 3)
     lifting.wait()
@@ -1074,7 +1109,7 @@
             pltpu.VMEM((256, act.shape[1]), BF), pltpu.VMEM((256, features), F32),
             pltpu.VMEM((own_rows, features), BF), pltpu.VMEM((own_rows, features), BF), pltpu.SemaphoreType.DMA((2,)),
         ]
-        + scatter_scratch(shapes),
+        + scatter_scratch(shapes, 2),
         compiler_params=pltpu.CompilerParams(collective_id=1, has_side_effects=True, vmem_limit_bytes=62 << 20),
         name="tail",
     )(grad_up, grad_proj, sums, bias_rows, gain, shift, back, weight, norm, tokens, grad_middle, down, act, middle)
@@ -1108,24 +1143,35 @@
 ):
     token_out[...] = token_ref[...]
     block_out[...] = block_ref[...]
-    up_out[...] = up_ref[...]
-    qkv_out[...] = qkv_ref[...]
-    proj_out[...] = proj_ref[...]
-    down_out[...] = down_ref[...]
-    shard = vec_out.shape[1]
-    vec_out[...] = packed_ref[:shard].T[:8]
-    bias_out[...] = packed_ref[shard : shard + 1]
+
+    @pl.when(pl.program_id(0) == 0)
+    def _():
+        up_out[...] = up_ref[...]
+        qkv_out[...] = qkv_ref[...]
+        proj_out[...] = proj_ref[...]
+        down_out[...] = down_ref[...]
+        shard = vec_out.shape[1]
+        vec_out[...] = packed_ref[:shard].T[:8]
+        bias_out[...] = packed_ref[shard : shard + 1]
 
 
 def finish(up, qkv, proj, down, tokens, block, packed, shard, unit):
     if lax.axis_size(AX) != 32:
         return up, qkv, proj, down, tokens, block, packed[:shard, :8].T, packed[shard : shard + 1, :unit]
+    size = tokens.shape[0] // 4
+    passed = [rows_spec(size, tokens.shape[1])] * 2
+
+    def kept(shape):
+        return pl.BlockSpec(shape, lambda i: (0, 0))
+
+    summed = [whole_spec(a.shape) for a in (up, qkv, proj, down)]
     return pl.pallas_call(
         finish_kernel,
+        grid=(4,),
         out_shape=[jax.ShapeDtypeStruct(a.shape, a.dtype) for a in (up, qkv, proj, down, tokens, block)]
         + [jax.ShapeDtypeStruct((8, shard), F32), jax.ShapeDtypeStruct((1, unit), F32)],
-        in_specs=[pl.BlockSpec(memory_space=pltpu.VMEM)] * 7,
-        out_specs=[pl.BlockSpec(memory_space=pltpu.VMEM)] * 8,
+        in_specs=summed + passed + [whole_spec(packed.shape)],
+        out_specs=[kept(a.shape) for a in (up, qkv, proj, down)] + passed + [kept((8, shard)), kept((1, unit))],
         compiler_params=PARAMS,
         name="finish",
     )(up, qkv, proj, down, tokens, block, packed)

time: 392 us -> 382 us (0.974)
  Pallas kernels: 330 us -> 320 us
    pallas_call x1, Pallas kernels: 99.1 us -> 90.5 us  [tail(): pl.pallas_call(functools.partial(tail_kernel, kinds), out_shape=scatter_s...]
  transfers between devices with their start and end apart: 10 -> 10, of which waited for: 3 -> 3; matrix products, arithmetic and copies ran while one was open for 4% -> 4% of each run, Pallas kernels for 47% -> 48%
where the time goes in v6:
time: 382 us; the launch traced here: 380 us
  Pallas kernels  320 us (84%)
  local copies, waits for them, and re-layouts  17 us (4%)
  waiting for transfers between devices  16 us (4%)
  between operations  14.4 us (4%)
  matrix products  5.83 us (2%)
    pallas_call x1, Pallas kernels, tail(): pl.pallas_call(functools.partial(tail_kernel, kinds), out_shape=scatter_s...  90.5 us
    pallas_call x1, Pallas kernels, gather_chips(): pl.pallas_call(gather_kernel, out_shape=[jax.ShapeDtypeStruct((chips, 2,...  67.5 us
    pallas_call x1, Pallas kernels, attend_back(): pl.pallas_call(functools.partial(attend_back_kernel, 256), grid=(clips, p...  51.7 us
    pallas_call x1, Pallas kernels, attend(): pl.pallas_call(functools.partial(attend_kernel, 256), grid=(clips, pairs)...  34.2 us
    pallas_call x1, Pallas kernels, feed(): pl.pallas_call(functools.partial(feed_kernel, steps, unit), grid=(2 * ste...  31.7 us
    all_gather x1, waiting for transfers between devices, per_device(): lax.all_gather(pack(up_weight, down_weight), AX, axis=0, tiled=True)  11.7 us
    pallas_call x1, Pallas kernels, project(): pl.pallas_call(functools.partial(project_kernel, steps), grid=(2 * steps,...  11.3 us
    pallas_call x1, Pallas kernels, outer(): pl.pallas_call(outer_kernel, grid=(columns // size,), in_specs=[pl.BlockS...  10.7 us
  transfers between devices with their start and end apart: 10, of which 3 were waited for; matrix products, arithmetic and copies ran while one was open for 4% of the time, Pallas kernels for 48%

profile of v6, /device:TPU:0, one launch (start us, length us, event | category | flops | bytes accessed | tf_op | source)
XLA Modules:
  0.0 379.6 jit_solution(4197938420570452176)
XLA Ops:
  7.2 0.0 all-gather.2.cloned.1.call-start
  7.2 1.9 pack.1
  9.1 0.0 all-gather.2.cloned.1.call-update
  9.1 0.6 collective-permute-start
  9.7 0.1 collective-permute-start.1
  9.7 0.8 stack.50
  10.5 0.1 copy.72
  10.6 0.7 dynamic_update_slice.3.packed_ref
  11.3 0.6 copy-done.9
  11.9 67.5 %gather_chips.1 = (bf16[16,2,32,1536]{3,2,1,0:T(8,128)(2,1)}, bf16[16,2,32,512]{3,2,1,0:T(8,128)(2,1)}, bf16[16,2,48,128]{3,2,1,0:T(8,128)(2,1)}) custom-call(bf16[32,3072]{1,0:T(8,128)(2,1)} %qkv_ref.1, bf16[32,1024]{1,0:T(8,128)(2,1)} %proj_ref.1, bf16[48,128]{1,0:T(8,128)(2,1)} %copy-done.9), custom_call_target="tpu_custom_call" | custom-call | flops 40000000000 | bytes 150000000 | tf_op jit(solution)/shard_map/gather_chips/pallas_call | solution.py:154
  79.4 0.0 copy-start.10
  79.4 1.3 dynamic-slice_bitcast_fusion.1
  80.8 0.1 collective-permute-start.2
  80.9 0.1 bitcast_convert_fusion
  80.9 0.2 copy.77
  81.1 0.6 fusion.2
  81.7 0.6 fusion.1.bias_ref
  82.3 0.0 collective-permute-done.1
  82.4 0.4 copy.74
  82.7 0.1 broadcast_select_fusion.penalty_ref.refs_3_
  82.9 0.3 maximum_select_fusion.weight_ref
  83.2 0.0 collective-permute-done.other_ref
  83.2 11.3 %project.1 = (bf16[1536,1024]{1,0:T(8,128)(2,1)}, bf16[1536,1536]{1,0:T(8,128)(2,1)}) custom-call(bf16[768,1024]{1,0:T(8,128)(2,1)} %bitcast.77, bf16[768,1024]{1,0:T(8,128)(2,1)} %collective-permute-done.other_ref, f32[1,1024]{1,0:T(1,128)} %get-tuple-element.110.gain_ref, f32[1,1024]{1,0:T(1,128)} %get-tuple-element.109.shift_ref, ...), custom_call_target="tpu_custom_call" | custom-call | tf_op jit(solution)/shard_map/project/pallas_call | solution.py:711
  94.5 34.2 %attend.1 = (bf16[2,2,384,512]{3,2,1,0:T(8,128)(2,1)S(1)}, f32[2,4,2,768]{3,2,1,0:T(2,128)S(1)}) custom-call(bf16[2,2,384,1536]{3,2,1,0:T(8,128)(2,1)} %bitcast.70, bf16[2,2,384,1536]{3,2,1,0:T(8,128)(2,1)} %bitcast.71, bf16[2,2,384,1536]{3,2,1,0:T(8,128)(2,1)} %bitcast.72, f32[2,2,384,1]{3,2,1,0:T(8,128)S(1)} %broadcast_select_fusion.penalty_ref.refs_3_), custom_call_target="tpu_custom_call" | custom-call | flops 2415919104 | bytes 6291456 | tf_op jit(solution)/shard_map/attend/pallas_call | solution.py:490
  128.7 0.0 copy-start
  128.7 0.0 copy-start.3
  128.7 0.1 slice.78
  128.8 1.0 convolution_convert_fusion.1
  129.8 0.1 copy-done
  129.9 0.5 collective-permute-start.3
  130.4 0.1 collective-permute-start.5
  130.4 3.0 collective-permute-done.3.recv_ref
  133.4 1.1 copy-done.7
  134.5 6.3 %second_norm.1 = (f32[768,1024]{1,0:T(8,128)}, bf16[768,1024]{1,0:T(8,128)(2,1)}) custom-call(bf16[1536,512]{1,0:T(8,128)(2,1)} %bitcast.68, bf16[512,1024]{1,0:T(8,128)(2,1)} %copy-done.4, bf16[768,1024]{1,0:T(8,128)(2,1)} %bitcast.78, bf16[768,1024]{1,0:T(8,128)(2,1)} %copy-done.7, f32[1,1024]{1,0:T(1,128)} %get-tuple-element.106.bias_ref, ...), custom_call_target="tpu_custom_call" | custom-call | tf_op jit(solution)/shard_map/second_norm/pallas_call | solution.py:746
  140.9 0.5 collective-permute-start.4
  141.3 0.8 slice.83
  142.2 0.6 bitcast_convert_fusion.1.bias_ref
  142.8 1.6 reshape.179.mark_ref
  144.4 1.4 collective-permute-done.4.other_ref
  145.8 11.7 %all-gather.2.cloned.1.call-done.refs_0_ = bf16[1024,8192]{1,0:T(8,128)(2,1)} async-done(((bf16[32,8192]{1,0:T(8,128)(2,1)}), bf16[1024,8192]{1,0:T(8,128)(2,1)}) %all-gather.2.cloned.1.call-update) | async-done | bytes 16777232 | tf_op jit(solution)/shard_map/all_gather | solution.py:1200
  157.4 31.7 %feed.1 = (bf16[1536,2048]{1,0:T(8,128)(2,1)}, bf16[1536,2048]{1,0:T(8,128)(2,1)}, bf16[1536,1024]{1,0:T(8,128)(2,1)}, bf16[1536,1024]{1,0:T(8,128)(2,1)}, f32[7...) custom-call(bf16[768,1024]{1,0:T(8,128)(2,1)} %get-tuple-element.63.own_ref, ...), custom_call_target="tpu_custom_call" | custom-call | flops 19327352832 | bytes 16777216 | tf_op jit(solution)/shard_map/feed/pallas_call | solution.py:845
  189.2 0.3 collective-permute-start.6
  189.5 10.7 %outer.1 = bf16[2048,1024]{1,0:T(8,128)(2,1)} custom-call(bf16[1536,2048]{1,0:T(8,128)(2,1)} %get-tuple-element.66.left_ref.act_hbm, bf16[1536,1024]{1,0:T(8,128)(2,1)} %get-tuple-element.67.right_ref.out_ref), custom_call_target="tpu_custom_call" | custom-call | flops 6442450944 | bytes 13631488 | tf_op jit(solution)/shard_map/outer/pallas_call | solution.py:882
  200.2 1.2 copy-done.6
  201.4 8.0 %second_back.1 = (f32[768,1024]{1,0:T(8,128)}, bf16[768,1024]{1,0:T(8,128)(2,1)}, f32[8,1024]{1,0:T(8,128)}) custom-call(f32[768,1024]{1,0:T(8,128)} %get-tuple-element.64.grad_ref, bf16[768,1024]{1,0:T(8,128)(2,1)} %copy-done.6, f32[768,1024]{1,0:T(8,128)} %get-tuple-element.69.middle_ref.sum_hbm, bf16[1536,1024]{1,0:T(8,128)(2,1)} %get-tuple-element.67.right_ref.out_ref, ...), custom_call_target="tpu_custom_call" | custom-call | tf_op jit(solution)/shard_map/second_back/pallas_call | solution.py:925
  209.4 0.3 collective-permute-start.7
  209.7 0.9 fusion
  210.6 0.7 pad.13.bias_ref
  211.3 0.8 slice.85
  212.1 1.5 constant_dynamic-update-slice_fusion.1
  213.6 0.9 fusion.3
  214.5 0.1 constant_dynamic-update-slice_fusion
  214.6 0.2 copy-done.5
  214.9 3.0 convolution_convert_fusion
  217.9 1.8 convolution_convert_fusion.2
  219.7 0.1 constant_dynamic-slice_fusion.1
  219.8 0.3 collective-permute-start.8
  220.2 51.7 %attend_back.1 = (bf16[2,2,384,1536]{3,2,1,0:T(8,128)(2,1)}, f32[2,4,2,128]{3,2,1,0:T(2,128)}, f32[128,1024]{1,0:T(8,128)}, bf16[1024,2048]{1,0:T(8,128)(2,1)}) custom-call(bf16[2,2,384,1536]{3,2,1,0:T(8,128)(2,1)} %bitcast.73, bf16[2,2,384,1536]{3,2,1,0:T(8,128)(2,1)} %bitcast.74, bf16[2,2,384,1536]{3,2,1,0:T(8,128)(2,1)} %bitcast.75, ...), custom_call_target="tpu_custom_call" | custom-call | flops 6039797760 | bytes 14155776 | tf_op jit(solution)/shard_map/attend_back/pallas_call | solution.py:647
  271.9 0.7 reduce_sum.9
  272.6 0.7 concatenate.48.sums_ref
  273.3 1.4 maximum_select_fusion.1
  274.7 90.5 %tail.1 = (f32[32,4096]{1,0:T(8,128)}, f32[32,3072]{1,0:T(8,128)}, f32[32,1024]{1,0:T(8,128)}, f32[48,128]{1,0:T(8,128)}, f32[768,1024]{1,0:T(8,128)}, /*index=5*/bf16[768,1024]{1,0:T(8,128)(2,1)}) custom-call(bf16[16,2,32,2048]{3,2,1,0:T(8,128)(2,1)} %bitcast.85, bf16[16,2,32,512]{3,2,1,0:T(8,128)(2,1)} %bitcast.84, f32[8,1024]{1,0:T(8,128)} %concatenate.48.sums_ref, ...), custom_call_target="tpu_custom_call" | custom-call | tf_op jit(solution)/shard_map/tail/pallas_call | solution.py:1097
  365.2 6.1 %finish.1 = (f32[32,4096]{1,0:T(8,128)}, f32[32,3072]{1,0:T(8,128)}, f32[32,1024]{1,0:T(8,128)}, f32[128,1024]{1,0:T(8,128)}, f32[768,1024]{1,0:T(8,128)}, /*ind...) custom-call(f32[32,4096]{1,0:T(8,128)} %get-tuple-element.84.up_ref, ...), custom_call_target="tpu_custom_call" | custom-call | tf_op jit(solution)/shard_map/finish/pallas_call | solution.py:1168
  371.3 1.5 slice_bitcast_fusion
  (34 shorter events, 0.1 us)
Async XLA Ops:
  7.2 150.2 %all-gather.2.cloned.1.call-start = ((), (), s32[]{:S(2)}) async-start(), calls=%async_computation | async-start | bytes 17301504 | tf_op jit(solution)/shard_map/all_gather | solution.py:1200
  9.1 74.1 %collective-permute-start = (bf16[768,1024]{1,0:T(8,128)(2,1)}, bf16[768,1024]{1,0:T(8,128)(2,1)}, u32[]{:S(2)}, u32[]{:S(2)}) collective-permute-start(bf16[768,1024]{1,0:T(8,128)(2,1)} %bitcast.76), channel_id=1, source_target_pairs={{0,1},{1,0},{2,3},{3,2},{4,5},{5,4},{6,7},{7,6},{8,9},{9,8},{10,11... | collective-permute-start | bytes 4718600 | tf_op jit(solution)/shard_map/ppermute | solution.py:34
  9.7 72.7 %collective-permute-start.1 = (s32[2,384]{1,0:T(2,128)}, s32[2,384]{1,0:T(2,128)S(1)}, u32[]{:S(2)}, u32[]{:S(2)}) collective-permute-start(s32[2,384]{1,0:T(2,128)} %param.17), channel_id=1, source_target_pairs={{0,1},{1,0},{2,3},{3,2},{4,5},{5,4},{6,7},{7,6},{8,9},{9,8},{10,11... | collective-permute-start | bytes 9224 | tf_op jit(solution)/shard_map/ppermute | solution.py:34
  11.3 0.6 copy-start.9
  79.4 1.4 copy-start.8
  79.4 3.0 copy-start.10
  80.8 2.1 collective-permute-start.2
  82.8 11.7 %copy-start.2 = (f32[2,2,384,1]{3,2,1,0:T(8,128)}, f32[2,2,384,1]{3,2,1,0:T(8,128)S(1)}, u32[]{:S(2)}) copy-start(f32[2,2,384,1]{3,2,1,0:T(8,128)S(1)} %broadcast_select_fusion.penalty_ref.refs_3_) | copy-start | bytes 18436
  83.2 45.6 %copy-start.4 = (bf16[512,1024]{1,0:T(8,128)(2,1)}, bf16[512,1024]{1,0:T(8,128)(2,1)S(1)}, u32[]{:S(2)}) copy-start(bf16[512,1024]{1,0:T(8,128)(2,1)S(1)} %maximum_select_fusion.weight_ref) | copy-start | bytes 3145732
  128.7 1.1 copy-start
  128.7 1.1 copy-start.3
  129.9 3.5 collective-permute-start.3
  130.4 14.0 %collective-permute-start.5 = (bf16[768,1024]{1,0:T(8,128)(2,1)}, bf16[768,1024]{1,0:T(8,128)(2,1)S(1)}, u32[]{:S(2)}, u32[]{:S(2)}) collective-permute-start(bf16[768,1024]{1,0:T(8,128)(2,1)} %bitcast.23.grad_own_ref), channel_id=1, source_target_pairs={{0,1},{1,0},{2,3},{3,2},{4,5},{5,4},{6,7},{7,6},{8,9},{9,8},{10,11... | collective-permute-start | bytes 4718600 | tf_op jit(solution)/shard_map/ppermute | solution.py:34
  133.4 1.1 copy-start.7
  140.9 4.9 %collective-permute-start.4 = (bf16[768,1024]{1,0:T(8,128)(2,1)}, bf16[768,1024]{1,0:T(8,128)(2,1)S(1)}, u32[]{:S(2)}, u32[]{:S(2)}) collective-permute-start(bf16[768,1024]{1,0:T(8,128)(2,1)} %get-tuple-element.63.own_ref), channel_id=1, source_target_pairs={{0,1},{1,0},{2,3},{3,2},{4,5},{5,4},{6,7},{7,6},{8,9},{9,8},{10,11... | collective-permute-start | bytes 4718600 | tf_op jit(solution)/shard_map/ppermute | solution.py:34
  144.4 13.0 %copy-start.11 = (bf16[768,1024]{1,0:T(8,128)(2,1)}, bf16[768,1024]{1,0:T(8,128)(2,1)S(1)}, u32[]{:S(2)}) copy-start(bf16[768,1024]{1,0:T(8,128)(2,1)S(1)} %collective-permute-done.5.grad_other_ref) | copy-start | bytes 4718596
  145.8 11.7 %copy-start.12 = (bf16[768,1024]{1,0:T(8,128)(2,1)}, bf16[768,1024]{1,0:T(8,128)(2,1)S(1)}, u32[]{:S(2)}) copy-start(bf16[768,1024]{1,0:T(8,128)(2,1)S(1)} %collective-permute-done.4.other_ref) | copy-start | bytes 4718596
  189.2 11.1 %collective-permute-start.6 = (bf16[768,1024]{1,0:T(8,128)(2,1)}, bf16[768,1024]{1,0:T(8,128)(2,1)S(1)}, u32[]{:S(2)}, u32[]{:S(2)}) collective-permute-start(bf16[768,1024]{1,0:T(8,128)(2,1)} %get-tuple-element.65), channel_id=1, source_target_pairs={{0,1},{1,0},{2,3},{3,2},{4,5},{5,4},{6,7},{7,6},{8,9},{9,8},{10,11... | collective-permute-start | bytes 4718600 | tf_op jit(solution)/shard_map/ppermute | solution.py:34
  200.2 1.2 copy-start.6
  209.4 5.0 %collective-permute-start.7 = (bf16[768,1024]{1,0:T(8,128)(2,1)}, bf16[768,1024]{1,0:T(8,128)(2,1)S(1)}, u32[]{:S(2)}, u32[]{:S(2)}) collective-permute-start(bf16[768,1024]{1,0:T(8,128)(2,1)} %get-tuple-element.70), channel_id=1, source_target_pairs={{0,1},{1,0},{2,3},{3,2},{4,5},{5,4},{6,7},{7,6},{8,9},{9,8},{10,11... | collective-permute-start | bytes 4718600 | tf_op jit(solution)/shard_map/ppermute | solution.py:34
  213.6 1.3 copy-start.5
  214.8 3.1 copy-start.1
  219.8 53.5 %collective-permute-start.8 = (bf16[512,512]{1,0:T(8,128)(2,1)S(1)}, bf16[512,512]{1,0:T(8,128)(2,1)S(1)}, u32[]{:S(2)}, u32[]{:S(2)}) collective-permute-start(bf16[512,512]{1,0:T(8,128)(2,1)S(1)} %get-tuple-element.100), channel_id=1, source_target_pairs={{0,1},{1,0},{2,3},{3,2},{4,5},{5,4},{6,7},{7,6},{8,9},{9,8},{10,11... | collective-permute-start | bytes 1572872 | tf_op jit(solution)/shard_map/ppermute | solution.py:34
Sparse Core Ops, SparseCore 0:
  11.4 145.9 all-gather.1

commit v7 on v6

--- a/solution.py
+++ b/solution.py
@@ -172,8 +172,9 @@
 
 
 class Scatter:
-    def __init__(self, kinds, ins, outs, scratch, early=None):
+    def __init__(self, kinds, ins, outs, scratch, early=None, origins=None):
         count = len(kinds)
+        self.origins = origins or ins
         self.early = early
         if early is not None:
             self.plane, scratch = scratch[-1], scratch[:-1]
@@ -211,10 +212,13 @@
     def source(self, w, chip):
         return (self.plane, chip % 4) if w == self.early else (self.ins[w], chip)
 
+    def origin(self, w, chip):
+        return (self.plane, chip % 4) if w == self.early else (self.origins[w], chip)
+
     def along(self, w):
         for j in (1, 2, 3):
             layer = pl.multiple_of(self.own[j] // 4 * 4, 4)
-            self.send(w, 23 + j, self.ins[w].at[pl.ds(layer, 4)], self.recv_z[w].at[j - 1], self.peers_z[j - 1])
+            self.send(w, 23 + j, self.origins[w].at[pl.ds(layer, 4)], self.recv_z[w].at[j - 1], self.peers_z[j - 1])
 
     def layer_sum(self, w):
         for j in range(3):
@@ -233,15 +237,15 @@
             self.strips(w, body)
 
     def far(self, w, j):
-        ref, at = self.source(w, self.at_xy[j])
+        ref, at = self.origin(w, self.at_xy[j])
         block = ref.at[at]
         self.send(w, j, block.at[0], self.recv_a[w].at[j], self.peer_y)
         self.send(w, 4 + j, block.at[1], self.recv_b[w].at[j], self.peer_x)
 
     def near(self, w, j):
-        ref, at = self.source(w, self.at_x[j])
+        ref, at = self.origin(w, self.at_x[j])
         self.send(w, 8 + j, ref.at[at, 1], self.recv_x[w].at[j, 1], self.peer_x)
-        ref, at = self.source(w, self.at_y[j])
+        ref, at = self.origin(w, self.at_y[j])
         self.send(w, 12 + j, ref.at[at, 0], self.recv_y[w].at[j, 0], self.peer_y)
 
     def strips(self, w, body):
@@ -511,7 +515,7 @@
         attend_back_step(chunk, *refs)
         return
     inputs, (down_ref, norm_hbm, pre_hbm), (back_out, bias_out, down_out, up_out) = refs[:7], refs[7:10], refs[10:14]
-    buffers, (norm, pre, load_sem), scratch = refs[14:21], refs[21:24], refs[24:]
+    buffers, (norm, pre, up_buf, load_sem), scratch = refs[14:21], refs[21:25], refs[25:]
     scatter = Scatter(("rows",), (down_ref,), (down_out,), scratch)
     step = pl.program_id(0) * pl.num_programs(1) + pl.program_id(1)
     total = pl.num_programs(0) * pl.num_programs(1)
@@ -542,13 +546,17 @@
         pltpu.make_async_copy(norm_hbm, norm, load_sem.at[0]).wait()
         pltpu.make_async_copy(pre_hbm, pre, load_sem.at[1]).wait()
 
-        @pl.loop(0, norm.shape[1] // 256)
+        @pl.loop(0, norm.shape[1] // 512)
         def _(i):
-            part = pl.ds(pl.multiple_of(i * 256, 256), 256)
-            up_out[part] = product_left_t(norm[:, part], pre[...]).astype(BF)
+            part = pl.ds(pl.multiple_of(i * 512, 512), 512)
+            up_buf[part] = product_left_t(norm[:, part], pre[...]).astype(BF)
+            pltpu.make_async_copy(up_buf.at[part], up_out.at[part], load_sem.at[2 + i]).start()
 
         scatter.last(0)
         scatter.drain()
+        for i in range(norm.shape[1] // 512):
+            part = pl.ds(i * 512, 512)
+            pltpu.make_async_copy(up_buf.at[part], up_out.at[part], load_sem.at[2 + i]).wait()
 
     for place, work in ((0, start), (2, two), (4, four), (5, five), (6, six), (7, seven)):
         pl.when(step == place)(work)
@@ -638,10 +646,11 @@
         sums = scatter_shapes([grad_down.shape], ("rows",))
         in_specs += [pl.BlockSpec(grad_down.shape, lambda i, j: (0, 0, 0, 0), pipeline_mode=pl.Buffered(1))]
         in_specs += [pl.BlockSpec(memory_space=pl.ANY)] * 2
-        out_specs += [pl.BlockSpec(sums[0].shape, lambda i, j: (0, 0)), pl.BlockSpec(up_shape, lambda i, j: (0, 0))]
+        out_specs += [pl.BlockSpec(sums[0].shape, lambda i, j: (0, 0)), pl.BlockSpec(memory_space=pl.ANY)]
         out_shape += [sums[0], jax.ShapeDtypeStruct(up_shape, BF)]
         operands += [grad_down, norm_two, grad_pre]
-        scratch += [pltpu.VMEM(norm_two.shape, BF), pltpu.VMEM(grad_pre.shape, BF), pltpu.SemaphoreType.DMA((2,))]
+        scratch += [pltpu.VMEM(norm_two.shape, BF), pltpu.VMEM(grad_pre.shape, BF), pltpu.VMEM(up_shape, BF)]
+        scratch += [pltpu.SemaphoreType.DMA((2 + up_shape[0] // 512,))]
         scratch += scatter_scratch([grad_down.shape])
         params = pltpu.CompilerParams(vmem_limit_bytes=60 << 20, collective_id=2, has_side_effects=True)
     outs = pl.pallas_call(
@@ -965,13 +974,16 @@
 
 
 def tail_kernel(
-    kinds, up_ref, proj_ref, sums_ref, bias_ref, gain_ref, shift_ref,
+    kinds, sums_ref, bias_ref, gain_ref, shift_ref, up_hbm, proj_hbm,
     back_hbm, weight_hbm, norm_hbm, token_hbm, middle_hbm, down_hbm, act_hbm, sum_hbm,
     up_out, qkv_out, proj_out, packed_out, tokens_out, block_out, *refs
 ):
     back, weight, norm, token, middle, down, qkv, packed, vectors, stage, land, load_sem, pass_sem = refs[:13]
-    act, total, lift_stage, lift_land, block_sem = refs[13:18]
-    scatter = Scatter(kinds, (up_ref, qkv, proj_ref, packed), (up_out, qkv_out, proj_out, packed_out), refs[18:], 2)
+    act, total, lift_stage, lift_land, block_sem, up_ref, proj_ref = refs[13:20]
+    scatter = Scatter(
+        kinds, (up_ref, qkv, proj_ref, packed), (up_out, qkv_out, proj_out, packed_out), refs[20:], 2,
+        (up_hbm, qkv, proj_hbm, packed),
+    )
     chips, _, shard, triple = qkv.shape
     own_rows = token.shape[0]
     loads = [
@@ -979,15 +991,15 @@
         for i, (source, target) in enumerate(
             (
                 (back_hbm, back), (weight_hbm, weight), (norm_hbm, norm), (token_hbm, token), (middle_hbm, middle),
-                (down_hbm, down),
+                (down_hbm, down), (up_hbm, up_ref), (proj_hbm, proj_ref),
             )
         )
     ]
-    for load in loads:
-        load.start()
     scatter.meet()
     scatter.opening(0)
     scatter.along(2)
+    for place in (0, 1, 6, 2, 7, 3, 4, 5):
+        loads[place].start()
     vectors[...] = jnp.zeros_like(vectors)
     vectors[0:8] = sums_ref[...]
     loads[0].wait(), loads[1].wait()
@@ -1002,6 +1014,7 @@
         device_id=(scatter.mate,), device_id_type=MESH,
     )
     passing.start()
+    loads[6].wait(), loads[7].wait()
     scatter.relay(0, 1), scatter.far(0, 3), scatter.near(0, 2)
     loads[2].wait()
 
@@ -1098,21 +1111,22 @@
         functools.partial(tail_kernel, kinds),
         out_shape=scatter_shapes(shapes, kinds)
         + [jax.ShapeDtypeStruct((own_rows, features), F32), jax.ShapeDtypeStruct((own_rows, features), BF)],
-        in_specs=[vmem] * 6 + [pl.BlockSpec(memory_space=pl.ANY)] * 8,
+        in_specs=[vmem] * 4 + [pl.BlockSpec(memory_space=pl.ANY)] * 10,
         out_specs=[vmem] * 6,
         scratch_shapes=[
             pltpu.VMEM(back.shape, BF), pltpu.VMEM(weight.shape, BF), pltpu.VMEM(norm.shape, BF),
             pltpu.VMEM(tokens.shape, BF), pltpu.VMEM(middle.shape, F32), pltpu.VMEM(down.shape, BF),
             pltpu.VMEM(shapes[1], BF), pltpu.VMEM(shapes[3], BF), pltpu.VMEM((PARAM_COLS, features), F32),
             pltpu.VMEM((own_rows, features), BF), pltpu.VMEM((own_rows, features), BF),
-            pltpu.SemaphoreType.DMA((6,)), pltpu.SemaphoreType.DMA((4,)),
+            pltpu.SemaphoreType.DMA((8,)), pltpu.SemaphoreType.DMA((4,)),
             pltpu.VMEM((256, act.shape[1]), BF), pltpu.VMEM((256, features), F32),
             pltpu.VMEM((own_rows, features), BF), pltpu.VMEM((own_rows, features), BF), pltpu.SemaphoreType.DMA((2,)),
+            pltpu.VMEM(grad_up.shape, BF), pltpu.VMEM(grad_proj.shape, BF),
         ]
         + scatter_scratch(shapes, 2),
         compiler_params=pltpu.CompilerParams(collective_id=1, has_side_effects=True, vmem_limit_bytes=62 << 20),
         name="tail",
-    )(grad_up, grad_proj, sums, bias_rows, gain, shift, back, weight, norm, tokens, grad_middle, down, act, middle)
+    )(sums, bias_rows, gain, shift, grad_up, grad_proj, back, weight, norm, tokens, grad_middle, down, act, middle)
 
 
 def pack_kernel(up_ref, down_ref, out_ref):
@@ -1143,35 +1157,24 @@
 ):
     token_out[...] = token_ref[...]
     block_out[...] = block_ref[...]
-
-    @pl.when(pl.program_id(0) == 0)
-    def _():
-        up_out[...] = up_ref[...]
-        qkv_out[...] = qkv_ref[...]
-        proj_out[...] = proj_ref[...]
-        down_out[...] = down_ref[...]
-        shard = vec_out.shape[1]
-        vec_out[...] = packed_ref[:shard].T[:8]
-        bias_out[...] = packed_ref[shard : shard + 1]
+    up_out[...] = up_ref[...]
+    qkv_out[...] = qkv_ref[...]
+    proj_out[...] = proj_ref[...]
+    down_out[...] = down_ref[...]
+    shard = vec_out.shape[1]
+    vec_out[...] = packed_ref[:shard].T[:8]
+    bias_out[...] = packed_ref[shard : shard + 1]
 
 
 def finish(up, qkv, proj, down, tokens, block, packed, shard, unit):
     if lax.axis_size(AX) != 32:
         return up, qkv, proj, down, tokens, block, packed[:shard, :8].T, packed[shard : shard + 1, :unit]
-    size = tokens.shape[0] // 4
-    passed = [rows_spec(size, tokens.shape[1])] * 2
-
-    def kept(shape):
-        return pl.BlockSpec(shape, lambda i: (0, 0))
-
-    summed = [whole_spec(a.shape) for a in (up, qkv, proj, down)]
     return pl.pallas_call(
         finish_kernel,
-        grid=(4,),
         out_shape=[jax.ShapeDtypeStruct(a.shape, a.dtype) for a in (up, qkv, proj, down, tokens, block)]
         + [jax.ShapeDtypeStruct((8, shard), F32), jax.ShapeDtypeStruct((1, unit), F32)],
-        in_specs=summed + passed + [whole_spec(packed.shape)],
-        out_specs=[kept(a.shape) for a in (up, qkv, proj, down)] + passed + [kept((8, shard)), kept((1, unit))],
+        in_specs=[pl.BlockSpec(memory_space=pltpu.VMEM)] * 7,
+        out_specs=[pl.BlockSpec(memory_space=pltpu.VMEM)] * 8,
         compiler_params=PARAMS,
         name="finish",
     )(up, qkv, proj, down, tokens, block, packed)

time: 382 us -> 379 us (level)
  no operation moved by 1% of the time
where the time goes in v7:
time: 379 us; the launch traced here: 377 us
  Pallas kernels  317 us (84%)
  local copies, waits for them, and re-layouts  17.1 us (5%)
  waiting for transfers between devices  16 us (4%)
  between operations  14.4 us (4%)
  matrix products  5.83 us (2%)
  other arithmetic  3.82 us (1%)
    pallas_call x1, Pallas kernels, tail(): pl.pallas_call(functools.partial(tail_kernel, kinds), out_shape=scatter_s...  89.1 us
    pallas_call x1, Pallas kernels, gather_chips(): pl.pallas_call(gather_kernel, out_shape=[jax.ShapeDtypeStruct((chips, 2,...  67.5 us
    pallas_call x1, Pallas kernels, attend_back(): pl.pallas_call(functools.partial(attend_back_kernel, 256), grid=(clips, p...  50.4 us
    pallas_call x1, Pallas kernels, attend(): pl.pallas_call(functools.partial(attend_kernel, 256), grid=(clips, pairs)...  34.2 us
    pallas_call x1, Pallas kernels, feed(): pl.pallas_call(functools.partial(feed_kernel, steps, unit), grid=(2 * ste...  31.7 us
    all_gather x1, waiting for transfers between devices, per_device(): lax.all_gather(pack(up_weight, down_weight), AX, axis=0, tiled=True)  11.7 us
    pallas_call x1, Pallas kernels, project(): pl.pallas_call(functools.partial(project_kernel, steps), grid=(2 * steps,...  11.3 us
    pallas_call x1, Pallas kernels, outer(): pl.pallas_call(outer_kernel, grid=(columns // size,), in_specs=[pl.BlockS...  10.7 us
  transfers between devices with their start and end apart: 10, of which 3 were waited for; matrix products, arithmetic and copies ran while one was open for 4% of the time, Pallas kernels for 48%

profile of v7, /device:TPU:0, one launch (start us, length us, event | category | flops | bytes accessed | tf_op | source)
XLA Modules:
  0.0 376.7 jit_solution(4639181337832996036)
XLA Ops:
  7.2 0.0 all-gather.2.cloned.1.call-start
  7.2 1.9 pack.1
  9.1 0.0 all-gather.2.cloned.1.call-update
  9.1 0.6 collective-permute-start
  9.7 0.1 collective-permute-start.1
  9.7 0.8 stack.50
  10.5 0.1 copy.72
  10.6 0.7 dynamic_update_slice.3.packed_ref
  11.3 0.6 copy-done.9
  11.9 67.5 %gather_chips.1 = (bf16[16,2,32,1536]{3,2,1,0:T(8,128)(2,1)}, bf16[16,2,32,512]{3,2,1,0:T(8,128)(2,1)}, bf16[16,2,48,128]{3,2,1,0:T(8,128)(2,1)}) custom-call(bf16[32,3072]{1,0:T(8,128)(2,1)} %qkv_ref.1, bf16[32,1024]{1,0:T(8,128)(2,1)} %proj_ref.1, bf16[48,128]{1,0:T(8,128)(2,1)} %copy-done.9), custom_call_target="tpu_custom_call" | custom-call | flops 40000000000 | bytes 150000000 | tf_op jit(solution)/shard_map/gather_chips/pallas_call | solution.py:154
  79.4 0.0 copy-start.10
  79.4 1.3 dynamic-slice_bitcast_fusion.1
  80.8 0.1 collective-permute-start.2
  80.9 0.1 bitcast_convert_fusion
  80.9 0.2 copy.77
  81.1 0.6 fusion.2
  81.7 0.6 fusion.1.bias_ref
  82.4 0.0 collective-permute-done.1
  82.4 0.4 copy.74
  82.8 0.1 broadcast_select_fusion.penalty_ref.refs_3_
  82.9 0.3 maximum_select_fusion.weight_ref
  83.2 11.3 %project.1 = (bf16[1536,1024]{1,0:T(8,128)(2,1)}, bf16[1536,1536]{1,0:T(8,128)(2,1)}) custom-call(bf16[768,1024]{1,0:T(8,128)(2,1)} %bitcast.77, bf16[768,1024]{1,0:T(8,128)(2,1)} %collective-permute-done.other_ref, f32[1,1024]{1,0:T(1,128)} %get-tuple-element.110.gain_ref, f32[1,1024]{1,0:T(1,128)} %get-tuple-element.109.shift_ref, ...), custom_call_target="tpu_custom_call" | custom-call | tf_op jit(solution)/shard_map/project/pallas_call | solution.py:720
  94.5 34.2 %attend.1 = (bf16[2,2,384,512]{3,2,1,0:T(8,128)(2,1)S(1)}, f32[2,4,2,768]{3,2,1,0:T(2,128)S(1)}) custom-call(bf16[2,2,384,1536]{3,2,1,0:T(8,128)(2,1)} %bitcast.70, bf16[2,2,384,1536]{3,2,1,0:T(8,128)(2,1)} %bitcast.71, bf16[2,2,384,1536]{3,2,1,0:T(8,128)(2,1)} %bitcast.72, f32[2,2,384,1]{3,2,1,0:T(8,128)S(1)} %broadcast_select_fusion.penalty_ref.refs_3_), custom_call_target="tpu_custom_call" | custom-call | flops 2415919104 | bytes 6291456 | tf_op jit(solution)/shard_map/attend/pallas_call | solution.py:494
  128.7 0.0 copy-start
  128.7 0.0 copy-start.3
  128.7 0.1 slice.78
  128.8 1.0 convolution_convert_fusion.1
  129.8 0.1 copy-done
  129.9 0.5 collective-permute-start.3
  130.4 0.1 collective-permute-start.5
  130.4 3.0 collective-permute-done.3.recv_ref
  133.4 1.1 copy-done.7
  134.5 6.3 %second_norm.1 = (f32[768,1024]{1,0:T(8,128)}, bf16[768,1024]{1,0:T(8,128)(2,1)}) custom-call(bf16[1536,512]{1,0:T(8,128)(2,1)} %bitcast.68, bf16[512,1024]{1,0:T(8,128)(2,1)} %copy-done.4, bf16[768,1024]{1,0:T(8,128)(2,1)} %bitcast.78, bf16[768,1024]{1,0:T(8,128)(2,1)} %copy-done.7, f32[1,1024]{1,0:T(1,128)} %get-tuple-element.106.bias_ref, ...), custom_call_target="tpu_custom_call" | custom-call | tf_op jit(solution)/shard_map/second_norm/pallas_call | solution.py:755
  140.9 0.5 collective-permute-start.4
  141.3 0.8 slice.83
  142.2 0.6 bitcast_convert_fusion.1.bias_ref
  142.8 1.6 reshape.179.mark_ref
  144.4 1.4 collective-permute-done.4.other_ref
  145.8 11.7 %all-gather.2.cloned.1.call-done.refs_0_ = bf16[1024,8192]{1,0:T(8,128)(2,1)} async-done(((bf16[32,8192]{1,0:T(8,128)(2,1)}), bf16[1024,8192]{1,0:T(8,128)(2,1)}) %all-gather.2.cloned.1.call-update) | async-done | bytes 16777232 | tf_op jit(solution)/shard_map/all_gather | solution.py:1203
  157.4 31.7 %feed.1 = (bf16[1536,2048]{1,0:T(8,128)(2,1)}, bf16[1536,2048]{1,0:T(8,128)(2,1)}, bf16[1536,1024]{1,0:T(8,128)(2,1)}, bf16[1536,1024]{1,0:T(8,128)(2,1)}, f32[7...) custom-call(bf16[768,1024]{1,0:T(8,128)(2,1)} %get-tuple-element.63.own_ref, ...), custom_call_target="tpu_custom_call" | custom-call | flops 19327352832 | bytes 16777216 | tf_op jit(solution)/shard_map/feed/pallas_call | solution.py:854
  189.2 0.3 collective-permute-start.6
  189.5 10.7 %outer.1 = bf16[2048,1024]{1,0:T(8,128)(2,1)} custom-call(bf16[1536,2048]{1,0:T(8,128)(2,1)} %get-tuple-element.66.left_ref.act_hbm, bf16[1536,1024]{1,0:T(8,128)(2,1)} %get-tuple-element.67.right_ref.out_ref), custom_call_target="tpu_custom_call" | custom-call | flops 6442450944 | bytes 13631488 | tf_op jit(solution)/shard_map/outer/pallas_call | solution.py:891
  200.2 1.2 copy-done.6
  201.4 8.0 %second_back.1 = (f32[768,1024]{1,0:T(8,128)}, bf16[768,1024]{1,0:T(8,128)(2,1)}, f32[8,1024]{1,0:T(8,128)}) custom-call(f32[768,1024]{1,0:T(8,128)} %get-tuple-element.64.grad_ref, bf16[768,1024]{1,0:T(8,128)(2,1)} %copy-done.6, f32[768,1024]{1,0:T(8,128)} %get-tuple-element.69.middle_ref.sum_hbm, bf16[1536,1024]{1,0:T(8,128)(2,1)} %get-tuple-element.67.right_ref.out_ref, ...), custom_call_target="tpu_custom_call" | custom-call | tf_op jit(solution)/shard_map/second_back/pallas_call | solution.py:934
  209.4 0.3 collective-permute-start.7
  209.7 0.9 fusion
  210.6 0.7 pad.13.bias_ref
  211.3 0.8 slice.85
  212.1 1.5 constant_dynamic-update-slice_fusion.1
  213.6 0.0 copy-start.1
  213.6 0.9 fusion.3
  214.5 0.1 constant_dynamic-update-slice_fusion
  214.6 0.4 copy-done.1
  215.0 1.8 convolution_convert_fusion.2
  216.9 3.0 convolution_convert_fusion
  219.9 0.1 constant_dynamic-slice_fusion.1
  220.0 0.3 collective-permute-start.8
  220.3 50.4 %attend_back.1 = (bf16[2,2,384,1536]{3,2,1,0:T(8,128)(2,1)}, f32[2,4,2,128]{3,2,1,0:T(2,128)}, f32[128,1024]{1,0:T(8,128)}, bf16[1024,2048]{1,0:T(8,128)(2,1)}) custom-call(bf16[2,2,384,1536]{3,2,1,0:T(8,128)(2,1)} %bitcast.73, bf16[2,2,384,1536]{3,2,1,0:T(8,128)(2,1)} %bitcast.74, bf16[2,2,384,1536]{3,2,1,0:T(8,128)(2,1)} %bitcast.75, ...), custom_call_target="tpu_custom_call" | custom-call | flops 6039797760 | bytes 14155776 | tf_op jit(solution)/shard_map/attend_back/pallas_call | solution.py:656
  270.8 0.7 reduce_sum.9
  271.5 0.7 concatenate.46.sums_ref
  272.2 1.4 maximum_select_fusion.1
  273.6 89.1 %tail.1 = (f32[32,4096]{1,0:T(8,128)}, f32[32,3072]{1,0:T(8,128)}, f32[32,1024]{1,0:T(8,128)}, f32[48,128]{1,0:T(8,128)}, f32[768,1024]{1,0:T(8,128)}, /*index=5*/bf16[768,1024]{1,0:T(8,128)(2,1)}) custom-call(f32[8,1024]{1,0:T(8,128)} %concatenate.46.sums_ref, bf16[16,2,16,128]{3,2,1,0:T(8,128)(2,1)} %pad.13.bias_ref, ...), custom_call_target="tpu_custom_call" | custom-call | tf_op jit(solution)/shard_map/tail/pallas_call | solution.py:1110
  362.8 5.6 %finish.1 = (f32[32,4096]{1,0:T(8,128)}, f32[32,3072]{1,0:T(8,128)}, f32[32,1024]{1,0:T(8,128)}, f32[128,1024]{1,0:T(8,128)}, f32[768,1024]{1,0:T(8,128)}, /*ind...) custom-call(f32[32,4096]{1,0:T(8,128)} %get-tuple-element.84.up_ref, ...), custom_call_target="tpu_custom_call" | custom-call | tf_op jit(solution)/shard_map/finish/pallas_call | solution.py:1172
  368.3 1.5 slice_bitcast_fusion
  (34 shorter events, 0.1 us)
Async XLA Ops:
  7.2 150.2 %all-gather.2.cloned.1.call-start = ((), (), s32[]{:S(2)}) async-start(), calls=%async_computation | async-start | bytes 17301504 | tf_op jit(solution)/shard_map/all_gather | solution.py:1203
  9.1 74.1 %collective-permute-start = (bf16[768,1024]{1,0:T(8,128)(2,1)}, bf16[768,1024]{1,0:T(8,128)(2,1)}, u32[]{:S(2)}, u32[]{:S(2)}) collective-permute-start(bf16[768,1024]{1,0:T(8,128)(2,1)} %bitcast.76), channel_id=1, source_target_pairs={{0,1},{1,0},{2,3},{3,2},{4,5},{5,4},{6,7},{7,6},{8,9},{9,8},{10,11... | collective-permute-start | bytes 4718600 | tf_op jit(solution)/shard_map/ppermute | solution.py:34
  9.7 72.7 %collective-permute-start.1 = (s32[2,384]{1,0:T(2,128)}, s32[2,384]{1,0:T(2,128)S(1)}, u32[]{:S(2)}, u32[]{:S(2)}) collective-permute-start(s32[2,384]{1,0:T(2,128)} %param.17), channel_id=1, source_target_pairs={{0,1},{1,0},{2,3},{3,2},{4,5},{5,4},{6,7},{7,6},{8,9},{9,8},{10,11... | collective-permute-start | bytes 9224 | tf_op jit(solution)/shard_map/ppermute | solution.py:34
  11.3 0.6 copy-start.9
  79.4 1.5 copy-start.8
  79.4 3.0 copy-start.10
  80.8 2.1 collective-permute-start.2
  82.8 11.7 %copy-start.2 = (f32[2,2,384,1]{3,2,1,0:T(8,128)}, f32[2,2,384,1]{3,2,1,0:T(8,128)S(1)}, u32[]{:S(2)}) copy-start(f32[2,2,384,1]{3,2,1,0:T(8,128)S(1)} %broadcast_select_fusion.penalty_ref.refs_3_) | copy-start | bytes 18436
  83.2 45.6 %copy-start.4 = (bf16[512,1024]{1,0:T(8,128)(2,1)}, bf16[512,1024]{1,0:T(8,128)(2,1)S(1)}, u32[]{:S(2)}) copy-start(bf16[512,1024]{1,0:T(8,128)(2,1)S(1)} %maximum_select_fusion.weight_ref) | copy-start | bytes 3145732
  128.7 1.1 copy-start
  128.7 1.1 copy-start.3
  129.9 3.5 collective-permute-start.3
  130.4 14.0 %collective-permute-start.5 = (bf16[768,1024]{1,0:T(8,128)(2,1)}, bf16[768,1024]{1,0:T(8,128)(2,1)S(1)}, u32[]{:S(2)}, u32[]{:S(2)}) collective-permute-start(bf16[768,1024]{1,0:T(8,128)(2,1)} %bitcast.23.grad_own_ref), channel_id=1, source_target_pairs={{0,1},{1,0},{2,3},{3,2},{4,5},{5,4},{6,7},{7,6},{8,9},{9,8},{10,11... | collective-permute-start | bytes 4718600 | tf_op jit(solution)/shard_map/ppermute | solution.py:34
  133.4 1.1 copy-start.7
  140.9 4.9 %collective-permute-start.4 = (bf16[768,1024]{1,0:T(8,128)(2,1)}, bf16[768,1024]{1,0:T(8,128)(2,1)S(1)}, u32[]{:S(2)}, u32[]{:S(2)}) collective-permute-start(bf16[768,1024]{1,0:T(8,128)(2,1)} %get-tuple-element.63.own_ref), channel_id=1, source_target_pairs={{0,1},{1,0},{2,3},{3,2},{4,5},{5,4},{6,7},{7,6},{8,9},{9,8},{10,11... | collective-permute-start | bytes 4718600 | tf_op jit(solution)/shard_map/ppermute | solution.py:34
  144.4 13.0 %copy-start.11 = (bf16[768,1024]{1,0:T(8,128)(2,1)}, bf16[768,1024]{1,0:T(8,128)(2,1)S(1)}, u32[]{:S(2)}) copy-start(bf16[768,1024]{1,0:T(8,128)(2,1)S(1)} %collective-permute-done.5.grad_other_ref) | copy-start | bytes 4718596
  145.8 11.7 %copy-start.12 = (bf16[768,1024]{1,0:T(8,128)(2,1)}, bf16[768,1024]{1,0:T(8,128)(2,1)S(1)}, u32[]{:S(2)}) copy-start(bf16[768,1024]{1,0:T(8,128)(2,1)S(1)} %collective-permute-done.4.other_ref) | copy-start | bytes 4718596
  189.2 11.1 %collective-permute-start.6 = (bf16[768,1024]{1,0:T(8,128)(2,1)}, bf16[768,1024]{1,0:T(8,128)(2,1)S(1)}, u32[]{:S(2)}, u32[]{:S(2)}) collective-permute-start(bf16[768,1024]{1,0:T(8,128)(2,1)} %get-tuple-element.65), channel_id=1, source_target_pairs={{0,1},{1,0},{2,3},{3,2},{4,5},{5,4},{6,7},{7,6},{8,9},{9,8},{10,11... | collective-permute-start | bytes 4718600 | tf_op jit(solution)/shard_map/ppermute | solution.py:34
  200.2 1.2 copy-start.6
  209.4 5.1 %collective-permute-start.7 = (bf16[768,1024]{1,0:T(8,128)(2,1)}, bf16[768,1024]{1,0:T(8,128)(2,1)S(1)}, u32[]{:S(2)}, u32[]{:S(2)}) collective-permute-start(bf16[768,1024]{1,0:T(8,128)(2,1)} %get-tuple-element.70), channel_id=1, source_target_pairs={{0,1},{1,0},{2,3},{3,2},{4,5},{5,4},{6,7},{7,6},{8,9},{9,8},{10,11... | collective-permute-start | bytes 4718600 | tf_op jit(solution)/shard_map/ppermute | solution.py:34
  213.6 1.4 copy-start.1
  215.0 1.8 copy-start.5
  220.0 52.2 %collective-permute-start.8 = (bf16[512,512]{1,0:T(8,128)(2,1)S(1)}, bf16[512,512]{1,0:T(8,128)(2,1)S(1)}, u32[]{:S(2)}, u32[]{:S(2)}) collective-permute-start(bf16[512,512]{1,0:T(8,128)(2,1)S(1)} %get-tuple-element.100), channel_id=1, source_target_pairs={{0,1},{1,0},{2,3},{3,2},{4,5},{5,4},{6,7},{7,6},{8,9},{9,8},{10,11... | collective-permute-start | bytes 1572872 | tf_op jit(solution)/shard_map/ppermute | solution.py:34
Sparse Core Ops, SparseCore 0:
  11.4 145.9 all-gather.1

commit v8 on v7

--- a/solution.py
+++ b/solution.py
@@ -514,9 +514,14 @@
     if len(refs) == 16:
         attend_back_step(chunk, *refs)
         return
-    inputs, (down_ref, norm_hbm, pre_hbm), (back_out, bias_out, down_out, up_out) = refs[:7], refs[7:10], refs[10:14]
-    buffers, (norm, pre, up_buf, load_sem), scratch = refs[14:21], refs[21:25], refs[25:]
-    scatter = Scatter(("rows",), (down_ref,), (down_out,), scratch)
+    inputs, (down_hbm, norm_hbm, pre_hbm), (back_out, bias_out, down_out, up_out) = refs[:7], refs[7:10], refs[10:14]
+    buffers, (norm, pre, up_buf, down_ref, load_sem), scratch = refs[14:21], refs[21:26], refs[26:]
+    width = down_out.shape[1]
+    parts = pl.ds(0, width - width // 8), pl.ds(width - width // 8, width // 8)
+    scatter = Scatter(
+        ("rows", "rows"), [down_ref.at[:, :, :, part] for part in parts], [down_out.at[:, part] for part in parts],
+        scratch, 1, [down_hbm.at[:, :, :, part] for part in parts],
+    )
     step = pl.program_id(0) * pl.num_programs(1) + pl.program_id(1)
     total = pl.num_programs(0) * pl.num_programs(1)
 
@@ -525,8 +530,11 @@
         pltpu.make_async_copy(pre_hbm, pre, load_sem.at[1]).start()
         scatter.meet()
         scatter.opening(0)
+        scatter.along(1)
+        pltpu.make_async_copy(down_hbm, down_ref, load_sem.at[load_sem.shape[0] - 1]).start()
 
     def two():
+        pltpu.make_async_copy(down_hbm, down_ref, load_sem.at[load_sem.shape[0] - 1]).wait()
         scatter.relay(0, 1), scatter.far(0, 3), scatter.near(0, 2)
 
     def four():
@@ -534,6 +542,8 @@
 
     def five():
         scatter.relay(0, 3), scatter.near(0, 0)
+        scatter.layer_sum(1)
+        scatter.far(1, 0), scatter.near(1, 0)
 
     def six():
         scatter.cross(0, 2)
@@ -543,6 +553,7 @@
 
     def end():
         scatter.cross(0, 3)
+        scatter.relay(1, 0)
         pltpu.make_async_copy(norm_hbm, norm, load_sem.at[0]).wait()
         pltpu.make_async_copy(pre_hbm, pre, load_sem.at[1]).wait()
 
@@ -552,6 +563,7 @@
             up_buf[part] = product_left_t(norm[:, part], pre[...]).astype(BF)
             pltpu.make_async_copy(up_buf.at[part], up_out.at[part], load_sem.at[2 + i]).start()
 
+        scatter.last(1)
         scatter.last(0)
         scatter.drain()
         for i in range(norm.shape[1] // 512):
@@ -644,14 +656,16 @@
     if fused:
         up_shape = (norm_two.shape[1], grad_pre.shape[1])
         sums = scatter_shapes([grad_down.shape], ("rows",))
-        in_specs += [pl.BlockSpec(grad_down.shape, lambda i, j: (0, 0, 0, 0), pipeline_mode=pl.Buffered(1))]
-        in_specs += [pl.BlockSpec(memory_space=pl.ANY)] * 2
+        in_specs += [pl.BlockSpec(memory_space=pl.ANY)] * 3
         out_specs += [pl.BlockSpec(sums[0].shape, lambda i, j: (0, 0)), pl.BlockSpec(memory_space=pl.ANY)]
         out_shape += [sums[0], jax.ShapeDtypeStruct(up_shape, BF)]
         operands += [grad_down, norm_two, grad_pre]
         scratch += [pltpu.VMEM(norm_two.shape, BF), pltpu.VMEM(grad_pre.shape, BF), pltpu.VMEM(up_shape, BF)]
-        scratch += [pltpu.SemaphoreType.DMA((2 + up_shape[0] // 512,))]
-        scratch += scatter_scratch([grad_down.shape])
+        scratch += [pltpu.VMEM(grad_down.shape, BF), pltpu.SemaphoreType.DMA((3 + up_shape[0] // 512,))]
+        most = grad_down.shape[3] - grad_down.shape[3] // 8
+        scratch += scatter_scratch(
+            [grad_down.shape[:3] + (most,), grad_down.shape[:3] + (grad_down.shape[3] - most,)], 1
+        )
         params = pltpu.CompilerParams(vmem_limit_bytes=60 << 20, collective_id=2, has_side_effects=True)
     outs = pl.pallas_call(
         functools.partial(attend_back_kernel, 256),

time: 379 us -> 376 us (level)
  Pallas kernels: 317 us -> 313 us
where the time goes in v8:
time: 376 us; the launch traced here: 373 us
  Pallas kernels  313 us (83%)
  local copies, waits for them, and re-layouts  17.1 us (5%)
  waiting for transfers between devices  16 us (4%)
  between operations  14.4 us (4%)
  matrix products  5.83 us (2%)
  other arithmetic  3.82 us (1%)
    pallas_call x1, Pallas kernels, tail(): pl.pallas_call(functools.partial(tail_kernel, kinds), out_shape=scatter_s...  88.4 us
    pallas_call x1, Pallas kernels, gather_chips(): pl.pallas_call(gather_kernel, out_shape=[jax.ShapeDtypeStruct((chips, 2,...  67.5 us
    pallas_call x1, Pallas kernels, attend_back(): pl.pallas_call(functools.partial(attend_back_kernel, 256), grid=(clips, p...  47.7 us
    pallas_call x1, Pallas kernels, attend(): pl.pallas_call(functools.partial(attend_kernel, 256), grid=(clips, pairs)...  34.2 us
    pallas_call x1, Pallas kernels, feed(): pl.pallas_call(functools.partial(feed_kernel, steps, unit), grid=(2 * ste...  31.7 us
    all_gather x1, waiting for transfers between devices, per_device(): lax.all_gather(pack(up_weight, down_weight), AX, axis=0, tiled=True)  11.7 us
    pallas_call x1, Pallas kernels, project(): pl.pallas_call(functools.partial(project_kernel, steps), grid=(2 * steps,...  11.3 us
    pallas_call x1, Pallas kernels, outer(): pl.pallas_call(outer_kernel, grid=(columns // size,), in_specs=[pl.BlockS...  10.7 us
  transfers between devices with their start and end apart: 10, of which 3 were waited for; matrix products, arithmetic and copies ran while one was open for 4% of the time, Pallas kernels for 48%

profile of v8, /device:TPU:0, one launch (start us, length us, event | category | flops | bytes accessed | tf_op | source)
XLA Modules:
  0.0 373.2 jit_solution(14440752011325461928)
XLA Ops:
  7.2 0.0 all-gather.2.cloned.1.call-start
  7.2 1.9 pack.1
  9.1 0.0 all-gather.2.cloned.1.call-update
  9.1 0.6 collective-permute-start
  9.7 0.1 collective-permute-start.1
  9.7 0.8 stack.50
  10.5 0.1 copy.72
  10.6 0.7 dynamic_update_slice.3.packed_ref
  11.3 0.6 copy-done.9
  11.9 67.5 %gather_chips.1 = (bf16[16,2,32,1536]{3,2,1,0:T(8,128)(2,1)}, bf16[16,2,32,512]{3,2,1,0:T(8,128)(2,1)}, bf16[16,2,48,128]{3,2,1,0:T(8,128)(2,1)}) custom-call(bf16[32,3072]{1,0:T(8,128)(2,1)} %qkv_ref.1, bf16[32,1024]{1,0:T(8,128)(2,1)} %proj_ref.1, bf16[48,128]{1,0:T(8,128)(2,1)} %copy-done.9), custom_call_target="tpu_custom_call" | custom-call | flops 40000000000 | bytes 150000000 | tf_op jit(solution)/shard_map/gather_chips/pallas_call | solution.py:154
  79.4 0.0 copy-start.10
  79.4 1.3 dynamic-slice_bitcast_fusion.1
  80.8 0.1 collective-permute-start.2
  80.9 0.1 bitcast_convert_fusion
  80.9 0.2 copy.77
  81.1 0.6 fusion.2
  81.7 0.6 fusion.1.bias_ref
  82.4 0.0 collective-permute-done.1
  82.4 0.4 copy.74
  82.8 0.1 broadcast_select_fusion.penalty_ref.refs_3_
  82.9 0.3 maximum_select_fusion.weight_ref
  83.2 11.3 %project.1 = (bf16[1536,1024]{1,0:T(8,128)(2,1)}, bf16[1536,1536]{1,0:T(8,128)(2,1)}) custom-call(bf16[768,1024]{1,0:T(8,128)(2,1)} %bitcast.77, bf16[768,1024]{1,0:T(8,128)(2,1)} %collective-permute-done.other_ref, f32[1,1024]{1,0:T(1,128)} %get-tuple-element.110.gain_ref, f32[1,1024]{1,0:T(1,128)} %get-tuple-element.109.shift_ref, ...), custom_call_target="tpu_custom_call" | custom-call | tf_op jit(solution)/shard_map/project/pallas_call | solution.py:734
  94.5 34.2 %attend.1 = (bf16[2,2,384,512]{3,2,1,0:T(8,128)(2,1)S(1)}, f32[2,4,2,768]{3,2,1,0:T(2,128)S(1)}) custom-call(bf16[2,2,384,1536]{3,2,1,0:T(8,128)(2,1)} %bitcast.70, bf16[2,2,384,1536]{3,2,1,0:T(8,128)(2,1)} %bitcast.71, bf16[2,2,384,1536]{3,2,1,0:T(8,128)(2,1)} %bitcast.72, f32[2,2,384,1]{3,2,1,0:T(8,128)S(1)} %broadcast_select_fusion.penalty_ref.refs_3_), custom_call_target="tpu_custom_call" | custom-call | flops 2415919104 | bytes 6291456 | tf_op jit(solution)/shard_map/attend/pallas_call | solution.py:494
  128.7 0.0 copy-start
  128.7 0.0 copy-start.3
  128.7 0.1 slice.78
  128.8 1.0 convolution_convert_fusion.1
  129.8 0.1 copy-done
  129.9 0.5 collective-permute-start.3
  130.4 0.1 collective-permute-start.5
  130.4 3.0 collective-permute-done.3.recv_ref
  133.4 1.1 copy-done.7
  134.5 6.3 %second_norm.1 = (f32[768,1024]{1,0:T(8,128)}, bf16[768,1024]{1,0:T(8,128)(2,1)}) custom-call(bf16[1536,512]{1,0:T(8,128)(2,1)} %bitcast.68, bf16[512,1024]{1,0:T(8,128)(2,1)} %copy-done.4, bf16[768,1024]{1,0:T(8,128)(2,1)} %bitcast.78, bf16[768,1024]{1,0:T(8,128)(2,1)} %copy-done.7, f32[1,1024]{1,0:T(1,128)} %get-tuple-element.106.bias_ref, ...), custom_call_target="tpu_custom_call" | custom-call | tf_op jit(solution)/shard_map/second_norm/pallas_call | solution.py:769
  140.9 0.5 collective-permute-start.4
  141.3 0.8 slice.83
  142.2 0.6 bitcast_convert_fusion.1.bias_ref
  142.8 1.6 reshape.179.mark_ref
  144.4 1.4 collective-permute-done.4.other_ref
  145.8 11.7 %all-gather.2.cloned.1.call-done.refs_0_ = bf16[1024,8192]{1,0:T(8,128)(2,1)} async-done(((bf16[32,8192]{1,0:T(8,128)(2,1)}), bf16[1024,8192]{1,0:T(8,128)(2,1)}) %all-gather.2.cloned.1.call-update) | async-done | bytes 16777232 | tf_op jit(solution)/shard_map/all_gather | solution.py:1217
  157.4 31.7 %feed.1 = (bf16[1536,2048]{1,0:T(8,128)(2,1)}, bf16[1536,2048]{1,0:T(8,128)(2,1)}, bf16[1536,1024]{1,0:T(8,128)(2,1)}, bf16[1536,1024]{1,0:T(8,128)(2,1)}, f32[7...) custom-call(bf16[768,1024]{1,0:T(8,128)(2,1)} %get-tuple-element.63.own_ref, ...), custom_call_target="tpu_custom_call" | custom-call | flops 19327352832 | bytes 16777216 | tf_op jit(solution)/shard_map/feed/pallas_call | solution.py:868
  189.2 0.3 collective-permute-start.6
  189.5 10.7 %outer.1 = bf16[2048,1024]{1,0:T(8,128)(2,1)} custom-call(bf16[1536,2048]{1,0:T(8,128)(2,1)} %get-tuple-element.66.left_ref.act_hbm, bf16[1536,1024]{1,0:T(8,128)(2,1)} %get-tuple-element.67.right_ref.out_ref), custom_call_target="tpu_custom_call" | custom-call | flops 6442450944 | bytes 13631488 | tf_op jit(solution)/shard_map/outer/pallas_call | solution.py:905
  200.2 1.2 copy-done.6
  201.4 8.0 %second_back.1 = (f32[768,1024]{1,0:T(8,128)}, bf16[768,1024]{1,0:T(8,128)(2,1)}, f32[8,1024]{1,0:T(8,128)}) custom-call(f32[768,1024]{1,0:T(8,128)} %get-tuple-element.64.grad_ref, bf16[768,1024]{1,0:T(8,128)(2,1)} %copy-done.6, f32[768,1024]{1,0:T(8,128)} %get-tuple-element.69.middle_ref.sum_hbm, bf16[1536,1024]{1,0:T(8,128)(2,1)} %get-tuple-element.67.right_ref.out_ref, ...), custom_call_target="tpu_custom_call" | custom-call | tf_op jit(solution)/shard_map/second_back/pallas_call | solution.py:948
  209.4 0.3 collective-permute-start.7
  209.7 0.9 fusion
  210.6 0.7 pad.13.bias_ref
  211.3 0.8 slice.85
  212.1 1.5 constant_dynamic-update-slice_fusion.1
  213.6 0.0 copy-start.1
  213.6 0.9 fusion.3
  214.5 0.1 constant_dynamic-update-slice_fusion
  214.6 0.4 copy-done.1
  215.0 1.8 convolution_convert_fusion.2
  216.9 3.0 convolution_convert_fusion
  219.9 0.1 constant_dynamic-slice_fusion.1
  220.0 0.3 collective-permute-start.8
  220.3 47.7 %attend_back.1 = (bf16[2,2,384,1536]{3,2,1,0:T(8,128)(2,1)}, f32[2,4,2,128]{3,2,1,0:T(2,128)}, f32[128,1024]{1,0:T(8,128)}, bf16[1024,2048]{1,0:T(8,128)(2,1)}) custom-call(bf16[2,2,384,1536]{3,2,1,0:T(8,128)(2,1)} %bitcast.73, bf16[2,2,384,1536]{3,2,1,0:T(8,128)(2,1)} %bitcast.74, bf16[2,2,384,1536]{3,2,1,0:T(8,128)(2,1)} %bitcast.75, ...), custom_call_target="tpu_custom_call" | custom-call | flops 6039797760 | bytes 14155776 | tf_op jit(solution)/shard_map/attend_back/pallas_call | solution.py:670
  268.1 0.7 reduce_sum.9
  268.8 0.7 concatenate.46.sums_ref
  269.5 1.4 maximum_select_fusion.1
  270.9 88.4 %tail.1 = (f32[32,4096]{1,0:T(8,128)}, f32[32,3072]{1,0:T(8,128)}, f32[32,1024]{1,0:T(8,128)}, f32[48,128]{1,0:T(8,128)}, f32[768,1024]{1,0:T(8,128)}, /*index=5*/bf16[768,1024]{1,0:T(8,128)(2,1)}) custom-call(f32[8,1024]{1,0:T(8,128)} %concatenate.46.sums_ref, bf16[16,2,16,128]{3,2,1,0:T(8,128)(2,1)} %pad.13.bias_ref, ...), custom_call_target="tpu_custom_call" | custom-call | tf_op jit(solution)/shard_map/tail/pallas_call | solution.py:1124
  359.3 5.6 %finish.1 = (f32[32,4096]{1,0:T(8,128)}, f32[32,3072]{1,0:T(8,128)}, f32[32,1024]{1,0:T(8,128)}, f32[128,1024]{1,0:T(8,128)}, f32[768,1024]{1,0:T(8,128)}, /*ind...) custom-call(f32[32,4096]{1,0:T(8,128)} %get-tuple-element.84.up_ref, ...), custom_call_target="tpu_custom_call" | custom-call | tf_op jit(solution)/shard_map/finish/pallas_call | solution.py:1186
  364.9 1.5 slice_bitcast_fusion
  (34 shorter events, 0.1 us)
Async XLA Ops:
  7.2 150.2 %all-gather.2.cloned.1.call-start = ((), (), s32[]{:S(2)}) async-start(), calls=%async_computation | async-start | bytes 17301504 | tf_op jit(solution)/shard_map/all_gather | solution.py:1217
  9.1 74.1 %collective-permute-start = (bf16[768,1024]{1,0:T(8,128)(2,1)}, bf16[768,1024]{1,0:T(8,128)(2,1)}, u32[]{:S(2)}, u32[]{:S(2)}) collective-permute-start(bf16[768,1024]{1,0:T(8,128)(2,1)} %bitcast.76), channel_id=1, source_target_pairs={{0,1},{1,0},{2,3},{3,2},{4,5},{5,4},{6,7},{7,6},{8,9},{9,8},{10,11... | collective-permute-start | bytes 4718600 | tf_op jit(solution)/shard_map/ppermute | solution.py:34
  9.7 72.7 %collective-permute-start.1 = (s32[2,384]{1,0:T(2,128)}, s32[2,384]{1,0:T(2,128)S(1)}, u32[]{:S(2)}, u32[]{:S(2)}) collective-permute-start(s32[2,384]{1,0:T(2,128)} %param.17), channel_id=1, source_target_pairs={{0,1},{1,0},{2,3},{3,2},{4,5},{5,4},{6,7},{7,6},{8,9},{9,8},{10,11... | collective-permute-start | bytes 9224 | tf_op jit(solution)/shard_map/ppermute | solution.py:34
  11.3 0.6 copy-start.9
  79.4 1.5 copy-start.8
  79.4 3.0 copy-start.10
  80.8 2.1 collective-permute-start.2
  82.8 11.7 %copy-start.2 = (f32[2,2,384,1]{3,2,1,0:T(8,128)}, f32[2,2,384,1]{3,2,1,0:T(8,128)S(1)}, u32[]{:S(2)}) copy-start(f32[2,2,384,1]{3,2,1,0:T(8,128)S(1)} %broadcast_select_fusion.penalty_ref.refs_3_) | copy-start | bytes 18436
  83.2 45.6 %copy-start.4 = (bf16[512,1024]{1,0:T(8,128)(2,1)}, bf16[512,1024]{1,0:T(8,128)(2,1)S(1)}, u32[]{:S(2)}) copy-start(bf16[512,1024]{1,0:T(8,128)(2,1)S(1)} %maximum_select_fusion.weight_ref) | copy-start | bytes 3145732
  128.7 1.1 copy-start
  128.7 1.1 copy-start.3
  129.9 3.5 collective-permute-start.3
  130.4 14.0 %collective-permute-start.5 = (bf16[768,1024]{1,0:T(8,128)(2,1)}, bf16[768,1024]{1,0:T(8,128)(2,1)S(1)}, u32[]{:S(2)}, u32[]{:S(2)}) collective-permute-start(bf16[768,1024]{1,0:T(8,128)(2,1)} %bitcast.23.grad_own_ref), channel_id=1, source_target_pairs={{0,1},{1,0},{2,3},{3,2},{4,5},{5,4},{6,7},{7,6},{8,9},{9,8},{10,11... | collective-permute-start | bytes 4718600 | tf_op jit(solution)/shard_map/ppermute | solution.py:34
  133.4 1.1 copy-start.7
  140.9 4.9 %collective-permute-start.4 = (bf16[768,1024]{1,0:T(8,128)(2,1)}, bf16[768,1024]{1,0:T(8,128)(2,1)S(1)}, u32[]{:S(2)}, u32[]{:S(2)}) collective-permute-start(bf16[768,1024]{1,0:T(8,128)(2,1)} %get-tuple-element.63.own_ref), channel_id=1, source_target_pairs={{0,1},{1,0},{2,3},{3,2},{4,5},{5,4},{6,7},{7,6},{8,9},{9,8},{10,11... | collective-permute-start | bytes 4718600 | tf_op jit(solution)/shard_map/ppermute | solution.py:34
  144.4 13.0 %copy-start.11 = (bf16[768,1024]{1,0:T(8,128)(2,1)}, bf16[768,1024]{1,0:T(8,128)(2,1)S(1)}, u32[]{:S(2)}) copy-start(bf16[768,1024]{1,0:T(8,128)(2,1)S(1)} %collective-permute-done.5.grad_other_ref) | copy-start | bytes 4718596
  145.8 11.7 %copy-start.12 = (bf16[768,1024]{1,0:T(8,128)(2,1)}, bf16[768,1024]{1,0:T(8,128)(2,1)S(1)}, u32[]{:S(2)}) copy-start(bf16[768,1024]{1,0:T(8,128)(2,1)S(1)} %collective-permute-done.4.other_ref) | copy-start | bytes 4718596
  189.2 11.1 %collective-permute-start.6 = (bf16[768,1024]{1,0:T(8,128)(2,1)}, bf16[768,1024]{1,0:T(8,128)(2,1)S(1)}, u32[]{:S(2)}, u32[]{:S(2)}) collective-permute-start(bf16[768,1024]{1,0:T(8,128)(2,1)} %get-tuple-element.65), channel_id=1, source_target_pairs={{0,1},{1,0},{2,3},{3,2},{4,5},{5,4},{6,7},{7,6},{8,9},{9,8},{10,11... | collective-permute-start | bytes 4718600 | tf_op jit(solution)/shard_map/ppermute | solution.py:34
  200.2 1.2 copy-start.6
  209.4 5.1 %collective-permute-start.7 = (bf16[768,1024]{1,0:T(8,128)(2,1)}, bf16[768,1024]{1,0:T(8,128)(2,1)S(1)}, u32[]{:S(2)}, u32[]{:S(2)}) collective-permute-start(bf16[768,1024]{1,0:T(8,128)(2,1)} %get-tuple-element.70), channel_id=1, source_target_pairs={{0,1},{1,0},{2,3},{3,2},{4,5},{5,4},{6,7},{7,6},{8,9},{9,8},{10,11... | collective-permute-start | bytes 4718600 | tf_op jit(solution)/shard_map/ppermute | solution.py:34
  213.6 1.4 copy-start.1
  215.0 1.8 copy-start.5
  220.0 49.4 %collective-permute-start.8 = (bf16[512,512]{1,0:T(8,128)(2,1)S(1)}, bf16[512,512]{1,0:T(8,128)(2,1)S(1)}, u32[]{:S(2)}, u32[]{:S(2)}) collective-permute-start(bf16[512,512]{1,0:T(8,128)(2,1)S(1)} %get-tuple-element.100), channel_id=1, source_target_pairs={{0,1},{1,0},{2,3},{3,2},{4,5},{5,4},{6,7},{7,6},{8,9},{9,8},{10,11... | collective-permute-start | bytes 1572872 | tf_op jit(solution)/shard_map/ppermute | solution.py:34
Sparse Core Ops, SparseCore 0:
  11.4 145.9 all-gather.1
